TPU v7x, 32 devices: a whole 2x2x4 slice. The times are simulated.
32 devices in a mesh: seg: 8 (over z, x), seq: 4 (over y, core).
Axes of the slice: x: 2, y: 2, z: 4, core: 2. Of those that a mesh axis runs over, the one named last changes fastest.
Arguments:
- tokens: bfloat16 [8, 1024, 2048], P('seg', 'seq'), may hold values from -6 to 6
- norm_gain: bfloat16 [2048], P(('seg', 'seq')), may hold values from 0.5 to 1.5
- in_proj: bfloat16 [2048, 8192], P(('seg', 'seq')), may hold values from -0.125 to 0.125
- conv_weight: bfloat16 [4, 4096], P(None, ('seg', 'seq')), may hold values from -3 to 3
- conv_bias: bfloat16 [4096], P(('seg', 'seq')), may hold values from -3 to 3
- x_proj: bfloat16 [4096, 160], P(('seg', 'seq')), may hold values from -0.09375 to 0.09375
- dt_proj: bfloat16 [128, 4096], P(None, ('seg', 'seq')), may hold values from -0.5 to 0.5
- dt_bias: bfloat16 [4096], P(('seg', 'seq')), may hold values from -16 to 0
- a_log: bfloat16 [16, 4096], P(None, ('seg', 'seq')), may hold values from 0 to 2.765625
- d_skip: bfloat16 [4096], P(('seg', 'seq')), may hold values from 0.5 to 1.5
- out_proj: bfloat16 [4096, 2048], P(('seg', 'seq')), may hold values from -0.375 to 0.375
- init_state: float32 [8, 16, 4096], P('seg'), may hold values from -6 to 6
- init_conv: float32 [8, 3, 4096], P('seg'), may hold values from -6 to 6
- cotangent: bfloat16 [8, 1024, 2048], P('seg', 'seq'), may hold values from -6 to 6
Outputs:
- mixed: bfloat16 [8, 1024, 2048], P('seg', 'seq')
- final_state: float32 [8, 16, 4096], P('seg', None, 'seq')
- final_conv: float32 [8, 3, 4096], P('seg', None, 'seq')
- input_grad: bfloat16 [8, 1024, 2048], P('seg', 'seq')
- init_state_grad: float32 [8, 16, 4096], P('seg', None, 'seq')
- init_conv_grad: float32 [8, 3, 4096], P('seg', None, 'seq')
- gain_grad: float32 [2048], P(('seg', 'seq'))
- in_proj_grad: float32 [2048, 8192], P(('seg', 'seq'))
- conv_weight_grad: float32 [4, 4096], P(None, ('seg', 'seq'))
- conv_bias_grad: float32 [4096], P(('seg', 'seq'))
- x_proj_grad: float32 [4096, 160], P(('seg', 'seq'))
- dt_proj_grad: float32 [128, 4096], P(None, ('seg', 'seq'))
- dt_bias_grad: float32 [4096], P(('seg', 'seq'))
- a_log_grad: float32 [16, 4096], P(None, ('seg', 'seq'))
- d_skip_grad: float32 [4096], P(('seg', 'seq'))
- out_proj_grad: float32 [4096, 2048], P(('seg', 'seq'))
All inputs are finite; a program needn't handle non-finite values.
Results may differ from a plain program's by a relative error of at most 0.0095.
Values may be sent and summed in bfloat16 or wider, within the bound.
A program may use at most 320 MiB of HBM per device.

v0:
```python
import math

import jax
import jax.numpy as jnp
from jax import lax
from jax.sharding import PartitionSpec as P

EPSILON = 1e-05


def shifted(value, axis, steps):
    count = lax.axis_size(axis)
    first, last = (max(0, -steps), min(count, count - steps))
    return lax.ppermute(value, axis, [(source, source + steps) for source in range(first, last)])


def prefix(shard, axis, combine, identity, reverse):
    devices, position = (lax.axis_size(axis), lax.axis_index(axis))
    everything = jax.tree.map(
        lambda part, kind: lax.all_gather(part.astype(kind), axis),
        shard,
        (jnp.bfloat16, jnp.bfloat16),
    )
    start = jax.tree.map(
        lambda part, zero: jnp.broadcast_to(jnp.asarray(zero, part.dtype), part.shape),
        shard,
        identity,
    )

    def step(k, before):
        at = devices - 1 - k if reverse else k
        reached = at > position if reverse else at < position
        new = combine(
            before, jax.tree.map(lambda part, own: part[at].astype(own.dtype), everything, shard)
        )
        return jax.tree.map(lambda a, b: jnp.where(reached, a, b), new, before)

    return lax.fori_loop(0, devices, step, start)


def shortened(shard):
    return jax.tree.map(lambda a: a.astype(jnp.bfloat16) if a.dtype == jnp.float32 else a, shard)


def broadcast(block, axis, owner):
    block = jnp.where(lax.axis_index(axis) == owner, block, jnp.zeros_like(block))
    return lax.psum(block, axis)


def compose(earlier_pair, later_pair):
    return (later_pair[0] * earlier_pair[0], later_pair[0] * earlier_pair[1] + later_pair[1])


def contract_rows(first_op, second_op):
    return lax.dot_general(
        first_op, second_op, (((0,), (0,)), ((), ())), preferred_element_type=jnp.float32
    )


def contract_cols(first_op, second_op):
    return lax.dot_general(
        first_op, second_op, (((1,), (1,)), ((), ())), preferred_element_type=jnp.float32
    )


def blocked(values_in, block_len):
    return values_in.reshape((values_in.shape[0] // block_len, block_len) + values_in.shape[1:])


def own_part(values_in, seq_place, parts):
    part_width = values_in.shape[-1] // parts
    return lax.dynamic_slice_in_dim(
        values_in, seq_place * part_width, part_width, values_in.ndim - 1
    )


def forward_scan(start_state, rate_rows, value_rows, b_rows, c_rows, a_mat, block_len):

    def advance(carry_state, block_items):
        rate_b, value_b, b_blk, c_blk = block_items
        first_state = carry_state
        drive_rows = rate_b * value_b
        outputs = []
        for i in range(block_len):
            carry_state = (
                jnp.exp(rate_b[i][None, :] * a_mat) * carry_state
                + b_blk[i][:, None] * drive_rows[i][None, :]
            )
            outputs.append(jnp.sum(c_blk[i][:, None] * carry_state, axis=0))
        return (carry_state, (jnp.stack(outputs), first_state))

    block_items = (
        blocked(rate_rows, block_len),
        blocked(value_rows, block_len),
        blocked(b_rows, block_len),
        blocked(c_rows, block_len),
    )
    end_state, (outputs, block_starts) = lax.scan(advance, start_state, block_items)
    return (end_state, outputs.reshape(rate_rows.shape), block_starts)


def backward_scan(
    grad_end,
    rate_rows,
    value_rows,
    b_rows,
    c_rows,
    a_mat,
    g_rows,
    block_starts,
    block_len,
    complete,
):

    def retreat(grad_carry, block_items):
        rate_b, value_b, b_blk, c_blk, g_blk, first_state = block_items
        decays = [jnp.exp(rate_b[i][None, :] * a_mat) for i in range(block_len)]
        if not complete:
            for i in reversed(range(block_len)):
                grad_carry = decays[i] * (c_blk[i][:, None] * g_blk[i][None, :] + grad_carry)
            return (grad_carry, None)
        drive_rows = rate_b * value_b
        state_list = [first_state]
        for i in range(block_len):
            state_list.append(
                decays[i] * state_list[-1] + b_blk[i][:, None] * drive_rows[i][None, :]
            )
        g_rate = [None] * block_len
        g_value = [None] * block_len
        g_brow = [None] * block_len
        g_crow = [None] * block_len
        g_amat = jnp.zeros_like(a_mat)
        for i in reversed(range(block_len)):
            multiplier = c_blk[i][:, None] * g_blk[i][None, :] + grad_carry
            weighted = multiplier * state_list[i] * decays[i]
            through_b = jnp.sum(multiplier * b_blk[i][:, None], axis=0)
            g_rate[i] = jnp.sum(weighted * a_mat, axis=0) + value_b[i] * through_b
            g_value[i] = rate_b[i] * through_b
            g_amat = g_amat + weighted * rate_b[i][None, :]
            g_brow[i] = jnp.sum(multiplier * drive_rows[i][None, :], axis=1)
            g_crow[i] = jnp.sum(state_list[i + 1] * g_blk[i][None, :], axis=1)
            grad_carry = decays[i] * multiplier
        return (
            grad_carry,
            (jnp.stack(g_rate), jnp.stack(g_value), g_amat, jnp.stack(g_brow), jnp.stack(g_crow)),
        )

    block_items = (
        blocked(rate_rows, block_len),
        blocked(value_rows, block_len),
        blocked(b_rows, block_len),
        blocked(c_rows, block_len),
        blocked(g_rows, block_len),
        block_starts,
    )
    grad_start, results = lax.scan(retreat, grad_end, block_items, reverse=True)
    if not complete:
        return (grad_start, None)
    g_rate, g_value, g_amat, g_brow, g_crow = results
    return (
        grad_start,
        (
            g_rate.reshape(rate_rows.shape),
            g_value.reshape(rate_rows.shape),
            jnp.sum(g_amat, axis=0),
            g_brow.reshape(b_rows.shape),
            g_crow.reshape(c_rows.shape),
        ),
    )


def body(
    tokens,
    norm_gain,
    in_proj,
    conv_weight,
    conv_bias,
    x_proj,
    dt_proj,
    dt_bias,
    a_log,
    d_skip,
    out_proj,
    init_state,
    init_conv,
    cotangent,
):
    seq_count = lax.axis_size("seq")
    seq_place = lax.axis_index("seq")
    gathered = (
        lax.all_gather(norm_gain, ("seg", "seq"), axis=0, tiled=True),
        lax.all_gather(in_proj, ("seg", "seq"), axis=0, tiled=True),
        lax.all_gather(conv_weight, ("seg", "seq"), axis=1, tiled=True),
        lax.all_gather(conv_bias, ("seg", "seq"), axis=0, tiled=True),
        lax.all_gather(x_proj, ("seg", "seq"), axis=0, tiled=True),
        lax.all_gather(dt_proj, ("seg", "seq"), axis=1, tiled=True),
        lax.all_gather(dt_bias, ("seg", "seq"), axis=0, tiled=True),
        lax.all_gather(a_log, ("seg", "seq"), axis=1, tiled=True),
        lax.all_gather(d_skip, ("seg", "seq"), axis=0, tiled=True),
        lax.all_gather(out_proj, ("seg", "seq"), axis=0, tiled=True),
    )
    gain_vec, w_in, w_conv, b_conv, w_x, w_dt, b_dt, log_a, skip_vec, w_out = gathered
    row_count = tokens.shape[1]
    history = init_conv.shape[1]
    block_len = math.gcd(row_count, 32)
    inputs = tokens[0].astype(jnp.float32)
    rstd_col = lax.rsqrt(jnp.mean(inputs * inputs, axis=1, keepdims=True) + EPSILON)
    normed = (inputs * rstd_col * gain_vec.astype(jnp.float32)).astype(jnp.bfloat16)
    projected = jnp.dot(normed, w_in, preferred_element_type=jnp.float32)
    inner_width = projected.shape[1] // 2
    x_in = projected[:, :inner_width]
    gate_in = projected[:, inner_width:]
    previous = shifted(x_in[row_count - history :].astype(jnp.bfloat16), "seq", 1).astype(
        jnp.float32
    )
    previous = jnp.where(seq_place == 0, init_conv[0], previous)
    padded = jnp.concatenate([previous, x_in], axis=0)
    kernel = w_conv.astype(jnp.float32)
    tap_count = kernel.shape[0]
    conv_out = b_conv.astype(jnp.float32) + sum(
        (kernel[k] * padded[k : k + row_count] for k in range(tap_count))
    )
    activated = jax.nn.silu(conv_out).astype(jnp.bfloat16)
    act_float = activated.astype(jnp.float32)
    mixed_x = jnp.dot(activated, w_x, preferred_element_type=jnp.float32)
    low_rank = w_dt.shape[0]
    state_width = log_a.shape[0]
    dt_low = mixed_x[:, :low_rank].astype(jnp.bfloat16)
    b_mat = mixed_x[:, low_rank : low_rank + state_width]
    c_mat = mixed_x[:, low_rank + state_width :]
    dt_pre = jnp.dot(dt_low, w_dt, preferred_element_type=jnp.float32) + b_dt.astype(jnp.float32)
    rate_rows = jax.nn.softplus(dt_pre)
    a_mat = -jnp.exp(log_a.astype(jnp.float32))
    decay_total = jnp.exp(a_mat * jnp.sum(rate_rows, axis=0)[None, :])
    zero_state = jnp.zeros_like(a_mat)
    ones_state = jnp.ones_like(a_mat)
    local_end, _, _ = forward_scan(zero_state, rate_rows, act_float, b_mat, c_mat, a_mat, block_len)
    prior_pair = prefix((decay_total, local_end), "seq", compose, (ones_state, zero_state), False)
    start_state = prior_pair[1] + prior_pair[0] * init_state[0]
    end_state, scanned, block_starts = forward_scan(
        start_state, rate_rows, act_float, b_mat, c_mat, a_mat, block_len
    )
    y_val = scanned + skip_vec.astype(jnp.float32) * act_float
    gate_act = jax.nn.silu(gate_in)
    gated = (y_val * gate_act).astype(jnp.bfloat16)
    mixed_out = (jnp.dot(gated, w_out, preferred_element_type=jnp.float32) + inputs).astype(
        jnp.bfloat16
    )
    final_h, final_c = (
        broadcast(shortened(end_state), "seq", seq_count - 1).astype(end_state.dtype),
        broadcast(x_in[row_count - history :].astype(jnp.bfloat16), "seq", seq_count - 1).astype(
            jnp.float32
        ),
    )
    again = (
        lax.all_gather(norm_gain, ("seg", "seq"), axis=0, tiled=True),
        lax.all_gather(in_proj, ("seg", "seq"), axis=0, tiled=True),
        lax.all_gather(conv_weight, ("seg", "seq"), axis=1, tiled=True),
        lax.all_gather(conv_bias, ("seg", "seq"), axis=0, tiled=True),
        lax.all_gather(x_proj, ("seg", "seq"), axis=0, tiled=True),
        lax.all_gather(dt_proj, ("seg", "seq"), axis=1, tiled=True),
        lax.all_gather(dt_bias, ("seg", "seq"), axis=0, tiled=True),
        lax.all_gather(a_log, ("seg", "seq"), axis=1, tiled=True),
        lax.all_gather(d_skip, ("seg", "seq"), axis=0, tiled=True),
        lax.all_gather(out_proj, ("seg", "seq"), axis=0, tiled=True),
    )
    back_gain = again[0].astype(jnp.float32)
    back_w_in = again[1]
    back_kernel = again[2].astype(jnp.float32)
    back_w_x = again[4]
    back_w_dt = again[5]
    back_skip = again[8].astype(jnp.float32)
    back_w_out = again[9]
    g_out = cotangent[0]
    out_grad = contract_rows(gated, g_out)
    g_gated = contract_cols(g_out, back_w_out)
    sig_gate = jax.nn.sigmoid(gate_in)
    g_y = g_gated * gate_act
    g_gate = g_gated * y_val * sig_gate * (1.0 + gate_in * (1.0 - sig_gate))
    skip_grad = jnp.sum(g_y * act_float, axis=0)
    local_grad, _ = backward_scan(
        zero_state, rate_rows, act_float, b_mat, c_mat, a_mat, g_y, block_starts, block_len, False
    )
    later_pair = prefix((decay_total, local_grad), "seq", compose, (ones_state, zero_state), True)
    start_grad, scan_grads = backward_scan(
        later_pair[1], rate_rows, act_float, b_mat, c_mat, a_mat, g_y, block_starts, block_len, True
    )
    g_rate, g_value, g_amat, g_brow, g_crow = scan_grads
    a_grad = g_amat * a_mat
    g_dtpre = (g_rate * jax.nn.sigmoid(dt_pre)).astype(jnp.bfloat16)
    dtb_grad = jnp.sum(g_dtpre.astype(jnp.float32), axis=0)
    dtp_grad = contract_rows(dt_low, g_dtpre)
    g_dtlow = contract_cols(g_dtpre, back_w_dt)
    g_mixed = jnp.concatenate([g_dtlow, g_brow, g_crow], axis=1).astype(jnp.bfloat16)
    xp_grad = contract_rows(activated, g_mixed)
    g_act = g_y * back_skip + g_value + contract_cols(g_mixed, back_w_x)
    sig_conv = jax.nn.sigmoid(conv_out)
    g_conv = g_act * sig_conv * (1.0 + conv_out * (1.0 - sig_conv))
    cb_grad = jnp.sum(g_conv, axis=0)
    cw_grad = jnp.stack(
        [jnp.sum(g_conv * padded[k : k + row_count], axis=0) for k in range(tap_count)]
    )
    g_padded = sum(
        (
            jnp.pad(back_kernel[k] * g_conv, ((k, tap_count - 1 - k), (0, 0)))
            for k in range(tap_count)
        )
    )
    head_grad = g_padded[:history]
    next_head = shifted(shortened(head_grad), "seq", -1).astype(head_grad.dtype)
    g_xin = g_padded[history:] + jnp.pad(next_head, ((row_count - history, 0), (0, 0)))
    g_proj = jnp.concatenate([g_xin, g_gate], axis=1).astype(jnp.bfloat16)
    inp_grad = contract_rows(normed, g_proj)
    g_normed = contract_cols(g_proj, back_w_in)
    gain_grad = jnp.sum(g_normed * inputs * rstd_col, axis=0)
    scaled = g_normed * back_gain
    input_grad = (
        g_out.astype(jnp.float32)
        + rstd_col * scaled
        - inputs
        * (rstd_col * rstd_col * rstd_col)
        * jnp.mean(scaled * inputs, axis=1, keepdims=True)
    ).astype(jnp.bfloat16)
    init_h_grad, init_c_grad = (
        broadcast(shortened(start_grad), "seq", 0).astype(start_grad.dtype),
        broadcast(shortened(head_grad), "seq", 0).astype(head_grad.dtype),
    )
    grad_shards = (
        lax.psum_scatter(gain_grad, ("seg", "seq"), scatter_dimension=0, tiled=True),
        lax.psum_scatter(inp_grad, ("seg", "seq"), scatter_dimension=0, tiled=True),
        lax.psum_scatter(cw_grad, ("seg", "seq"), scatter_dimension=1, tiled=True),
        lax.psum_scatter(cb_grad, ("seg", "seq"), scatter_dimension=0, tiled=True),
        lax.psum_scatter(xp_grad, ("seg", "seq"), scatter_dimension=0, tiled=True),
        lax.psum_scatter(dtp_grad, ("seg", "seq"), scatter_dimension=1, tiled=True),
        lax.psum_scatter(dtb_grad, ("seg", "seq"), scatter_dimension=0, tiled=True),
        lax.psum_scatter(a_grad, ("seg", "seq"), scatter_dimension=1, tiled=True),
        lax.psum_scatter(skip_grad, ("seg", "seq"), scatter_dimension=0, tiled=True),
        lax.psum_scatter(out_grad, ("seg", "seq"), scatter_dimension=0, tiled=True),
    )
    return (
        mixed_out[None],
        own_part(final_h, seq_place, seq_count)[None],
        own_part(final_c, seq_place, seq_count)[None],
        input_grad[None],
        own_part(init_h_grad, seq_place, seq_count)[None],
        own_part(init_c_grad, seq_place, seq_count)[None],
        grad_shards[0],
        grad_shards[1],
        grad_shards[2],
        grad_shards[3],
        grad_shards[4],
        grad_shards[5],
        grad_shards[6],
        grad_shards[7],
        grad_shards[8],
        grad_shards[9],
    )


def solution(mesh):
    placed = (
        P("seg", "seq", None),
        P(("seg", "seq")),
        P(("seg", "seq"), None),
        P(None, ("seg", "seq")),
        P(("seg", "seq")),
        P(("seg", "seq"), None),
        P(None, ("seg", "seq")),
        P(("seg", "seq")),
        P(None, ("seg", "seq")),
        P(("seg", "seq")),
        P(("seg", "seq"), None),
        P("seg", None, None),
        P("seg", None, None),
        P("seg", "seq", None),
    )
    return jax.shard_map(
        body,
        mesh=mesh,
        in_specs=placed,
        out_specs=(
            P("seg", "seq", None),
            P("seg", None, "seq"),
            P("seg", None, "seq"),
            P("seg", "seq", None),
            P("seg", None, "seq"),
            P("seg", None, "seq"),
            P(("seg", "seq")),
            P(("seg", "seq"), None),
            P(None, ("seg", "seq")),
            P(("seg", "seq")),
            P(("seg", "seq"), None),
            P(None, ("seg", "seq")),
            P(("seg", "seq")),
            P(None, ("seg", "seq")),
            P(("seg", "seq")),
            P(("seg", "seq"), None),
        ),
        check_vma=False,
    )
```

profile of v0, /device:TPU:1, one launch (start us, length us, event | category | flops | bytes accessed | tf_op | source)
XLA Modules:
  0.0 2799.0 jit_solution(18270522138560760385)
XLA Ops:
  10.9 43.6 %all-reduce.5 = bf16[2048]{0:T(1024)(128)(2,1)S(1)} all-reduce(bf16[2048]{0:T(1024)(128)(2,1)S(1)} %dynamic-update-slice), channel_id=1, replica_groups=mesh['seg'=8,'seq'=4] {'seg','seq'}, use_global_device_ids=true, to_apply=%add.5 | all-reduce | flops 2048 | bytes 8192
  57.0 43.0 %all_gather.59 = bf16[4,4096]{1,0:T(4,128)(2,1)S(1)} all-gather(bf16[4,128]{1,0:T(4,128)(2,1)} %param.29), channel_id=1, replica_groups=mesh['seg'=8,'seq'=4] {'seg','seq'}, dimensions={1}, use_global_device_ids=true | all-gather | bytes 33792 | tf_op jit(solution)/shard_map/all_gather | solution.py:193
  100.1 108.7 %all-gather.11.cloned.1.call-done = bf16[2048,8192]{1,0:T(8,128)(2,1)} async-done(((bf16[64,8192]{1,0:T(8,128)(2,1)}), bf16[2048,8192]{1,0:T(8,128)(2,1)}) %all-gather.11.cloned.1.call-update) | async-done | bytes 33554448 | tf_op jit(solution)/shard_map/all_gather | solution.py:192
  208.8 17.9 fusion.369
  228.2 3.2 collective-permute-start
  231.4 38.9 %all_gather.57 = bf16[16,4096]{1,0:T(8,128)(2,1)S(1)} all-gather(bf16[16,128]{1,0:T(8,128)(2,1)S(1)} %copy-done.36), channel_id=1, replica_groups=mesh['seg'=8,'seq'=4] {'seg','seq'}, dimensions={1}, use_global_device_ids=true | all-gather | bytes 135168 | tf_op jit(solution)/shard_map/all_gather | solution.py:198
  270.3 38.1 %all-gather.3 = bf16[32,1,128]{2,1,0:T(2,128)(2,1)S(1)} all-gather(bf16[1,1,128]{2,1,0:T(2,128)(2,1)S(1)} %bitcast.2914), channel_id=1, replica_groups=mesh['seg'=8,'seq'=4] {'seg','seq'}, dimensions={0}, use_global_device_ids=true | all-gather | bytes 8448 | tf_op jit(solution)/shard_map/all_gather | solution.py:194
  308.4 38.3 %all-gather.5 = bf16[32,1,128]{2,1,0:T(2,128)(2,1)S(1)} all-gather(bf16[1,1,128]{2,1,0:T(2,128)(2,1)S(1)} %bitcast.2915), channel_id=1, replica_groups=mesh['seg'=8,'seq'=4] {'seg','seq'}, dimensions={0}, use_global_device_ids=true | all-gather | bytes 8448 | tf_op jit(solution)/shard_map/all_gather | solution.py:199
  347.3 36.9 %all-gather.4 = bf16[32,1,128]{2,1,0:T(2,128)(2,1)S(1)} all-gather(bf16[1,1,128]{2,1,0:T(2,128)(2,1)S(1)} %bitcast.2916), channel_id=1, replica_groups=mesh['seg'=8,'seq'=4] {'seg','seq'}, dimensions={0}, use_global_device_ids=true | all-gather | bytes 8448 | tf_op jit(solution)/shard_map/all_gather | solution.py:197
  384.2 4.6 slice.4298
  389.0 21.6 multiply_reduce_fusion.160
  410.6 2.9 fusion.391
  413.5 12.1 all-gather.15.cloned.1.call-done
  425.6 7.2 compare_select_fusion
  432.9 7.7 all-gather
  443.1 76.7 %while.98 = (s32[]{:T(128)}, f32[16,4096]{1,0:T(8,128)}, f32[8,32,4096]{2,1,0:T(8,128)}, f32[16,4096]{1,0:T(8,128)S(1)}, f32[8,32,16]{2,1,0:T(8,128)S(1)}, /*ind...) while((s32[]{:T(128)}, f32[16,4096]{1,0:T(8,128)}, ...), condition=%wide.region_3.4_spmd.clone, body=%wide.region_2.3_spmd.clone.sunk | while | flops 8585250 | bytes 7609367 | solution.py:98
  520.9 7.7 all-gather.1
  533.8 125.5 %while.96 = (s32[]{:T(128)}, f32[16,4096]{1,0:T(8,128)S(1)}, f32[8,32,4096]{2,1,0:T(8,128)}, f32[8,16,4096]{2,1,0:T(8,128)}, f32[8,32,4096]{2,1,0:T(8,128)}, /*i...) while((s32[]{:T(128)}, f32[16,4096]{1,0:T(8,128)S(1)}, ...), condition=%wide.region_39.40_spmd, body=%wide.region_6.39_spmd.sunk | while | flops 18874400 | bytes 15481405 | solution.py:98
  542.2 3.1 multiply_reduce_fusion.190
  552.2 2.9 constant_dynamic-slice_fusion.428
  558.5 3.1 multiply_reduce_fusion.190
  574.2 3.1 multiply_reduce_fusion.190
  589.8 3.1 multiply_reduce_fusion.190
  605.1 3.1 multiply_reduce_fusion.190
  620.6 3.1 multiply_reduce_fusion.190
  636.3 3.1 multiply_reduce_fusion.190
  652.1 3.1 multiply_reduce_fusion.190
  659.4 83.2 %while.100 = (s32[]{:T(128)}, f32[16,4096]{1,0:T(8,128)S(1)}, f32[8,32,4096]{2,1,0:T(8,128)}, f32[16,4096]{1,0:T(8,128)S(1)}, f32[8,32,16]{2,1,0:T(8,128)S(1)}, ...) while((s32[]{:T(128)}, f32[16,4096]{1,0:T(8,128)S(1)}, ...), condition=%wide.region_43.44_spmd.clone, body=%wide.region_42.43_spmd.clone.sunk | while | flops 8454179 | bytes 3939383 | solution.py:156
  659.4 2.9 constant_dynamic-slice_fusion.435
  669.4 2.9 constant_dynamic-slice_fusion.435
  679.8 3.0 constant_dynamic-slice_fusion.435
  690.2 2.9 constant_dynamic-slice_fusion.435
  700.7 2.8 constant_dynamic-slice_fusion.435
  710.9 3.2 constant_dynamic-slice_fusion.435
  721.2 3.3 constant_dynamic-slice_fusion.435
  732.1 2.9 constant_dynamic-slice_fusion.435
  742.6 7.3 all-gather.2
  757.3 358.1 %while.97 = (s32[]{:T(128)}, f32[16,4096]{1,0:T(8,128)S(1)}, f32[8,32,4096]{2,1,0:T(8,128)}, f32[8,32,4096]{2,1,0:T(8,128)}, f32[8,16,4096]{2,1,0:T(8,128)}, /*i...) while((s32[]{:T(128)}, f32[16,4096]{1,0:T(8,128)S(1)}, ...), condition=%wide.region_175.176_spmd, body=%wide.region_46.175_spmd.sunk | while | flops 58784800 | bytes 39608088 | solution.py:156
  769.2 8.2 bitcast_dynamic-update-slice_fusion.11
  813.5 8.2 bitcast_dynamic-update-slice_fusion.11
  858.1 8.2 bitcast_dynamic-update-slice_fusion.11
  902.8 8.2 bitcast_dynamic-update-slice_fusion.11
  947.2 8.2 bitcast_dynamic-update-slice_fusion.11
  991.8 8.2 bitcast_dynamic-update-slice_fusion.11
  1036.8 8.2 bitcast_dynamic-update-slice_fusion.11
  1081.8 8.2 bitcast_dynamic-update-slice_fusion.11
  1116.3 9.1 convert_reduce_fusion
  1127.7 15.0 fusion.380
  1148.2 3.4 fusion.374
  1155.3 14.4 fusion.363
  1169.8 8.1 pad_add_fusion
  1180.4 3.2 collective-permute-done.1
  1185.4 25.6 fusion.349
  1211.8 11.8 all-reduce.11
  1224.8 12.1 fusion.352
  1236.9 16.1 fusion.361
  1253.0 39.9 %all-reduce.10 = (f32[2048]{0:T(1024)S(1)}, f32[4096]{0:T(1024)S(1)}, f32[4096]{0:T(1024)S(1)}, f32[4096]{0:T(1024)S(1)}) all-reduce(f32[2048]{0:T(1024)S(1)} %get-tuple-element.1072, f32[4096]{0:T(1024)S(1)} %get-tuple-element.1067, f32[4096]{0:T(1024)S(1)} %get-tuple-element.1211, ...), channel_id=5, replica_groups=mesh['seg'=8,'seq'=4] {'seg','seq'}, use_global_device_ids=true, to_apply=%region_180.181.clone | all-reduce | flops 14336 | bytes 114688
  1295.3 3.2 fusion.362
  1300.1 11.8 all-reduce.15.cloned.1.call-done
  1313.3 132.9 %reduce-scatter.15.cloned.1.call-done = f32[16,128]{1,0:T(8,128)} async-done(((f32[16,4096]{1,0:T(8,128)}), f32[16,128]{1,0:T(8,128)}) %reduce-scatter.15.cloned.1.call-update) | async-done | bytes 8208 | tf_op jit(solution)/shard_map/reduce_scatter | solution.py:336
  1446.2 137.3 %reduce-scatter.13.cloned.1.call-done = f32[128,128]{1,0:T(8,128)} async-done(((f32[128,4096]{1,0:T(8,128)}), f32[128,128]{1,0:T(8,128)}) %reduce-scatter.13.cloned.1.call-update) | async-done | bytes 65552 | tf_op jit(solution)/shard_map/reduce_scatter | solution.py:334
  1583.5 137.9 %reduce-scatter.11.cloned.1.call-done = f32[128,160]{0,1:T(8,128)} async-done(((f32[4096,160]{0,1:T(8,128)}), f32[128,160]{0,1:T(8,128)}) %reduce-scatter.11.cloned.1.call-update) | async-done | bytes 81936 | tf_op jit(solution)/shard_map/reduce_scatter | solution.py:333
  1721.4 362.0 %reduce-scatter.17.cloned.1.call-done = f32[128,2048]{1,0:T(8,128)} async-done(((f32[4096,2048]{1,0:T(8,128)}), f32[128,2048]{1,0:T(8,128)}) %reduce-scatter.17.cloned.1.call-update) | async-done | bytes 1048592 | tf_op jit(solution)/shard_map/reduce_scatter | solution.py:338
  2083.4 708.9 %reduce-scatter.9.cloned.1.call-done = f32[64,8192]{1,0:T(8,128)} async-done(((f32[2048,8192]{1,0:T(8,128)}), f32[64,8192]{1,0:T(8,128)}) %reduce-scatter.9.cloned.1.call-update) | async-done | bytes 2097168 | tf_op jit(solution)/shard_map/reduce_scatter | solution.py:330
  (944 shorter events, 571.5 us)
Async XLA Ops:
  7.2 201.6 %all-gather.11.cloned.1.call-start = ((), (), s32[]{:S(2)}) async-start(), calls=%async_computation.6 | async-start | bytes 34603008 | tf_op jit(solution)/shard_map/all_gather | solution.py:192
  7.9 381.1 %all-gather.17.cloned.1.call-start = ((), (), s32[]{:S(2)}) async-start(), calls=%async_computation.9 | async-start | bytes 17301504 | tf_op jit(solution)/shard_map/all_gather | solution.py:200
  8.7 401.9 %all-gather.13.cloned.1.call-start = ((), (), s32[]{:S(2)}) async-start(), calls=%async_computation.7 | async-start | bytes 1351680 | tf_op jit(solution)/shard_map/all_gather | solution.py:195
  9.4 416.2 %all-gather.15.cloned.1.call-start = ((), (), s32[]{:S(2)}) async-start(), calls=%async_computation.8 | async-start | bytes 1081344 | tf_op jit(solution)/shard_map/all_gather | solution.py:196
  10.0 1288.6 %reduce-scatter.19.cloned.1.call-start = ((), (), s32[]{:S(2)}) async-start(), calls=%async_computation.15 | async-start | bytes 2162688
  54.5 172.1 %copy-start.12 = (f32[2048]{0:T(1024)}, f32[2048]{0:T(1024)S(1)}, u32[]{:S(2)}) copy-start(f32[2048]{0:T(1024)S(1)} %convert_element_type.154) | copy-start | bytes 24580
  57.0 169.7 %copy-start.21 = (f32[256]{0:T(256)}, f32[256]{0:T(256)S(1)}, u32[]{:S(2)}) copy-start(f32[256]{0:T(256)S(1)} %get-tuple-element.1794) | copy-start | bytes 3076
  100.0 288.9 %copy-start.28 = (f32[1,4096]{1,0:T(1,128)}, f32[1,4096]{1,0:T(1,128)S(1)}, u32[]{:S(2)}) copy-start(f32[1,4096]{1,0:T(1,128)S(1)} %get-tuple-element.1789) | copy-start | bytes 49156
  100.1 288.9 %copy-start.30 = (f32[1,4096]{1,0:T(1,128)}, f32[1,4096]{1,0:T(1,128)S(1)}, u32[]{:S(2)}) copy-start(f32[1,4096]{1,0:T(1,128)S(1)} %get-tuple-element.1790) | copy-start | bytes 49156
  100.1 288.9 %copy-start.32 = (f32[1,4096]{1,0:T(1,128)}, f32[1,4096]{1,0:T(1,128)S(1)}, u32[]{:S(2)}) copy-start(f32[1,4096]{1,0:T(1,128)S(1)} %get-tuple-element.1791) | copy-start | bytes 49156
  100.1 288.9 %copy-start.34 = (f32[1,4096]{1,0:T(1,128)}, f32[1,4096]{1,0:T(1,128)S(1)}, u32[]{:S(2)}) copy-start(f32[1,4096]{1,0:T(1,128)S(1)} %get-tuple-element.1792) | copy-start | bytes 49156
  208.8 22.7 copy-start.36
  208.8 61.5 %copy-start.38 = (bf16[128]{0:T(256)(128)(2,1)S(1)}, bf16[128]{0:T(256)(128)(2,1)}, u32[]{:S(2)}) copy-start(bf16[128]{0:T(256)(128)(2,1)} %param.30) | copy-start | bytes 772
  208.8 99.7 %copy-start.39 = (bf16[128]{0:T(256)(128)(2,1)S(1)}, bf16[128]{0:T(256)(128)(2,1)}, u32[]{:S(2)}) copy-start(bf16[128]{0:T(256)(128)(2,1)} %param.35) | copy-start | bytes 772
  208.8 138.6 %copy-start.40 = (bf16[128]{0:T(256)(128)(2,1)S(1)}, bf16[128]{0:T(256)(128)(2,1)}, u32[]{:S(2)}) copy-start(bf16[128]{0:T(256)(128)(2,1)} %param.33) | copy-start | bytes 772
  228.2 160.7 %collective-permute-start = (bf16[3,4096]{1,0:T(4,128)(2,1)S(1)}, bf16[3,4096]{1,0:T(4,128)(2,1)S(1)}, u32[]{:S(2)}, u32[]{:S(2)}) collective-permute-start(bf16[3,4096]{1,0:T(4,128)(2,1)S(1)} %get-tuple-element.1216), channel_id=1, source_target_pairs={{0,1},{1,2},{2,3},{4,5},{5,6},{6,7},{8,9},{9,10},{10,11},{12,13},{... | collective-permute-start | bytes 73736 | tf_op jit(solution)/shard_map/ppermute | solution.py:14
  384.2 4.7 copy-start.26
  388.9 21.6 copy-start.23
  410.6 30.1 %copy-start = (bf16[256,4096]{1,0:T(8,128)(2,1)}, bf16[256,4096]{1,0:T(8,128)(2,1)S(1)}, u32[]{:S(2)}) copy-start(bf16[256,4096]{1,0:T(8,128)(2,1)S(1)} %get-tuple-element.1209) | copy-start | bytes 6291460
  413.5 19.3 copy-start.14
  443.1 85.4 %copy-start.5 = (bf16[64,4096]{1,0:T(8,128)(2,1)S(1)}, bf16[64,4096]{1,0:T(8,128)(2,1)}, u32[]{:S(2)}) copy-start(bf16[64,4096]{1,0:T(8,128)(2,1)} %all-gather) | copy-start | bytes 1572868
  443.1 6.8 copy-start.17
  452.1 0.7 copy-start.18
  452.8 7.2 copy-start.17
  462.2 0.7 copy-start.18
  462.9 6.7 copy-start.17
  471.7 0.7 copy-start.18
  472.4 6.7 copy-start.17
  481.3 0.7 copy-start.18
  482.0 6.4 copy-start.17
  491.3 6.5 copy-start.17
  500.6 6.8 copy-start.17
  510.3 6.7 copy-start.17
  519.9 9.9 copy-start.19
  533.8 125.5 %copy-start.16 = (f32[16,4096]{1,0:T(8,128)S(1)}, f32[16,4096]{1,0:T(8,128)}, u32[]{:S(2)}) copy-start(f32[16,4096]{1,0:T(8,128)} %custom-call.3) | copy-start | bytes 786436
  757.3 359.0 %copy-start.25 = (f32[32,1,128]{2,1,0:T(1,128)S(1)}, f32[32,1,128]{2,1,0:T(1,128)}, u32[]{:S(2)}) copy-start(f32[32,1,128]{2,1,0:T(1,128)} %convert_element_type.183) | copy-start | bytes 49156
  1116.2 10.5 copy-start.11
  1116.3 11.3 copy-start.1
  1116.3 11.4 copy-start.6
  1116.3 11.5 copy-start.7
  1116.3 11.5 copy-start.24
  1116.3 11.4 copy-start.29
  1116.3 11.4 copy-start.31
  1116.3 11.4 copy-start.33
  1116.3 11.4 copy-start.35
  1125.4 1.3 copy-start.2
  1142.7 5.5 copy-start.15
  1144.9 167.0 %all-reduce.15.cloned.1.call-start = ((), (), s32[]{:S(2)}) async-start(), calls=%async_computation.16 | async-start | bytes 524288 | tf_op jit(solution)/shard_map/psum | solution.py:47
  1147.3 298.9 %reduce-scatter.15.cloned.1.call-start = ((), (), s32[]{:S(2)}) async-start(), calls=%async_computation.13 | async-start | bytes 270336 | tf_op jit(solution)/shard_map/reduce_scatter | solution.py:336
  1148.2 435.3 %reduce-scatter.13.cloned.1.call-start = ((), (), s32[]{:S(2)}) async-start(), calls=%async_computation.12 | async-start | bytes 2162688 | tf_op jit(solution)/shard_map/reduce_scatter | solution.py:334
  1151.7 569.8 %reduce-scatter.11.cloned.1.call-start = ((), (), s32[]{:S(2)}) async-start(), calls=%async_computation.11 | async-start | bytes 2703360 | tf_op jit(solution)/shard_map/reduce_scatter | solution.py:333
  1153.7 1.6 copy-start.9
  1153.8 929.6 %reduce-scatter.17.cloned.1.call-start = ((), (), s32[]{:S(2)}) async-start(), calls=%async_computation.14 | async-start | bytes 34603008 | tf_op jit(solution)/shard_map/reduce_scatter | solution.py:338
  1169.7 1622.5 %reduce-scatter.9.cloned.1.call-start = ((), (), s32[]{:S(2)}) async-start(), calls=%async_computation.10 | async-start | bytes 69206016 | tf_op jit(solution)/shard_map/reduce_scatter | solution.py:330
  1177.9 7.5 copy-start.3
  1177.9 7.5 copy-start.13
  1177.9 7.5 copy-start.22
  1178.0 5.6 collective-permute-start.1
  1211.0 0.8 copy-start.20
  1224.8 12.1 copy-start.4
  1224.8 12.1 copy-start.10
  1236.9 16.1 copy-start.27
  1236.9 58.4 %copy-start.8 = (bf16[1,256,2048]{2,1,0:T(8,128)(2,1)S(1)}, bf16[1,256,2048]{2,1,0:T(8,128)(2,1)}, u32[]{:S(2)}) copy-start(bf16[1,256,2048]{2,1,0:T(8,128)(2,1)} %param.39) | copy-start | bytes 3145732
  1236.9 58.4 %copy-start.37 = (f32[256]{0:T(256)S(1)}, f32[256]{0:T(256)}, u32[]{:S(2)}) copy-start(f32[256]{0:T(256)} %get-tuple-element.1793) | copy-start | bytes 3076
  (4 other events, 2.8 us)
Sparse Core Ops, SparseCore 0:
  10.9 197.8 all-gather.10
  211.6 112.9 all-gather.16
  327.5 47.5 all-gather.12
  377.8 47.7 all-gather.14
  1145.0 132.4 reduce-scatter.18
  1279.8 32.0 all-reduce.14
  1314.6 131.4 reduce-scatter.14
  1449.0 134.4 reduce-scatter.12
  1586.3 135.0 reduce-scatter.10
  1724.1 359.2 reduce-scatter.16
  2086.3 705.9 reduce-scatter.8
where the time goes:
time: 2810 us; the launch traced here: 2800 us
  waiting for transfers between devices  1620 us (58%)
  other arithmetic  391 us (14%)
  local copies, waits for them, and re-layouts  313 us (11%)
  blocking collectives  313 us (11%)
  matrix products  139 us (5%)
    reduce_scatter x1, waiting for transfers between devices, body(): lax.psum_scatter(inp_grad, ('seg', 'seq'), scatter_dimension=0, tiled=True)  709 us
    reduce_scatter x1, waiting for transfers between devices, body(): lax.psum_scatter(out_grad, ('seg', 'seq'), scatter_dimension=0, tiled=True)  362 us
    reduce_scatter x1, waiting for transfers between devices, body(): lax.psum_scatter(xp_grad, ('seg', 'seq'), scatter_dimension=0, tiled=True)  138 us
    reduce_scatter x1, waiting for transfers between devices, body(): lax.psum_scatter(dtp_grad, ('seg', 'seq'), scatter_dimension=1, tiled=True)  137 us
    reduce_scatter x1, waiting for transfers between devices, body(): lax.psum_scatter(a_grad, ('seg', 'seq'), scatter_dimension=1, tiled=True)  133 us
    all_gather x1, waiting for transfers between devices, body(): lax.all_gather(in_proj, ('seg', 'seq'), axis=0, tiled=True)  109 us
    unnamed x2, blocking collectives  83.6 us
    slice x32, local copies, waits for them, and re-layouts, advance(): rate_b[i][None, :] * a_mat  76 us
  transfers between devices with their start and end apart: 13, of which 9 were waited for; matrix products, arithmetic and copies ran while one was open for 5% of the time, Pallas kernels for 0%

commit v1 on v0

v1 whole, which is shorter than its diff:
```python
import functools

import jax
import jax.numpy as jnp
from jax import lax
from jax.experimental import pallas as pl
from jax.experimental.pallas import tpu as pltpu
from jax.sharding import PartitionSpec as P

EPSILON = 1e-05
LOG2E = 1.4426950408889634
LANES = 128
UNROLL = 8
F32 = jnp.float32
BF16 = jnp.bfloat16


def sigmoid(v):
    return 1.0 / (1.0 + jnp.exp(-v))


def softplus(v):
    return jnp.maximum(v, 0.0) + jnp.log1p(jnp.exp(-jnp.abs(v)))


def to_planes(planes_ref, rows):
    count = rows.shape[0]
    for s in range(rows.shape[1] // LANES):
        planes_ref[pl.ds(s * count, count), :] = rows[:, s * LANES : (s + 1) * LANES]


def from_planes(planes_ref, count, planes):
    return jnp.concatenate(
        [planes_ref[pl.ds(s * count, count), :] for s in range(planes)], axis=1
    )


def forward_kernel(
    pre_ref, act_ref, gate_ref, bc_ref, a_ref, skip_ref, init_ref,
    y_ref, gated_ref, check_ref, final_ref,
    state, rate_pl, drive_pl, y_pl,
):
    count = pre_ref.shape[0]
    width, planes, _ = a_ref.shape

    @pl.when(pl.program_id(0) == 0)
    def _():
        state[...] = init_ref[...]

    rate = softplus(pre_ref[...])
    act = act_ref[...].astype(F32)
    to_planes(rate_pl, rate)
    to_planes(drive_pl, rate * act)

    def group(k, carry):
        first = k * UNROLL
        rates = [rate_pl[pl.ds(first + i, planes, stride=count), :] for i in range(UNROLL)]
        drives = [drive_pl[pl.ds(first + i, planes, stride=count), :] for i in range(UNROLL)]
        sums = [None] * UNROLL
        for n in range(width):
            a = a_ref[n]
            h = state[n]
            check_ref[k, n] = h
            for i in range(UNROLL):
                h = jnp.exp2(rates[i] * a) * h + bc_ref[first + i, n] * drives[i]
                term = bc_ref[first + i, width + n] * h
                sums[i] = term if n == 0 else sums[i] + term
            state[n] = h
        for i in range(UNROLL):
            y_pl[pl.ds(first + i, planes, stride=count), :] = sums[i]
        return carry

    lax.fori_loop(0, count // UNROLL, group, 0)
    y_val = from_planes(y_pl, count, planes) + skip_ref[...] * act
    gate = gate_ref[...]
    y_ref[...] = y_val
    gated_ref[...] = (y_val * gate * sigmoid(gate)).astype(BF16)

    @pl.when(pl.program_id(0) == pl.num_programs(0) - 1)
    def _():
        final_ref[...] = state[...]


def backward_kernel(
    pre_ref, act_ref, gy_ref, bc_ref, a_ref, skip_ref, check_ref,
    gdt_ref, gact_ref, gbc_ref, agrad_ref, start_ref, dtb_ref, sgrad_ref,
    carry_s, rate_pl, drive_pl, gy_pl, grate_pl, thr_pl, prod, part,
):
    count = pre_ref.shape[0]
    width, planes, _ = a_ref.shape

    @pl.when(pl.program_id(0) == 0)
    def _():
        carry_s[...] = jnp.zeros_like(carry_s)
        agrad_ref[...] = jnp.zeros_like(agrad_ref)
        dtb_ref[...] = jnp.zeros_like(dtb_ref)
        sgrad_ref[...] = jnp.zeros_like(sgrad_ref)

    pre = pre_ref[...]
    rate = softplus(pre)
    act = act_ref[...].astype(F32)
    gy = gy_ref[...]
    to_planes(rate_pl, rate)
    to_planes(drive_pl, rate * act)
    to_planes(gy_pl, gy)
    groups = count // UNROLL

    def group(j, carry):
        k = groups - 1 - j
        first = k * UNROLL
        rates = [rate_pl[pl.ds(first + i, planes, stride=count), :] for i in range(UNROLL)]
        drives = [drive_pl[pl.ds(first + i, planes, stride=count), :] for i in range(UNROLL)]
        gys = [gy_pl[pl.ds(first + i, planes, stride=count), :] for i in range(UNROLL)]
        g_rate = [None] * UNROLL
        through = [None] * UNROLL
        for n in range(width):
            a = a_ref[n]
            states = [check_ref[k, n]]
            decays = []
            for i in range(UNROLL):
                decays.append(jnp.exp2(rates[i] * a))
                states.append(decays[i] * states[i] + bc_ref[first + i, n] * drives[i])
            lam = carry_s[n]
            acc = agrad_ref[n]
            for i in reversed(range(UNROLL)):
                lam = lam + bc_ref[first + i, width + n] * gys[i]
                b_term = bc_ref[first + i, n] * lam
                prod[pl.ds((i * 2 * width + n) * planes, planes), :] = lam * drives[i]
                prod[pl.ds((i * 2 * width + width + n) * planes, planes), :] = (
                    states[i + 1] * gys[i]
                )
                lam = decays[i] * lam
                weighted = lam * states[i]
                acc = acc + weighted * rates[i]
                a_term = weighted * a
                g_rate[i] = a_term if n == 0 else g_rate[i] + a_term
                through[i] = b_term if n == 0 else through[i] + b_term
            carry_s[n] = lam
            agrad_ref[n] = acc
        for i in range(UNROLL):
            grate_pl[pl.ds(first + i, planes, stride=count), :] = g_rate[i]
            thr_pl[pl.ds(first + i, planes, stride=count), :] = through[i]
            for q in range(2 * width // 8):
                base = (i * 2 * width + q * 8) * planes
                total = prod[pl.ds(base, 8, stride=planes), :]
                for s in range(1, planes):
                    total = total + prod[pl.ds(base + s, 8, stride=planes), :]
                row = pl.multiple_of((first + i) * 2 * width + q * 8, 8)
                part[pl.ds(row, 8), :] = total
        return carry

    lax.fori_loop(0, groups, group, 0)
    g_rate = from_planes(grate_pl, count, planes) * (1.0 / LOG2E)
    through = from_planes(thr_pl, count, planes)
    g_dtpre = ((g_rate + act * through) * sigmoid(pre)).astype(BF16)
    gdt_ref[...] = g_dtpre
    gact_ref[...] = gy * skip_ref[...] + rate * through
    dtb_ref[...] += jnp.sum(g_dtpre.astype(F32), axis=0, keepdims=True)
    sgrad_ref[...] += jnp.sum(gy * act, axis=0, keepdims=True)
    rows = 2 * width
    ones = jnp.ones((LANES, LANES), F32)
    sums = jnp.dot(part[...], ones, preferred_element_type=F32)
    sums = sums.reshape(count, rows, LANES)
    pick = lax.broadcasted_iota(jnp.int32, (1, rows, LANES), 1) == lax.broadcasted_iota(
        jnp.int32, (1, rows, LANES), 2
    )
    gbc_ref[...] = jnp.sum(jnp.where(pick, sums, 0.0), axis=1)

    @pl.when(pl.program_id(0) == pl.num_programs(0) - 1)
    def _():
        start_ref[...] = carry_s[...]


def forward_scan(pre, act, gate, bc, a2, skip, init, block):
    length, features = pre.shape
    width, planes, _ = a2.shape
    steps = length // block
    rows = pl.BlockSpec((block, features), lambda i: (i, 0))
    whole = pl.BlockSpec((width, planes, LANES), lambda i: (0, 0, 0))
    plane = pltpu.VMEM((planes * block, LANES), F32)
    return pl.pallas_call(
        forward_kernel,
        grid=(steps,),
        in_specs=[
            rows, rows, rows,
            pl.BlockSpec((block, 2 * width), lambda i: (i, 0), memory_space=pltpu.SMEM),
            whole,
            pl.BlockSpec((1, features), lambda i: (0, 0)),
            whole,
        ],
        out_specs=[
            rows, rows,
            pl.BlockSpec((block // UNROLL, width, planes, LANES), lambda i: (i, 0, 0, 0)),
            whole,
        ],
        out_shape=[
            jax.ShapeDtypeStruct((length, features), F32),
            jax.ShapeDtypeStruct((length, features), BF16),
            jax.ShapeDtypeStruct((length // UNROLL, width, planes, LANES), F32),
            jax.ShapeDtypeStruct((width, planes, LANES), F32),
        ],
        scratch_shapes=[pltpu.VMEM((width, planes, LANES), F32), plane, plane, plane],
        cost_estimate=pl.CostEstimate(
            flops=8 * length * features * width,
            bytes_accessed=24 * length * features,
            transcendentals=length * features * width,
        ),
        name="scan_forward",
    )(pre, act, gate, bc, a2, skip, init)


def backward_scan(pre, act, gy, bc, a2, skip, checks, block):
    length, features = pre.shape
    width, planes, _ = a2.shape
    steps = length // block
    rows = pl.BlockSpec((block, features), lambda i: (steps - 1 - i, 0))
    whole = pl.BlockSpec((width, planes, LANES), lambda i: (0, 0, 0))
    line = pl.BlockSpec((1, features), lambda i: (0, 0))
    plane = pltpu.VMEM((planes * block, LANES), F32)
    return pl.pallas_call(
        backward_kernel,
        grid=(steps,),
        in_specs=[
            rows, rows, rows,
            pl.BlockSpec(
                (block, 2 * width), lambda i: (steps - 1 - i, 0), memory_space=pltpu.SMEM
            ),
            whole, line,
            pl.BlockSpec(
                (block // UNROLL, width, planes, LANES), lambda i: (steps - 1 - i, 0, 0, 0)
            ),
        ],
        out_specs=[
            rows, rows,
            pl.BlockSpec((block, LANES), lambda i: (steps - 1 - i, 0)),
            whole, whole, line, line,
        ],
        out_shape=[
            jax.ShapeDtypeStruct((length, features), BF16),
            jax.ShapeDtypeStruct((length, features), F32),
            jax.ShapeDtypeStruct((length, LANES), F32),
            jax.ShapeDtypeStruct((width, planes, LANES), F32),
            jax.ShapeDtypeStruct((width, planes, LANES), F32),
            jax.ShapeDtypeStruct((1, features), F32),
            jax.ShapeDtypeStruct((1, features), F32),
        ],
        scratch_shapes=[pltpu.VMEM((width, planes, LANES), F32)]
        + [plane] * 5
        + [
            pltpu.VMEM((UNROLL * 2 * width * planes, LANES), F32),
            pltpu.VMEM((block * 2 * width, LANES), F32),
        ],
        cost_estimate=pl.CostEstimate(
            flops=20 * length * features * width,
            bytes_accessed=28 * length * features,
            transcendentals=length * features * width,
        ),
        name="scan_backward",
    )(pre, act, gy, bc, a2, skip, checks)


def dot_nn(a, b):
    return jnp.dot(a, b, preferred_element_type=F32)


def dot_tn(a, b):
    return lax.dot_general(a, b, (((0,), (0,)), ((), ())), preferred_element_type=F32)


def dot_nt(a, b):
    return lax.dot_general(a, b, (((1,), (1,)), ((), ())), preferred_element_type=F32)


def body(
    tokens, norm_gain, in_proj, conv_weight, conv_bias, x_proj, dt_proj, dt_bias,
    a_log, d_skip, out_proj, init_state, init_conv, cotangent,
):
    segs, seqs = lax.axis_size("seg"), lax.axis_size("seq")
    place = lax.axis_index("seq")
    own_rows, both = in_proj.shape
    part = conv_bias.shape[0]
    feats = segs * part
    taps = conv_weight.shape[0]
    width = a_log.shape[0]
    low_rank = dt_proj.shape[0]
    planes = feats // LANES
    own_len, model = tokens.shape[1:]
    length = own_len * seqs
    block = 64

    def mine(rows):
        shaped = rows.reshape(rows.shape[0], segs, seqs, part)
        return lax.dynamic_index_in_dim(shaped, place, 2, keepdims=False).reshape(
            rows.shape[0], feats
        )

    def to_contiguous(rows):
        count = rows.shape[0]
        shaped = rows.reshape(count, seqs, (segs // seqs) * part)
        got = lax.all_to_all(shaped, "seq", 1, 0, tiled=False)
        return (
            got.reshape(seqs, count, segs // seqs, part)
            .transpose(1, 2, 0, 3)
            .reshape(count, feats)
        )

    gain_col = norm_gain.astype(F32)[:, None]
    own_weight = in_proj.astype(F32)
    scaled = (own_weight * gain_col).astype(BF16)
    scaled = scaled.reshape(own_rows, 2, segs, seqs, part).transpose(3, 1, 0, 2, 4)
    scaled = scaled.reshape(seqs, 2, own_rows, feats)
    swapped = lax.all_to_all(scaled, "seq", 0, 0, tiled=False)
    w_x_half = lax.all_gather(
        swapped[:, 0].reshape(seqs * own_rows, feats), "seg", axis=0, tiled=True
    )
    tok = lax.all_gather(tokens[0], "seq", axis=0, tiled=True)
    small = jnp.concatenate(
        [
            dt_proj, x_proj.T, a_log, conv_weight, conv_bias[None], dt_bias[None], d_skip[None],
        ],
        axis=0,
    )
    small_all = lax.all_gather(small, "seg", axis=0, tiled=False)
    w_g_half = lax.all_gather(
        swapped[:, 1].reshape(seqs * own_rows, feats), "seg", axis=0, tiled=True
    )
    w_out = lax.all_gather(out_proj, "seg", axis=0, tiled=True)
    cot = lax.all_gather(cotangent[0], "seq", axis=0, tiled=True)

    small_all = small_all.transpose(1, 0, 2).reshape(small.shape[0], feats)
    w_dt = small_all[:low_rank]
    w_xt = small_all[low_rank : low_rank + x_proj.shape[1]]
    rest = small_all[low_rank + x_proj.shape[1] :].astype(F32)
    a_mat = -jnp.exp(rest[:width])
    a2 = (a_mat * LOG2E).reshape(width, planes, LANES)
    kernel = rest[width : width + taps]
    b_conv = rest[width + taps][None]
    b_dt = rest[width + taps + 1][None]
    skip = rest[width + taps + 2][None]

    tok_float = tok.astype(F32)
    rstd = lax.rsqrt(jnp.mean(tok_float * tok_float, axis=1, keepdims=True) + EPSILON)
    x_in = rstd * dot_nn(tok, w_x_half)
    history = init_conv.shape[1]
    head = mine(init_conv[0])
    padded = jnp.concatenate([head, x_in], axis=0)
    conv_out = b_conv + sum(kernel[k] * padded[k : k + length] for k in range(taps))
    act = jax.nn.silu(conv_out).astype(BF16)
    mixed_x = lax.psum(dot_nt(act, w_xt), "seq")
    dt_low = mixed_x[:, :low_rank].astype(BF16)
    bc = mixed_x[:, low_rank:]
    pre = dot_nn(dt_low, w_dt) + b_dt
    gate = rstd * dot_nn(tok, w_g_half)
    init = mine(init_state[0]).reshape(width, planes, LANES)
    y_val, gated, checks, final = forward_scan(pre, act, gate, bc, a2, skip, init, block)
    out_part = dot_nn(gated, w_out).astype(BF16)
    mixed_out = lax.psum_scatter(out_part, "seq", scatter_dimension=0, tiled=True)
    mixed_out = (mixed_out.astype(F32) + tokens[0].astype(F32)).astype(BF16)

    g_gated = dot_nt(cot, w_out)
    sig_gate = jax.nn.sigmoid(gate)
    gy = g_gated * gate * sig_gate
    gs_gate = (
        rstd * g_gated * y_val * sig_gate * (1.0 + gate * (1.0 - sig_gate))
    ).astype(BF16)
    out_grad = lax.psum_scatter(
        dot_tn(gated, cot).astype(BF16), "seg", scatter_dimension=0, tiled=True
    )
    gate_grad = lax.psum_scatter(
        dot_tn(tok, gs_gate).astype(BF16), "seg", scatter_dimension=0, tiled=True
    )
    g_dtpre, g_actp, g_bc, a_sum, start, dtb_grad, skip_grad = backward_scan(
        pre, act, gy, bc, a2, skip, checks, block
    )
    g_mixed = jnp.concatenate([dot_nt(g_dtpre, w_dt), g_bc[:, : 2 * width]], axis=1)
    g_mixed = lax.psum(g_mixed, "seq").astype(BF16)
    g_act = g_actp + dot_nn(g_mixed, w_xt)
    sig_conv = jax.nn.sigmoid(conv_out)
    g_conv = g_act * sig_conv * (1.0 + conv_out * (1.0 - sig_conv))
    tail = jnp.concatenate([g_conv, jnp.zeros((history, feats), F32)], axis=0)
    whole = jnp.concatenate([jnp.zeros((history, feats), F32), tail], axis=0)
    g_xin = sum(kernel[k] * tail[history - k : history - k + length] for k in range(taps))
    head_grad = sum(kernel[k] * whole[history - k : 2 * history - k] for k in range(taps))
    gs_x = (rstd * g_xin).astype(BF16)
    x_grad = lax.psum_scatter(
        dot_tn(tok, gs_x).astype(BF16), "seg", scatter_dimension=0, tiled=True
    )
    q_part = (dot_nt(gs_gate, w_g_half) + dot_nt(gs_x, w_x_half)).astype(BF16)
    q_own = lax.psum_scatter(q_part, "seq", scatter_dimension=0, tiled=True).astype(F32)

    cw_grad = jnp.stack([jnp.sum(g_conv * padded[k : k + length], axis=0) for k in range(taps)])
    grads = jnp.concatenate(
        [
            dot_tn(dt_low, g_dtpre),
            dot_tn(g_mixed, act),
            a_sum.reshape(width, feats) * a_mat,
            cw_grad,
            jnp.sum(g_conv, axis=0, keepdims=True),
            dtb_grad,
            skip_grad,
        ],
        axis=0,
    )
    grads = grads.reshape(grads.shape[0], segs, part).transpose(1, 0, 2).astype(BF16)
    grads = lax.psum_scatter(grads, "seg", scatter_dimension=0, tiled=False).astype(F32)

    own = tokens[0].astype(F32)
    own_rstd = lax.rsqrt(jnp.mean(own * own, axis=1, keepdims=True) + EPSILON)
    input_grad = (
        cotangent[0].astype(F32)
        + q_own
        - own * (own_rstd * own_rstd) * jnp.mean(q_own * own, axis=1, keepdims=True)
    ).astype(BF16)

    halves = jnp.stack([x_grad, gate_grad]).reshape(2, seqs, own_rows, feats)
    halves = lax.all_to_all(halves, "seq", 1, 0, tiled=False)
    raw_grad = (
        halves.reshape(seqs, 2, own_rows, segs, part)
        .transpose(2, 1, 3, 0, 4)
        .reshape(own_rows, both)
        .astype(F32)
    )
    in_grad = raw_grad * gain_col
    gain_grad = jnp.sum(raw_grad * own_weight, axis=1)

    ends = to_contiguous(
        jnp.concatenate(
            [
                final.reshape(width, feats),
                x_in[length - history :],
                start.reshape(width, feats),
                head_grad,
            ],
            axis=0,
        )
    )
    at = width + history
    xp_at = low_rank + x_proj.shape[1]
    return (
        mixed_out[None],
        ends[None, :width],
        ends[None, width:at],
        input_grad[None],
        ends[None, at : at + width],
        ends[None, at + width :],
        gain_grad,
        in_grad,
        grads[xp_at + width : xp_at + width + taps],
        grads[xp_at + width + taps],
        grads[low_rank:xp_at].T,
        grads[:low_rank],
        grads[xp_at + width + taps + 1],
        grads[xp_at : xp_at + width],
        grads[xp_at + width + taps + 2],
        out_grad.astype(F32),
    )


def solution(mesh):
    spread = ("seg", "seq")
    placed = (
        P("seg", "seq", None),
        P(spread),
        P(spread, None),
        P(None, spread),
        P(spread),
        P(spread, None),
        P(None, spread),
        P(spread),
        P(None, spread),
        P(spread),
        P(spread, None),
        P("seg", None, None),
        P("seg", None, None),
        P("seg", "seq", None),
    )
    return jax.shard_map(
        body,
        mesh=mesh,
        in_specs=placed,
        out_specs=(
            P("seg", "seq", None),
            P("seg", None, "seq"),
            P("seg", None, "seq"),
            P("seg", "seq", None),
            P("seg", None, "seq"),
            P("seg", None, "seq"),
            P(spread),
            P(spread, None),
            P(None, spread),
            P(spread),
            P(spread, None),
            P(None, spread),
            P(spread),
            P(None, spread),
            P(spread),
            P(spread, None),
        ),
        check_vma=False,
    )
```

time: 2810 us -> 945 us (0.34)
  waiting for transfers between devices: 1620 us -> 568 us
  other arithmetic: 391 us -> 28.3 us
  local copies, waits for them, and re-layouts: 313 us -> 29.1 us
  blocking collectives: 313 us -> 77.3 us
  Pallas kernels: 0 us -> 119 us
  matrix products: 139 us -> 96.4 us
    reduce_scatter x5, waiting for transfers between devices: 1480 us -> 348 us  [the longest x1 90.8 us: body(): lax.psum_scatter(dot_tn(tok, gs_gate).astype(BF16), 'seg', scatter_dimens...]
    slice x139 -> x16, local copies, waits for them, and re-layouts: 230 us -> 8.71 us  [the longest x1 1.87 us: body(): bc = mixed_x[:, low_rank:]]
    all_gather x8 -> x1, blocking collectives: 218 us -> 25.9 us  [body(): small_all = lax.all_gather(small, 'seg', axis=0, tiled=False)]
    reduce_sum x203 -> x3, other arithmetic: 157 us -> 9.63 us  [the longest x1 4.71 us: body(): jnp.sum(g_conv * padded[k:k + length], axis=0)]
    pallas_call x0 -> x2, Pallas kernels: none -> 119 us  [the longest x1 86.8 us: backward_scan(): pl.pallas_call(backward_kernel, grid=(steps,), in_specs=[rows, rows, rows...]
    add x58 -> x1, other arithmetic: 91.4 us -> 0.89 us  [body(): sum((kernel[k] * whole[history - k:2 * history - k] for k in range(taps)))]
    unnamed x2 -> x0, blocking collectives: 83.6 us -> none
    all_gather x4 -> x5, waiting for transfers between devices: 121 us -> 189 us  [the longest x1 72.7 us: body(): w_out = lax.all_gather(out_proj, 'seg', axis=0, tiled=True)]
  transfers between devices with their start and end apart: 13 -> 13, of which waited for: 9 -> 9; matrix products, arithmetic and copies ran while one was open for 5% -> 12% of each run, Pallas kernels for 0% -> 3%
where the time goes in v1:
time: 945 us; the launch traced here: 939 us
  waiting for transfers between devices  568 us (60%)
  Pallas kernels  119 us (13%)
  matrix products  96.4 us (10%)
  blocking collectives  77.3 us (8%)
  local copies, waits for them, and re-layouts  29.1 us (3%)
  other arithmetic  28.3 us (3%)
  between operations  15.1 us (2%)
    reduce_scatter x1, waiting for transfers between devices, body(): lax.psum_scatter(dot_tn(tok, gs_gate).astype(BF16), 'seg', scatter_dimens...  90.8 us
    pallas_call x1, Pallas kernels, backward_scan(): pl.pallas_call(backward_kernel, grid=(steps,), in_specs=[rows, rows, rows...  86.8 us
    reduce_scatter x1, waiting for transfers between devices, body(): lax.psum_scatter(dot_tn(gated, cot).astype(BF16), 'seg', scatter_dimensio...  84.3 us
    reduce_scatter x1, waiting for transfers between devices, body(): lax.psum_scatter(dot_tn(tok, gs_x).astype(BF16), 'seg', scatter_dimension...  82.9 us
    all_gather x1, waiting for transfers between devices, body(): w_out = lax.all_gather(out_proj, 'seg', axis=0, tiled=True)  72.7 us
    all_gather x1, waiting for transfers between devices, body(): lax.all_gather(swapped[:, 0].reshape(seqs * own_rows, feats), 'seg', axis...  59.4 us
    all_gather x1, waiting for transfers between devices, body(): lax.all_gather(swapped[:, 1].reshape(seqs * own_rows, feats), 'seg', axis...  56.4 us
    reduce_scatter x1, waiting for transfers between devices, body(): lax.psum_scatter(out_part, 'seq', scatter_dimension=0, tiled=True)  45.3 us
  transfers between devices with their start and end apart: 13, of which 9 were waited for; matrix products, arithmetic and copies ran while one was open for 12% of the time, Pallas kernels for 3%

profile of v1, /device:TPU:1, one launch (start us, length us, event | category | flops | bytes accessed | tf_op | source)
XLA Modules:
  0.0 938.6 jit_solution(14221552561535500551)
XLA Ops:
  7.2 0.7 all-gather.16.cloned.1.call-update
  8.0 0.7 convert_element_type.98
  8.6 1.5 fusion.26
  10.1 0.8 reshape.158
  11.6 25.1 %all_to_all.32 = bf16[4,2,64,1024]{3,2,1,0:T(8,128)(2,1)S(1)} all-to-all(bf16[4,2,64,1024]{3,2,1,0:T(8,128)(2,1)S(1)} %reshape.159), channel_id=1, replica_groups=mesh['seg'=8,'seq'=4] {'seq'}, dimensions={0} | all-to-all | bytes 2097152 | tf_op jit(solution)/shard_map/all_to_all | solution.py:312
  36.7 1.1 fusion.57
  37.9 0.7 all-gather.12.cloned.1.call-update
  38.7 25.9 %all-gather.3 = bf16[8,311,128]{2,1,0:T(8,128)(2,1)S(1)} all-gather(bf16[1,311,128]{2,1,0:T(8,128)(2,1)S(1)} %bitcast.213), channel_id=2, replica_groups=mesh['seg'=8,'seq'=4] {'seg'}, dimensions={0}, use_global_device_ids=true | all-gather | bytes 716544 | tf_op jit(solution)/shard_map/all_gather | solution.py:323
  65.5 3.2 multiply_reduce_fusion
  68.7 59.4 %all-gather.10.cloned.1.call-done = bf16[2048,1024]{1,0:T(8,128)(2,1)} async-done(((bf16[256,1024]{1,0:T(8,128)(2,1)}), bf16[2048,1024]{1,0:T(8,128)(2,1)}) %all-gather.10.cloned.1.call-update) | async-done | bytes 4194320 | tf_op jit(solution)/shard_map/all_gather | solution.py:313
  128.1 7.5 multiply_bitcast_fusion.1
  135.7 4.5 multiply_convert_fusion.2
  140.1 1.7 fusion.39
  143.3 1.1 reshape_squeeze.19
  144.4 0.7 constant_dynamic-slice_fusion
  145.1 0.6 fusion.51.a_ref
  145.7 56.4 %all-gather.12.cloned.1.call-done = bf16[2048,1024]{1,0:T(8,128)(2,1)} async-done(((bf16[256,1024]{1,0:T(8,128)(2,1)}), bf16[2048,1024]{1,0:T(8,128)(2,1)}) %all-gather.12.cloned.1.call-update) | async-done | bytes 4194320 | tf_op jit(solution)/shard_map/all_gather | solution.py:324
  202.2 9.9 %multiply_bitcast_fusion.gate_ref = f32[1024,1024]{1,0:T(8,128)} fusion(bf16[2048,1024]{1,0:T(8,128)(2,1)} %all-gather.12.cloned.1.call-done, bf16[1,1024,2048]{2,1,0:T(8,128)(2,1)} %all-gather.16.cloned.1.call-done, f32[1024]{0:T(1024)S(1)} %add_rsqrt_fusion), kind=kOutput, calls=%fused_computation.32 | convolution fusion | flops 4296015872 | bytes 12587008 | tf_op jit(solution)/shard_map/dot_general | solution.py:263
  212.1 28.6 %all-reduce.6.cloned.1.call-done = f32[1024,160]{1,0:T(8,128)} async-done(((f32[1024,160]{1,0:T(8,128)}), f32[1024,160]{1,0:T(8,128)}) %all-reduce.6.cloned.1.call-update) | async-done | bytes 655376 | tf_op jit(solution)/shard_map/psum | solution.py:349
  240.7 1.9 slice.226.bc_ref
  242.6 3.7 convolution_add_fusion.pre_ref
  246.3 32.0 %scan_forward.1 = (f32[1024,1024]{1,0:T(8,128)}, bf16[1024,1024]{1,0:T(8,128)(2,1)}, f32[128,16,8,128]{3,2,1,0:T(8,128)}, f32[16,8,128]{2,1,0:T(8,128)}) custom-call(f32[1024,1024]{1,0:T(8,128)} %convolution_add_fusion.pre_ref, bf16[1024,1024]{1,0:T(8,128)(2,1)} %copy-done.6, f32[1024,1024]{1,0:T(8,128)} %multiply_bitcast_fusion.gate_ref, ...), custom_call_target="tpu_custom_call" | custom-call | flops 134217728 | bytes 25165824 | tf_op jit(solution)/shard_map/scan_forward/pallas_call | solution.py:181
  278.3 72.7 %all-gather.14.cloned.1.call-done = bf16[1024,2048]{1,0:T(8,128)(2,1)} async-done(((bf16[128,2048]{1,0:T(8,128)(2,1)}), bf16[1024,2048]{1,0:T(8,128)(2,1)}) %all-gather.14.cloned.1.call-update) | async-done | bytes 4194320 | tf_op jit(solution)/shard_map/all_gather | solution.py:327
  351.0 14.2 %multiply_convert_fusion.1 = (bf16[1024,1024]{1,0:T(8,128)(2,1)}, f32[1024,1024]{1,0:T(8,128)}) fusion(f32[1024,1024]{1,0:T(8,128)} %multiply_bitcast_fusion.gate_ref, f32[1024,1024]{1,0:T(8,128)} %get-tuple-element.34, f32[1024]{0:T(1024)S(1)} %add_rsqrt_fusion, bf16[1024,2048]{1,0:T(8,128)(2,1)} %all-gather.14.cloned.1.call-done, ...), kind=kOutput, calls=%fused_computation.28 | convolution fusion | flops 4308598784 | bytes 23072768 | tf_op jit(solution)/shard_map/dot_general | solution.py:271
  365.2 86.8 %scan_backward.1 = (bf16[1024,1024]{1,0:T(8,128)(2,1)}, f32[1024,1024]{1,0:T(8,128)}, f32[1024,128]{1,0:T(8,128)}, f32[16,8,128]{2,1,0:T(8,128)}, f32[16,8,128]{...) custom-call(f32[1024,1024]{1,0:T(8,128)} %convolution_add_fusion.pre_ref, bf16[1024,1024]{1,0:T(8,128)(2,1)} %copy-done.6, ...), custom_call_target="tpu_custom_call" | custom-call | flops 335544320 | bytes 29360128 | tf_op jit(solution)/shard_map/scan_backward/pallas_call | solution.py:220
  452.1 3.4 fusion.43
  455.4 1.2 copy.185
  456.6 1.1 pad_maximum_fusion.2
  457.7 18.9 %all-reduce.7 = bf16[1024,160]{0,1:T(8,128)(2,1)S(1)} all-reduce(f32[1024,160]{0,1:T(8,128)S(1)} %pad_maximum_fusion.2), channel_id=1, replica_groups=mesh['seg'=8,'seq'=4] {'seq'}, use_global_device_ids=true, to_apply=%region_3.4 | all-reduce | flops 163840 | bytes 983040 | tf_op jit(solution)/shard_map/psum | solution.py:376
  477.2 2.5 fusion.35
  479.8 4.2 add_multiply_fusion
  484.1 4.7 multiply_reduce_fusion.2
  489.0 3.4 concatenate.73
  492.5 8.4 convert_bitcast_fusion.1
  500.9 9.4 %convert_bitcast_fusion = bf16[2048,1024]{0,1:T(8,128)(2,1)} fusion(bf16[1024,1024]{1,0:T(8,128)(2,1)} %get-tuple-element.95, bf16[1,1024,2048]{2,1,0:T(8,128)(2,1)} %all-gather.16.cloned.1.call-done), kind=kOutput, calls=%fused_computation.23 | convolution fusion | flops 4297064448 | bytes 10485760 | tf_op jit(solution)/shard_map/dot_general | solution.py:267
  510.9 9.4 %fusion.19 = bf16[1024,2048]{1,0:T(8,128)(2,1)} fusion(bf16[1024,1024]{1,0:T(8,128)(2,1)} %get-tuple-element.27, bf16[1,1024,2048]{2,1,0:T(8,128)(2,1)} %all-gather.18.cloned.1.call-done), kind=kOutput, calls=%fused_computation.39 | convolution fusion | flops 4297064448 | bytes 10485760 | tf_op jit(solution)/shard_map/dot_general | solution.py:267
  520.3 7.2 fusion.61
  527.5 6.2 add_convert_fusion
  533.8 1.5 copy-done.24
  535.3 8.3 convolution_convert_fusion
  543.6 0.8 slice.229
  544.4 0.9 fusion.56
  545.8 7.4 all_to_all.33
  553.3 0.7 broadcast_in_dim.36
  554.0 0.7 broadcast_in_dim.39
  554.7 0.6 copy.191
  555.9 0.9 convert_element_type.122
  558.5 0.6 slice_bitcast_fusion.1
  559.1 0.6 slice_bitcast_fusion
  559.8 82.9 %reduce-scatter.13.cloned.1.call-done = bf16[256,1024]{0,1:T(8,128)(2,1)} async-done(((bf16[2048,1024]{0,1:T(8,128)(2,1)}), bf16[256,1024]{0,1:T(8,128)(2,1)}) %reduce-scatter.13.cloned.1.call-update) | async-done | bytes 524304 | tf_op jit(solution)/shard_map/reduce_scatter | solution.py:385
  642.6 1.2 copy.194
  643.9 90.8 %reduce-scatter.15.cloned.1.call-done = bf16[256,1024]{0,1:T(8,128)(2,1)} async-done(((bf16[2048,1024]{0,1:T(8,128)(2,1)}), bf16[256,1024]{0,1:T(8,128)(2,1)}) %reduce-scatter.15.cloned.1.call-update) | async-done | bytes 524304 | tf_op jit(solution)/shard_map/reduce_scatter | solution.py:369
  734.6 1.2 copy.195
  736.0 1.1 copy.196
  737.1 4.7 all-to-all-start.2
  741.8 84.3 %reduce-scatter.17.cloned.1.call-done = bf16[128,2048]{1,0:T(8,128)(2,1)} async-done(((bf16[1024,2048]{1,0:T(8,128)(2,1)}), bf16[128,2048]{1,0:T(8,128)(2,1)}) %reduce-scatter.17.cloned.1.call-update) | async-done | bytes 524304 | tf_op jit(solution)/shard_map/reduce_scatter | solution.py:366
  826.1 2.1 convert_element_type.124
  828.2 44.9 %reduce-scatter.11.cloned.1.call-done = bf16[256,2048]{1,0:T(8,128)(2,1)} async-done(((bf16[1024,2048]{1,0:T(8,128)(2,1)}), bf16[256,2048]{1,0:T(8,128)(2,1)}) %reduce-scatter.11.cloned.1.call-update) | async-done | bytes 1048592 | tf_op jit(solution)/shard_map/reduce_scatter | solution.py:389
  873.1 1.7 fusion.31
  874.8 45.3 %reduce-scatter.9.cloned.1.call-done = bf16[256,2048]{1,0:T(8,128)(2,1)} async-done(((bf16[1024,2048]{1,0:T(8,128)(2,1)}), bf16[256,2048]{1,0:T(8,128)(2,1)}) %reduce-scatter.9.cloned.1.call-update) | async-done | bytes 1048592 | tf_op jit(solution)/shard_map/reduce_scatter | solution.py:357
  920.1 3.6 fusion.37
  924.4 2.7 copy.197
  927.1 2.2 reshape.160
  929.3 2.2 broadcast_multiply_fusion
  (121 shorter events, 8.3 us)
Async XLA Ops:
  7.2 57.6 %copy-start = (f32[1,3,4096]{2,0,1:T(1,128)S(1)}, f32[1,3,4096]{2,0,1:T(1,128)}, u32[]{:S(2)}) copy-start(f32[1,3,4096]{2,0,1:T(1,128)} %param.26) | copy-start | bytes 147460
  7.2 58.3 %all-gather.16.cloned.1.call-start = ((), (), s32[]{:S(2)}) async-start(), calls=%async_computation.18 | async-start | bytes 5242880 | tf_op jit(solution)/shard_map/all_gather | solution.py:316
  7.9 120.2 %all-gather.10.cloned.1.call-start = ((), (), s32[]{:S(2)}) async-start(), calls=%async_computation.9 | async-start | bytes 4718592 | tf_op jit(solution)/shard_map/all_gather | solution.py:313
  11.0 27.6 %copy-start.14 = (bf16[128,160]{0,1:T(8,128)(2,1)S(1)}, bf16[128,160]{0,1:T(8,128)(2,1)}, u32[]{:S(2)}) copy-start(bf16[128,160]{0,1:T(8,128)(2,1)} %param.19) | copy-start | bytes 122884
  11.0 27.6 %copy-start.15 = (bf16[128,128]{1,0:T(8,128)(2,1)S(1)}, bf16[128,128]{1,0:T(8,128)(2,1)}, u32[]{:S(2)}) copy-start(bf16[128,128]{1,0:T(8,128)(2,1)} %param.20) | copy-start | bytes 98308
  11.0 27.6 %copy-start.16 = (bf16[16,128]{1,0:T(8,128)(2,1)S(1)}, bf16[16,128]{1,0:T(8,128)(2,1)}, u32[]{:S(2)}) copy-start(bf16[16,128]{1,0:T(8,128)(2,1)} %param.22) | copy-start | bytes 12292
  11.1 27.6 %copy-start.19 = (bf16[4,128]{1,0:T(4,128)(2,1)S(1)}, bf16[4,128]{1,0:T(4,128)(2,1)}, u32[]{:S(2)}) copy-start(bf16[4,128]{1,0:T(4,128)(2,1)} %param.17) | copy-start | bytes 3076
  11.1 27.6 %copy-start.20 = (bf16[128]{0:T(256)(128)(2,1)S(1)}, bf16[128]{0:T(256)(128)(2,1)}, u32[]{:S(2)}) copy-start(bf16[128]{0:T(256)(128)(2,1)} %param.18) | copy-start | bytes 772
  11.1 27.6 %copy-start.21 = (bf16[128]{0:T(256)(128)(2,1)S(1)}, bf16[128]{0:T(256)(128)(2,1)}, u32[]{:S(2)}) copy-start(bf16[128]{0:T(256)(128)(2,1)} %param.21) | copy-start | bytes 772
  11.1 27.6 %copy-start.22 = (bf16[128]{0:T(256)(128)(2,1)S(1)}, bf16[128]{0:T(256)(128)(2,1)}, u32[]{:S(2)}) copy-start(bf16[128]{0:T(256)(128)(2,1)} %param.23) | copy-start | bytes 772
  37.8 164.4 %all-gather.12.cloned.1.call-start = ((), (), s32[]{:S(2)}) async-start(), calls=%async_computation.11 | async-start | bytes 4718592 | tf_op jit(solution)/shard_map/all_gather | solution.py:324
  38.5 202.2 %all-reduce.6.cloned.1.call-start = ((), (), s32[]{:S(2)}) async-start(), calls=%async_computation.10 | async-start | bytes 2097152 | tf_op jit(solution)/shard_map/psum | solution.py:349
  135.6 4.5 copy-start.2
  140.1 2.9 copy-start.6
  141.8 136.5 %all-gather.18.cloned.1.call-start = ((), (), s32[]{:S(2)}) async-start(), calls=%async_computation.19 | async-start | bytes 5242880 | tf_op jit(solution)/shard_map/all_gather | solution.py:328
  142.4 208.6 %all-gather.14.cloned.1.call-start = ((), (), s32[]{:S(2)}) async-start(), calls=%async_computation.12 | async-start | bytes 4718592 | tf_op jit(solution)/shard_map/all_gather | solution.py:327
  143.0 412.9 %reduce-scatter.19.cloned.1.call-start = ((), (), s32[]{:S(2)}) async-start(), calls=%async_computation.20 | async-start | bytes 718848
  452.0 24.6 %copy-start.7 = (bf16[1024,1024]{1,0:T(8,128)(2,1)S(1)}, bf16[1024,1024]{1,0:T(8,128)(2,1)}, u32[]{:S(2)}) copy-start(bf16[1024,1024]{1,0:T(8,128)(2,1)} %copy-done.6) | copy-start | bytes 6291460
  476.6 3.2 copy-start.8
  479.8 4.2 copy-start.3
  484.0 4.8 copy-start.4
  484.1 4.8 copy-start.13
  484.1 4.9 copy-start.17
  484.1 4.9 copy-start.18
  492.4 150.2 %reduce-scatter.13.cloned.1.call-start = ((), (), s32[]{:S(2)}) async-start(), calls=%async_computation.15 | async-start | bytes 4718592 | tf_op jit(solution)/shard_map/reduce_scatter | solution.py:385
  500.9 233.8 %reduce-scatter.15.cloned.1.call-start = ((), (), s32[]{:S(2)}) async-start(), calls=%async_computation.16 | async-start | bytes 4718592 | tf_op jit(solution)/shard_map/reduce_scatter | solution.py:369
  510.4 315.7 %reduce-scatter.17.cloned.1.call-start = ((), (), s32[]{:S(2)}) async-start(), calls=%async_computation.17 | async-start | bytes 4718592 | tf_op jit(solution)/shard_map/reduce_scatter | solution.py:366
  520.3 352.8 %reduce-scatter.11.cloned.1.call-start = ((), (), s32[]{:S(2)}) async-start(), calls=%async_computation.14 | async-start | bytes 5242880 | tf_op jit(solution)/shard_map/reduce_scatter | solution.py:389
  520.3 7.2 copy-start.23
  533.7 1.6 copy-start.24
  533.7 386.3 %reduce-scatter.9.cloned.1.call-start = ((), (), s32[]{:S(2)}) async-start(), calls=%async_computation.13 | async-start | bytes 5242880 | tf_op jit(solution)/shard_map/reduce_scatter | solution.py:357
  543.5 1.8 copy-start.12
  543.6 1.9 copy-start.11
  735.9 137.2 %copy-start.5 = (bf16[1,256,2048]{2,1,0:T(8,128)(2,1)S(1)}, bf16[1,256,2048]{2,1,0:T(8,128)(2,1)}, u32[]{:S(2)}) copy-start(bf16[1,256,2048]{2,1,0:T(8,128)(2,1)} %param.14) | copy-start | bytes 3145732
  736.0 184.1 %copy-start.10 = (bf16[1,256,2048]{2,1,0:T(8,128)(2,1)S(1)}, bf16[1,256,2048]{2,1,0:T(8,128)(2,1)}, u32[]{:S(2)}) copy-start(bf16[1,256,2048]{2,1,0:T(8,128)(2,1)} %param.27) | copy-start | bytes 3145732
  737.1 186.6 %all-to-all-start.2 = ((bf16[1,2,4,64,1024]{4,3,1,0,2:T(8,128)(2,1)}), bf16[1,2,4,64,1024]{4,3,1,0,2:T(8,128)(2,1)S(1)}, u32[]{:S(2)}, u32[]{:S(2)}) async-start(bf16[1,2,4,64,1024]{4,3,1,0,2:T(8,128)(2,1)} %copy.196), calls=%async_computation.6 | async-start | bytes 2097152 | tf_op jit(solution)/shard_map/all_to_all | solution.py:416
  924.4 4.9 copy-start.9
  924.4 7.1 copy-start.1
Sparse Core Ops, SparseCore 0:
  9.6 44.3 all-gather.15
  56.6 71.4 all-gather.9
  130.8 71.3 all-gather.11
  205.0 35.6 all-reduce.5
  242.1 35.6 all-gather.17
  279.8 71.1 all-gather.13
  492.6 57.1 reduce-scatter.18
  553.3 89.2 reduce-scatter.12
  646.3 88.3 reduce-scatter.14
  738.1 87.9 reduce-scatter.16
  828.6 44.4 reduce-scatter.10
  875.5 44.5 reduce-scatter.8

commit v2 on v1

--- a/solution.py
+++ b/solution.py
@@ -259,6 +259,554 @@
     )(pre, act, gy, bc, a2, skip, checks)
 
 
+MESH_ID = pl.DeviceIdType.MESH
+VMEM_MOST = 60 * 1024 * 1024
+
+
+class Grid:
+    def __init__(self, axis, lines, fast):
+        self.axis, self.lines, self.fast = axis, lines, fast
+        self.here = lax.axis_index(axis)
+        self.line = self.here // fast
+        self.lane = self.here - self.line * fast
+
+    def at(self, line, lane):
+        return line * self.fast + lane
+
+    def line_peer(self, k):
+        return lax.rem(self.line + k, self.lines)
+
+    def lane_peer(self, e):
+        return lax.rem(self.lane + e, self.fast)
+
+    def copy(self, src, dst, sent, got, index):
+        return pltpu.make_async_remote_copy(
+            src_ref=src, dst_ref=dst, send_sem=sent, recv_sem=got,
+            device_id={self.axis: index}, device_id_type=MESH_ID,
+        )
+
+
+def meet(groups):
+    barrier = pltpu.get_barrier_semaphore()
+    total = 0
+    for grid in groups:
+        size = grid.lines * grid.fast
+        for k in range(1, size):
+            pl.semaphore_signal(
+                barrier, inc=1, device_id={grid.axis: lax.rem(grid.here + k, size)},
+                device_id_type=MESH_ID,
+            )
+        total += size - 1
+    pl.semaphore_wait(barrier, total)
+
+
+class Gather:
+    def __init__(self, grid, own, out, sems):
+        self.grid, self.own, self.out = grid, own, out
+        self.up_s, self.up_r, self.dn_s, self.dn_r, self.x_s, self.x_r = sems
+
+    @staticmethod
+    def semaphores(lines, fast):
+        hops = pltpu.SemaphoreType.DMA((lines,))
+        across = pltpu.SemaphoreType.DMA((lines, fast))
+        return [hops, hops, hops, hops, across, across]
+
+    def block(self, line, lane=None):
+        grid = self.grid
+        return self.out.at[grid.at(line, grid.lane if lane is None else lane)]
+
+    def up(self, k):
+        grid = self.grid
+        block = self.block(jnp.maximum(grid.line - k, 0))
+        return grid.copy(
+            self.own if k == 0 else block, block, self.up_s.at[k], self.up_r.at[k],
+            grid.at(jnp.minimum(grid.line + 1, grid.lines - 1), grid.lane),
+        )
+
+    def down(self, k):
+        grid = self.grid
+        block = self.block(jnp.minimum(grid.line + k, grid.lines - 1))
+        return grid.copy(
+            self.own if k == 0 else block, block, self.dn_s.at[k], self.dn_r.at[k],
+            grid.at(jnp.maximum(grid.line - 1, 0), grid.lane),
+        )
+
+    def sends_up(self, k):
+        return jnp.logical_and(self.grid.line + 1 < self.grid.lines, self.grid.line >= k)
+
+    def sends_down(self, k):
+        return jnp.logical_and(self.grid.line > 0, self.grid.line + k < self.grid.lines)
+
+    def across(self, line, slot, e, own=False):
+        grid = self.grid
+        block = self.block(line)
+        return grid.copy(
+            self.own if own else block, block, self.x_s.at[slot, e], self.x_r.at[slot, e],
+            grid.at(grid.line, grid.lane_peer(e)),
+        )
+
+    def slots(self):
+        return range(self.grid.lines)
+
+    def begin(self):
+        grid = self.grid
+        for when, copy in ((self.sends_up(0), self.up(0)), (self.sends_down(0), self.down(0))):
+            pl.when(when)(copy.start)
+        for e in range(1, grid.fast):
+            self.across(grid.line, 0, e, own=True).start()
+
+    def step(self, k):
+        grid = self.grid
+
+        def arrived(copy, line, slot, forward, onward):
+            copy.wait_recv()
+            if k < grid.lines - 1:
+                pl.when(forward(k))(onward(k).start)
+            for e in range(1, grid.fast):
+                self.across(line, slot, e).start()
+
+        below, above = grid.line - k, grid.line + k
+
+        @pl.when(below >= 0)
+        def _():
+            arrived(self.up(k - 1), below, grid.lines - k, self.sends_up, self.up)
+
+        @pl.when(above < grid.lines)
+        def _():
+            arrived(self.down(k - 1), above, k, self.sends_down, self.down)
+
+    def finish(self):
+        grid = self.grid
+        for k in range(grid.lines - 1):
+            pl.when(self.sends_up(k))(self.up(k).wait_send)
+            pl.when(self.sends_down(k))(self.down(k).wait_send)
+        for slot in self.slots():
+            for e in range(1, grid.fast):
+                copy = self.across(grid.line_peer(slot), slot, e, own=slot == 0)
+                copy.wait_send()
+                copy.wait_recv()
+
+
+class Scatter:
+    def __init__(self, grid, src, scratch):
+        self.grid, self.src = grid, src
+        (
+            self.xbuf, self.own, self.stage, self.zbuf, self.acc,
+            self.x_s, self.x_r, self.z_s, self.z_r, self.o_s,
+        ) = scratch
+
+    @staticmethod
+    def scratch(lines, fast, shape):
+        dma = pltpu.SemaphoreType.DMA
+        return [
+            pltpu.VMEM((lines, fast - 1) + shape, BF16),
+            pltpu.VMEM((lines,) + shape, BF16),
+            pltpu.VMEM((lines - 1,) + shape, BF16),
+            pltpu.VMEM((lines - 1,) + shape, BF16),
+            pltpu.VMEM(shape, F32),
+            dma((lines, fast)), dma((lines, fast)), dma((lines,)), dma((lines,)), dma((lines,)),
+        ]
+
+    def across(self, k, e):
+        grid = self.grid
+        lane = grid.lane_peer(e)
+        return grid.copy(
+            self.src.at[grid.at(grid.line_peer(k), lane)], self.xbuf.at[k, e - 1],
+            self.x_s.at[k, e], self.x_r.at[k, e], grid.at(grid.line, lane),
+        )
+
+    def local(self, k):
+        grid = self.grid
+        return pltpu.make_async_copy(
+            self.src.at[grid.at(grid.line_peer(k), grid.lane)], self.own.at[k], self.o_s.at[k]
+        )
+
+    def along(self, k):
+        grid = self.grid
+        return grid.copy(
+            self.stage.at[k - 1], self.zbuf.at[k - 1], self.z_s.at[k], self.z_r.at[k],
+            grid.at(grid.line_peer(k), grid.lane),
+        )
+
+    def order(self):
+        return list(range(self.grid.lines - 1, -1, -1))
+
+    def begin(self):
+        for k in self.order():
+            for e in range(1, self.grid.fast):
+                self.across(k, e).start()
+            self.local(k).start()
+
+    def rows(self, step):
+        count = self.acc.shape[0]
+        size = 16 if count % 16 == 0 else 8
+        def run(i, carry):
+            step(pl.ds(pl.multiple_of(i * size, size), size))
+            return carry
+        lax.fori_loop(0, count // size, run, 0)
+
+    def middle(self, k):
+        for e in range(1, self.grid.fast):
+            self.across(k, e).wait_recv()
+        self.local(k).wait()
+
+        def add(at):
+            total = self.own[k, at, :].astype(F32)
+            for e in range(self.grid.fast - 1):
+                total = total + self.xbuf[k, e, at, :].astype(F32)
+            if k > 0:
+                self.stage[k - 1, at, :] = total.astype(BF16)
+            else:
+                self.acc[at, :] = total
+
+        self.rows(add)
+        if k > 0:
+            self.along(k).start()
+
+    def finish(self, out_ref):
+        for k in range(1, self.grid.lines):
+            self.along(k).wait_recv()
+
+        def add(at):
+            total = self.acc[at, :]
+            for k in range(self.grid.lines - 1):
+                total = total + self.zbuf[k, at, :].astype(F32)
+            out_ref[at, :] = total.astype(out_ref.dtype)
+
+        self.rows(add)
+
+    def drain(self):
+        for k in self.order():
+            for e in range(1, self.grid.fast):
+                self.across(k, e).wait_send()
+            if k > 0:
+                self.along(k).wait_send()
+
+
+class Exchange:
+    def __init__(self, grid, src, dst, sems):
+        self.grid, self.src, self.dst = grid, src, dst
+        self.sent, self.got = sems
+        self.size = grid.lines * grid.fast
+
+    @staticmethod
+    def semaphores(size):
+        return [pltpu.SemaphoreType.DMA((size,)), pltpu.SemaphoreType.DMA((size,))]
+
+    def one(self, k):
+        grid = self.grid
+        peer = lax.rem(grid.here + k, self.size)
+        return grid.copy(
+            self.src(peer), self.dst(grid.here), self.sent.at[k], self.got.at[k], peer
+        )
+
+    def begin(self):
+        for k in range(1, self.size):
+            self.one(k).start()
+
+    def arrived(self):
+        for k in range(1, self.size):
+            self.one(k).wait_recv()
+
+    def drain(self):
+        for k in range(1, self.size):
+            self.one(k).wait_send()
+
+
+ANY = pl.BlockSpec(memory_space=pl.ANY)
+INSIDE = pl.BlockSpec(memory_space=pltpu.VMEM)
+
+
+def comm_params(collective_id):
+    return pltpu.CompilerParams(
+        collective_id=collective_id, has_side_effects=True, vmem_limit_bytes=VMEM_MOST
+    )
+
+
+def grids(shape):
+    lines, fast, seq_lines = shape
+    return Grid("seg", lines, fast), Grid("seq", seq_lines, 2)
+
+
+def gather_kernel(
+    shape, scaled, small, tokens,
+    w_x, small_all, tok, g_part,
+    x_part, tok_in, g_own, local_s, x_sems, small_sems, tok_sems, swap_x, swap_g,
+):
+    seg, seq = grids(shape)
+    load_tok = pltpu.make_async_copy(tokens, tok_in, local_s.at[0])
+    load_own = pltpu.make_async_copy(scaled.at[seq.here, 0], x_part.at[seq.here], local_s.at[1])
+    load_gate = pltpu.make_async_copy(scaled.at[seq.here, 1], g_own, local_s.at[3])
+    load_tok.start()
+    load_own.start()
+    load_gate.start()
+    meet((seg, seq))
+    swap_x = Exchange(seq, lambda p: scaled.at[p, 0], lambda m: x_part.at[m], swap_x)
+    swap_g = Exchange(seq, lambda p: scaled.at[p, 1], lambda m: g_part.at[m], swap_g)
+    swap_x.begin()
+    smalls = Gather(seg, small, small_all, small_sems)
+    smalls.begin()
+    load_tok.wait()
+    toks = Gather(seq, tok_in, tok, tok_sems)
+    toks.begin()
+    store_tok = pltpu.make_async_copy(tok_in, tok.at[seq.here], local_s.at[0])
+    store_small = pltpu.make_async_copy(small, small_all.at[seg.here], local_s.at[2])
+    store_tok.start()
+    store_small.start()
+    load_gate.wait()
+    store_gate = pltpu.make_async_copy(g_own, g_part.at[seq.here], local_s.at[3])
+    store_gate.start()
+    load_own.wait()
+    swap_x.arrived()
+    halves = Gather(seg, x_part, w_x, x_sems)
+    halves.begin()
+    store_own = pltpu.make_async_copy(x_part, w_x.at[seg.here], local_s.at[1])
+    store_own.start()
+    swap_g.begin()
+    for k in range(1, seq.lines):
+        toks.step(k)
+    for k in range(1, seg.lines):
+        smalls.step(k)
+        halves.step(k)
+    toks.finish()
+    smalls.finish()
+    halves.finish()
+    swap_g.arrived()
+    swap_x.drain()
+    swap_g.drain()
+    store_tok.wait()
+    store_small.wait()
+    store_gate.wait()
+    store_own.wait()
+
+
+def gather_start(shape, scaled, small, tokens):
+    lines, fast, seq_lines = shape
+    segs, seqs = lines * fast, seq_lines * 2
+    rows, feats = scaled.shape[2:]
+    sems = Gather.semaphores
+    flat = [
+        pltpu.VMEM((seqs, rows, feats), BF16),
+        pltpu.VMEM(tokens.shape, BF16),
+        pltpu.VMEM((rows, feats), BF16),
+        pltpu.SemaphoreType.DMA((4,)),
+        *sems(lines, fast), *sems(lines, fast), *sems(seq_lines, 2),
+        *Exchange.semaphores(seqs), *Exchange.semaphores(seqs),
+    ]
+
+    def kernel(*refs):
+        ins, rest = refs[:7], refs[7:]
+        gather_kernel(
+            shape, *ins, *rest[:4], rest[4:10], rest[10:16], rest[16:22], rest[22:24], rest[24:26]
+        )
+
+    w_x, small_all, tok, g_part = pl.pallas_call(
+        kernel,
+        in_specs=[ANY, INSIDE, ANY],
+        out_specs=[ANY] * 4,
+        out_shape=[
+            jax.ShapeDtypeStruct((segs, seqs, rows, feats), BF16),
+            jax.ShapeDtypeStruct((segs,) + small.shape, BF16),
+            jax.ShapeDtypeStruct((seqs,) + tokens.shape, BF16),
+            jax.ShapeDtypeStruct((seqs, rows, feats), BF16),
+        ],
+        scratch_shapes=flat,
+        compiler_params=comm_params(1),
+        name="gather_start",
+    )(scaled, small, tokens)
+    return w_x.reshape(-1, feats), small_all, tok.reshape(-1, tokens.shape[1]), g_part
+
+
+def total_kernel(shape, call, x_ref, out_ref, half, got, mine, others, whole, sems):
+    _, seq = grids(shape)
+    lane_s, lane_r, line_s, line_r, back_s, back_r = sems
+    width = x_ref.shape[1] // 2
+    lines = seq.lines
+    barrier = pltpu.get_barrier_semaphore()
+    other = 1 - seq.lane
+    for peer in [seq.at(seq.line, other)] + [
+        seq.at(seq.line_peer(k), seq.lane) for k in range(1, lines)
+    ]:
+        pl.semaphore_signal(barrier, inc=1, device_id={"seq": peer}, device_id_type=MESH_ID)
+    pl.semaphore_wait(barrier, lines)
+    left = pl.ds(0, width)
+    right = pl.ds(width, width)
+
+    @pl.when(seq.lane == 0)
+    def _():
+        half[...] = x_ref[:, right].astype(BF16)
+
+    @pl.when(seq.lane == 1)
+    def _():
+        half[...] = x_ref[:, left].astype(BF16)
+
+    swap = seq.copy(half, got, lane_s, lane_r, seq.at(seq.line, other))
+    swap.start()
+    swap.wait()
+
+    @pl.when(seq.lane == 0)
+    def _():
+        mine[...] = (x_ref[:, left] + got[...].astype(F32)).astype(BF16)
+
+    @pl.when(seq.lane == 1)
+    def _():
+        mine[...] = (x_ref[:, right] + got[...].astype(F32)).astype(BF16)
+
+    copies = [
+        seq.copy(
+            mine, others.at[k - 1], line_s.at[k], line_r.at[k], seq.at(seq.line_peer(k), seq.lane)
+        )
+        for k in range(1, lines)
+    ]
+    for copy in copies:
+        copy.start()
+    for copy in copies:
+        copy.wait()
+    total = mine[...].astype(F32)
+    for k in range(lines - 1):
+        total = total + others[k].astype(F32)
+    whole[seq.lane] = total.astype(BF16)
+    back = seq.copy(
+        whole.at[seq.lane], whole.at[seq.lane], back_s, back_r, seq.at(seq.line, other)
+    )
+    back.start()
+    back.wait()
+    out_ref[:, left] = whole[0]
+    out_ref[:, right] = whole[1]
+
+
+def total_over_seq(shape, x, collective_id):
+    lines = shape[2]
+    rows, width = x.shape
+    part = pltpu.VMEM((rows, width // 2), BF16)
+    dma = pltpu.SemaphoreType.DMA
+
+    def kernel(x_ref, out_ref, half, got, mine, others, whole, *sems):
+        total_kernel(shape, collective_id, x_ref, out_ref, half, got, mine, others, whole, sems)
+
+    return pl.pallas_call(
+        kernel,
+        in_specs=[INSIDE],
+        out_specs=INSIDE,
+        out_shape=jax.ShapeDtypeStruct(x.shape, BF16),
+        scratch_shapes=[
+            part, part, part,
+            pltpu.VMEM((max(lines - 1, 1), rows, width // 2), BF16),
+            pltpu.VMEM((2, rows, width // 2), BF16),
+            dma, dma, dma((lines,)), dma((lines,)), dma, dma,
+        ],
+        compiler_params=comm_params(collective_id),
+        name="total_over_seq",
+    )(x)
+
+
+def scatter_end(shape, over_seg, over_seq, ends):
+    lines, fast, seq_lines = shape
+    seqs = seq_lines * 2
+    count = len(over_seg)
+    blocks = [a.shape[1:] for a in over_seg]
+    own_rows = blocks[1][0] // seqs
+    feats = blocks[1][1]
+    scratch = []
+    spans = []
+    for block in blocks:
+        part = Scatter.scratch(lines, fast, tuple(block))
+        spans.append((len(scratch), len(scratch) + len(part)))
+        scratch += part
+    part = Scatter.scratch(seq_lines, 2, tuple(over_seq.shape[1:]))
+    spans.append((len(scratch), len(scratch) + len(part)))
+    scratch += part
+    tail = len(scratch)
+    scratch += [
+        pltpu.VMEM((2, blocks[1][0], feats), BF16),
+        *Exchange.semaphores(seqs), *Exchange.semaphores(seqs), *Exchange.semaphores(seqs),
+        pltpu.SemaphoreType.DMA((3,)),
+    ]
+
+    def kernel(*refs):
+        srcs = refs[:count]
+        q_src, ends_in = refs[count : count + 2]
+        small_out, out_out, halves_out, q_out, ends_out = refs[count + 2 : count + 7]
+        sc = refs[count + 7 :]
+        seg, seq = grids(shape)
+        meet((seg, seq))
+        scatters = [Scatter(seg, s, sc[a:b]) for s, (a, b) in zip(srcs, spans)]
+        q_sum = Scatter(seq, q_src, sc[spans[-1][0] : spans[-1][1]])
+        halves = sc[tail]
+        sems = sc[tail + 1 : tail + 7]
+        local = sc[tail + 7]
+        end_swap = Exchange(
+            seq, lambda p: ends_in.at[p], lambda m: ends_out.at[m], sems[:2]
+        )
+        end_swap.begin()
+        q_sum.begin()
+        for s in scatters:
+            s.begin()
+
+        def swap(half, pair):
+            return Exchange(
+                seq,
+                lambda p: halves.at[half, pl.ds(pl.multiple_of(p * own_rows, own_rows), own_rows)],
+                lambda m: halves_out.at[half, m],
+                pair,
+            )
+
+        swaps = [swap(0, sems[2:4]), swap(1, sems[4:6])]
+        small, x_half, g_half, out = scatters
+        outs = {0: small_out, 1: halves.at[0], 2: halves.at[1], 3: out_out}
+        for k in q_sum.order():
+            q_sum.middle(k)
+        for i, s in enumerate(scatters):
+            for j, k in enumerate(s.order()):
+                s.middle(k)
+                if i > 0 and j == min(1, lines - 1):
+                    scatters[i - 1].finish(outs[i - 1])
+                    if i - 1 in (1, 2):
+                        swaps[i - 2].begin()
+            if i == 0:
+                q_sum.finish(q_out)
+        out.finish(out_out)
+        own = []
+        for half in (0, 1):
+            own.append(
+                pltpu.make_async_copy(
+                    halves.at[
+                        half, pl.ds(pl.multiple_of(seq.here * own_rows, own_rows), own_rows)
+                    ],
+                    halves_out.at[half, seq.here],
+                    local.at[half],
+                )
+            )
+        own.append(
+            pltpu.make_async_copy(ends_in.at[seq.here], ends_out.at[seq.here], local.at[2])
+        )
+        for copy in own:
+            copy.start()
+        for s in scatters + [q_sum]:
+            s.drain()
+        for e in swaps + [end_swap]:
+            e.arrived()
+            e.drain()
+        for copy in own:
+            copy.wait()
+
+    return pl.pallas_call(
+        kernel,
+        in_specs=[ANY] * (count + 1) + [INSIDE],
+        out_specs=[INSIDE] * 5,
+        out_shape=[
+            jax.ShapeDtypeStruct(blocks[0], F32),
+            jax.ShapeDtypeStruct(blocks[3], F32),
+            jax.ShapeDtypeStruct((2, seqs, own_rows, feats), BF16),
+            jax.ShapeDtypeStruct(over_seq.shape[1:], F32),
+            jax.ShapeDtypeStruct(ends.shape, F32),
+        ],
+        scratch_shapes=scratch,
+        compiler_params=comm_params(4),
+        name="scatter_end",
+    )(*over_seg, over_seq, ends)
+
+
 def dot_nn(a, b):
     return jnp.dot(a, b, preferred_element_type=F32)
 
@@ -287,21 +835,13 @@
     own_len, model = tokens.shape[1:]
     length = own_len * seqs
     block = 64
+    seq_lines = seqs // 2
+    shape = (segs // seq_lines, seq_lines, seq_lines)
 
     def mine(rows):
         shaped = rows.reshape(rows.shape[0], segs, seqs, part)
         return lax.dynamic_index_in_dim(shaped, place, 2, keepdims=False).reshape(
             rows.shape[0], feats
-        )
-
-    def to_contiguous(rows):
-        count = rows.shape[0]
-        shaped = rows.reshape(count, seqs, (segs // seqs) * part)
-        got = lax.all_to_all(shaped, "seq", 1, 0, tiled=False)
-        return (
-            got.reshape(seqs, count, segs // seqs, part)
-            .transpose(1, 2, 0, 3)
-            .reshape(count, feats)
         )
 
     gain_col = norm_gain.astype(F32)[:, None]
@@ -309,20 +849,16 @@
     scaled = (own_weight * gain_col).astype(BF16)
     scaled = scaled.reshape(own_rows, 2, segs, seqs, part).transpose(3, 1, 0, 2, 4)
     scaled = scaled.reshape(seqs, 2, own_rows, feats)
-    swapped = lax.all_to_all(scaled, "seq", 0, 0, tiled=False)
-    w_x_half = lax.all_gather(
-        swapped[:, 0].reshape(seqs * own_rows, feats), "seg", axis=0, tiled=True
-    )
-    tok = lax.all_gather(tokens[0], "seq", axis=0, tiled=True)
     small = jnp.concatenate(
         [
             dt_proj, x_proj.T, a_log, conv_weight, conv_bias[None], dt_bias[None], d_skip[None],
         ],
         axis=0,
     )
-    small_all = lax.all_gather(small, "seg", axis=0, tiled=False)
+    small = jnp.pad(small, ((0, -small.shape[0] % 16), (0, 0)))
+    w_x_half, small_all, tok, g_part = gather_start(shape, scaled, small, tokens[0])
     w_g_half = lax.all_gather(
-        swapped[:, 1].reshape(seqs * own_rows, feats), "seg", axis=0, tiled=True
+        g_part.reshape(seqs * own_rows, feats), "seg", axis=0, tiled=True
     )
     w_out = lax.all_gather(out_proj, "seg", axis=0, tiled=True)
     cot = lax.all_gather(cotangent[0], "seq", axis=0, tiled=True)
@@ -346,10 +882,10 @@
     padded = jnp.concatenate([head, x_in], axis=0)
     conv_out = b_conv + sum(kernel[k] * padded[k : k + length] for k in range(taps))
     act = jax.nn.silu(conv_out).astype(BF16)
-    mixed_x = lax.psum(dot_nt(act, w_xt), "seq")
-    dt_low = mixed_x[:, :low_rank].astype(BF16)
-    bc = mixed_x[:, low_rank:]
-    pre = dot_nn(dt_low, w_dt) + b_dt
+    mixed_x = total_over_seq(shape, dot_nt(w_xt, act), 2)
+    dt_low = mixed_x[:low_rank]
+    bc = mixed_x[low_rank:].astype(F32).T
+    pre = dot_tn(dt_low, w_dt) + b_dt
     gate = rstd * dot_nn(tok, w_g_half)
     init = mine(init_state[0]).reshape(width, planes, LANES)
     y_val, gated, checks, final = forward_scan(pre, act, gate, bc, a2, skip, init, block)
@@ -363,18 +899,14 @@
     gs_gate = (
         rstd * g_gated * y_val * sig_gate * (1.0 + gate * (1.0 - sig_gate))
     ).astype(BF16)
-    out_grad = lax.psum_scatter(
-        dot_tn(gated, cot).astype(BF16), "seg", scatter_dimension=0, tiled=True
-    )
-    gate_grad = lax.psum_scatter(
-        dot_tn(tok, gs_gate).astype(BF16), "seg", scatter_dimension=0, tiled=True
-    )
+    out_grad = dot_tn(gated, cot).astype(BF16)
+    gate_grad = dot_tn(tok, gs_gate).astype(BF16)
     g_dtpre, g_actp, g_bc, a_sum, start, dtb_grad, skip_grad = backward_scan(
         pre, act, gy, bc, a2, skip, checks, block
     )
-    g_mixed = jnp.concatenate([dot_nt(g_dtpre, w_dt), g_bc[:, : 2 * width]], axis=1)
-    g_mixed = lax.psum(g_mixed, "seq").astype(BF16)
-    g_act = g_actp + dot_nn(g_mixed, w_xt)
+    g_mixed = jnp.concatenate([dot_nt(w_dt, g_dtpre), g_bc[:, : 2 * width].T], axis=0)
+    g_mixed = total_over_seq(shape, g_mixed, 3)
+    g_act = g_actp + dot_tn(g_mixed, w_xt)
     sig_conv = jax.nn.sigmoid(conv_out)
     g_conv = g_act * sig_conv * (1.0 + conv_out * (1.0 - sig_conv))
     tail = jnp.concatenate([g_conv, jnp.zeros((history, feats), F32)], axis=0)
@@ -382,17 +914,14 @@
     g_xin = sum(kernel[k] * tail[history - k : history - k + length] for k in range(taps))
     head_grad = sum(kernel[k] * whole[history - k : 2 * history - k] for k in range(taps))
     gs_x = (rstd * g_xin).astype(BF16)
-    x_grad = lax.psum_scatter(
-        dot_tn(tok, gs_x).astype(BF16), "seg", scatter_dimension=0, tiled=True
-    )
+    x_grad = dot_tn(tok, gs_x).astype(BF16)
     q_part = (dot_nt(gs_gate, w_g_half) + dot_nt(gs_x, w_x_half)).astype(BF16)
-    q_own = lax.psum_scatter(q_part, "seq", scatter_dimension=0, tiled=True).astype(F32)
 
     cw_grad = jnp.stack([jnp.sum(g_conv * padded[k : k + length], axis=0) for k in range(taps)])
     grads = jnp.concatenate(
         [
-            dot_tn(dt_low, g_dtpre),
-            dot_tn(g_mixed, act),
+            dot_nn(dt_low, g_dtpre),
+            dot_nn(g_mixed, act),
             a_sum.reshape(width, feats) * a_mat,
             cw_grad,
             jnp.sum(g_conv, axis=0, keepdims=True),
@@ -401,9 +930,34 @@
         ],
         axis=0,
     )
+    grads = jnp.pad(grads, ((0, -grads.shape[0] % 16), (0, 0)))
     grads = grads.reshape(grads.shape[0], segs, part).transpose(1, 0, 2).astype(BF16)
-    grads = lax.psum_scatter(grads, "seg", scatter_dimension=0, tiled=False).astype(F32)
-
+    ends = jnp.concatenate(
+        [
+            final.reshape(width, feats),
+            x_in[length - history :],
+            start.reshape(width, feats),
+            head_grad,
+        ],
+        axis=0,
+    )
+    ends = jnp.pad(ends, ((0, -ends.shape[0] % 8), (0, 0)))
+    grads, out_grad, halves, q_own, ends = scatter_end(
+        shape,
+        [
+            grads,
+            x_grad.reshape(segs, seqs * own_rows, feats),
+            gate_grad.reshape(segs, seqs * own_rows, feats),
+            out_grad.reshape(segs, part, model),
+        ],
+        q_part.reshape(seqs, own_len, model),
+        ends.reshape(ends.shape[0], seqs, feats // seqs).transpose(1, 0, 2),
+    )
+    ends = (
+        ends.reshape(seqs, ends.shape[1], segs // seqs, part)
+        .transpose(1, 2, 0, 3)
+        .reshape(ends.shape[1], feats)
+    )
     own = tokens[0].astype(F32)
     own_rstd = lax.rsqrt(jnp.mean(own * own, axis=1, keepdims=True) + EPSILON)
     input_grad = (
@@ -412,28 +966,15 @@
         - own * (own_rstd * own_rstd) * jnp.mean(q_own * own, axis=1, keepdims=True)
     ).astype(BF16)
 
-    halves = jnp.stack([x_grad, gate_grad]).reshape(2, seqs, own_rows, feats)
-    halves = lax.all_to_all(halves, "seq", 1, 0, tiled=False)
     raw_grad = (
-        halves.reshape(seqs, 2, own_rows, segs, part)
-        .transpose(2, 1, 3, 0, 4)
+        halves.reshape(2, seqs, own_rows, segs, part)
+        .transpose(2, 0, 3, 1, 4)
         .reshape(own_rows, both)
         .astype(F32)
     )
     in_grad = raw_grad * gain_col
     gain_grad = jnp.sum(raw_grad * own_weight, axis=1)
 
-    ends = to_contiguous(
-        jnp.concatenate(
-            [
-                final.reshape(width, feats),
-                x_in[length - history :],
-                start.reshape(width, feats),
-                head_grad,
-            ],
-            axis=0,
-        )
-    )
     at = width + history
     xp_at = low_rank + x_proj.shape[1]
     return (
@@ -442,7 +983,7 @@
         ends[None, width:at],
         input_grad[None],
         ends[None, at : at + width],
-        ends[None, at + width :],
+        ends[None, at + width : at + width + history],
         gain_grad,
         in_grad,
         grads[xp_at + width : xp_at + width + taps],
@@ -452,7 +993,7 @@
         grads[xp_at + width + taps + 1],
         grads[xp_at : xp_at + width],
         grads[xp_at + width + taps + 2],
-        out_grad.astype(F32),
+        out_grad,
     )
 
 

time: 945 us -> 656 us (0.69)
  waiting for transfers between devices: 568 us -> 99 us
  Pallas kernels: 119 us -> 391 us
  blocking collectives: 77.3 us -> 0 us
  matrix products: 96.4 us -> 86.3 us
    reduce_scatter x4 -> x0, waiting for transfers between devices: 303 us -> none  [the longest x1 90.8 us: body(): lax.psum_scatter(dot_tn(tok, gs_gate).astype(BF16), 'seg', scatter_dimens...]
    pallas_call x0 -> x4, Pallas kernels: none -> 272 us  [the longest x1 171 us: scatter_end(): pl.pallas_call(kernel, in_specs=[ANY] * (count + 1) + [INSIDE], out_specs...]
    all_gather x3 -> x1, waiting for transfers between devices: 116 us -> 30 us  [body(): lax.all_gather(g_part.reshape(seqs * own_rows, feats), 'seg', axis=0, til...]
    reduce_scatter x1, waiting for transfers between devices: 45.3 us -> 0.01 us  [body(): lax.psum_scatter(out_part, 'seq', scatter_dimension=0, tiled=True)]
    all_to_all x2 -> x0, blocking collectives: 32.5 us -> none  [the longest x1 25.1 us: body(): swapped = lax.all_to_all(scaled, 'seq', 0, 0, tiled=False)]
    psum x1 -> x0, waiting for transfers between devices: 28.6 us -> none  [body(): mixed_x = lax.psum(dot_nt(act, w_xt), 'seq')]
    all_gather x1 -> x0, blocking collectives: 25.9 us -> none  [body(): small_all = lax.all_gather(small, 'seg', axis=0, tiled=False)]
    psum x1 -> x0, blocking collectives: 18.9 us -> none  [body(): g_mixed = lax.psum(g_mixed, 'seq').astype(BF16)]
  transfers between devices with their start and end apart: 13 -> 4, of which waited for: 9 -> 2; matrix products, arithmetic and copies ran while one was open for 12% -> 15% of each run, Pallas kernels for 3% -> 33%
where the time goes in v2:
time: 656 us; the launch traced here: 649 us
  Pallas kernels  391 us (60%)
  waiting for transfers between devices  99 us (15%)
  matrix products  86.3 us (13%)
  local copies, waits for them, and re-layouts  29.2 us (4%)
  other arithmetic  28.4 us (4%)
  between operations  14.6 us (2%)
    pallas_call x1, Pallas kernels, scatter_end(): pl.pallas_call(kernel, in_specs=[ANY] * (count + 1) + [INSIDE], out_specs...  171 us
    pallas_call x1, Pallas kernels, backward_scan(): pl.pallas_call(backward_kernel, grid=(steps,), in_specs=[rows, rows, rows...  86.8 us
    pallas_call x1, Pallas kernels, gather_start(): pl.pallas_call(kernel, in_specs=[ANY, INSIDE, ANY], out_specs=[ANY] * 4,...  74.7 us
    all_gather x1, waiting for transfers between devices, body(): w_out = lax.all_gather(out_proj, 'seg', axis=0, tiled=True)  67.6 us
    dot_general x5, matrix products, dot_tn(): lax.dot_general(a, b, (((0,), (0,)), ((), ())), preferred_element_type=F32)  32.7 us
    pallas_call x1, Pallas kernels, forward_scan(): pl.pallas_call(forward_kernel, grid=(steps,), in_specs=[rows, rows, rows,...  32 us
    all_gather x1, waiting for transfers between devices, body(): lax.all_gather(g_part.reshape(seqs * own_rows, feats), 'seg', axis=0, til...  30 us
    dot_general x5, matrix products, dot_nt(): lax.dot_general(a, b, (((1,), (1,)), ((), ())), preferred_element_type=F32)  28.9 us
  transfers between devices with their start and end apart: 4, of which 2 were waited for; matrix products, arithmetic and copies ran while one was open for 15% of the time, Pallas kernels for 33%

profile of v2, /device:TPU:1, one launch (start us, length us, event | category | flops | bytes accessed | tf_op | source)
XLA Modules:
  0.0 648.9 jit_solution(298804504754828465)
XLA Ops:
  7.2 0.7 convert_element_type.82
  8.0 1.5 fusion.10
  9.5 0.8 reshape.152
  10.4 1.3 reshape.153.refs_0_
  11.8 0.6 pad.16.refs_1_
  12.4 74.7 %gather_start.1 = (bf16[8,4,64,1024]{3,2,1,0:T(8,128)(2,1)}, bf16[8,320,128]{2,1,0:T(8,128)(2,1)}, bf16[4,256,2048]{2,1,0:T(8,128)(2,1)}, bf16[4,64,1024]{2,1,0:T(8,128)(2,1)}) custom-call(bf16[4,2,64,1024]{3,2,1,0:T(8,128)(2,1)} %reshape.153.refs_0_, bf16[320,128]{1,0:T(8,128)(2,1)} %pad.16.refs_1_, bf16[256,2048]{1,0:T(8,128)(2,1)} %bitcast.151), custom_call_target="tpu_custom_call" | custom-call | tf_op jit(solution)/shard_map/gather_start/pallas_call | solution.py:603
  87.3 0.7 all-gather.9.cloned.1.call-update
  88.0 0.7 all-gather.7.cloned.1.call-update
  88.8 1.5 copy.92
  90.3 3.1 multiply_reduce_fusion
  93.5 7.7 %convolution_multiply_fusion.1 = f32[1024,1024]{1,0:T(8,128)S(1)} fusion(bf16[1024,2048]{1,0:T(8,128)(2,1)} %bitcast.153, bf16[2048,1024]{1,0:T(8,128)(2,1)} %bitcast.195, f32[1024]{0:T(1024)S(1)} %bitcast.184), kind=kOutput, calls=%fused_computation.38 | convolution fusion | flops 4296015872 | bytes 12587008 | tf_op jit(solution)/shard_map/dot_general | solution.py:811
  101.2 0.7 fusion.41
  101.9 4.1 multiply_convert_fusion.2
  106.0 1.7 fusion.21.x_ref
  107.7 14.0 %total_over_seq.2 = bf16[160,1024]{1,0:T(8,128)(2,1)} custom-call(f32[160,1024]{1,0:T(8,128)} %fusion.21.x_ref), custom_call_target="tpu_custom_call" | custom-call | tf_op jit(solution)/shard_map/total_over_seq/pallas_call | solution.py:687
  121.6 0.9 slice.159
  122.5 0.2 copy.55
  122.7 1.2 reshape_squeeze.7
  123.8 0.7 constant_dynamic-slice_fusion
  124.5 0.6 fusion.33.a_ref
  125.2 0.8 convert_bitcast_fusion.bc_ref
  126.0 3.7 convolution_add_fusion.pre_ref
  129.7 30.0 %all-gather.5.cloned.1.call-done = bf16[2048,1024]{1,0:T(8,128)(2,1)} async-done(((bf16[256,1024]{1,0:T(8,128)(2,1)}), bf16[2048,1024]{1,0:T(8,128)(2,1)}) %all-gather.5.cloned.1.call-update) | async-done | bytes 4194320 | tf_op jit(solution)/shard_map/all_gather | solution.py:860
  159.7 9.9 %convolution_multiply_fusion.gate_ref = f32[1024,1024]{1,0:T(8,128)} fusion(bf16[1024,2048]{1,0:T(8,128)(2,1)} %bitcast.154, bf16[2048,1024]{1,0:T(8,128)(2,1)} %all-gather.5.cloned.1.call-done, f32[1024]{0:T(1024)S(1)} %bitcast.185), kind=kOutput, calls=%fused_computation.37 | convolution fusion | flops 4296015872 | bytes 12587008 | tf_op jit(solution)/shard_map/dot_general | solution.py:811
  169.6 32.0 %scan_forward.1 = (f32[1024,1024]{1,0:T(8,128)}, bf16[1024,1024]{1,0:T(8,128)(2,1)}, f32[128,16,8,128]{3,2,1,0:T(8,128)}, f32[16,8,128]{2,1,0:T(8,128)}) custom-call(f32[1024,1024]{1,0:T(8,128)} %convolution_add_fusion.pre_ref, bf16[1024,1024]{1,0:T(8,128)(2,1)} %copy-done.2, f32[1024,1024]{1,0:T(8,128)} %convolution_multiply_fusion.gate_ref, ...), custom_call_target="tpu_custom_call" | custom-call | flops 134217728 | bytes 25165824 | tf_op jit(solution)/shard_map/scan_forward/pallas_call | solution.py:181
  201.7 67.6 %all-gather.7.cloned.1.call-done = bf16[1024,2048]{1,0:T(8,128)(2,1)} async-done(((bf16[128,2048]{1,0:T(8,128)(2,1)}), bf16[1024,2048]{1,0:T(8,128)(2,1)}) %all-gather.7.cloned.1.call-update) | async-done | bytes 4194320 | tf_op jit(solution)/shard_map/all_gather | solution.py:863
  269.3 14.2 %multiply_convert_fusion = (bf16[1024,1024]{1,0:T(8,128)(2,1)}, f32[1024,1024]{1,0:T(8,128)}) fusion(f32[1024,1024]{1,0:T(8,128)} %convolution_multiply_fusion.gate_ref, f32[1024,1024]{1,0:T(8,128)} %get-tuple-element.48, f32[1024]{0:T(1024)S(1)} %bitcast.186, bf16[1024,2048]{1,0:T(8,128)(2,1)} %all-gather.7.cloned.1.call-done, ...), kind=kOutput, calls=%fused_computation.11 | convolution fusion | flops 4308598784 | bytes 23072768 | tf_op jit(solution)/shard_map/dot_general | solution.py:819
  283.4 86.8 %scan_backward.1 = (bf16[1024,1024]{1,0:T(8,128)(2,1)}, f32[1024,1024]{1,0:T(8,128)}, f32[1024,128]{1,0:T(8,128)}, f32[16,8,128]{2,1,0:T(8,128)}, f32[16,8,128]{...) custom-call(f32[1024,1024]{1,0:T(8,128)} %convolution_add_fusion.pre_ref, bf16[1024,1024]{1,0:T(8,128)(2,1)} %copy-done.2, ...), custom_call_target="tpu_custom_call" | custom-call | flops 335544320 | bytes 29360128 | tf_op jit(solution)/shard_map/scan_backward/pallas_call | solution.py:220
  370.3 2.4 fusion.25
  372.7 1.2 copy.46
  374.0 0.9 pad_maximum_fusion.1.x_ref
  374.8 12.9 %total_over_seq.3 = bf16[160,1024]{1,0:T(8,128)(2,1)} custom-call(f32[160,1024]{1,0:T(8,128)} %pad_maximum_fusion.1.x_ref), custom_call_target="tpu_custom_call" | custom-call | tf_op jit(solution)/shard_map/total_over_seq/pallas_call | solution.py:687
  387.8 5.5 add_multiply_fusion
  393.3 5.5 multiply_reduce_fusion.2
  398.8 6.1 convolution_convert_fusion.2
  405.0 0.7 copy-done.16
  405.8 1.3 fusion.38
  407.1 0.7 copy.93
  408.0 0.4 convolution_convert_fusion.4
  408.5 0.5 convolution_convert_fusion.3
  409.0 0.4 concatenate.28
  409.3 1.0 bitcast_bitcast_fusion.refs_0_
  410.3 10.8 %convolution_convert_fusion.1 = bf16[2048,1024]{1,0:T(8,128)(2,1)} fusion(bf16[1024,2048]{1,0:T(8,128)(2,1)} %bitcast.155, bf16[1024,1024]{1,0:T(8,128)(2,1)} %get-tuple-element.67), kind=kOutput, calls=%fused_computation.29 | convolution fusion | flops 4297064448 | bytes 10485760 | tf_op jit(solution)/shard_map/dot_general | solution.py:815
  421.1 6.5 %convolution_convert_fusion = bf16[2048,1024]{1,0:T(8,128)(2,1)} fusion(bf16[1024,2048]{1,0:T(8,128)(2,1)S(1)} %bitcast.156, bf16[1024,1024]{1,0:T(8,128)(2,1)S(1)} %copy-done.33), kind=kOutput, calls=%fused_computation.28 | convolution fusion | flops 4297064448 | bytes 10485760 | tf_op jit(solution)/shard_map/dot_general | solution.py:815
  427.6 4.5 fusion.42
  432.2 6.3 fusion.7
  438.5 6.1 add_convert_fusion
  444.6 170.8 %scatter_end.1 = (f32[320,128]{1,0:T(8,128)}, f32[128,2048]{1,0:T(8,128)}, bf16[2,4,64,1024]{3,2,1,0:T(8,128)(2,1)}, f32[256,2048]{1,0:T(8,128)}, f32[4,40,256]{2,1,0:T(8,128)}) custom-call(bf16[8,320,128]{2,1,0:T(8,128)(2,1)} %bitcast_bitcast_fusion.refs_0_, bf16[8,256,1024]{2,1,0:T(8,128)(2,1)} %bitcast.158, bf16[8,256,1024]{2,1,0:T(8,128)(2,1)} %bitcast.159, ...), custom_call_target="tpu_custom_call" | custom-call | tf_op jit(solution)/shard_map/scatter_end/pallas_call | solution.py:793
  615.4 1.5 slice.178
  616.9 1.3 slice.180
  618.2 1.3 slice.175
  619.5 1.5 copy.66
  621.0 2.7 copy.53
  623.6 2.2 reshape.166
  626.0 0.7 broadcast_in_dim.40
  626.7 0.7 broadcast_in_dim.43
  627.4 0.6 copy.50
  628.0 0.6 copy.52
  628.6 2.1 fusion.13
  630.7 1.3 slice_bitcast_fusion.8
  632.0 1.5 slice_bitcast_fusion.1
  633.5 3.5 broadcast_multiply_fusion
  637.0 4.3 fusion.18
  641.3 1.0 copy.97
  (105 shorter events, 1.0 us)
Async XLA Ops:
  7.2 86.3 %copy-start = (f32[1,3,4096]{2,0,1:T(1,128)S(1)}, f32[1,3,4096]{2,0,1:T(1,128)}, u32[]{:S(2)}) copy-start(f32[1,3,4096]{2,0,1:T(1,128)} %param.26) | copy-start | bytes 147460
  7.2 152.5 %all-gather.5.cloned.1.call-start = ((), (), s32[]{:S(2)}) async-start(), calls=%async_computation.1 | async-start | bytes 4718592 | tf_op jit(solution)/shard_map/all_gather | solution.py:860
  7.9 3.8 copy-start.18
  7.9 3.8 copy-start.19
  7.9 3.8 copy-start.20
  7.9 3.8 copy-start.23
  7.9 3.8 copy-start.24
  7.9 3.8 copy-start.25
  7.9 3.8 copy-start.26
  87.2 114.5 %all-gather.9.cloned.1.call-start = ((), (), s32[]{:S(2)}) async-start(), calls=%async_computation.4 | async-start | bytes 5242880 | tf_op jit(solution)/shard_map/all_gather | solution.py:864
  88.0 181.3 %all-gather.7.cloned.1.call-start = ((), (), s32[]{:S(2)}) async-start(), calls=%async_computation.2 | async-start | bytes 4718592 | tf_op jit(solution)/shard_map/all_gather | solution.py:863
  88.7 548.3 %reduce-scatter.2.cloned.1.call-start = ((), (), s32[]{:S(2)}) async-start(), calls=%async_computation.3 | async-start | bytes 5242880 | tf_op jit(solution)/shard_map/reduce_scatter | solution.py:893
  101.2 4.8 copy-start.4
  106.0 23.7 %copy-start.2 = (bf16[1024,1024]{1,0:T(8,128)(2,1)}, bf16[1024,1024]{1,0:T(8,128)(2,1)S(1)}, u32[]{:S(2)}) copy-start(bf16[1024,1024]{1,0:T(8,128)(2,1)S(1)} %get-tuple-element.63.act_ref) | copy-start | bytes 6291460
  387.8 5.5 copy-start.5
  393.3 5.5 copy-start.6
  393.3 5.5 copy-start.30
  393.3 5.5 copy-start.31
  404.9 0.8 copy-start.16
  404.9 0.9 copy-start.17
  404.9 3.0 copy-start.15
  404.9 3.0 copy-start.22
  404.9 3.0 copy-start.21
  404.9 3.1 copy-start.8
  404.9 3.1 copy-start.10
  405.0 3.5 copy-start.3
  405.0 3.5 copy-start.12
  410.3 10.8 %copy-start.9 = (bf16[4,256,2048]{2,1,0:T(8,128)(2,1)S(1)}, bf16[4,256,2048]{2,1,0:T(8,128)(2,1)}, u32[]{:S(2)}) copy-start(bf16[4,256,2048]{2,1,0:T(8,128)(2,1)} %get-tuple-element.37) | copy-start | bytes 12582916
  410.3 10.8 %copy-start.33 = (bf16[1024,1024]{1,0:T(8,128)(2,1)S(1)}, bf16[1024,1024]{1,0:T(8,128)(2,1)}, u32[]{:S(2)}) copy-start(bf16[1024,1024]{1,0:T(8,128)(2,1)} %get-tuple-element.65) | copy-start | bytes 6291460
  421.1 6.5 %copy-start.28 = (bf16[2048,1024]{1,0:T(8,128)(2,1)S(1)}, bf16[2048,1024]{1,0:T(8,128)(2,1)}, u32[]{:S(2)}) copy-start(bf16[2048,1024]{1,0:T(8,128)(2,1)} %all-gather.5.cloned.1.call-done) | copy-start | bytes 12582916
  427.6 4.6 copy-start.29
  427.6 4.6 copy-start.32
  432.2 6.3 copy-start.11
  432.2 6.3 copy-start.27
  621.0 4.9 copy-start.14
  621.0 7.6 %copy-start.7 = (bf16[1,256,2048]{2,1,0:T(8,128)(2,1)S(1)}, bf16[1,256,2048]{2,1,0:T(8,128)(2,1)}, u32[]{:S(2)}) copy-start(bf16[1,256,2048]{2,1,0:T(8,128)(2,1)} %param.14) | copy-start | bytes 3145732
  633.5 8.7 %copy-start.1 = (f32[1,3,4096]{2,0,1:T(1,128)S(1)}, f32[1,3,4096]{2,0,1:T(1,128)}, u32[]{:S(2)}) copy-start(f32[1,3,4096]{2,0,1:T(1,128)} %param.26) | copy-start | bytes 147460
  637.0 4.3 copy-start.13
Sparse Core Ops, SparseCore 0:
  87.3 72.3 all-gather.4
  161.3 34.6 all-gather.8
  198.1 71.1 all-gather.6
  405.1 42.4 reduce-scatter.1

commit v3 on v2

--- a/solution.py
+++ b/solution.py
@@ -35,16 +35,298 @@
     )
 
 
+MESH_ID = pl.DeviceIdType.MESH
+VMEM_MOST = 60 * 1024 * 1024
+
+
+class Grid:
+    def __init__(self, axis, lines, fast):
+        self.axis, self.lines, self.fast = axis, lines, fast
+        self.here = lax.axis_index(axis)
+        self.line = self.here // fast
+        self.lane = self.here - self.line * fast
+
+    def at(self, line, lane):
+        return line * self.fast + lane
+
+    def line_peer(self, k):
+        return lax.rem(self.line + k, self.lines)
+
+    def lane_peer(self, e):
+        return lax.rem(self.lane + e, self.fast)
+
+    def copy(self, src, dst, sent, got, index):
+        return pltpu.make_async_remote_copy(
+            src_ref=src, dst_ref=dst, send_sem=sent, recv_sem=got,
+            device_id={self.axis: index}, device_id_type=MESH_ID,
+        )
+
+
+def meet(groups):
+    barrier = pltpu.get_barrier_semaphore()
+    total = 0
+    for grid in groups:
+        size = grid.lines * grid.fast
+        for k in range(1, size):
+            pl.semaphore_signal(
+                barrier, inc=1, device_id={grid.axis: lax.rem(grid.here + k, size)},
+                device_id_type=MESH_ID,
+            )
+        total += size - 1
+    pl.semaphore_wait(barrier, total)
+
+
+class Gather:
+    def __init__(self, grid, own, out, sems):
+        self.grid, self.own, self.out = grid, own, out
+        self.up_s, self.up_r, self.dn_s, self.dn_r, self.x_s, self.x_r = sems
+
+    @staticmethod
+    def semaphores(lines, fast):
+        hops = pltpu.SemaphoreType.DMA((lines,))
+        across = pltpu.SemaphoreType.DMA((lines, fast))
+        return [hops, hops, hops, hops, across, across]
+
+    def block(self, line, lane=None):
+        grid = self.grid
+        return self.out.at[grid.at(line, grid.lane if lane is None else lane)]
+
+    def up(self, k):
+        grid = self.grid
+        block = self.block(jnp.maximum(grid.line - k, 0))
+        return grid.copy(
+            self.own if k == 0 else block, block, self.up_s.at[k], self.up_r.at[k],
+            grid.at(jnp.minimum(grid.line + 1, grid.lines - 1), grid.lane),
+        )
+
+    def down(self, k):
+        grid = self.grid
+        block = self.block(jnp.minimum(grid.line + k, grid.lines - 1))
+        return grid.copy(
+            self.own if k == 0 else block, block, self.dn_s.at[k], self.dn_r.at[k],
+            grid.at(jnp.maximum(grid.line - 1, 0), grid.lane),
+        )
+
+    def sends_up(self, k):
+        return jnp.logical_and(self.grid.line + 1 < self.grid.lines, self.grid.line >= k)
+
+    def sends_down(self, k):
+        return jnp.logical_and(self.grid.line > 0, self.grid.line + k < self.grid.lines)
+
+    def across(self, line, slot, e, own=False):
+        grid = self.grid
+        block = self.block(line)
+        return grid.copy(
+            self.own if own else block, block, self.x_s.at[slot, e], self.x_r.at[slot, e],
+            grid.at(grid.line, grid.lane_peer(e)),
+        )
+
+    def slots(self):
+        return range(self.grid.lines)
+
+    def begin(self):
+        grid = self.grid
+        for when, copy in ((self.sends_up(0), self.up(0)), (self.sends_down(0), self.down(0))):
+            pl.when(when)(copy.start)
+        for e in range(1, grid.fast):
+            self.across(grid.line, 0, e, own=True).start()
+
+    def step(self, k):
+        grid = self.grid
+
+        def arrived(copy, line, slot, forward, onward):
+            copy.wait_recv()
+            if k < grid.lines - 1:
+                pl.when(forward(k))(onward(k).start)
+            for e in range(1, grid.fast):
+                self.across(line, slot, e).start()
+
+        below, above = grid.line - k, grid.line + k
+
+        @pl.when(below >= 0)
+        def _():
+            arrived(self.up(k - 1), below, grid.lines - k, self.sends_up, self.up)
+
+        @pl.when(above < grid.lines)
+        def _():
+            arrived(self.down(k - 1), above, k, self.sends_down, self.down)
+
+    def finish(self):
+        grid = self.grid
+        for k in range(grid.lines - 1):
+            pl.when(self.sends_up(k))(self.up(k).wait_send)
+            pl.when(self.sends_down(k))(self.down(k).wait_send)
+        for slot in self.slots():
+            for e in range(1, grid.fast):
+                copy = self.across(grid.line_peer(slot), slot, e, own=slot == 0)
+                copy.wait_send()
+                copy.wait_recv()
+
+
+class Scatter:
+    def __init__(self, grid, src, scratch):
+        self.grid, self.src = grid, src
+        (
+            self.xbuf, self.own, self.stage, self.zbuf, self.acc,
+            self.x_s, self.x_r, self.z_s, self.z_r, self.o_s,
+        ) = scratch
+
+    @staticmethod
+    def scratch(lines, fast, shape):
+        dma = pltpu.SemaphoreType.DMA
+        return [
+            pltpu.VMEM((lines, fast - 1) + shape, BF16),
+            pltpu.VMEM((lines,) + shape, BF16),
+            pltpu.VMEM((lines - 1,) + shape, BF16),
+            pltpu.VMEM((lines - 1,) + shape, BF16),
+            pltpu.VMEM(shape, F32),
+            dma((lines, fast)), dma((lines, fast)), dma((lines,)), dma((lines,)), dma((lines,)),
+        ]
+
+    def across(self, k, e):
+        grid = self.grid
+        lane = grid.lane_peer(e)
+        return grid.copy(
+            self.src.at[grid.at(grid.line_peer(k), lane)], self.xbuf.at[k, e - 1],
+            self.x_s.at[k, e], self.x_r.at[k, e], grid.at(grid.line, lane),
+        )
+
+    def local(self, k):
+        grid = self.grid
+        return pltpu.make_async_copy(
+            self.src.at[grid.at(grid.line_peer(k), grid.lane)], self.own.at[k], self.o_s.at[k]
+        )
+
+    def along(self, k):
+        grid = self.grid
+        return grid.copy(
+            self.stage.at[k - 1], self.zbuf.at[k - 1], self.z_s.at[k], self.z_r.at[k],
+            grid.at(grid.line_peer(k), grid.lane),
+        )
+
+    def order(self):
+        return list(range(self.grid.lines - 1, -1, -1))
+
+    def begin(self):
+        for k in self.order():
+            for e in range(1, self.grid.fast):
+                self.across(k, e).start()
+            self.local(k).start()
+
+    def rows(self, step):
+        count = self.acc.shape[0]
+        size = 16 if count % 16 == 0 else 8
+        def run(i, carry):
+            step(pl.ds(pl.multiple_of(i * size, size), size))
+            return carry
+        lax.fori_loop(0, count // size, run, 0)
+
+    def middle(self, k):
+        for e in range(1, self.grid.fast):
+            self.across(k, e).wait_recv()
+        self.local(k).wait()
+
+        def add(at):
+            total = self.own[k, at, :].astype(F32)
+            for e in range(self.grid.fast - 1):
+                total = total + self.xbuf[k, e, at, :].astype(F32)
+            if k > 0:
+                self.stage[k - 1, at, :] = total.astype(BF16)
+            else:
+                self.acc[at, :] = total
+
+        self.rows(add)
+        if k > 0:
+            self.along(k).start()
+
+    def finish(self, out_ref):
+        for k in range(1, self.grid.lines):
+            self.along(k).wait_recv()
+
+        def add(at):
+            total = self.acc[at, :]
+            for k in range(self.grid.lines - 1):
+                total = total + self.zbuf[k, at, :].astype(F32)
+            out_ref[at, :] = total.astype(out_ref.dtype)
+
+        self.rows(add)
+
+    def drain(self):
+        for k in self.order():
+            for e in range(1, self.grid.fast):
+                self.across(k, e).wait_send()
+            if k > 0:
+                self.along(k).wait_send()
+
+
+class Exchange:
+    def __init__(self, grid, src, dst, sems):
+        self.grid, self.src, self.dst = grid, src, dst
+        self.sent, self.got = sems
+        self.size = grid.lines * grid.fast
+
+    @staticmethod
+    def semaphores(size):
+        return [pltpu.SemaphoreType.DMA((size,)), pltpu.SemaphoreType.DMA((size,))]
+
+    def one(self, k):
+        grid = self.grid
+        peer = lax.rem(grid.here + k, self.size)
+        return grid.copy(
+            self.src(peer), self.dst(grid.here), self.sent.at[k], self.got.at[k], peer
+        )
+
+    def begin(self):
+        for k in range(1, self.size):
+            self.one(k).start()
+
+    def arrived(self):
+        for k in range(1, self.size):
+            self.one(k).wait_recv()
+
+    def drain(self):
+        for k in range(1, self.size):
+            self.one(k).wait_send()
+
+
+ANY = pl.BlockSpec(memory_space=pl.ANY)
+INSIDE = pl.BlockSpec(memory_space=pltpu.VMEM)
+
+
+def comm_params(collective_id):
+    return pltpu.CompilerParams(
+        collective_id=collective_id, has_side_effects=True, vmem_limit_bytes=VMEM_MOST
+    )
+
+
+def grids(shape):
+    lines, fast, seq_lines = shape
+    return Grid("seg", lines, fast), Grid("seq", seq_lines, 2)
+
+
 def forward_kernel(
-    pre_ref, act_ref, gate_ref, bc_ref, a_ref, skip_ref, init_ref,
-    y_ref, gated_ref, check_ref, final_ref,
-    state, rate_pl, drive_pl, y_pl,
+    shape, steps,
+    pre_ref, act_ref, bc_ref, a_ref, skip_ref, init_ref, weight_ref, cot_ref,
+    y_ref, check_ref, final_ref, weights_ref, cots_ref,
+    state, rate_pl, drive_pl, y_pl, local_s, *sems,
 ):
     count = pre_ref.shape[0]
     width, planes, _ = a_ref.shape
+    seg, seq = grids(shape)
+    weights = Gather(seg, weight_ref, weights_ref, sems[:6])
+    cots = Gather(seq, cot_ref, cots_ref, sems[6:])
+    keep = [
+        pltpu.make_async_copy(weight_ref, weights_ref.at[seg.here], local_s.at[0]),
+        pltpu.make_async_copy(cot_ref, cots_ref.at[seq.here], local_s.at[1]),
+    ]
 
     @pl.when(pl.program_id(0) == 0)
     def _():
+        meet((seg, seq))
+        weights.begin()
+        cots.begin()
+        for copy in keep:
+            copy.start()
         state[...] = init_ref[...]
 
     rate = softplus(pre_ref[...])
@@ -71,26 +353,44 @@
         return carry
 
     lax.fori_loop(0, count // UNROLL, group, 0)
-    y_val = from_planes(y_pl, count, planes) + skip_ref[...] * act
-    gate = gate_ref[...]
-    y_ref[...] = y_val
-    gated_ref[...] = (y_val * gate * sigmoid(gate)).astype(BF16)
-
-    @pl.when(pl.program_id(0) == pl.num_programs(0) - 1)
+    y_ref[...] = from_planes(y_pl, count, planes) + skip_ref[...] * act
+
+    for k in range(1, seg.lines):
+
+        @pl.when(pl.program_id(0) == (steps - 1) * k // (seg.lines - 1))
+        def _():
+            weights.step(k)
+            if k < seq.lines:
+                cots.step(k)
+
+    @pl.when(pl.program_id(0) == steps - 1)
     def _():
         final_ref[...] = state[...]
+        weights.finish()
+        cots.finish()
+        for copy in keep:
+            copy.wait()
 
 
 def backward_kernel(
-    pre_ref, act_ref, gy_ref, bc_ref, a_ref, skip_ref, check_ref,
-    gdt_ref, gact_ref, gbc_ref, agrad_ref, start_ref, dtb_ref, sgrad_ref,
-    carry_s, rate_pl, drive_pl, gy_pl, grate_pl, thr_pl, prod, part,
+    shape, steps,
+    pre_ref, act_ref, gy_ref, bc_ref, a_ref, skip_ref, check_ref, first_src, second_src,
+    gdt_ref, gact_ref, gbc_ref, agrad_ref, start_ref, dtb_ref, sgrad_ref, first_out, second_out,
+    carry_s, rate_pl, drive_pl, gy_pl, grate_pl, thr_pl, prod, part, *scratch,
 ):
     count = pre_ref.shape[0]
     width, planes, _ = a_ref.shape
+    seg, _ = grids(shape)
+    half = len(scratch) // 2
+    first, second = (
+        Scatter(seg, first_src, scratch[:half]), Scatter(seg, second_src, scratch[half:])
+    )
 
     @pl.when(pl.program_id(0) == 0)
     def _():
+        meet((seg,))
+        first.begin()
+        second.begin()
         carry_s[...] = jnp.zeros_like(carry_s)
         agrad_ref[...] = jnp.zeros_like(agrad_ref)
         dtb_ref[...] = jnp.zeros_like(dtb_ref)
@@ -166,12 +466,24 @@
     )
     gbc_ref[...] = jnp.sum(jnp.where(pick, sums, 0.0), axis=1)
 
-    @pl.when(pl.program_id(0) == pl.num_programs(0) - 1)
+    events = [(s, k) for s in (first, second) for k in s.order()]
+    for j, (scatter, k) in enumerate(events):
+
+        @pl.when(pl.program_id(0) == min(steps - 1, steps * (j + 1) // len(events)))
+        def _():
+            scatter.middle(k)
+
+    @pl.when(pl.program_id(0) == steps - 1)
     def _():
         start_ref[...] = carry_s[...]
-
-
-def forward_scan(pre, act, gate, bc, a2, skip, init, block):
+        first.finish(first_out)
+        second.finish(second_out)
+        first.drain()
+        second.drain()
+
+
+def forward_scan(shape, pre, act, bc, a2, skip, init, weight, cot, block):
+    lines, fast, seq_lines = shape
     length, features = pre.shape
     width, planes, _ = a2.shape
     steps = length // block
@@ -179,37 +491,45 @@
     whole = pl.BlockSpec((width, planes, LANES), lambda i: (0, 0, 0))
     plane = pltpu.VMEM((planes * block, LANES), F32)
     return pl.pallas_call(
-        forward_kernel,
+        functools.partial(forward_kernel, shape, steps),
         grid=(steps,),
         in_specs=[
-            rows, rows, rows,
+            rows, rows,
             pl.BlockSpec((block, 2 * width), lambda i: (i, 0), memory_space=pltpu.SMEM),
             whole,
             pl.BlockSpec((1, features), lambda i: (0, 0)),
             whole,
+            pl.BlockSpec(weight.shape, lambda i: (0, 0)),
+            pl.BlockSpec(cot.shape, lambda i: (0, 0)),
         ],
         out_specs=[
-            rows, rows,
+            rows,
             pl.BlockSpec((block // UNROLL, width, planes, LANES), lambda i: (i, 0, 0, 0)),
-            whole,
+            whole, ANY, ANY,
         ],
         out_shape=[
             jax.ShapeDtypeStruct((length, features), F32),
-            jax.ShapeDtypeStruct((length, features), BF16),
             jax.ShapeDtypeStruct((length // UNROLL, width, planes, LANES), F32),
             jax.ShapeDtypeStruct((width, planes, LANES), F32),
-        ],
-        scratch_shapes=[pltpu.VMEM((width, planes, LANES), F32), plane, plane, plane],
+            jax.ShapeDtypeStruct((lines * fast,) + weight.shape, BF16),
+            jax.ShapeDtypeStruct((seq_lines * 2,) + cot.shape, BF16),
+        ],
+        scratch_shapes=[
+            pltpu.VMEM((width, planes, LANES), F32), plane, plane, plane,
+            pltpu.SemaphoreType.DMA((2,)),
+            *Gather.semaphores(lines, fast), *Gather.semaphores(seq_lines, 2),
+        ],
+        compiler_params=comm_params(5),
         cost_estimate=pl.CostEstimate(
             flops=8 * length * features * width,
             bytes_accessed=24 * length * features,
             transcendentals=length * features * width,
         ),
         name="scan_forward",
-    )(pre, act, gate, bc, a2, skip, init)
-
-
-def backward_scan(pre, act, gy, bc, a2, skip, checks, block):
+    )(pre, act, bc, a2, skip, init, weight, cot)
+
+
+def backward_scan(shape, pre, act, gy, bc, a2, skip, checks, first, second, block):
     length, features = pre.shape
     width, planes, _ = a2.shape
     steps = length // block
@@ -218,7 +538,7 @@
     line = pl.BlockSpec((1, features), lambda i: (0, 0))
     plane = pltpu.VMEM((planes * block, LANES), F32)
     return pl.pallas_call(
-        backward_kernel,
+        functools.partial(backward_kernel, shape, steps),
         grid=(steps,),
         in_specs=[
             rows, rows, rows,
@@ -229,11 +549,14 @@
             pl.BlockSpec(
                 (block // UNROLL, width, planes, LANES), lambda i: (steps - 1 - i, 0, 0, 0)
             ),
+            ANY, ANY,
         ],
         out_specs=[
             rows, rows,
             pl.BlockSpec((block, LANES), lambda i: (steps - 1 - i, 0)),
             whole, whole, line, line,
+            pl.BlockSpec(first.shape[1:], lambda i: (0, 0)),
+            pl.BlockSpec(second.shape[1:], lambda i: (0, 0)),
         ],
         out_shape=[
             jax.ShapeDtypeStruct((length, features), BF16),
@@ -243,289 +566,25 @@
             jax.ShapeDtypeStruct((width, planes, LANES), F32),
             jax.ShapeDtypeStruct((1, features), F32),
             jax.ShapeDtypeStruct((1, features), F32),
+            jax.ShapeDtypeStruct(first.shape[1:], BF16),
+            jax.ShapeDtypeStruct(second.shape[1:], F32),
         ],
         scratch_shapes=[pltpu.VMEM((width, planes, LANES), F32)]
         + [plane] * 5
         + [
             pltpu.VMEM((UNROLL * 2 * width * planes, LANES), F32),
             pltpu.VMEM((block * 2 * width, LANES), F32),
-        ],
+            *Scatter.scratch(shape[0], shape[1], tuple(first.shape[1:])),
+            *Scatter.scratch(shape[0], shape[1], tuple(second.shape[1:])),
+        ],
+        compiler_params=comm_params(6),
         cost_estimate=pl.CostEstimate(
             flops=20 * length * features * width,
             bytes_accessed=28 * length * features,
             transcendentals=length * features * width,
         ),
         name="scan_backward",
-    )(pre, act, gy, bc, a2, skip, checks)
-
-
-MESH_ID = pl.DeviceIdType.MESH
-VMEM_MOST = 60 * 1024 * 1024
-
-
-class Grid:
-    def __init__(self, axis, lines, fast):
-        self.axis, self.lines, self.fast = axis, lines, fast
-        self.here = lax.axis_index(axis)
-        self.line = self.here // fast
-        self.lane = self.here - self.line * fast
-
-    def at(self, line, lane):
-        return line * self.fast + lane
-
-    def line_peer(self, k):
-        return lax.rem(self.line + k, self.lines)
-
-    def lane_peer(self, e):
-        return lax.rem(self.lane + e, self.fast)
-
-    def copy(self, src, dst, sent, got, index):
-        return pltpu.make_async_remote_copy(
-            src_ref=src, dst_ref=dst, send_sem=sent, recv_sem=got,
-            device_id={self.axis: index}, device_id_type=MESH_ID,
-        )
-
-
-def meet(groups):
-    barrier = pltpu.get_barrier_semaphore()
-    total = 0
-    for grid in groups:
-        size = grid.lines * grid.fast
-        for k in range(1, size):
-            pl.semaphore_signal(
-                barrier, inc=1, device_id={grid.axis: lax.rem(grid.here + k, size)},
-                device_id_type=MESH_ID,
-            )
-        total += size - 1
-    pl.semaphore_wait(barrier, total)
-
-
-class Gather:
-    def __init__(self, grid, own, out, sems):
-        self.grid, self.own, self.out = grid, own, out
-        self.up_s, self.up_r, self.dn_s, self.dn_r, self.x_s, self.x_r = sems
-
-    @staticmethod
-    def semaphores(lines, fast):
-        hops = pltpu.SemaphoreType.DMA((lines,))
-        across = pltpu.SemaphoreType.DMA((lines, fast))
-        return [hops, hops, hops, hops, across, across]
-
-    def block(self, line, lane=None):
-        grid = self.grid
-        return self.out.at[grid.at(line, grid.lane if lane is None else lane)]
-
-    def up(self, k):
-        grid = self.grid
-        block = self.block(jnp.maximum(grid.line - k, 0))
-        return grid.copy(
-            self.own if k == 0 else block, block, self.up_s.at[k], self.up_r.at[k],
-            grid.at(jnp.minimum(grid.line + 1, grid.lines - 1), grid.lane),
-        )
-
-    def down(self, k):
-        grid = self.grid
-        block = self.block(jnp.minimum(grid.line + k, grid.lines - 1))
-        return grid.copy(
-            self.own if k == 0 else block, block, self.dn_s.at[k], self.dn_r.at[k],
-            grid.at(jnp.maximum(grid.line - 1, 0), grid.lane),
-        )
-
-    def sends_up(self, k):
-        return jnp.logical_and(self.grid.line + 1 < self.grid.lines, self.grid.line >= k)
-
-    def sends_down(self, k):
-        return jnp.logical_and(self.grid.line > 0, self.grid.line + k < self.grid.lines)
-
-    def across(self, line, slot, e, own=False):
-        grid = self.grid
-        block = self.block(line)
-        return grid.copy(
-            self.own if own else block, block, self.x_s.at[slot, e], self.x_r.at[slot, e],
-            grid.at(grid.line, grid.lane_peer(e)),
-        )
-
-    def slots(self):
-        return range(self.grid.lines)
-
-    def begin(self):
-        grid = self.grid
-        for when, copy in ((self.sends_up(0), self.up(0)), (self.sends_down(0), self.down(0))):
-            pl.when(when)(copy.start)
-        for e in range(1, grid.fast):
-            self.across(grid.line, 0, e, own=True).start()
-
-    def step(self, k):
-        grid = self.grid
-
-        def arrived(copy, line, slot, forward, onward):
-            copy.wait_recv()
-            if k < grid.lines - 1:
-                pl.when(forward(k))(onward(k).start)
-            for e in range(1, grid.fast):
-                self.across(line, slot, e).start()
-
-        below, above = grid.line - k, grid.line + k
-
-        @pl.when(below >= 0)
-        def _():
-            arrived(self.up(k - 1), below, grid.lines - k, self.sends_up, self.up)
-
-        @pl.when(above < grid.lines)
-        def _():
-            arrived(self.down(k - 1), above, k, self.sends_down, self.down)
-
-    def finish(self):
-        grid = self.grid
-        for k in range(grid.lines - 1):
-            pl.when(self.sends_up(k))(self.up(k).wait_send)
-            pl.when(self.sends_down(k))(self.down(k).wait_send)
-        for slot in self.slots():
-            for e in range(1, grid.fast):
-                copy = self.across(grid.line_peer(slot), slot, e, own=slot == 0)
-                copy.wait_send()
-                copy.wait_recv()
-
-
-class Scatter:
-    def __init__(self, grid, src, scratch):
-        self.grid, self.src = grid, src
-        (
-            self.xbuf, self.own, self.stage, self.zbuf, self.acc,
-            self.x_s, self.x_r, self.z_s, self.z_r, self.o_s,
-        ) = scratch
-
-    @staticmethod
-    def scratch(lines, fast, shape):
-        dma = pltpu.SemaphoreType.DMA
-        return [
-            pltpu.VMEM((lines, fast - 1) + shape, BF16),
-            pltpu.VMEM((lines,) + shape, BF16),
-            pltpu.VMEM((lines - 1,) + shape, BF16),
-            pltpu.VMEM((lines - 1,) + shape, BF16),
-            pltpu.VMEM(shape, F32),
-            dma((lines, fast)), dma((lines, fast)), dma((lines,)), dma((lines,)), dma((lines,)),
-        ]
-
-    def across(self, k, e):
-        grid = self.grid
-        lane = grid.lane_peer(e)
-        return grid.copy(
-            self.src.at[grid.at(grid.line_peer(k), lane)], self.xbuf.at[k, e - 1],
-            self.x_s.at[k, e], self.x_r.at[k, e], grid.at(grid.line, lane),
-        )
-
-    def local(self, k):
-        grid = self.grid
-        return pltpu.make_async_copy(
-            self.src.at[grid.at(grid.line_peer(k), grid.lane)], self.own.at[k], self.o_s.at[k]
-        )
-
-    def along(self, k):
-        grid = self.grid
-        return grid.copy(
-            self.stage.at[k - 1], self.zbuf.at[k - 1], self.z_s.at[k], self.z_r.at[k],
-            grid.at(grid.line_peer(k), grid.lane),
-        )
-
-    def order(self):
-        return list(range(self.grid.lines - 1, -1, -1))
-
-    def begin(self):
-        for k in self.order():
-            for e in range(1, self.grid.fast):
-                self.across(k, e).start()
-            self.local(k).start()
-
-    def rows(self, step):
-        count = self.acc.shape[0]
-        size = 16 if count % 16 == 0 else 8
-        def run(i, carry):
-            step(pl.ds(pl.multiple_of(i * size, size), size))
-            return carry
-        lax.fori_loop(0, count // size, run, 0)
-
-    def middle(self, k):
-        for e in range(1, self.grid.fast):
-            self.across(k, e).wait_recv()
-        self.local(k).wait()
-
-        def add(at):
-            total = self.own[k, at, :].astype(F32)
-            for e in range(self.grid.fast - 1):
-                total = total + self.xbuf[k, e, at, :].astype(F32)
-            if k > 0:
-                self.stage[k - 1, at, :] = total.astype(BF16)
-            else:
-                self.acc[at, :] = total
-
-        self.rows(add)
-        if k > 0:
-            self.along(k).start()
-
-    def finish(self, out_ref):
-        for k in range(1, self.grid.lines):
-            self.along(k).wait_recv()
-
-        def add(at):
-            total = self.acc[at, :]
-            for k in range(self.grid.lines - 1):
-                total = total + self.zbuf[k, at, :].astype(F32)
-            out_ref[at, :] = total.astype(out_ref.dtype)
-
-        self.rows(add)
-
-    def drain(self):
-        for k in self.order():
-            for e in range(1, self.grid.fast):
-                self.across(k, e).wait_send()
-            if k > 0:
-                self.along(k).wait_send()
-
-
-class Exchange:
-    def __init__(self, grid, src, dst, sems):
-        self.grid, self.src, self.dst = grid, src, dst
-        self.sent, self.got = sems
-        self.size = grid.lines * grid.fast
-
-    @staticmethod
-    def semaphores(size):
-        return [pltpu.SemaphoreType.DMA((size,)), pltpu.SemaphoreType.DMA((size,))]
-
-    def one(self, k):
-        grid = self.grid
-        peer = lax.rem(grid.here + k, self.size)
-        return grid.copy(
-            self.src(peer), self.dst(grid.here), self.sent.at[k], self.got.at[k], peer
-        )
-
-    def begin(self):
-        for k in range(1, self.size):
-            self.one(k).start()
-
-    def arrived(self):
-        for k in range(1, self.size):
-            self.one(k).wait_recv()
-
-    def drain(self):
-        for k in range(1, self.size):
-            self.one(k).wait_send()
-
-
-ANY = pl.BlockSpec(memory_space=pl.ANY)
-INSIDE = pl.BlockSpec(memory_space=pltpu.VMEM)
-
-
-def comm_params(collective_id):
-    return pltpu.CompilerParams(
-        collective_id=collective_id, has_side_effects=True, vmem_limit_bytes=VMEM_MOST
-    )
-
-
-def grids(shape):
-    lines, fast, seq_lines = shape
-    return Grid("seg", lines, fast), Grid("seq", seq_lines, 2)
+    )(pre, act, gy, bc, a2, skip, checks, first, second)
 
 
 def gather_kernel(
@@ -700,7 +759,7 @@
     )(x)
 
 
-def scatter_end(shape, over_seg, over_seq, ends):
+def scatter_end(shape, over_seg, over_seq, g_half, ends):
     lines, fast, seq_lines = shape
     seqs = seq_lines * 2
     count = len(over_seg)
@@ -718,21 +777,21 @@
     scratch += part
     tail = len(scratch)
     scratch += [
-        pltpu.VMEM((2, blocks[1][0], feats), BF16),
+        pltpu.VMEM((blocks[1][0], feats), BF16),
         *Exchange.semaphores(seqs), *Exchange.semaphores(seqs), *Exchange.semaphores(seqs),
         pltpu.SemaphoreType.DMA((3,)),
     ]
 
     def kernel(*refs):
         srcs = refs[:count]
-        q_src, ends_in = refs[count : count + 2]
-        small_out, out_out, halves_out, q_out, ends_out = refs[count + 2 : count + 7]
+        q_src, g_in, ends_in = refs[count : count + 3]
+        small_out, halves_out, q_out, ends_out = refs[count + 3 : count + 7]
         sc = refs[count + 7 :]
         seg, seq = grids(shape)
         meet((seg, seq))
         scatters = [Scatter(seg, s, sc[a:b]) for s, (a, b) in zip(srcs, spans)]
         q_sum = Scatter(seq, q_src, sc[spans[-1][0] : spans[-1][1]])
-        halves = sc[tail]
+        halves = (sc[tail], g_in)
         sems = sc[tail + 1 : tail + 7]
         local = sc[tail + 7]
         end_swap = Exchange(
@@ -746,32 +805,30 @@
         def swap(half, pair):
             return Exchange(
                 seq,
-                lambda p: halves.at[half, pl.ds(pl.multiple_of(p * own_rows, own_rows), own_rows)],
+                lambda p: halves[half].at[pl.ds(pl.multiple_of(p * own_rows, own_rows), own_rows)],
                 lambda m: halves_out.at[half, m],
                 pair,
             )
 
         swaps = [swap(0, sems[2:4]), swap(1, sems[4:6])]
-        small, x_half, g_half, out = scatters
-        outs = {0: small_out, 1: halves.at[0], 2: halves.at[1], 3: out_out}
-        for k in q_sum.order():
-            q_sum.middle(k)
-        for i, s in enumerate(scatters):
-            for j, k in enumerate(s.order()):
-                s.middle(k)
-                if i > 0 and j == min(1, lines - 1):
-                    scatters[i - 1].finish(outs[i - 1])
-                    if i - 1 in (1, 2):
-                        swaps[i - 2].begin()
-            if i == 0:
-                q_sum.finish(q_out)
-        out.finish(out_out)
+        swaps[1].begin()
+        small, x_half = scatters
+        for k in small.order():
+            small.middle(k)
+        for j, k in enumerate(x_half.order()):
+            x_half.middle(k)
+            if j < seq_lines:
+                q_sum.middle(q_sum.order()[j])
+        small.finish(small_out)
+        q_sum.finish(q_out)
+        x_half.finish(halves[0])
+        swaps[0].begin()
         own = []
         for half in (0, 1):
             own.append(
                 pltpu.make_async_copy(
-                    halves.at[
-                        half, pl.ds(pl.multiple_of(seq.here * own_rows, own_rows), own_rows)
+                    halves[half].at[
+                        pl.ds(pl.multiple_of(seq.here * own_rows, own_rows), own_rows)
                     ],
                     halves_out.at[half, seq.here],
                     local.at[half],
@@ -792,11 +849,10 @@
 
     return pl.pallas_call(
         kernel,
-        in_specs=[ANY] * (count + 1) + [INSIDE],
-        out_specs=[INSIDE] * 5,
+        in_specs=[ANY] * (count + 1) + [INSIDE, INSIDE],
+        out_specs=[INSIDE] * 4,
         out_shape=[
             jax.ShapeDtypeStruct(blocks[0], F32),
-            jax.ShapeDtypeStruct(blocks[3], F32),
             jax.ShapeDtypeStruct((2, seqs, own_rows, feats), BF16),
             jax.ShapeDtypeStruct(over_seq.shape[1:], F32),
             jax.ShapeDtypeStruct(ends.shape, F32),
@@ -804,7 +860,7 @@
         scratch_shapes=scratch,
         compiler_params=comm_params(4),
         name="scatter_end",
-    )(*over_seg, over_seq, ends)
+    )(*over_seg, over_seq, g_half, ends)
 
 
 def dot_nn(a, b):
@@ -860,8 +916,6 @@
     w_g_half = lax.all_gather(
         g_part.reshape(seqs * own_rows, feats), "seg", axis=0, tiled=True
     )
-    w_out = lax.all_gather(out_proj, "seg", axis=0, tiled=True)
-    cot = lax.all_gather(cotangent[0], "seq", axis=0, tiled=True)
 
     small_all = small_all.transpose(1, 0, 2).reshape(small.shape[0], feats)
     w_dt = small_all[:low_rank]
@@ -886,9 +940,15 @@
     dt_low = mixed_x[:low_rank]
     bc = mixed_x[low_rank:].astype(F32).T
     pre = dot_tn(dt_low, w_dt) + b_dt
+    init = mine(init_state[0]).reshape(width, planes, LANES)
+    y_val, checks, final, w_out, cot = forward_scan(
+        shape, pre, act, bc, a2, skip, init, out_proj, cotangent[0], block
+    )
+    w_out = w_out.reshape(feats, model)
+    cot = cot.reshape(length, model)
+    y_val, w_g_half = lax.optimization_barrier((y_val, w_g_half))
     gate = rstd * dot_nn(tok, w_g_half)
-    init = mine(init_state[0]).reshape(width, planes, LANES)
-    y_val, gated, checks, final = forward_scan(pre, act, gate, bc, a2, skip, init, block)
+    gated = (y_val * jax.nn.silu(gate)).astype(BF16)
     out_part = dot_nn(gated, w_out).astype(BF16)
     mixed_out = lax.psum_scatter(out_part, "seq", scatter_dimension=0, tiled=True)
     mixed_out = (mixed_out.astype(F32) + tokens[0].astype(F32)).astype(BF16)
@@ -901,8 +961,11 @@
     ).astype(BF16)
     out_grad = dot_tn(gated, cot).astype(BF16)
     gate_grad = dot_tn(tok, gs_gate).astype(BF16)
-    g_dtpre, g_actp, g_bc, a_sum, start, dtb_grad, skip_grad = backward_scan(
-        pre, act, gy, bc, a2, skip, checks, block
+    g_dtpre, g_actp, g_bc, a_sum, start, dtb_grad, skip_grad, g_half, out_grad = backward_scan(
+        shape, pre, act, gy, bc, a2, skip, checks,
+        gate_grad.reshape(segs, seqs * own_rows, feats),
+        out_grad.reshape(segs, part, model),
+        block,
     )
     g_mixed = jnp.concatenate([dot_nt(w_dt, g_dtpre), g_bc[:, : 2 * width].T], axis=0)
     g_mixed = total_over_seq(shape, g_mixed, 3)
@@ -942,15 +1005,11 @@
         axis=0,
     )
     ends = jnp.pad(ends, ((0, -ends.shape[0] % 8), (0, 0)))
-    grads, out_grad, halves, q_own, ends = scatter_end(
+    grads, halves, q_own, ends = scatter_end(
         shape,
-        [
-            grads,
-            x_grad.reshape(segs, seqs * own_rows, feats),
-            gate_grad.reshape(segs, seqs * own_rows, feats),
-            out_grad.reshape(segs, part, model),
-        ],
+        [grads, x_grad.reshape(segs, seqs * own_rows, feats)],
         q_part.reshape(seqs, own_len, model),
+        g_half,
         ends.reshape(ends.shape[0], seqs, feats // seqs).transpose(1, 0, 2),
     )
     ends = (

time: 656 us -> 536 us (0.82)
  waiting for transfers between devices: 99 us -> 0.06 us
  Pallas kernels: 391 us -> 375 us
  other arithmetic: 28.4 us -> 38.2 us
  matrix products: 86.3 us -> 77.9 us
    all_gather x2 -> x0, waiting for transfers between devices: 67.6 us -> none  [the longest x1 67.6 us: body(): w_out = lax.all_gather(out_proj, 'seg', axis=0, tiled=True)]
    all_gather x1, waiting for transfers between devices: 30 us -> 0.02 us  [body(): lax.all_gather(g_part.reshape(seqs * own_rows, feats), 'seg', axis=0, til...]
    pallas_call x3, Pallas kernels: 290 us -> 274 us  [the longest x1 112 us: backward_scan(): pl.pallas_call(functools.partial(backward_kernel, shape, steps), grid=(st...]
    reduce_sum x1, other arithmetic: 5.47 us -> 14.2 us  [body(): jnp.sum(g_conv * padded[k:k + length], axis=0)]
  transfers between devices with their start and end apart: 4 -> 2, of which waited for: 2 -> 0; matrix products, arithmetic and copies ran while one was open for 15% -> 19% of each run, Pallas kernels for 33% -> 56%
where the time goes in v3:
time: 536 us; the launch traced here: 534 us
  Pallas kernels  375 us (70%)
  matrix products  77.9 us (15%)
  other arithmetic  38.2 us (7%)
  local copies, waits for them, and re-layouts  28.3 us (5%)
  between operations  14.9 us (3%)
    pallas_call x1, Pallas kernels, backward_scan(): pl.pallas_call(functools.partial(backward_kernel, shape, steps), grid=(st...  112 us
    pallas_call x1, Pallas kernels, forward_scan(): pl.pallas_call(functools.partial(forward_kernel, shape, steps), grid=(ste...  82.2 us
    pallas_call x1, Pallas kernels, scatter_end(): pl.pallas_call(kernel, in_specs=[ANY] * (count + 1) + [INSIDE, INSIDE], o...  79.8 us
    pallas_call x1, Pallas kernels, gather_start(): pl.pallas_call(kernel, in_specs=[ANY, INSIDE, ANY], out_specs=[ANY] * 4,...  74.7 us
    dot_general x5, matrix products, dot_tn(): lax.dot_general(a, b, (((0,), (0,)), ((), ())), preferred_element_type=F32)  30 us
    dot_general x5, matrix products, dot_nt(): lax.dot_general(a, b, (((1,), (1,)), ((), ())), preferred_element_type=F32)  27 us
    pallas_call x2, Pallas kernels, total_over_seq(): pl.pallas_call(kernel, in_specs=[INSIDE], out_specs=INSIDE, out_shape=jax...  26.2 us
    dot_general x5, matrix products, dot_nn(): return jnp.dot(a, b, preferred_element_type=F32)  21 us
  transfers between devices with their start and end apart: 2, of which 0 were waited for; matrix products, arithmetic and copies ran while one was open for 19% of the time, Pallas kernels for 56%

profile of v3, /device:TPU:1, one launch (start us, length us, event | category | flops | bytes accessed | tf_op | source)
XLA Modules:
  0.0 534.4 jit_solution(13786924234001702871)
XLA Ops:
  7.2 0.7 convert_element_type.85
  8.0 1.5 fusion.3
  9.5 0.8 reshape.158
  10.4 1.3 reshape.159.refs_0_
  11.8 0.6 pad.16.refs_1_
  12.5 74.7 %gather_start.1 = (bf16[8,4,64,1024]{3,2,1,0:T(8,128)(2,1)}, bf16[8,320,128]{2,1,0:T(8,128)(2,1)}, bf16[4,256,2048]{2,1,0:T(8,128)(2,1)}, bf16[4,64,1024]{2,1,0:T(8,128)(2,1)}) custom-call(bf16[4,2,64,1024]{3,2,1,0:T(8,128)(2,1)} %reshape.159.refs_0_, bf16[320,128]{1,0:T(8,128)(2,1)} %pad.16.refs_1_, bf16[256,2048]{1,0:T(8,128)(2,1)} %bitcast.145), custom_call_target="tpu_custom_call" | custom-call | tf_op jit(solution)/shard_map/gather_start/pallas_call | solution.py:662
  87.3 1.5 copy.92
  88.9 0.2 reshape_squeeze.7
  89.1 3.2 multiply_reduce_fusion
  92.4 0.2 copy-done.8
  92.6 6.3 %convolution_multiply_fusion = f32[1024,1024]{1,0:T(8,128)S(1)} fusion(bf16[1024,2048]{1,0:T(8,128)(2,1)S(1)} %bitcast.151, bf16[2048,1024]{1,0:T(8,128)(2,1)} %bitcast.187, f32[1024]{0:T(1024)S(1)} %bitcast.177), kind=kOutput, calls=%fused_computation.34 | convolution fusion | flops 4296015872 | bytes 12587008 | tf_op jit(solution)/shard_map/dot_general | solution.py:867
  98.9 0.7 fusion.34
  99.6 4.1 multiply_convert_fusion.3
  103.6 1.7 fusion.14.x_ref
  105.3 13.9 %total_over_seq.2 = bf16[160,1024]{1,0:T(8,128)(2,1)} custom-call(f32[160,1024]{1,0:T(8,128)} %fusion.14.x_ref), custom_call_target="tpu_custom_call" | custom-call | tf_op jit(solution)/shard_map/total_over_seq/pallas_call | solution.py:746
  119.2 0.8 slice.159
  120.1 0.2 copy.55
  120.3 0.7 constant_dynamic-slice_fusion
  121.0 0.6 fusion.26.a_ref
  121.6 0.8 convert_bitcast_fusion.bc_ref
  122.4 3.8 convolution_add_fusion.pre_ref
  126.2 82.2 %scan_forward.1 = (f32[1024,1024]{1,0:T(8,128)}, f32[128,16,8,128]{3,2,1,0:T(8,128)}, f32[16,8,128]{2,1,0:T(8,128)}, bf16[8,128,2048]{2,1,0:T(8,128)(2,1)}, bf16[4,256,2048]{2,1,0:T(8,128)(2,1)}) custom-call(f32[1024,1024]{1,0:T(8,128)} %convolution_add_fusion.pre_ref, bf16[1024,1024]{1,0:T(8,128)(2,1)} %copy-done.2, f32[1024,32]{1,0:T(8,128)} %convert_bitcast_fusion.bc_ref, ...), custom_call_target="tpu_custom_call" | custom-call | flops 134217728 | bytes 25165824 | tf_op jit(solution)/shard_map/scan_forward/pallas_call | solution.py:493
  208.4 7.7 %fusion.35 = f32[1024,1024]{1,0:T(8,128)S(1)} fusion(bf16[1024,2048]{1,0:T(8,128)(2,1)} %bitcast.149, bf16[2048,1024]{1,0:T(8,128)(2,1)} %all-gather.2.cloned.1.call-done), kind=kOutput, calls=%fused_computation.107 | convolution fusion | flops 4294967296 | bytes 12582912 | tf_op jit(solution)/shard_map/dot_general | solution.py:867
  216.1 9.6 %multiply_convert_fusion.1 = (bf16[1024,1024]{1,0:T(8,128)(2,1)S(1)}, f32[1024,1024]{1,0:T(8,128)}, bf16[1024,1024]{1,0:T(8,128)(2,1)S(1)}) fusion(f32[1024,1024]{1,0:T(8,128)} %get-tuple-element.45, f32[1024,1024]{1,0:T(8,128)S(1)} %fusion.35, f32[1024]{0:T(1024)S(1)} %bitcast.178, bf16[1024,2048]{1,0:T(8,128)(2,1)S(1)} %bitcast.192, ...), kind=kOutput, calls=%fused_computation.15 | convolution fusion | flops 4312793088 | bytes 25169920 | tf_op jit(solution)/shard_map/dot_general | solution.py:875
  225.7 6.2 %convolution_convert_fusion.1 = bf16[1024,2048]{1,0:T(8,128)(2,1)} fusion(bf16[1024,1024]{1,0:T(8,128)(2,1)S(1)} %get-tuple-element.75, bf16[1024,2048]{1,0:T(8,128)(2,1)S(1)} %bitcast.193), kind=kOutput, calls=%fused_computation.25 | convolution fusion | flops 4297064448 | bytes 10485760 | tf_op jit(solution)/shard_map/dot_general | solution.py:871
  231.9 6.1 %convolution_convert_fusion.3 = bf16[1024,2048]{1,0:T(8,128)(2,1)} fusion(bf16[1024,1024]{1,0:T(8,128)(2,1)S(1)} %get-tuple-element.75, bf16[1024,2048]{1,0:T(8,128)(2,1)S(1)} %bitcast.191), kind=kOutput, calls=%fused_computation.27 | convolution fusion | flops 4297064448 | bytes 10485760 | tf_op jit(solution)/shard_map/dot_general | solution.py:867
  238.1 8.4 %convolution_convert_fusion.2 = bf16[2048,1024]{1,0:T(8,128)(2,1)} fusion(bf16[1024,2048]{1,0:T(8,128)(2,1)} %bitcast.150, bf16[1024,1024]{1,0:T(8,128)(2,1)S(1)} %get-tuple-element.73), kind=kOutput, calls=%fused_computation.26 | convolution fusion | flops 4297064448 | bytes 10485760 | tf_op jit(solution)/shard_map/dot_general | solution.py:871
  246.4 112.0 %scan_backward.1 = (bf16[1024,1024]{1,0:T(8,128)(2,1)}, f32[1024,1024]{1,0:T(8,128)}, f32[1024,128]{1,0:T(8,128)}, f32[16,8,128]{2,1,0:T(8,128)}, f32[16,8,128]{...) custom-call(f32[1024,1024]{1,0:T(8,128)} %convolution_add_fusion.pre_re, ...), custom_call_target="tpu_custom_call" | custom-call | flops 335544320 | bytes 29360128 | tf_op jit(solution)/shard_map/scan_backward/pallas_call | solution.py:540
  358.5 0.9 multiply_convert_fusion.4
  359.3 1.2 copy.46
  360.6 0.7 convert.50
  361.3 0.7 convert.51
  362.0 2.4 fusion.18
  364.4 0.9 pad_maximum_fusion.1.x_ref
  365.3 12.3 %total_over_seq.3 = bf16[160,1024]{1,0:T(8,128)(2,1)} custom-call(f32[160,1024]{1,0:T(8,128)} %pad_maximum_fusion.1.x_ref), custom_call_target="tpu_custom_call" | custom-call | tf_op jit(solution)/shard_map/total_over_seq/pallas_call | solution.py:746
  377.6 5.4 %add_multiply_fusion = f32[1024,1024]{1,0:T(8,128)S(1)} fusion(f32[1024,1024]{1,0:T(8,128)} %get-tuple-element.72, f32[1024,1024]{1,0:T(8,128)} %get-tuple-element.53, bf16[160,1024]{1,0:T(8,128)(2,1)} %total_over_seq.3, bf16[20,8,8,128]{3,2,1,0:T(8,128)(2,1)S(1)} %bitcast.160), kind=kOutput, calls=%fused_computation.14 | convolution fusion | flops 344981504 | bytes 13238272 | tf_op jit(solution)/shard_map/dot_general | solution.py:871
  383.1 0.7 copy.93
  383.8 1.4 copy-done.5
  385.2 14.2 %multiply_reduce_fusion.2 = (bf16[1024]{0:T(1024)(128)(2,1)S(1)}, bf16[1024]{0:T(1024)(128)(2,1)S(1)}, bf16[1024]{0:T(1024)(128)(2,1)S(1)}, bf16[1024]{0:T(1024)...) fusion(f32[1024,1024]{1,0:T(8,128)S(1)} %add_multiply_fusion, f32[1024,1024]{1,0:T(8,128)S(1)} %copy-done.5, ...), kind=kLoop, calls=%fused_computation.11 | loop fusion | flops 22014976 | bytes 10528768 | tf_op jit(solution)/shard_map/reduce_sum | solution.py:983
  399.6 0.4 convolution_convert_fusion.5
  400.0 0.5 convolution_convert_fusion.4
  400.6 0.4 concatenate.28
  400.9 1.0 bitcast_bitcast_fusion.refs_0_
  401.9 7.1 %fusion.36 = f32[1024,2048]{1,0:T(8,128)S(1)} fusion(bf16[1024,1024]{1,0:T(8,128)(2,1)} %copy-done.27, bf16[2048,1024]{1,0:T(8,128)(2,1)} %all-gather.2.cloned.1.call-done), kind=kOutput, calls=%fused_computation.108 | convolution fusion | flops 4294967296 | bytes 14680064 | tf_op jit(solution)/shard_map/dot_general | solution.py:875
  409.1 6.2 %convolution_convert_fusion = bf16[2048,1024]{1,0:T(8,128)(2,1)} fusion(bf16[1024,2048]{1,0:T(8,128)(2,1)S(1)} %bitcast.152, bf16[1024,1024]{1,0:T(8,128)(2,1)S(1)} %get-tuple-element.76), kind=kOutput, calls=%fused_computation.24 | convolution fusion | flops 4297064448 | bytes 10485760 | tf_op jit(solution)/shard_map/dot_general | solution.py:871
  415.3 6.2 %add_convert_fusion = bf16[1024,2048]{1,0:T(8,128)(2,1)} fusion(f32[1024,2048]{1,0:T(8,128)S(1)} %fusion.36, bf16[1024,1024]{1,0:T(8,128)(2,1)S(1)} %get-tuple-element.76, bf16[2048,1024]{1,0:T(8,128)(2,1)S(1)} %bitcast.188), kind=kOutput, calls=%fused_computation | convolution fusion | flops 4299161600 | bytes 18874368 | tf_op jit(solution)/shard_map/dot_general | solution.py:875
  421.5 79.8 %scatter_end.1 = (f32[320,128]{1,0:T(8,128)}, bf16[2,4,64,1024]{3,2,1,0:T(8,128)(2,1)}, f32[256,2048]{1,0:T(8,128)}, f32[4,40,256]{2,1,0:T(8,128)}) custom-call(bf16[8,320,128]{2,1,0:T(8,128)(2,1)} %bitcast_bitcast_fusion.refs_0_, bf16[8,256,1024]{2,1,0:T(8,128)(2,1)} %bitcast.147, bf16[4,256,2048]{2,1,0:T(8,128)(2,1)} %bitcast.148, ...), custom_call_target="tpu_custom_call" | custom-call | tf_op jit(solution)/shard_map/scatter_end/pallas_call | solution.py:850
  501.3 1.3 slice.175
  502.6 1.3 slice.180
  503.9 1.5 slice.178
  505.4 1.0 reshape.173
  506.4 0.7 broadcast_in_dim.43
  507.1 0.6 copy.52
  507.7 0.6 copy.50
  508.3 0.7 broadcast_in_dim.40
  509.0 1.5 copy.66
  510.5 2.7 copy.53
  513.2 2.2 reshape.174
  515.4 2.1 fusion.6
  517.5 0.5 slice_bitcast_fusion.8
  518.0 0.6 slice_bitcast_fusion.1
  518.7 3.5 broadcast_multiply_fusion
  522.1 4.3 fusion.11
  526.4 1.0 copy.97
  (87 shorter events, 0.8 us)
Async XLA Ops:
  7.2 81.7 %copy-start = (f32[1,3,4096]{2,0,1:T(1,128)S(1)}, f32[1,3,4096]{2,0,1:T(1,128)}, u32[]{:S(2)}) copy-start(f32[1,3,4096]{2,0,1:T(1,128)} %param.26) | copy-start | bytes 147460
  7.2 201.2 %all-gather.2.cloned.1.call-start = ((), (), s32[]{:S(2)}) async-start(), calls=%async_computation.1 | async-start | bytes 4718592 | tf_op jit(solution)/shard_map/all_gather | solution.py:916
  7.9 3.8 copy-start.17
  7.9 3.8 copy-start.18
  7.9 3.8 copy-start.19
  7.9 3.8 copy-start.20
  7.9 3.8 copy-start.21
  7.9 3.8 copy-start.22
  7.9 3.8 copy-start.23
  10.4 78.5 %copy-start.13 = (f32[1,16,4096]{2,1,0:T(8,128)S(1)}, f32[1,16,4096]{2,1,0:T(8,128)}, u32[]{:S(2)}) copy-start(f32[1,16,4096]{2,1,0:T(8,128)} %param.25) | copy-start | bytes 786436
  87.2 434.9 %reduce-scatter.2.cloned.1.call-start = ((), (), s32[]{:S(2)}) async-start(), calls=%async_computation.2 | async-start | bytes 5242880 | tf_op jit(solution)/shard_map/reduce_scatter | solution.py:953
  89.1 3.5 copy-start.8
  98.8 4.8 copy-start.4
  103.6 22.6 %copy-start.2 = (bf16[1024,1024]{1,0:T(8,128)(2,1)}, bf16[1024,1024]{1,0:T(8,128)(2,1)S(1)}, u32[]{:S(2)}) copy-start(bf16[1024,1024]{1,0:T(8,128)(2,1)S(1)} %get-tuple-element.71.act_ref) | copy-start | bytes 6291460
  208.4 7.7 %copy-start.25 = (bf16[8,128,2048]{2,1,0:T(8,128)(2,1)S(1)}, bf16[8,128,2048]{2,1,0:T(8,128)(2,1)}, u32[]{:S(2)}) copy-start(bf16[8,128,2048]{2,1,0:T(8,128)(2,1)} %get-tuple-element.47) | copy-start | bytes 12582916
  208.4 7.7 %copy-start.26 = (bf16[4,256,2048]{2,1,0:T(8,128)(2,1)S(1)}, bf16[4,256,2048]{2,1,0:T(8,128)(2,1)}, u32[]{:S(2)}) copy-start(bf16[4,256,2048]{2,1,0:T(8,128)(2,1)} %get-tuple-element.48) | copy-start | bytes 12582916
  225.7 12.4 %copy-start.27 = (bf16[1024,1024]{1,0:T(8,128)(2,1)}, bf16[1024,1024]{1,0:T(8,128)(2,1)S(1)}, u32[]{:S(2)}) copy-start(bf16[1024,1024]{1,0:T(8,128)(2,1)S(1)} %get-tuple-element.73) | copy-start | bytes 6291460
  377.6 5.4 %copy-start.15 = (f32[16,8,128]{2,1,0:T(8,128)S(1)}, f32[16,8,128]{2,1,0:T(8,128)}, u32[]{:S(2)}) copy-start(f32[16,8,128]{2,1,0:T(8,128)} %get-tuple-element.57) | copy-start | bytes 196612
  377.6 5.4 %copy-start.16 = (f32[16,8,128]{2,1,0:T(8,128)S(1)}, f32[16,8,128]{2,1,0:T(8,128)}, u32[]{:S(2)}) copy-start(f32[16,8,128]{2,1,0:T(8,128)} %get-tuple-element.58) | copy-start | bytes 196612
  383.0 2.2 copy-start.5
  385.2 14.3 %copy-start.7 = (bf16[1024,1024]{1,0:T(8,128)(2,1)S(1)}, bf16[1024,1024]{1,0:T(8,128)(2,1)}, u32[]{:S(2)}) copy-start(bf16[1024,1024]{1,0:T(8,128)(2,1)} %get-tuple-element.50) | copy-start | bytes 6291460
  385.2 14.3 %copy-start.10 = (bf16[160,1024]{1,0:T(8,128)(2,1)S(1)}, bf16[160,1024]{1,0:T(8,128)(2,1)}, u32[]{:S(2)}) copy-start(bf16[160,1024]{1,0:T(8,128)(2,1)} %total_over_seq.2) | copy-start | bytes 983044
  385.2 14.8 %copy-start.3 = (bf16[1024,1024]{1,0:T(8,128)(2,1)S(1)}, bf16[1024,1024]{1,0:T(8,128)(2,1)}, u32[]{:S(2)}) copy-start(bf16[1024,1024]{1,0:T(8,128)(2,1)} %copy-done.2) | copy-start | bytes 6291460
  385.2 14.8 %copy-start.11 = (bf16[160,1024]{1,0:T(8,128)(2,1)S(1)}, bf16[160,1024]{1,0:T(8,128)(2,1)}, u32[]{:S(2)}) copy-start(bf16[160,1024]{1,0:T(8,128)(2,1)} %total_over_seq.3) | copy-start | bytes 983044
  401.9 7.2 %copy-start.9 = (bf16[4,256,2048]{2,1,0:T(8,128)(2,1)S(1)}, bf16[4,256,2048]{2,1,0:T(8,128)(2,1)}, u32[]{:S(2)}) copy-start(bf16[4,256,2048]{2,1,0:T(8,128)(2,1)} %get-tuple-element.41) | copy-start | bytes 12582916
  409.0 6.2 %copy-start.24 = (bf16[8,4,64,1024]{3,2,1,0:T(8,128)(2,1)S(1)}, bf16[8,4,64,1024]{3,2,1,0:T(8,128)(2,1)}, u32[]{:S(2)}) copy-start(bf16[8,4,64,1024]{3,2,1,0:T(8,128)(2,1)} %get-tuple-element.42) | copy-start | bytes 12582916
  510.5 4.9 copy-start.6
  513.2 4.3 copy-start.14
  518.7 8.7 %copy-start.1 = (f32[1,3,4096]{2,0,1:T(1,128)S(1)}, f32[1,3,4096]{2,0,1:T(1,128)}, u32[]{:S(2)}) copy-start(f32[1,3,4096]{2,0,1:T(1,128)} %param.26) | copy-start | bytes 147460
  522.1 4.3 copy-start.12
Sparse Core Ops, SparseCore 0:
  87.4 90.6 all-gather.1
  238.2 42.8 reduce-scatter.1

commit v4 on v3

--- a/solution.py
+++ b/solution.py
@@ -15,6 +15,18 @@
 BF16 = jnp.bfloat16
 
 
+def dot_nn(a, b):
+    return jnp.dot(a, b, preferred_element_type=F32)
+
+
+def dot_tn(a, b):
+    return lax.dot_general(a, b, (((0,), (0,)), ((), ())), preferred_element_type=F32)
+
+
+def dot_nt(a, b):
+    return lax.dot_general(a, b, (((1,), (1,)), ((), ())), preferred_element_type=F32)
+
+
 def sigmoid(v):
     return 1.0 / (1.0 + jnp.exp(-v))
 
@@ -36,7 +48,7 @@
 
 
 MESH_ID = pl.DeviceIdType.MESH
-VMEM_MOST = 60 * 1024 * 1024
+VMEM_MOST = 63 * 1024 * 1024 + 512 * 1024
 
 
 class Grid:
@@ -164,37 +176,40 @@
 
 
 class Scatter:
-    def __init__(self, grid, src, scratch):
-        self.grid, self.src = grid, src
-        (
-            self.xbuf, self.own, self.stage, self.zbuf, self.acc,
-            self.x_s, self.x_r, self.z_s, self.z_r, self.o_s,
-        ) = scratch
+    def __init__(self, grid, src, scratch, inside=False):
+        self.grid, self.src, self.inside = grid, src, inside
+        if not inside:
+            self.own, self.o_s = scratch[:2]
+            scratch = scratch[2:]
+        self.xbuf, self.stage, self.zbuf, self.acc = scratch[:4]
+        self.x_s, self.x_r, self.z_s, self.z_r = scratch[4:]
 
     @staticmethod
-    def scratch(lines, fast, shape):
+    def scratch(lines, fast, shape, inside=False):
         dma = pltpu.SemaphoreType.DMA
-        return [
+        shape = tuple(shape)
+        loads = [] if inside else [pltpu.VMEM((lines,) + shape, BF16), dma((lines,))]
+        return loads + [
             pltpu.VMEM((lines, fast - 1) + shape, BF16),
-            pltpu.VMEM((lines,) + shape, BF16),
             pltpu.VMEM((lines - 1,) + shape, BF16),
             pltpu.VMEM((lines - 1,) + shape, BF16),
             pltpu.VMEM(shape, F32),
-            dma((lines, fast)), dma((lines, fast)), dma((lines,)), dma((lines,)), dma((lines,)),
+            dma((lines, fast)), dma((lines, fast)), dma((lines,)), dma((lines,)),
         ]
+
+    def index(self, k, e):
+        return self.grid.at(self.grid.line_peer(k), self.grid.lane_peer(e))
 
     def across(self, k, e):
         grid = self.grid
-        lane = grid.lane_peer(e)
         return grid.copy(
-            self.src.at[grid.at(grid.line_peer(k), lane)], self.xbuf.at[k, e - 1],
-            self.x_s.at[k, e], self.x_r.at[k, e], grid.at(grid.line, lane),
+            self.src.at[self.index(k, e)], self.xbuf.at[k, e - 1],
+            self.x_s.at[k, e], self.x_r.at[k, e], grid.at(grid.line, grid.lane_peer(e)),
         )
 
     def local(self, k):
-        grid = self.grid
         return pltpu.make_async_copy(
-            self.src.at[grid.at(grid.line_peer(k), grid.lane)], self.own.at[k], self.o_s.at[k]
+            self.src.at[self.index(k, 0)], self.own.at[k], self.o_s.at[k]
         )
 
     def along(self, k):
@@ -211,23 +226,30 @@
         for k in self.order():
             for e in range(1, self.grid.fast):
                 self.across(k, e).start()
-            self.local(k).start()
+            if not self.inside:
+                self.local(k).start()
 
     def rows(self, step):
         count = self.acc.shape[0]
         size = 16 if count % 16 == 0 else 8
+
         def run(i, carry):
             step(pl.ds(pl.multiple_of(i * size, size), size))
             return carry
+
         lax.fori_loop(0, count // size, run, 0)
 
     def middle(self, k):
         for e in range(1, self.grid.fast):
             self.across(k, e).wait_recv()
-        self.local(k).wait()
+        if self.inside:
+            own = self.src.at[self.index(k, 0)]
+        else:
+            self.local(k).wait()
+            own = self.own.at[k]
 
         def add(at):
-            total = self.own[k, at, :].astype(F32)
+            total = own[at, :].astype(F32)
             for e in range(self.grid.fast - 1):
                 total = total + self.xbuf[k, e, at, :].astype(F32)
             if k > 0:
@@ -239,7 +261,7 @@
         if k > 0:
             self.along(k).start()
 
-    def finish(self, out_ref):
+    def finish(self, write):
         for k in range(1, self.grid.lines):
             self.along(k).wait_recv()
 
@@ -247,7 +269,7 @@
             total = self.acc[at, :]
             for k in range(self.grid.lines - 1):
                 total = total + self.zbuf[k, at, :].astype(F32)
-            out_ref[at, :] = total.astype(out_ref.dtype)
+            write(at, total)
 
         self.rows(add)
 
@@ -259,6 +281,13 @@
                 self.along(k).wait_send()
 
 
+def into(ref):
+    def write(at, total):
+        ref[at, :] = total.astype(ref.dtype)
+
+    return write
+
+
 class Exchange:
     def __init__(self, grid, src, dst, sems):
         self.grid, self.src, self.dst = grid, src, dst
@@ -302,6 +331,57 @@
 def grids(shape):
     lines, fast, seq_lines = shape
     return Grid("seg", lines, fast), Grid("seq", seq_lines, 2)
+
+
+def sum_over_seq(seq, x_ref, out_ref, half, got, mine, others, whole, *sems):
+    lane_s, lane_r, line_s, line_r, back_s, back_r = sems
+    width = x_ref.shape[1] // 2
+    lines = seq.lines
+    other = 1 - seq.lane
+    left = pl.ds(0, width)
+    right = pl.ds(width, width)
+
+    @pl.when(seq.lane == 0)
+    def _():
+        half[...] = x_ref[:, right].astype(BF16)
+
+    @pl.when(seq.lane == 1)
+    def _():
+        half[...] = x_ref[:, left].astype(BF16)
+
+    swap = seq.copy(half, got, lane_s, lane_r, seq.at(seq.line, other))
+    swap.start()
+    swap.wait()
+
+    @pl.when(seq.lane == 0)
+    def _():
+        mine[...] = (x_ref[:, left] + got[...].astype(F32)).astype(BF16)
+
+    @pl.when(seq.lane == 1)
+    def _():
+        mine[...] = (x_ref[:, right] + got[...].astype(F32)).astype(BF16)
+
+    copies = [
+        seq.copy(
+            mine, others.at[k - 1], line_s.at[k], line_r.at[k], seq.at(seq.line_peer(k), seq.lane)
+        )
+        for k in range(1, lines)
+    ]
+    for copy in copies:
+        copy.start()
+    for copy in copies:
+        copy.wait()
+    total = mine[...].astype(F32)
+    for k in range(lines - 1):
+        total = total + others[k].astype(F32)
+    whole[seq.lane] = total.astype(BF16)
+    back = seq.copy(
+        whole.at[seq.lane], whole.at[seq.lane], back_s, back_r, seq.at(seq.line, other)
+    )
+    back.start()
+    back.wait()
+    out_ref[:, left] = whole[0]
+    out_ref[:, right] = whole[1]
 
 
 def forward_kernel(
@@ -374,43 +454,48 @@
 
 def backward_kernel(
     shape, steps,
-    pre_ref, act_ref, gy_ref, bc_ref, a_ref, skip_ref, check_ref, first_src, second_src,
-    gdt_ref, gact_ref, gbc_ref, agrad_ref, start_ref, dtb_ref, sgrad_ref, first_out, second_out,
-    carry_s, rate_pl, drive_pl, gy_pl, grate_pl, thr_pl, prod, part, *scratch,
+    pre_ref, act_ref, gy_ref, bc_ref, a_ref, skip_ref, check_ref, wdt_ref, low_ref, base_ref,
+    first_src, second_src, third_src,
+    gact_ref, agrad_ref, start_ref, dtb_ref, sgrad_ref, dtp_ref, mix_ref,
+    first_out, second_out, third_out,
+    carry_s, rate_pl, drive_pl, gy_pl, grate_pl, thr_pl, prod, part, mix_s, *scratch,
 ):
     count = pre_ref.shape[0]
     width, planes, _ = a_ref.shape
-    seg, _ = grids(shape)
-    half = len(scratch) // 2
-    first, second = (
-        Scatter(seg, first_src, scratch[:half]), Scatter(seg, second_src, scratch[half:])
-    )
-
-    @pl.when(pl.program_id(0) == 0)
+    low_rank = wdt_ref.shape[0]
+    seg, seq = grids(shape)
+    first, second, third = (
+        Scatter(grid, src, scratch[10 * i : 10 * i + 10])
+        for i, (grid, src) in enumerate(((seg, first_src), (seg, second_src), (seq, third_src)))
+    )
+    step = pl.program_id(0)
+
+    @pl.when(step == 0)
     def _():
-        meet((seg,))
+        meet((seg, seq))
         first.begin()
+        third.begin()
         second.begin()
         carry_s[...] = jnp.zeros_like(carry_s)
         agrad_ref[...] = jnp.zeros_like(agrad_ref)
         dtb_ref[...] = jnp.zeros_like(dtb_ref)
         sgrad_ref[...] = jnp.zeros_like(sgrad_ref)
+        dtp_ref[...] = jnp.zeros_like(dtp_ref)
 
     pre = pre_ref[...]
     rate = softplus(pre)
     act = act_ref[...].astype(F32)
-    gy = gy_ref[...]
     to_planes(rate_pl, rate)
     to_planes(drive_pl, rate * act)
-    to_planes(gy_pl, gy)
+    to_planes(gy_pl, gy_ref[...])
     groups = count // UNROLL
 
     def group(j, carry):
         k = groups - 1 - j
-        first = k * UNROLL
-        rates = [rate_pl[pl.ds(first + i, planes, stride=count), :] for i in range(UNROLL)]
-        drives = [drive_pl[pl.ds(first + i, planes, stride=count), :] for i in range(UNROLL)]
-        gys = [gy_pl[pl.ds(first + i, planes, stride=count), :] for i in range(UNROLL)]
+        at = k * UNROLL
+        rates = [rate_pl[pl.ds(at + i, planes, stride=count), :] for i in range(UNROLL)]
+        drives = [drive_pl[pl.ds(at + i, planes, stride=count), :] for i in range(UNROLL)]
+        gys = [gy_pl[pl.ds(at + i, planes, stride=count), :] for i in range(UNROLL)]
         g_rate = [None] * UNROLL
         through = [None] * UNROLL
         for n in range(width):
@@ -419,12 +504,12 @@
             decays = []
             for i in range(UNROLL):
                 decays.append(jnp.exp2(rates[i] * a))
-                states.append(decays[i] * states[i] + bc_ref[first + i, n] * drives[i])
+                states.append(decays[i] * states[i] + bc_ref[at + i, n] * drives[i])
             lam = carry_s[n]
             acc = agrad_ref[n]
             for i in reversed(range(UNROLL)):
-                lam = lam + bc_ref[first + i, width + n] * gys[i]
-                b_term = bc_ref[first + i, n] * lam
+                lam = lam + bc_ref[at + i, width + n] * gys[i]
+                b_term = bc_ref[at + i, n] * lam
                 prod[pl.ds((i * 2 * width + n) * planes, planes), :] = lam * drives[i]
                 prod[pl.ds((i * 2 * width + width + n) * planes, planes), :] = (
                     states[i + 1] * gys[i]
@@ -438,25 +523,54 @@
             carry_s[n] = lam
             agrad_ref[n] = acc
         for i in range(UNROLL):
-            grate_pl[pl.ds(first + i, planes, stride=count), :] = g_rate[i]
-            thr_pl[pl.ds(first + i, planes, stride=count), :] = through[i]
+            grate_pl[pl.ds(at + i, planes, stride=count), :] = g_rate[i]
+            thr_pl[pl.ds(at + i, planes, stride=count), :] = through[i]
             for q in range(2 * width // 8):
                 base = (i * 2 * width + q * 8) * planes
                 total = prod[pl.ds(base, 8, stride=planes), :]
                 for s in range(1, planes):
                     total = total + prod[pl.ds(base + s, 8, stride=planes), :]
-                row = pl.multiple_of((first + i) * 2 * width + q * 8, 8)
+                row = pl.multiple_of((at + i) * 2 * width + q * 8, 8)
                 part[pl.ds(row, 8), :] = total
         return carry
 
-    lax.fori_loop(0, groups, group, 0)
+    events = [functools.partial(s.middle, k) for s in (first, second) for k in s.order()]
+    ticks = 2 * steps
+    plan = [[] for _ in range(ticks)]
+    for j, event in enumerate(events):
+        plan[min(ticks - 1, ticks * (j + 1) // len(events))].append(event)
+    for k in third.order():
+        plan[min(ticks - 1, 2)].append(functools.partial(third.middle, k))
+
+    def add_base(at, total):
+        third_out[at, :] = (total + base_ref[at, :].astype(F32)).astype(BF16)
+
+    plan[min(ticks - 1, 9)].append(functools.partial(third.finish, add_base))
+
+    def part_of_step(h, carry):
+        lax.fori_loop(h * (groups // 2), (h + 1) * (groups // 2), group, 0)
+        for tick in range(ticks - 1):
+            if plan[tick]:
+
+                @pl.when(step * 2 + h == tick)
+                def _():
+                    for event in plan[tick]:
+                        event()
+
+        return carry
+
+    lax.fori_loop(0, 2, part_of_step, 0)
     g_rate = from_planes(grate_pl, count, planes) * (1.0 / LOG2E)
     through = from_planes(thr_pl, count, planes)
+    pre = pre_ref[...]
+    rate = softplus(pre)
+    act = act_ref[...].astype(F32)
+    gy = gy_ref[...]
     g_dtpre = ((g_rate + act * through) * sigmoid(pre)).astype(BF16)
-    gdt_ref[...] = g_dtpre
     gact_ref[...] = gy * skip_ref[...] + rate * through
     dtb_ref[...] += jnp.sum(g_dtpre.astype(F32), axis=0, keepdims=True)
     sgrad_ref[...] += jnp.sum(gy * act, axis=0, keepdims=True)
+    dtp_ref[...] += dot_nn(low_ref[...], g_dtpre)
     rows = 2 * width
     ones = jnp.ones((LANES, LANES), F32)
     sums = jnp.dot(part[...], ones, preferred_element_type=F32)
@@ -464,22 +578,21 @@
     pick = lax.broadcasted_iota(jnp.int32, (1, rows, LANES), 1) == lax.broadcasted_iota(
         jnp.int32, (1, rows, LANES), 2
     )
-    gbc_ref[...] = jnp.sum(jnp.where(pick, sums, 0.0), axis=1)
-
-    events = [(s, k) for s in (first, second) for k in s.order()]
-    for j, (scatter, k) in enumerate(events):
-
-        @pl.when(pl.program_id(0) == min(steps - 1, steps * (j + 1) // len(events)))
-        def _():
-            scatter.middle(k)
-
-    @pl.when(pl.program_id(0) == steps - 1)
+    g_bc = jnp.sum(jnp.where(pick, sums, 0.0), axis=1)
+    tokens_at = pl.ds(pl.multiple_of((steps - 1 - step) * count, count), count)
+    mix_s[pl.ds(0, low_rank), tokens_at] = dot_nt(wdt_ref[...], g_dtpre)
+    mix_s[pl.ds(low_rank, rows), tokens_at] = g_bc.T[:rows]
+
+    @pl.when(step == steps - 1)
     def _():
         start_ref[...] = carry_s[...]
-        first.finish(first_out)
-        second.finish(second_out)
-        first.drain()
-        second.drain()
+        sum_over_seq(seq, mix_s, mix_ref, *scratch[30:])
+        for event in plan[ticks - 1]:
+            event()
+        first.finish(into(first_out))
+        second.finish(into(second_out))
+        for scatter in (first, second, third):
+            scatter.drain()
 
 
 def forward_scan(shape, pre, act, bc, a2, skip, init, weight, cot, block):
@@ -529,14 +642,23 @@
     )(pre, act, bc, a2, skip, init, weight, cot)
 
 
-def backward_scan(shape, pre, act, gy, bc, a2, skip, checks, first, second, block):
+def backward_scan(
+    shape, pre, act, gy, bc, a2, skip, checks, w_dt, dt_low, base, first, second, third, block
+):
+    lines, fast, seq_lines = shape
     length, features = pre.shape
     width, planes, _ = a2.shape
+    low_rank = w_dt.shape[0]
     steps = length // block
     rows = pl.BlockSpec((block, features), lambda i: (steps - 1 - i, 0))
     whole = pl.BlockSpec((width, planes, LANES), lambda i: (0, 0, 0))
-    line = pl.BlockSpec((1, features), lambda i: (0, 0))
+
+    def all_of(rows, columns):
+        return pl.BlockSpec((rows, columns), lambda i: (0, 0))
+
+    line = all_of(1, features)
     plane = pltpu.VMEM((planes * block, LANES), F32)
+    mixed = (low_rank + 2 * width, length)
     return pl.pallas_call(
         functools.partial(backward_kernel, shape, steps),
         grid=(steps,),
@@ -549,33 +671,37 @@
             pl.BlockSpec(
                 (block // UNROLL, width, planes, LANES), lambda i: (steps - 1 - i, 0, 0, 0)
             ),
-            ANY, ANY,
+            all_of(low_rank, features),
+            pl.BlockSpec((low_rank, block), lambda i: (0, steps - 1 - i)),
+            all_of(*base.shape),
+            ANY, ANY, ANY,
         ],
         out_specs=[
-            rows, rows,
-            pl.BlockSpec((block, LANES), lambda i: (steps - 1 - i, 0)),
-            whole, whole, line, line,
-            pl.BlockSpec(first.shape[1:], lambda i: (0, 0)),
-            pl.BlockSpec(second.shape[1:], lambda i: (0, 0)),
+            rows, whole, whole, line, line, all_of(low_rank, features), all_of(*mixed),
+            all_of(*first.shape[1:]), all_of(*second.shape[1:]), all_of(*base.shape),
         ],
         out_shape=[
-            jax.ShapeDtypeStruct((length, features), BF16),
             jax.ShapeDtypeStruct((length, features), F32),
-            jax.ShapeDtypeStruct((length, LANES), F32),
             jax.ShapeDtypeStruct((width, planes, LANES), F32),
             jax.ShapeDtypeStruct((width, planes, LANES), F32),
             jax.ShapeDtypeStruct((1, features), F32),
             jax.ShapeDtypeStruct((1, features), F32),
+            jax.ShapeDtypeStruct((low_rank, features), F32),
+            jax.ShapeDtypeStruct(mixed, BF16),
             jax.ShapeDtypeStruct(first.shape[1:], BF16),
             jax.ShapeDtypeStruct(second.shape[1:], F32),
+            jax.ShapeDtypeStruct(base.shape, BF16),
         ],
         scratch_shapes=[pltpu.VMEM((width, planes, LANES), F32)]
         + [plane] * 5
         + [
             pltpu.VMEM((UNROLL * 2 * width * planes, LANES), F32),
             pltpu.VMEM((block * 2 * width, LANES), F32),
-            *Scatter.scratch(shape[0], shape[1], tuple(first.shape[1:])),
-            *Scatter.scratch(shape[0], shape[1], tuple(second.shape[1:])),
+            pltpu.VMEM(mixed, F32),
+            *Scatter.scratch(lines, fast, first.shape[1:]),
+            *Scatter.scratch(lines, fast, second.shape[1:]),
+            *Scatter.scratch(seq_lines, 2, third.shape[1:]),
+            *sum_scratch(seq_lines, *mixed),
         ],
         compiler_params=comm_params(6),
         cost_estimate=pl.CostEstimate(
@@ -584,7 +710,305 @@
             transcendentals=length * features * width,
         ),
         name="scan_backward",
-    )(pre, act, gy, bc, a2, skip, checks, first, second)
+    )(pre, act, gy, bc, a2, skip, checks, w_dt, dt_low, base, first, second, third)
+
+
+def finish_kernel(shape, taps, history, refs, scratch):
+    (
+        gact, x_in, act, tok, w_x, w_g, gs_gate,
+        mix, w_xt, head, kern, b_conv, dtp, a_grad, dtb, sgrad, g_half, own_tok, own_cot,
+        final, start,
+        small_out, halves_out, input_out, ends_out,
+    ) = refs
+    (
+        gc, xb, actb, tokb, wxb, wgb, gsg, gs_x, xg, q_src, pack, small_src, ends_src, x_half,
+        in_s, own_s,
+    ) = scratch[:16]
+    seg, seq = grids(shape)
+    length, feats = act.shape
+    at = 16
+    sets = []
+    for inside, size in ((True, 8), (True, 8), (True, 8)):
+        sets.append(scratch[at : at + size])
+        at += size
+    swaps_s = [scratch[at + 2 * i : at + 2 * i + 2] for i in range(3)]
+    small = Scatter(seg, small_src, sets[0], inside=True)
+    x_sum = Scatter(seg, xg, sets[1], inside=True)
+    q_sum = Scatter(seq, q_src, sets[2], inside=True)
+    loads = [
+        pltpu.make_async_copy(gact, gc.at[pl.ds(0, length)], in_s.at[0]),
+        pltpu.make_async_copy(x_in, xb.at[pl.ds(8, length)], in_s.at[1]),
+        pltpu.make_async_copy(tok, tokb, in_s.at[2]),
+        pltpu.make_async_copy(act, actb, in_s.at[3]),
+        pltpu.make_async_copy(gs_gate, gsg, in_s.at[4]),
+        pltpu.make_async_copy(w_g, wgb, in_s.at[5]),
+        pltpu.make_async_copy(w_x, wxb, in_s.at[6]),
+    ]
+    for load in loads:
+        load.start()
+    meet((seg, seq))
+    own_rows = g_half.shape[0] // (seq.lines * seq.fast)
+
+    def swap(half, src, sems):
+        return Exchange(
+            seq,
+            lambda p: src.at[pl.ds(pl.multiple_of(p * own_rows, own_rows), own_rows)],
+            lambda m: halves_out.at[half, m],
+            sems,
+        )
+
+    swap_g = swap(1, g_half, swaps_s[1])
+    swap_g.begin()
+    xb[pl.ds(0, 8), :] = head[...]
+    gc[pl.ds(length, 8), :] = jnp.zeros((8, feats), F32)
+    loads[0].wait()
+    big = LANES
+
+    def add_mixed(i, carry):
+        rows = pl.ds(pl.multiple_of(i * big, big), big)
+        gc[rows, :] += dot_tn(mix[:, rows], w_xt[...])
+        return carry
+
+    lax.fori_loop(0, length // big, add_mixed, 0)
+    loads[1].wait()
+    tall = 32
+    chunk = min(512, feats)
+    sums_at = 8 * (taps + 1)
+    pack[...] = jnp.zeros_like(pack)
+
+    def through_conv(i, carry):
+        t0 = pl.multiple_of(i * tall, tall)
+        for c in range(0, feats, chunk):
+            cols = pl.ds(c, chunk)
+            wide = xb[pl.ds(t0, tall + 8), cols]
+            rows = [wide[8 - history + k : 8 - history + k + tall] for k in range(taps)]
+            conv = b_conv[:, cols]
+            for k in range(taps):
+                conv = conv + kern[pl.ds(k, 1), cols] * rows[k]
+            sig = sigmoid(conv)
+            g_conv = gc[pl.ds(t0, tall), cols] * sig * (1.0 + conv * (1.0 - sig))
+            gc[pl.ds(t0, tall), cols] = g_conv
+            for k in range(taps):
+                term = g_conv * rows[k]
+                pack[pl.ds(8 * k, 8), cols] += sum(
+                    term[8 * j : 8 * j + 8] for j in range(tall // 8)
+                )
+            pack[pl.ds(8 * taps, 8), cols] += sum(
+                g_conv[8 * j : 8 * j + 8] for j in range(tall // 8)
+            )
+        return carry
+
+    lax.fori_loop(0, length // tall, through_conv, 0)
+    loads[2].wait()
+
+    def to_input(i, carry):
+        t0 = pl.multiple_of(i * tall, tall)
+        lines = tokb[pl.ds(t0, tall), :].astype(F32)
+        rstd = lax.rsqrt(jnp.mean(lines * lines, axis=1, keepdims=True) + EPSILON)
+        for c in range(0, feats, chunk):
+            cols = pl.ds(c, chunk)
+            wide = gc[pl.ds(t0, tall + 8), cols]
+            g_x = kern[pl.ds(0, 1), cols] * wide[history : history + tall]
+            for k in range(1, taps):
+                g_x = g_x + kern[pl.ds(k, 1), cols] * wide[history - k : history - k + tall]
+            gs_x[pl.ds(t0, tall), cols] = (rstd * g_x).astype(BF16)
+        return carry
+
+    lax.fori_loop(0, length // tall, to_input, 0)
+    loads[3].wait()
+    low_rank = dtp.shape[0]
+    mixes = mix.shape[0]
+    width = a_grad.shape[0]
+    part = small_src.shape[2]
+    xp = dot_nn(mix[...], actb[...])
+    for g in range(small_src.shape[0]):
+        cols = slice(g * part, (g + 1) * part)
+        small_src[g, pl.ds(0, low_rank), :] = dtp[:, cols].astype(BF16)
+        small_src[g, pl.ds(low_rank, mixes), :] = xp[:, cols].astype(BF16)
+        base = low_rank + mixes
+        small_src[g, pl.ds(base, width), :] = a_grad[:, cols].astype(BF16)
+        lines = [
+            jnp.sum(pack[pl.ds(8 * k, 8), cols], axis=0, keepdims=True) for k in range(taps + 1)
+        ]
+        lines += [dtb[:, cols], sgrad[:, cols]]
+        lines.append(jnp.zeros((16 - len(lines), part), F32))
+        small_src[g, pl.ds(base + width, 16), :] = jnp.concatenate(lines, axis=0).astype(BF16)
+    small.begin()
+
+    block_rows = xg.shape[1]
+
+    def partial(index):
+        cols = pl.ds(pl.multiple_of(index * block_rows, block_rows), block_rows)
+        xg[index] = dot_tn(tokb[:, cols], gs_x[...]).astype(BF16)
+
+    by_block = block_rows % LANES == 0
+    if not by_block:
+        for index in range(xg.shape[0]):
+            cols = slice(index * block_rows, (index + 1) * block_rows)
+            xg[index] = dot_tn(tokb[:, cols], gs_x[...]).astype(BF16)
+
+    def leave(j, carry):
+        k = seg.lines - 1 - j
+        for e in range(1, seg.fast):
+            if by_block:
+                partial(x_sum.index(k, e))
+            x_sum.across(k, e).start()
+        return carry
+
+    lax.fori_loop(0, seg.lines, leave, 0)
+    def stay(j, carry):
+        if by_block:
+            partial(x_sum.index(seg.lines - 1 - j, 0))
+        return carry
+
+    lax.fori_loop(0, seg.lines, stay, 0)
+    ends_in = jnp.concatenate(
+        [
+            final[...],
+            xb[pl.ds(length, 8), :][8 - history :],
+            start[...],
+            sum_head(gc, kern, history, taps),
+            jnp.zeros((ends_src.shape[1] - 2 * (width + history), feats), F32),
+        ],
+        axis=0,
+    )
+    piece = ends_src.shape[2]
+    for p in range(ends_src.shape[0]):
+        ends_src[p] = ends_in[:, p * piece : (p + 1) * piece]
+    end_swap = Exchange(seq, lambda p: ends_src.at[p], lambda m: ends_out.at[m], swaps_s[2])
+    end_swap.begin()
+    loads[4].wait()
+    loads[5].wait()
+    loads[6].wait()
+    own_len = own_tok.shape[0]
+    model = own_tok.shape[1]
+    wide = 512
+
+    def normed(index):
+        rows = pl.ds(pl.multiple_of(index * own_len, own_len), own_len)
+
+        def column(c, carry):
+            cols = pl.ds(pl.multiple_of(c * wide, wide), wide)
+            q_src[index, :, cols] = (
+                dot_nt(gsg[rows, :], wgb[cols, :]) + dot_nt(gs_x[rows, :], wxb[cols, :])
+            ).astype(BF16)
+            return carry
+
+        lax.fori_loop(0, model // wide, column, 0)
+
+    def leave_q(j, carry):
+        k = seq.lines - 1 - j
+        normed(q_sum.index(k, 1))
+        q_sum.across(k, 1).start()
+        return carry
+
+    def stay_q(j, carry):
+        normed(q_sum.index(seq.lines - 1 - j, 0))
+        return carry
+
+    lax.fori_loop(0, seq.lines, leave_q, 0)
+    lax.fori_loop(0, seq.lines, stay_q, 0)
+    for k in small.order():
+        small.middle(k)
+    for j, k in enumerate(x_sum.order()):
+        x_sum.middle(k)
+        if j == seg.lines - 2:
+            for m in q_sum.order():
+                q_sum.middle(m)
+
+    def input_grad(at, total):
+        own = own_tok[at, :].astype(F32)
+        square = 1.0 / (jnp.mean(own * own, axis=1, keepdims=True) + EPSILON)
+        input_out[at, :] = (
+            own_cot[at, :].astype(F32)
+            + total
+            - own * (square * jnp.mean(total * own, axis=1, keepdims=True))
+        ).astype(BF16)
+
+    q_sum.finish(input_grad)
+    small.finish(into(small_out))
+    x_sum.finish(into(x_half))
+    swap_x = swap(0, x_half, swaps_s[0])
+    swap_x.begin()
+    own = pl.ds(pl.multiple_of(seq.here * own_rows, own_rows), own_rows)
+    keeps = [
+        pltpu.make_async_copy(x_half.at[own], halves_out.at[0, seq.here], own_s.at[0]),
+        pltpu.make_async_copy(g_half.at[own], halves_out.at[1, seq.here], own_s.at[1]),
+        pltpu.make_async_copy(ends_src.at[seq.here], ends_out.at[seq.here], own_s.at[2]),
+    ]
+    for keep in keeps:
+        keep.start()
+    for scatter in (small, x_sum, q_sum):
+        scatter.drain()
+    for exchange in (swap_g, end_swap, swap_x):
+        exchange.arrived()
+        exchange.drain()
+    for keep in keeps:
+        keep.wait()
+
+
+def sum_head(gc, kern, history, taps):
+    top = gc[pl.ds(0, 8), :]
+    rows = []
+    for j in range(history):
+        rows.append(
+            sum(kern[pl.ds(k, 1), :] * top[j - k : j - k + 1] for k in range(min(j + 1, taps)))
+        )
+    return jnp.concatenate(rows, axis=0)
+
+
+def finish_all(shape, taps, history, big, small):
+    lines, fast, seq_lines = shape
+    segs, seqs = lines * fast, seq_lines * 2
+    gact, x_in, act, tok, w_x, w_g, gs_gate = big
+    mix, w_xt, head, kern, b_conv, dtp, a_grad, dtb, sgrad, g_half, own_tok, own_cot = small[:12]
+    length, feats = act.shape
+    own_len, model = own_tok.shape
+    width = a_grad.shape[0]
+    rows = dtp.shape[0] + mix.shape[0] + width + 16
+    block_rows = model // segs
+    own_rows = g_half.shape[0] // seqs
+    ends = (seqs, 2 * (width + history) + (-2 * (width + history)) % 8, feats // seqs)
+    dma = pltpu.SemaphoreType.DMA
+    scratch = [
+        pltpu.VMEM((length + 8, feats), F32),
+        pltpu.VMEM((length + 8, feats), F32),
+        pltpu.VMEM((length, feats), BF16),
+        pltpu.VMEM((length, model), BF16),
+        pltpu.VMEM((model, feats), BF16),
+        pltpu.VMEM((model, feats), BF16),
+        pltpu.VMEM((length, feats), BF16),
+        pltpu.VMEM((length, feats), BF16),
+        pltpu.VMEM((segs, block_rows, feats), BF16),
+        pltpu.VMEM((seqs, own_len, model), BF16),
+        pltpu.VMEM((8 * (taps + 1), feats), F32),
+        pltpu.VMEM((segs, rows, feats // segs), BF16),
+        pltpu.VMEM(ends, F32),
+        pltpu.VMEM((block_rows, feats), BF16),
+        dma((7,)), dma((3,)),
+        *Scatter.scratch(lines, fast, (rows, feats // segs), inside=True),
+        *Scatter.scratch(lines, fast, (block_rows, feats), inside=True),
+        *Scatter.scratch(seq_lines, 2, (own_len, model), inside=True),
+        *Exchange.semaphores(seqs), *Exchange.semaphores(seqs), *Exchange.semaphores(seqs),
+    ]
+
+    def kernel(*refs):
+        finish_kernel(shape, taps, history, refs[:25], refs[25:])
+
+    return pl.pallas_call(
+        kernel,
+        in_specs=[ANY] * 7 + [INSIDE] * 14,
+        out_specs=[INSIDE] * 4,
+        out_shape=[
+            jax.ShapeDtypeStruct((rows, feats // segs), F32),
+            jax.ShapeDtypeStruct((2, seqs, own_rows, feats), BF16),
+            jax.ShapeDtypeStruct((own_len, model), BF16),
+            jax.ShapeDtypeStruct(ends, F32),
+        ],
+        scratch_shapes=scratch,
+        compiler_params=comm_params(4),
+        name="finish",
+    )(*big, *small)
 
 
 def gather_kernel(
@@ -676,203 +1100,103 @@
     return w_x.reshape(-1, feats), small_all, tok.reshape(-1, tokens.shape[1]), g_part
 
 
-def total_kernel(shape, call, x_ref, out_ref, half, got, mine, others, whole, sems):
-    _, seq = grids(shape)
-    lane_s, lane_r, line_s, line_r, back_s, back_r = sems
-    width = x_ref.shape[1] // 2
-    lines = seq.lines
-    barrier = pltpu.get_barrier_semaphore()
-    other = 1 - seq.lane
-    for peer in [seq.at(seq.line, other)] + [
-        seq.at(seq.line_peer(k), seq.lane) for k in range(1, lines)
-    ]:
-        pl.semaphore_signal(barrier, inc=1, device_id={"seq": peer}, device_id_type=MESH_ID)
-    pl.semaphore_wait(barrier, lines)
-    left = pl.ds(0, width)
-    right = pl.ds(width, width)
-
-    @pl.when(seq.lane == 0)
-    def _():
-        half[...] = x_ref[:, right].astype(BF16)
-
-    @pl.when(seq.lane == 1)
-    def _():
-        half[...] = x_ref[:, left].astype(BF16)
-
-    swap = seq.copy(half, got, lane_s, lane_r, seq.at(seq.line, other))
-    swap.start()
-    swap.wait()
-
-    @pl.when(seq.lane == 0)
-    def _():
-        mine[...] = (x_ref[:, left] + got[...].astype(F32)).astype(BF16)
-
-    @pl.when(seq.lane == 1)
-    def _():
-        mine[...] = (x_ref[:, right] + got[...].astype(F32)).astype(BF16)
-
-    copies = [
-        seq.copy(
-            mine, others.at[k - 1], line_s.at[k], line_r.at[k], seq.at(seq.line_peer(k), seq.lane)
-        )
-        for k in range(1, lines)
-    ]
-    for copy in copies:
-        copy.start()
-    for copy in copies:
-        copy.wait()
-    total = mine[...].astype(F32)
-    for k in range(lines - 1):
-        total = total + others[k].astype(F32)
-    whole[seq.lane] = total.astype(BF16)
-    back = seq.copy(
-        whole.at[seq.lane], whole.at[seq.lane], back_s, back_r, seq.at(seq.line, other)
-    )
-    back.start()
-    back.wait()
-    out_ref[:, left] = whole[0]
-    out_ref[:, right] = whole[1]
-
-
-def total_over_seq(shape, x, collective_id):
-    lines = shape[2]
-    rows, width = x.shape
+def sum_scratch(seq_lines, rows, width):
     part = pltpu.VMEM((rows, width // 2), BF16)
     dma = pltpu.SemaphoreType.DMA
-
-    def kernel(x_ref, out_ref, half, got, mine, others, whole, *sems):
-        total_kernel(shape, collective_id, x_ref, out_ref, half, got, mine, others, whole, sems)
+    return [
+        part, part, part,
+        pltpu.VMEM((max(seq_lines - 1, 1), rows, width // 2), BF16),
+        pltpu.VMEM((2, rows, width // 2), BF16),
+        dma, dma, dma((seq_lines,)), dma((seq_lines,)), dma, dma,
+    ]
+
+
+def total_over_seq(shape, x, collective_id):
+    def kernel(x_ref, out_ref, *scratch):
+        _, seq = grids(shape)
+        meet((seq,))
+        sum_over_seq(seq, x_ref, out_ref, *scratch)
 
     return pl.pallas_call(
         kernel,
         in_specs=[INSIDE],
         out_specs=INSIDE,
         out_shape=jax.ShapeDtypeStruct(x.shape, BF16),
-        scratch_shapes=[
-            part, part, part,
-            pltpu.VMEM((max(lines - 1, 1), rows, width // 2), BF16),
-            pltpu.VMEM((2, rows, width // 2), BF16),
-            dma, dma, dma((lines,)), dma((lines,)), dma, dma,
-        ],
+        scratch_shapes=sum_scratch(shape[2], *x.shape),
         compiler_params=comm_params(collective_id),
         name="total_over_seq",
     )(x)
 
 
-def scatter_end(shape, over_seg, over_seq, g_half, ends):
-    lines, fast, seq_lines = shape
-    seqs = seq_lines * 2
-    count = len(over_seg)
-    blocks = [a.shape[1:] for a in over_seg]
-    own_rows = blocks[1][0] // seqs
-    feats = blocks[1][1]
-    scratch = []
-    spans = []
-    for block in blocks:
-        part = Scatter.scratch(lines, fast, tuple(block))
-        spans.append((len(scratch), len(scratch) + len(part)))
-        scratch += part
-    part = Scatter.scratch(seq_lines, 2, tuple(over_seq.shape[1:]))
-    spans.append((len(scratch), len(scratch) + len(part)))
-    scratch += part
-    tail = len(scratch)
-    scratch += [
-        pltpu.VMEM((blocks[1][0], feats), BF16),
-        *Exchange.semaphores(seqs), *Exchange.semaphores(seqs), *Exchange.semaphores(seqs),
-        pltpu.SemaphoreType.DMA((3,)),
-    ]
-
-    def kernel(*refs):
-        srcs = refs[:count]
-        q_src, g_in, ends_in = refs[count : count + 3]
-        small_out, halves_out, q_out, ends_out = refs[count + 3 : count + 7]
-        sc = refs[count + 7 :]
-        seg, seq = grids(shape)
-        meet((seg, seq))
-        scatters = [Scatter(seg, s, sc[a:b]) for s, (a, b) in zip(srcs, spans)]
-        q_sum = Scatter(seq, q_src, sc[spans[-1][0] : spans[-1][1]])
-        halves = (sc[tail], g_in)
-        sems = sc[tail + 1 : tail + 7]
-        local = sc[tail + 7]
-        end_swap = Exchange(
-            seq, lambda p: ends_in.at[p], lambda m: ends_out.at[m], sems[:2]
-        )
-        end_swap.begin()
-        q_sum.begin()
-        for s in scatters:
-            s.begin()
-
-        def swap(half, pair):
-            return Exchange(
-                seq,
-                lambda p: halves[half].at[pl.ds(pl.multiple_of(p * own_rows, own_rows), own_rows)],
-                lambda m: halves_out.at[half, m],
-                pair,
-            )
-
-        swaps = [swap(0, sems[2:4]), swap(1, sems[4:6])]
-        swaps[1].begin()
-        small, x_half = scatters
-        for k in small.order():
-            small.middle(k)
-        for j, k in enumerate(x_half.order()):
-            x_half.middle(k)
-            if j < seq_lines:
-                q_sum.middle(q_sum.order()[j])
-        small.finish(small_out)
-        q_sum.finish(q_out)
-        x_half.finish(halves[0])
-        swaps[0].begin()
-        own = []
-        for half in (0, 1):
-            own.append(
-                pltpu.make_async_copy(
-                    halves[half].at[
-                        pl.ds(pl.multiple_of(seq.here * own_rows, own_rows), own_rows)
-                    ],
-                    halves_out.at[half, seq.here],
-                    local.at[half],
-                )
-            )
-        own.append(
-            pltpu.make_async_copy(ends_in.at[seq.here], ends_out.at[seq.here], local.at[2])
-        )
-        for copy in own:
-            copy.start()
-        for s in scatters + [q_sum]:
-            s.drain()
-        for e in swaps + [end_swap]:
-            e.arrived()
-            e.drain()
-        for copy in own:
-            copy.wait()
-
+def unpack_kernel(
+    seqs, taps, history, low_rank, width,
+    small, halves, ends, mixed, input_grad, out_grad, weight, gain,
+    mixed_o, final_o, final_c, input_o, start_o, start_c, gain_o, in_o, cw_o, cb_o, xp_o, dtp_o,
+    dtb_o, a_o, skip_o, out_o,
+):
+    mixed_o[0] = mixed[...]
+    input_o[0] = input_grad[...]
+    out_o[...] = out_grad[...]
+    part = small.shape[1]
+    columns = xp_o.shape[1]
+    dtp_o[...] = small[pl.ds(0, low_rank), :]
+    turned = small[pl.ds(low_rank, low_rank), :].T
+    xp_o[:, pl.ds(0, low_rank)] = turned
+    xp_o[:, pl.ds(low_rank, columns - low_rank)] = small[
+        pl.ds(2 * low_rank, columns - low_rank), :
+    ].T
+    at = low_rank + columns
+    a_o[...] = small[pl.ds(at, width), :]
+    lines = small[pl.ds(at + width, 16), :]
+    cw_o[...] = lines[:taps]
+    cb_o[...] = lines[taps]
+    dtb_o[...] = lines[taps + 1]
+    skip_o[...] = lines[taps + 2]
+    each = final_o.shape[2] // part // seqs
+    for s in range(seqs):
+        rows = ends[s]
+        for g in range(each):
+            got = rows[:, g * part : (g + 1) * part]
+            cols = pl.ds((g * seqs + s) * part, part)
+            final_o[0, :, cols] = got[:width]
+            final_c[0, :, cols] = got[width : width + history]
+            start_o[0, :, cols] = got[width + history : 2 * width + history]
+            start_c[0, :, cols] = got[2 * width + history : 2 * (width + history)]
+    scale = gain[...]
+    total = jnp.zeros((in_o.shape[0], part), F32)
+    groups = halves.shape[3] // part
+    for half in range(2):
+        for s in range(seqs):
+            for g in range(groups):
+                raw = halves[half, s, :, g * part : (g + 1) * part].astype(F32)
+                cols = pl.ds(((half * groups + g) * seqs + s) * part, part)
+                in_o[:, cols] = raw * scale
+                total = total + raw * weight[:, cols].astype(F32)
+    gain_o[...] = jnp.sum(total.T, axis=0)
+
+
+def unpack(taps, history, low_rank, width, small, halves, ends, mixed, input_grad, out_grad,
+           weight, gain):
+    seqs, own_rows, feats = halves.shape[1:]
+    part = small.shape[1]
+    model = mixed.shape[1]
+    kept = ends.shape[2] * seqs
+    f32 = lambda *dims: jax.ShapeDtypeStruct(dims, F32)
     return pl.pallas_call(
-        kernel,
-        in_specs=[ANY] * (count + 1) + [INSIDE, INSIDE],
-        out_specs=[INSIDE] * 4,
+        functools.partial(unpack_kernel, seqs, taps, history, low_rank, width),
+        in_specs=[INSIDE] * 8,
+        out_specs=[INSIDE] * 16,
         out_shape=[
-            jax.ShapeDtypeStruct(blocks[0], F32),
-            jax.ShapeDtypeStruct((2, seqs, own_rows, feats), BF16),
-            jax.ShapeDtypeStruct(over_seq.shape[1:], F32),
-            jax.ShapeDtypeStruct(ends.shape, F32),
+            jax.ShapeDtypeStruct((1,) + mixed.shape, BF16),
+            f32(1, width, kept), f32(1, history, kept),
+            jax.ShapeDtypeStruct((1,) + input_grad.shape, BF16),
+            f32(1, width, kept), f32(1, history, kept),
+            f32(own_rows), f32(*weight.shape),
+            f32(taps, part), f32(part), f32(part, low_rank + 2 * width), f32(low_rank, part),
+            f32(part), f32(width, part), f32(part), f32(part, model),
         ],
-        scratch_shapes=scratch,
-        compiler_params=comm_params(4),
-        name="scatter_end",
-    )(*over_seg, over_seq, g_half, ends)
-
-
-def dot_nn(a, b):
-    return jnp.dot(a, b, preferred_element_type=F32)
-
-
-def dot_tn(a, b):
-    return lax.dot_general(a, b, (((0,), (0,)), ((), ())), preferred_element_type=F32)
-
-
-def dot_nt(a, b):
-    return lax.dot_general(a, b, (((1,), (1,)), ((), ())), preferred_element_type=F32)
+        name="unpack",
+    )(small, halves, ends, mixed, input_grad, out_grad, weight, gain)
 
 
 def body(
@@ -950,8 +1274,6 @@
     gate = rstd * dot_nn(tok, w_g_half)
     gated = (y_val * jax.nn.silu(gate)).astype(BF16)
     out_part = dot_nn(gated, w_out).astype(BF16)
-    mixed_out = lax.psum_scatter(out_part, "seq", scatter_dimension=0, tiled=True)
-    mixed_out = (mixed_out.astype(F32) + tokens[0].astype(F32)).astype(BF16)
 
     g_gated = dot_nt(cot, w_out)
     sig_gate = jax.nn.sigmoid(gate)
@@ -961,70 +1283,37 @@
     ).astype(BF16)
     out_grad = dot_tn(gated, cot).astype(BF16)
     gate_grad = dot_tn(tok, gs_gate).astype(BF16)
-    g_dtpre, g_actp, g_bc, a_sum, start, dtb_grad, skip_grad, g_half, out_grad = backward_scan(
-        shape, pre, act, gy, bc, a2, skip, checks,
-        gate_grad.reshape(segs, seqs * own_rows, feats),
-        out_grad.reshape(segs, part, model),
-        block,
-    )
-    g_mixed = jnp.concatenate([dot_nt(w_dt, g_dtpre), g_bc[:, : 2 * width].T], axis=0)
-    g_mixed = total_over_seq(shape, g_mixed, 3)
-    g_act = g_actp + dot_tn(g_mixed, w_xt)
-    sig_conv = jax.nn.sigmoid(conv_out)
-    g_conv = g_act * sig_conv * (1.0 + conv_out * (1.0 - sig_conv))
-    tail = jnp.concatenate([g_conv, jnp.zeros((history, feats), F32)], axis=0)
-    whole = jnp.concatenate([jnp.zeros((history, feats), F32), tail], axis=0)
-    g_xin = sum(kernel[k] * tail[history - k : history - k + length] for k in range(taps))
-    head_grad = sum(kernel[k] * whole[history - k : 2 * history - k] for k in range(taps))
-    gs_x = (rstd * g_xin).astype(BF16)
-    x_grad = dot_tn(tok, gs_x).astype(BF16)
-    q_part = (dot_nt(gs_gate, w_g_half) + dot_nt(gs_x, w_x_half)).astype(BF16)
-
-    cw_grad = jnp.stack([jnp.sum(g_conv * padded[k : k + length], axis=0) for k in range(taps)])
-    grads = jnp.concatenate(
-        [
-            dot_nn(dt_low, g_dtpre),
-            dot_nn(g_mixed, act),
-            a_sum.reshape(width, feats) * a_mat,
-            cw_grad,
-            jnp.sum(g_conv, axis=0, keepdims=True),
-            dtb_grad,
-            skip_grad,
-        ],
-        axis=0,
-    )
-    grads = jnp.pad(grads, ((0, -grads.shape[0] % 16), (0, 0)))
-    grads = grads.reshape(grads.shape[0], segs, part).transpose(1, 0, 2).astype(BF16)
-    ends = jnp.concatenate(
-        [
-            final.reshape(width, feats),
-            x_in[length - history :],
-            start.reshape(width, feats),
-            head_grad,
-        ],
-        axis=0,
-    )
-    ends = jnp.pad(ends, ((0, -ends.shape[0] % 8), (0, 0)))
-    grads, halves, q_own, ends = scatter_end(
-        shape,
-        [grads, x_grad.reshape(segs, seqs * own_rows, feats)],
-        q_part.reshape(seqs, own_len, model),
-        g_half,
-        ends.reshape(ends.shape[0], seqs, feats // seqs).transpose(1, 0, 2),
-    )
+    g_actp, a_sum, start, dtb_grad, skip_grad, dtp_grad, g_mixed, g_half, out_grad, mixed_out = (
+        backward_scan(
+            shape, pre, act, gy, bc, a2, skip, checks, w_dt, dt_low, tokens[0],
+            gate_grad.reshape(segs, seqs * own_rows, feats),
+            out_grad.reshape(segs, part, model),
+            out_part.reshape(seqs, own_len, model),
+            2 * block,
+        )
+    )
+    grads, halves, input_grad, ends = finish_all(
+        shape, taps, history,
+        (g_actp, x_in, act, tok, w_x_half, w_g_half, gs_gate),
+        (
+            g_mixed, w_xt,
+            jnp.pad(head, ((8 - history, 0), (0, 0))),
+            jnp.pad(kernel, ((0, -taps % 8), (0, 0))),
+            b_conv, dtp_grad, a_sum.reshape(width, feats) * a_mat, dtb_grad, skip_grad, g_half,
+            tokens[0], cotangent[0],
+            final.reshape(width, feats), start.reshape(width, feats),
+        ),
+    )
+    if part % LANES == 0:
+        return unpack(
+            taps, history, low_rank, width, grads, halves, ends, mixed_out, input_grad, out_grad,
+            in_proj, gain_col,
+        )
     ends = (
         ends.reshape(seqs, ends.shape[1], segs // seqs, part)
         .transpose(1, 2, 0, 3)
         .reshape(ends.shape[1], feats)
     )
-    own = tokens[0].astype(F32)
-    own_rstd = lax.rsqrt(jnp.mean(own * own, axis=1, keepdims=True) + EPSILON)
-    input_grad = (
-        cotangent[0].astype(F32)
-        + q_own
-        - own * (own_rstd * own_rstd) * jnp.mean(q_own * own, axis=1, keepdims=True)
-    ).astype(BF16)
-
     raw_grad = (
         halves.reshape(2, seqs, own_rows, segs, part)
         .transpose(2, 0, 3, 1, 4)

time: 536 us -> 486 us (0.907)
  other arithmetic: 38.2 us -> 11.2 us
  matrix products: 77.9 us -> 54.3 us
    pallas_call x1 -> x2, Pallas kernels: 79.8 us -> 108 us  [the longest x1 102 us: finish_all(): pl.pallas_call(kernel, in_specs=[ANY] * 7 + [INSIDE] * 14, out_specs=[INS...]
    reduce_sum x2 -> x0, other arithmetic: 16.3 us -> none  [the longest x1 14.2 us: body(): jnp.sum(g_conv * padded[k:k + length], axis=0)]
    dot_general x5 -> x2, matrix products: 27 us -> 11.6 us  [dot_nt(): lax.dot_general(a, b, (((1,), (1,)), ((), ())), preferred_element_type=F32)]
    dot_general x5 -> x3, matrix products: 30 us -> 16.3 us  [dot_tn(): lax.dot_general(a, b, (((0,), (0,)), ((), ())), preferred_element_type=F32)]
    pallas_call x1, Pallas kernels: 82.2 us -> 69.2 us  [forward_scan(): pl.pallas_call(functools.partial(forward_kernel, shape, steps), grid=(ste...]
    pallas_call x2 -> x1, Pallas kernels: 26.2 us -> 13.9 us  [total_over_seq(): pl.pallas_call(kernel, in_specs=[INSIDE], out_specs=INSIDE, out_shape=jax...]
    convert_element_type x3 -> x0, local copies, waits for them, and re-layouts: 5.84 us -> none  [the longest x2 4.88 us: body(): raw_grad = halves.reshape(2, seqs, own_rows, segs, part).transpose(2, 0,...]
    dot_general x5 -> x3, matrix products: 21 us -> 26.4 us  [dot_nn(): return jnp.dot(a, b, preferred_element_type=F32)]
  transfers between devices with their start and end apart: 2 -> 1, of which waited for: 0 -> 0; matrix products, arithmetic and copies ran while one was open for 19% -> 9% of each run, Pallas kernels for 56% -> 17%
where the time goes in v4:
time: 486 us
  Pallas kernels  380 us (78%)
  matrix products  54.3 us (11%)
  local copies, waits for them, and re-layouts  25.3 us (5%)
  between operations  14.3 us (3%)
  other arithmetic  11.2 us (2%)
    pallas_call x1, Pallas kernels, backward_scan(): pl.pallas_call(functools.partial(backward_kernel, shape, steps), grid=(st...  114 us
    pallas_call x1, Pallas kernels, finish_all(): pl.pallas_call(kernel, in_specs=[ANY] * 7 + [INSIDE] * 14, out_specs=[INS...  102 us
    pallas_call x1, Pallas kernels, gather_start(): pl.pallas_call(kernel, in_specs=[ANY, INSIDE, ANY], out_specs=[ANY] * 4,...  74.7 us
    pallas_call x1, Pallas kernels, forward_scan(): pl.pallas_call(functools.partial(forward_kernel, shape, steps), grid=(ste...  69.2 us
    dot_general x3, matrix products, dot_nn(): return jnp.dot(a, b, preferred_element_type=F32)  26.4 us
    dot_general x3, matrix products, dot_tn(): lax.dot_general(a, b, (((0,), (0,)), ((), ())), preferred_element_type=F32)  16.3 us
    pallas_call x1, Pallas kernels, total_over_seq(): pl.pallas_call(kernel, in_specs=[INSIDE], out_specs=INSIDE, out_shape=jax...  13.9 us
    dot_general x2, matrix products, dot_nt(): lax.dot_general(a, b, (((1,), (1,)), ((), ())), preferred_element_type=F32)  11.6 us
  transfers between devices with their start and end apart: 1, of which 0 were waited for; matrix products, arithmetic and copies ran while one was open for 9% of the time, Pallas kernels for 17%

profile of v4, /device:TPU:1, one launch (start us, length us, event | category | flops | bytes accessed | tf_op | source)
XLA Modules:
  0.0 485.6 jit_solution(952475318990924293)
XLA Ops:
  7.2 0.0 copy-start
  7.2 0.0 all-gather.2.cloned.1.call-start
  7.2 0.7 convert_bitcast_fusion.1
  7.9 0.0 copy-start.13
  7.9 0.0 copy-start.14
  7.9 0.0 copy-start.15
  8.0 1.5 multiply_convert_fusion.3
  9.5 0.8 reshape.118
  10.3 0.1 copy.61
  10.4 1.3 reshape.119.refs_0_
  11.7 0.0 copy-done.9
  11.7 0.0 copy-done.10
  11.7 0.0 copy-done.11
  11.7 0.0 copy-done.12
  11.7 0.0 copy-done.13
  11.7 0.0 copy-done.14
  11.7 0.0 copy-done.15
  11.7 0.1 concatenate.6
  11.8 0.6 pad.12.refs_1_
  12.4 74.7 %gather_start.1 = (bf16[8,4,64,1024]{3,2,1,0:T(8,128)(2,1)}, bf16[8,320,128]{2,1,0:T(8,128)(2,1)}, bf16[4,256,2048]{2,1,0:T(8,128)(2,1)}, bf16[4,64,1024]{2,1,0:T(8,128)(2,1)}) custom-call(bf16[4,2,64,1024]{3,2,1,0:T(8,128)(2,1)} %reshape.119.refs_0_, bf16[320,128]{1,0:T(8,128)(2,1)} %pad.12.refs_1_, bf16[256,2048]{1,0:T(8,128)(2,1)} %bitcast.97), custom_call_target="tpu_custom_call" | custom-call | tf_op jit(solution)/shard_map/gather_start/pallas_call | solution.py:1086
  87.2 0.0 all-gather.2.cloned.1.call-update
  87.2 1.5 copy.62
  88.8 0.7 slice.110
  89.5 3.1 multiply_reduce_fusion
  92.6 0.0 copy-done
  92.7 0.0 copy-start.6
  92.7 0.6 fusion.14
  93.3 7.6 %convolution_multiply_fusion.refs_1_ = f32[1024,1024]{1,0:T(8,128)S(1)} fusion(bf16[1024,2048]{1,0:T(8,128)(2,1)} %bitcast.93, bf16[2048,1024]{1,0:T(8,128)(2,1)} %bitcast.104, f32[1024]{0:T(1024)S(1)} %bitcast.131), kind=kOutput, calls=%fused_computation.21 | convolution fusion | flops 4296015872 | bytes 12587008 | tf_op jit(solution)/shard_map/dot_general | solution.py:19
  101.0 2.0 copy-done.4
  103.0 2.8 multiply_convert_fusion.2.act_ref.refs_2_
  105.8 0.0 copy-start.2
  105.8 1.3 copy-done.2
  107.1 1.7 fusion.13.x_ref
  108.8 13.9 %total_over_seq.1 = bf16[160,1024]{1,0:T(8,128)(2,1)} custom-call(f32[160,1024]{1,0:T(8,128)} %fusion.13.x_ref), custom_call_target="tpu_custom_call" | custom-call | tf_op jit(solution)/shard_map/total_over_seq/pallas_call | solution.py:1120
  122.7 0.9 slice.92
  123.5 1.7 slice.88.low_ref
  125.2 0.8 copy.63
  126.0 0.2 copy.40
  126.1 1.1 reshape_squeeze.7
  127.3 1.7 copy.64
  129.0 0.7 slice_bitcast_fusion
  129.7 0.6 pad.13.refs_9_
  130.3 0.6 pad.14.refs_10_
  130.9 0.7 copy.35.gain
  131.6 0.7 constant_dynamic-slice_fusion
  132.3 1.5 fusion.11.a_ref
  133.8 0.8 convert_bitcast_fusion.bc_ref
  134.6 3.7 convolution_add_fusion.pre_ref
  138.4 69.2 %scan_forward.1 = (f32[1024,1024]{1,0:T(8,128)}, f32[128,16,8,128]{3,2,1,0:T(8,128)}, f32[16,8,128]{2,1,0:T(8,128)}, bf16[8,128,2048]{2,1,0:T(8,128)(2,1)}, bf16[4,256,2048]{2,1,0:T(8,128)(2,1)}) custom-call(f32[1024,1024]{1,0:T(8,128)} %convolution_add_fusion.pre_ref, bf16[1024,1024]{1,0:T(8,128)(2,1)} %copy-done.2, f32[1024,32]{1,0:T(8,128)} %convert_bitcast_fusion.bc_ref, ...), custom_call_target="tpu_custom_call" | custom-call | flops 134217728 | bytes 25165824 | tf_op jit(solution)/shard_map/scan_forward/pallas_call | solution.py:606
  207.6 10.0 %fusion.15 = f32[1024,1024]{1,0:T(8,128)} fusion(bf16[1024,2048]{1,0:T(8,128)(2,1)} %bitcast.136, bf16[1024,2048]{1,0:T(8,128)(2,1)} %bitcast.138), kind=kOutput, calls=%fused_computation.53 | convolution fusion | flops 4294967296 | bytes 12582912 | tf_op jit(solution)/shard_map/dot_general | solution.py:27
  217.6 12.6 %multiply_convert_fusion = (bf16[1024,1024]{1,0:T(8,128)(2,1)S(1)}, bf16[1024,1024]{1,0:T(8,128)(2,1)S(1)}, f32[1024,1024]{1,0:T(8,128)}) fusion(f32[1024,1024]{1,0:T(8,128)} %get-tuple-element.50, f32[1024]{0:T(1024)S(1)} %bitcast.132, f32[1024,1024]{1,0:T(8,128)} %fusion.15, bf16[1024,2048]{1,0:T(8,128)(2,1)} %bitcast.94, ...), kind=kOutput, calls=%fused_computation.13 | convolution fusion | flops 4312793088 | bytes 25169920 | tf_op jit(solution)/shard_map/dot_general | solution.py:19
  230.2 6.1 %convolution_convert_fusion = bf16[1024,2048]{1,0:T(8,128)(2,1)} fusion(bf16[1024,1024]{1,0:T(8,128)(2,1)S(1)} %get-tuple-element.82, bf16[1024,2048]{1,0:T(8,128)(2,1)S(1)} %bitcast.139), kind=kOutput, calls=%fused_computation.18 | convolution fusion | flops 4297064448 | bytes 10485760 | tf_op jit(solution)/shard_map/dot_general | solution.py:19
  236.4 6.3 %convolution_convert_fusion.1 = bf16[1024,2048]{1,0:T(8,128)(2,1)} fusion(bf16[1024,1024]{1,0:T(8,128)(2,1)S(1)} %get-tuple-element.82, bf16[1024,2048]{1,0:T(8,128)(2,1)S(1)} %bitcast.137), kind=kOutput, calls=%fused_computation.19 | convolution fusion | flops 4297064448 | bytes 10485760 | tf_op jit(solution)/shard_map/dot_general | solution.py:23
  242.6 6.3 %convolution_convert_fusion.2 = bf16[2048,1024]{1,0:T(8,128)(2,1)} fusion(bf16[1024,2048]{1,0:T(8,128)(2,1)S(1)} %bitcast.96, bf16[1024,1024]{1,0:T(8,128)(2,1)S(1)} %get-tuple-element.83.refs_6_), kind=kOutput, calls=%fused_computation.20 | convolution fusion | flops 4297064448 | bytes 10485760 | tf_op jit(solution)/shard_map/dot_general | solution.py:23
  248.9 114.4 %scan_backward.1 = (f32[1024,1024]{1,0:T(8,128)}, f32[16,8,128]{2,1,0:T(8,128)}, f32[16,8,128]{2,1,0:T(8,128)}, f32[1,1024]{1,0:T(1,128)}, f32[1,1024]{1,0:T(1,1...) custom-call(f32[1024,1024]{1,0:T(8,128)} %convolution_add_fusion.pre, ...), custom_call_target="tpu_custom_call" | custom-call | flops 335544320 | bytes 29360128 | tf_op jit(solution)/shard_map/scan_backward/pallas_call | solution.py:662
  363.4 0.9 fusion.10
  364.2 0.6 copy.65
  364.9 0.0 copy-done.8
  364.9 1.5 copy_bitcast_fusion.4
  366.4 102.3 %finish.1 = (f32[320,128]{1,0:T(8,128)}, bf16[2,4,64,1024]{3,2,1,0:T(8,128)(2,1)}, bf16[256,2048]{1,0:T(8,128)(2,1)}, f32[4,40,256]{2,1,0:T(8,128)}) custom-call(f32[1024,1024]{1,0:T(8,128)} %get-tuple-element.51.refs_0_, f32[1024,1024]{1,0:T(8,128)} %copy-done.4, bf16[1024,1024]{1,0:T(8,128)(2,1)} %copy-done.2, bf16[1024,2048]{1,0:T(8,128)(2,1)} %bitcast.95, ...), custom_call_target="tpu_custom_call" | custom-call | tf_op jit(solution)/shard_map/finish/pallas_call | solution.py:998
  468.7 5.7 %unpack.1 = (bf16[1,256,2048]{2,1,0:T(8,128)(2,1)}, f32[1,16,1024]{2,1,0:T(8,128)}, f32[1,3,1024]{2,1,0:T(4,128)}, bf16[1,256,2048]{2,1,0:T(8,128)(2,1)}, f32[1,...) custom-call(f32[320,128]{1,0:T(8,128)} %get-tuple-element.60.small, ...), custom_call_target="tpu_custom_call" | custom-call | tf_op jit(solution)/shard_map/unpack/pallas_call | solution.py:1185
  474.4 1.6 copy.38
  476.1 1.3 copy.36
  477.4 1.3 copy.37
  (27 shorter events, 0.1 us)
Async XLA Ops:
  7.2 85.4 %copy-start = (f32[1,3,4096]{2,0,1:T(1,128)S(1)}, f32[1,3,4096]{2,0,1:T(1,128)}, u32[]{:S(2)}) copy-start(f32[1,3,4096]{2,0,1:T(1,128)} %param.26) | copy-start | bytes 147460
  7.2 210.4 %all-gather.2.cloned.1.call-start = ((), (), s32[]{:S(2)}) async-start(), calls=%async_computation | async-start | bytes 4718592 | tf_op jit(solution)/shard_map/all_gather | solution.py:1240
  7.9 3.8 copy-start.9
  7.9 3.8 copy-start.10
  7.9 3.8 copy-start.11
  7.9 3.8 copy-start.12
  7.9 3.8 copy-start.13
  7.9 3.8 copy-start.14
  7.9 3.8 copy-start.15
  92.7 8.3 %copy-start.6 = (f32[32,8,128]{2,1,0:T(8,128)}, f32[32,8,128]{2,1,0:T(8,128)S(1)}, u32[]{:S(2)}) copy-start(f32[32,8,128]{2,1,0:T(8,128)S(1)} %slice_convert_fusion) | copy-start | bytes 393220
  100.9 2.0 copy-start.4
  105.8 1.3 copy-start.2
  217.6 12.7 %copy-start.17 = (bf16[8,128,2048]{2,1,0:T(8,128)(2,1)S(1)}, bf16[8,128,2048]{2,1,0:T(8,128)(2,1)}, u32[]{:S(2)}) copy-start(bf16[8,128,2048]{2,1,0:T(8,128)(2,1)} %get-tuple-element.45) | copy-start | bytes 12582916
  230.2 12.4 %copy-start.5 = (bf16[1024,1024]{1,0:T(8,128)(2,1)}, bf16[1024,1024]{1,0:T(8,128)(2,1)S(1)}, u32[]{:S(2)}) copy-start(bf16[1024,1024]{1,0:T(8,128)(2,1)S(1)} %get-tuple-element.83.refs_6_) | copy-start | bytes 6291460
  230.2 6.1 %copy-start.16 = (bf16[4,256,2048]{2,1,0:T(8,128)(2,1)S(1)}, bf16[4,256,2048]{2,1,0:T(8,128)(2,1)}, u32[]{:S(2)}) copy-start(bf16[4,256,2048]{2,1,0:T(8,128)(2,1)} %get-tuple-element.44) | copy-start | bytes 12582916
  236.4 6.3 %copy-start.3 = (bf16[4,256,2048]{2,1,0:T(8,128)(2,1)S(1)}, bf16[4,256,2048]{2,1,0:T(8,128)(2,1)}, u32[]{:S(2)}) copy-start(bf16[4,256,2048]{2,1,0:T(8,128)(2,1)} %get-tuple-element.42) | copy-start | bytes 12582916
  248.9 114.4 %copy-start.7 = (f32[32,8,128]{2,1,0:T(8,128)S(1)}, f32[32,8,128]{2,1,0:T(8,128)}, u32[]{:S(2)}) copy-start(f32[32,8,128]{2,1,0:T(8,128)} %copy-done.6) | copy-start | bytes 393220
  248.9 116.0 %copy-start.8 = (f32[16,8,128]{2,1,0:T(8,128)S(1)}, f32[16,8,128]{2,1,0:T(8,128)}, u32[]{:S(2)}) copy-start(f32[16,8,128]{2,1,0:T(8,128)} %get-tuple-element.58) | copy-start | bytes 196612
  366.4 112.3 %copy-start.1 = (f32[1,3,4096]{2,0,1:T(1,128)S(1)}, f32[1,3,4096]{2,0,1:T(1,128)}, u32[]{:S(2)}) copy-start(f32[1,3,4096]{2,0,1:T(1,128)} %param.26) | copy-start | bytes 147460
Sparse Core Ops, SparseCore 0:
  87.3 80.9 all-gather.1

commit v5 on v4

--- a/solution.py
+++ b/solution.py
@@ -89,8 +89,8 @@
 
 
 class Gather:
-    def __init__(self, grid, own, out, sems):
-        self.grid, self.own, self.out = grid, own, out
+    def __init__(self, grid, own, out, sems, piece=None):
+        self.grid, self.own, self.out, self.piece = grid, own, out, piece
         self.up_s, self.up_r, self.dn_s, self.dn_r, self.x_s, self.x_r = sems
 
     @staticmethod
@@ -101,7 +101,8 @@
 
     def block(self, line, lane=None):
         grid = self.grid
-        return self.out.at[grid.at(line, grid.lane if lane is None else lane)]
+        index = grid.at(line, grid.lane if lane is None else lane)
+        return self.out.at[index] if self.piece is None else self.out.at[index, self.piece]
 
     def up(self, k):
         grid = self.grid
@@ -386,70 +387,123 @@
 
 def forward_kernel(
     shape, steps,
-    pre_ref, act_ref, bc_ref, a_ref, skip_ref, init_ref, weight_ref, cot_ref,
-    y_ref, check_ref, final_ref, weights_ref, cots_ref,
-    state, rate_pl, drive_pl, y_pl, local_s, *sems,
+    low_ref, wdt_ref, bias_ref, act_ref, bc_ref, a_ref, skip_ref, init_ref, weight_ref, cot_ref,
+    tok_ref, gate_one, gate_src,
+    y_ref, pre_ref, check_ref, final_ref, gate_ref, gated_ref, weights_ref, cots_ref, gate_two,
+    state, rate_pl, drive_pl, y_pl, w_one, w_two, local_s, *sems,
 ):
     count = pre_ref.shape[0]
     width, planes, _ = a_ref.shape
     seg, seq = grids(shape)
-    weights = Gather(seg, weight_ref, weights_ref, sems[:6])
-    cots = Gather(seq, cot_ref, cots_ref, sems[6:])
-    keep = [
+    gates = Gather(seg, gate_src.at[:, 1], gate_two, sems[:6])
+    weights = Gather(seg, weight_ref, weights_ref, sems[6:12])
+    cots = Gather(seq, cot_ref, cots_ref, sems[12:])
+    step = pl.program_id(0)
+    keeps = [
         pltpu.make_async_copy(weight_ref, weights_ref.at[seg.here], local_s.at[0]),
         pltpu.make_async_copy(cot_ref, cots_ref.at[seq.here], local_s.at[1]),
+        pltpu.make_async_copy(gate_src.at[:, 1], gate_two.at[seg.here], local_s.at[2]),
     ]
-
-    @pl.when(pl.program_id(0) == 0)
+    load_one = pltpu.make_async_copy(gate_one, w_one, local_s.at[3])
+
+    @pl.when(step == 0)
     def _():
         meet((seg, seq))
+        gates.begin()
         weights.begin()
         cots.begin()
-        for copy in keep:
-            copy.start()
+        for keep in keeps:
+            keep.start()
+        load_one.start()
         state[...] = init_ref[...]
 
-    rate = softplus(pre_ref[...])
+    pre = dot_tn(low_ref[...], wdt_ref[...]) + bias_ref[...]
+    pre_ref[...] = pre
+    rate = softplus(pre)
     act = act_ref[...].astype(F32)
     to_planes(rate_pl, rate)
     to_planes(drive_pl, rate * act)
+    groups = count // UNROLL
 
     def group(k, carry):
-        first = k * UNROLL
-        rates = [rate_pl[pl.ds(first + i, planes, stride=count), :] for i in range(UNROLL)]
-        drives = [drive_pl[pl.ds(first + i, planes, stride=count), :] for i in range(UNROLL)]
+        at = k * UNROLL
+        rates = [rate_pl[pl.ds(at + i, planes, stride=count), :] for i in range(UNROLL)]
+        drives = [drive_pl[pl.ds(at + i, planes, stride=count), :] for i in range(UNROLL)]
         sums = [None] * UNROLL
         for n in range(width):
             a = a_ref[n]
             h = state[n]
             check_ref[k, n] = h
             for i in range(UNROLL):
-                h = jnp.exp2(rates[i] * a) * h + bc_ref[first + i, n] * drives[i]
-                term = bc_ref[first + i, width + n] * h
+                h = jnp.exp2(rates[i] * a) * h + bc_ref[at + i, n] * drives[i]
+                term = bc_ref[at + i, width + n] * h
                 sums[i] = term if n == 0 else sums[i] + term
             state[n] = h
         for i in range(UNROLL):
-            y_pl[pl.ds(first + i, planes, stride=count), :] = sums[i]
+            y_pl[pl.ds(at + i, planes, stride=count), :] = sums[i]
         return carry
 
-    lax.fori_loop(0, count // UNROLL, group, 0)
-    y_ref[...] = from_planes(y_pl, count, planes) + skip_ref[...] * act
-
+    ticks = 2 * steps
+    plan = [[] for _ in range(ticks)]
+    late = []
     for k in range(1, seg.lines):
-
-        @pl.when(pl.program_id(0) == (steps - 1) * k // (seg.lines - 1))
-        def _():
-            weights.step(k)
-            if k < seq.lines:
-                cots.step(k)
-
-    @pl.when(pl.program_id(0) == steps - 1)
+        for gather, share in ((gates, 4 * k), (weights, 9 * k)):
+            tick = ticks * share // 16
+            (plan[tick - 1] if tick < ticks else late).append(functools.partial(gather.step, k))
+        if k < seq.lines:
+            plan[ticks - 1].append(functools.partial(cots.step, k))
+
+    def part_of_step(h, carry):
+        lax.fori_loop(h * (groups // 2), (h + 1) * (groups // 2), group, 0)
+        for tick in range(ticks):
+            if plan[tick]:
+
+                @pl.when(step * 2 + h == tick)
+                def _():
+                    for event in plan[tick]:
+                        event()
+
+        return carry
+
+    lax.fori_loop(0, 2, part_of_step, 0)
+    y_ref[pl.ds(pl.multiple_of(step * count, count), count), :] = (
+        from_planes(y_pl, count, planes) + skip_ref[...] * act_ref[...].astype(F32)
+    )
+
+    @pl.when(step == steps - 1)
     def _():
         final_ref[...] = state[...]
+        for event in late[:-1]:
+            event()
+        gates.finish()
+        keeps[2].wait()
+        load_one.wait()
+        load_two = pltpu.make_async_copy(gate_two, w_two, local_s.at[3])
+        load_two.start()
+        load_two.wait()
+        model = tok_ref.shape[1]
+        half = w_one.shape[3]
+        block = 256
+
+        def gating(i, carry):
+            rows = pl.ds(pl.multiple_of(i * block, block), block)
+            lines = tok_ref[rows, :].astype(F32)
+            rstd = lax.rsqrt(jnp.mean(lines * lines, axis=1, keepdims=True) + EPSILON)
+            for j, w in enumerate((w_one, w_two)):
+                cols = pl.ds(j * half, half)
+                gate = rstd * dot_nn(tok_ref[rows, :], w[...].reshape(model, half))
+                gate_ref[rows, cols] = gate
+                gated_ref[rows, cols] = (y_ref[rows, cols] * gate * sigmoid(gate)).astype(BF16)
+            return carry
+
+        blocks = y_ref.shape[0] // block
+        lax.fori_loop(0, blocks // 2, gating, 0)
+        late[-1]()
+        lax.fori_loop(blocks // 2, blocks, gating, 0)
         weights.finish()
         cots.finish()
-        for copy in keep:
-            copy.wait()
+        for keep in keeps[:2]:
+            keep.wait()
 
 
 def backward_kernel(
@@ -595,42 +649,54 @@
             scatter.drain()
 
 
-def forward_scan(shape, pre, act, bc, a2, skip, init, weight, cot, block):
+def forward_scan(
+    shape, low, w_dt, bias, act, bc, a2, skip, init, weight, cot, tok, gate_one, gate_part, block
+):
     lines, fast, seq_lines = shape
-    length, features = pre.shape
+    length, features = act.shape
     width, planes, _ = a2.shape
+    low_rank = w_dt.shape[0]
     steps = length // block
     rows = pl.BlockSpec((block, features), lambda i: (i, 0))
-    whole = pl.BlockSpec((width, planes, LANES), lambda i: (0, 0, 0))
+    one = pl.Buffered(1)
+
+    def whole(*dims):
+        return pl.BlockSpec(dims, lambda i: (0,) * len(dims), pipeline_mode=one)
+
     plane = pltpu.VMEM((planes * block, LANES), F32)
     return pl.pallas_call(
         functools.partial(forward_kernel, shape, steps),
         grid=(steps,),
         in_specs=[
-            rows, rows,
+            pl.BlockSpec((low_rank, block), lambda i: (0, i)),
+            whole(low_rank, features), whole(1, features), rows,
             pl.BlockSpec((block, 2 * width), lambda i: (i, 0), memory_space=pltpu.SMEM),
-            whole,
-            pl.BlockSpec((1, features), lambda i: (0, 0)),
-            whole,
-            pl.BlockSpec(weight.shape, lambda i: (0, 0)),
-            pl.BlockSpec(cot.shape, lambda i: (0, 0)),
+            whole(width, planes, LANES), whole(1, features), whole(width, planes, LANES),
+            whole(*weight.shape), whole(*cot.shape), whole(*tok.shape), ANY, ANY,
         ],
         out_specs=[
-            rows,
+            whole(length, features), rows,
             pl.BlockSpec((block // UNROLL, width, planes, LANES), lambda i: (i, 0, 0, 0)),
-            whole, ANY, ANY,
+            whole(width, planes, LANES), whole(length, features), whole(length, features),
+            ANY, ANY, ANY,
         ],
         out_shape=[
+            jax.ShapeDtypeStruct((length, features), F32),
             jax.ShapeDtypeStruct((length, features), F32),
             jax.ShapeDtypeStruct((length // UNROLL, width, planes, LANES), F32),
             jax.ShapeDtypeStruct((width, planes, LANES), F32),
+            jax.ShapeDtypeStruct((length, features), F32),
+            jax.ShapeDtypeStruct((length, features), BF16),
             jax.ShapeDtypeStruct((lines * fast,) + weight.shape, BF16),
             jax.ShapeDtypeStruct((seq_lines * 2,) + cot.shape, BF16),
+            jax.ShapeDtypeStruct(gate_one.shape, BF16),
         ],
         scratch_shapes=[
             pltpu.VMEM((width, planes, LANES), F32), plane, plane, plane,
-            pltpu.SemaphoreType.DMA((2,)),
-            *Gather.semaphores(lines, fast), *Gather.semaphores(seq_lines, 2),
+            pltpu.VMEM(gate_one.shape, BF16), pltpu.VMEM(gate_one.shape, BF16),
+            pltpu.SemaphoreType.DMA((4,)),
+            *Gather.semaphores(lines, fast), *Gather.semaphores(lines, fast),
+            *Gather.semaphores(seq_lines, 2),
         ],
         compiler_params=comm_params(5),
         cost_estimate=pl.CostEstimate(
@@ -639,7 +705,7 @@
             transcendentals=length * features * width,
         ),
         name="scan_forward",
-    )(pre, act, bc, a2, skip, init, weight, cot)
+    )(low, w_dt, bias, act, bc, a2, skip, init, weight, cot, tok, gate_one, gate_part)
 
 
 def backward_scan(
@@ -715,7 +781,7 @@
 
 def finish_kernel(shape, taps, history, refs, scratch):
     (
-        gact, x_in, act, tok, w_x, w_g, gs_gate,
+        gact, x_in, act, tok, w_x, w_g, w_h, gs_gate,
         mix, w_xt, head, kern, b_conv, dtp, a_grad, dtb, sgrad, g_half, own_tok, own_cot,
         final, start,
         small_out, halves_out, input_out, ends_out,
@@ -741,8 +807,9 @@
         pltpu.make_async_copy(tok, tokb, in_s.at[2]),
         pltpu.make_async_copy(act, actb, in_s.at[3]),
         pltpu.make_async_copy(gs_gate, gsg, in_s.at[4]),
-        pltpu.make_async_copy(w_g, wgb, in_s.at[5]),
-        pltpu.make_async_copy(w_x, wxb, in_s.at[6]),
+        pltpu.make_async_copy(w_g, wgb.at[0], in_s.at[5]),
+        pltpu.make_async_copy(w_h, wgb.at[1], in_s.at[6]),
+        pltpu.make_async_copy(w_x, wxb, in_s.at[7]),
     ]
     for load in loads:
         load.start()
@@ -880,9 +947,11 @@
     loads[4].wait()
     loads[5].wait()
     loads[6].wait()
+    loads[7].wait()
     own_len = own_tok.shape[0]
     model = own_tok.shape[1]
     wide = 512
+    half = feats // 2
 
     def normed(index):
         rows = pl.ds(pl.multiple_of(index * own_len, own_len), own_len)
@@ -890,7 +959,9 @@
         def column(c, carry):
             cols = pl.ds(pl.multiple_of(c * wide, wide), wide)
             q_src[index, :, cols] = (
-                dot_nt(gsg[rows, :], wgb[cols, :]) + dot_nt(gs_x[rows, :], wxb[cols, :])
+                dot_nt(gsg[rows, pl.ds(0, half)], wgb[0, cols, :])
+                + dot_nt(gsg[rows, pl.ds(half, half)], wgb[1, cols, :])
+                + dot_nt(gs_x[rows, :], wxb[cols, :])
             ).astype(BF16)
             return carry
 
@@ -960,7 +1031,7 @@
 def finish_all(shape, taps, history, big, small):
     lines, fast, seq_lines = shape
     segs, seqs = lines * fast, seq_lines * 2
-    gact, x_in, act, tok, w_x, w_g, gs_gate = big
+    gact, x_in, act, tok, w_x, w_g, w_h, gs_gate = big
     mix, w_xt, head, kern, b_conv, dtp, a_grad, dtb, sgrad, g_half, own_tok, own_cot = small[:12]
     length, feats = act.shape
     own_len, model = own_tok.shape
@@ -976,7 +1047,7 @@
         pltpu.VMEM((length, feats), BF16),
         pltpu.VMEM((length, model), BF16),
         pltpu.VMEM((model, feats), BF16),
-        pltpu.VMEM((model, feats), BF16),
+        pltpu.VMEM((2, model, feats // 2), BF16),
         pltpu.VMEM((length, feats), BF16),
         pltpu.VMEM((length, feats), BF16),
         pltpu.VMEM((segs, block_rows, feats), BF16),
@@ -985,7 +1056,7 @@
         pltpu.VMEM((segs, rows, feats // segs), BF16),
         pltpu.VMEM(ends, F32),
         pltpu.VMEM((block_rows, feats), BF16),
-        dma((7,)), dma((3,)),
+        dma((8,)), dma((3,)),
         *Scatter.scratch(lines, fast, (rows, feats // segs), inside=True),
         *Scatter.scratch(lines, fast, (block_rows, feats), inside=True),
         *Scatter.scratch(seq_lines, 2, (own_len, model), inside=True),
@@ -993,11 +1064,11 @@
     ]
 
     def kernel(*refs):
-        finish_kernel(shape, taps, history, refs[:25], refs[25:])
+        finish_kernel(shape, taps, history, refs[:26], refs[26:])
 
     return pl.pallas_call(
         kernel,
-        in_specs=[ANY] * 7 + [INSIDE] * 14,
+        in_specs=[ANY] * 8 + [INSIDE] * 14,
         out_specs=[INSIDE] * 4,
         out_shape=[
             jax.ShapeDtypeStruct((rows, feats // segs), F32),
@@ -1012,92 +1083,226 @@
 
 
 def gather_kernel(
-    shape, scaled, small, tokens,
-    w_x, small_all, tok, g_part,
-    x_part, tok_in, g_own, local_s, x_sems, small_sems, tok_sems, swap_x, swap_g,
+    shape, scaled_x, scaled_g, small, tokens, w_x, small_all, tok, g_part, x_part, tok_in, g_own,
+    local_s, small_sems, tok_sems, swap_x, swap_g, x_sems,
 ):
     seg, seq = grids(shape)
+    size = seq.lines * seq.fast
     load_tok = pltpu.make_async_copy(tokens, tok_in, local_s.at[0])
-    load_own = pltpu.make_async_copy(scaled.at[seq.here, 0], x_part.at[seq.here], local_s.at[1])
-    load_gate = pltpu.make_async_copy(scaled.at[seq.here, 1], g_own, local_s.at[3])
+    load_own = pltpu.make_async_copy(scaled_x.at[seq.here], x_part.at[seq.here], local_s.at[1])
+    load_gate = pltpu.make_async_copy(scaled_g.at[seq.here], g_own, local_s.at[3])
     load_tok.start()
     load_own.start()
     load_gate.start()
     meet((seg, seq))
-    swap_x = Exchange(seq, lambda p: scaled.at[p, 0], lambda m: x_part.at[m], swap_x)
-    swap_g = Exchange(seq, lambda p: scaled.at[p, 1], lambda m: g_part.at[m], swap_g)
+    swap_x = Exchange(seq, lambda p: scaled_x.at[p], lambda m: x_part.at[m], swap_x)
+    swap_g = Exchange(seq, lambda p: scaled_g.at[p], lambda m: g_part.at[m], swap_g)
     swap_x.begin()
+    pieces = []
+    for k in range(size):
+        place = lax.rem(seq.here - k + size, size)
+        pieces.append(Gather(seg, x_part.at[place], w_x, x_sems[6 * k : 6 * k + 6], place))
     smalls = Gather(seg, small, small_all, small_sems)
+    load_own.wait()
+    pieces[0].begin()
     smalls.begin()
     load_tok.wait()
     toks = Gather(seq, tok_in, tok, tok_sems)
+    for k in range(1, size):
+        swap_x.one(k).wait_recv()
+        pieces[k].begin()
     toks.begin()
-    store_tok = pltpu.make_async_copy(tok_in, tok.at[seq.here], local_s.at[0])
-    store_small = pltpu.make_async_copy(small, small_all.at[seg.here], local_s.at[2])
-    store_tok.start()
-    store_small.start()
+    swap_g.begin()
     load_gate.wait()
-    store_gate = pltpu.make_async_copy(g_own, g_part.at[seq.here], local_s.at[3])
-    store_gate.start()
-    load_own.wait()
-    swap_x.arrived()
-    halves = Gather(seg, x_part, w_x, x_sems)
-    halves.begin()
-    store_own = pltpu.make_async_copy(x_part, w_x.at[seg.here], local_s.at[1])
-    store_own.start()
-    swap_g.begin()
-    for k in range(1, seq.lines):
-        toks.step(k)
-    for k in range(1, seg.lines):
-        smalls.step(k)
-        halves.step(k)
+    keeps = [
+        pltpu.make_async_copy(tok_in, tok.at[seq.here], local_s.at[0]),
+        pltpu.make_async_copy(x_part, w_x.at[seg.here], local_s.at[1]),
+        pltpu.make_async_copy(small, small_all.at[seg.here], local_s.at[2]),
+        pltpu.make_async_copy(g_own, g_part.at[seq.here], local_s.at[3]),
+    ]
+    for keep in keeps:
+        keep.start()
+    for k in range(1, max(seg.lines, seq.lines)):
+        if k < seg.lines:
+            pieces[0].step(k)
+            smalls.step(k)
+            for piece in pieces[1:]:
+                piece.step(k)
+        if k < seq.lines:
+            toks.step(k)
     toks.finish()
     smalls.finish()
-    halves.finish()
+    for piece in pieces:
+        piece.finish()
     swap_g.arrived()
     swap_x.drain()
     swap_g.drain()
-    store_tok.wait()
-    store_small.wait()
-    store_gate.wait()
-    store_own.wait()
-
-
-def gather_start(shape, scaled, small, tokens):
+    for keep in keeps:
+        keep.wait()
+
+
+def gather_start(shape, scaled_x, scaled_g, small, tokens):
     lines, fast, seq_lines = shape
     segs, seqs = lines * fast, seq_lines * 2
-    rows, feats = scaled.shape[2:]
+    rows, feats = scaled_x.shape[1:]
     sems = Gather.semaphores
-    flat = [
-        pltpu.VMEM((seqs, rows, feats), BF16),
-        pltpu.VMEM(tokens.shape, BF16),
-        pltpu.VMEM((rows, feats), BF16),
-        pltpu.SemaphoreType.DMA((4,)),
-        *sems(lines, fast), *sems(lines, fast), *sems(seq_lines, 2),
-        *Exchange.semaphores(seqs), *Exchange.semaphores(seqs),
-    ]
 
     def kernel(*refs):
-        ins, rest = refs[:7], refs[7:]
+        ins, rest = refs[:11], refs[11:]
         gather_kernel(
-            shape, *ins, *rest[:4], rest[4:10], rest[10:16], rest[16:22], rest[22:24], rest[24:26]
+            shape, *ins, rest[0], rest[1:7], rest[7:13], rest[13:15], rest[15:17], rest[17:]
         )
 
     w_x, small_all, tok, g_part = pl.pallas_call(
         kernel,
-        in_specs=[ANY, INSIDE, ANY],
+        in_specs=[ANY, ANY, INSIDE, ANY],
         out_specs=[ANY] * 4,
         out_shape=[
             jax.ShapeDtypeStruct((segs, seqs, rows, feats), BF16),
             jax.ShapeDtypeStruct((segs,) + small.shape, BF16),
             jax.ShapeDtypeStruct((seqs,) + tokens.shape, BF16),
-            jax.ShapeDtypeStruct((seqs, rows, feats), BF16),
-        ],
-        scratch_shapes=flat,
+            jax.ShapeDtypeStruct((seqs,) + scaled_g.shape[1:], BF16),
+        ],
+        scratch_shapes=[
+            pltpu.VMEM((seqs, rows, feats), BF16),
+            pltpu.VMEM(tokens.shape, BF16),
+            pltpu.VMEM(scaled_g.shape[1:], BF16),
+            pltpu.SemaphoreType.DMA((4,)),
+            *sems(lines, fast), *sems(seq_lines, 2),
+            *Exchange.semaphores(seqs), *Exchange.semaphores(seqs),
+            *(sems(lines, fast) * seqs),
+        ],
         compiler_params=comm_params(1),
         name="gather_start",
-    )(scaled, small, tokens)
+    )(scaled_x, scaled_g, small, tokens)
     return w_x.reshape(-1, feats), small_all, tok.reshape(-1, tokens.shape[1]), g_part
+
+
+def front_kernel(
+    shape, steps, taps, history, width,
+    tok_ref, wx_ref, small_ref, head_ref, gate_src,
+    x_ref, act_ref, rstd_ref, wdt_ref, wxt_ref, par_ref, a2_ref, low_ref, bc_ref, gate_out,
+    xb, mix_s, mix, local_s, *scratch,
+):
+    seg, seq = grids(shape)
+    step = pl.program_id(0)
+    gates = Gather(seg, gate_src.at[:, 0], gate_out, scratch[:6])
+    count = tok_ref.shape[0]
+    low_rank = wdt_ref.shape[0]
+    mixes = wxt_ref.shape[0]
+    feats = wx_ref.shape[1]
+    part = small_ref.shape[2]
+
+    @pl.when(step == 0)
+    def _():
+        meet((seg, seq))
+        gates.begin()
+        xb[pl.ds(0, 8), :] = head_ref[...]
+        for g in range(small_ref.shape[0]):
+            cols = slice(g * part, (g + 1) * part)
+            wdt_ref[:, cols] = small_ref[g, pl.ds(0, low_rank), :]
+            wxt_ref[:, cols] = small_ref[g, pl.ds(low_rank, mixes), :]
+            rest = small_ref[g, pl.ds(low_rank + mixes, width + 16), :].astype(F32)
+            par_ref[:, cols] = rest
+        a_mat = -jnp.exp(par_ref[pl.ds(0, width), :])
+        par_ref[pl.ds(0, width), :] = a_mat
+        for s in range(feats // LANES):
+            a2_ref[:, s, :] = a_mat[:, s * LANES : (s + 1) * LANES] * LOG2E
+
+    kern = par_ref[pl.ds(width, 8), :]
+    rows = tok_ref[...].astype(F32)
+    rstd = lax.rsqrt(jnp.mean(rows * rows, axis=1, keepdims=True) + EPSILON)
+    rstd_ref[...] = jnp.broadcast_to(rstd, rstd_ref.shape)
+    x_in = rstd * dot_nn(tok_ref[...], wx_ref[...])
+    x_ref[...] = x_in
+    xb[pl.ds(8, count), :] = x_in
+    tall = 32
+    chunk = min(512, feats)
+
+    def through_conv(i, carry):
+        t0 = pl.multiple_of(i * tall, tall)
+        for c in range(0, feats, chunk):
+            cols = slice(c, c + chunk)
+            wide = xb[pl.ds(t0, tall + 8), pl.ds(c, chunk)]
+            conv = kern[taps : taps + 1, cols]
+            for k in range(taps):
+                conv = conv + kern[k : k + 1, cols] * wide[8 - history + k : 8 - history + k + tall]
+            act_ref[pl.ds(t0, tall), pl.ds(c, chunk)] = (conv * sigmoid(conv)).astype(BF16)
+        return carry
+
+    lax.fori_loop(0, count // tall, through_conv, 0)
+    xb[pl.ds(0, 8), :] = xb[pl.ds(count, 8), :]
+    mix_s[:, pl.ds(pl.multiple_of(step * count, count), count)] = dot_nt(wxt_ref[...], act_ref[...])
+    for k in range(1, seg.lines - 1):
+
+        @pl.when(step == min(steps - 1, 2 * k - 1))
+        def _():
+            gates.step(k)
+
+    @pl.when(step == steps - 1)
+    def _():
+        sum_over_seq(seq, mix_s, mix, *scratch[6:])
+        low_ref[...] = mix[pl.ds(0, low_rank), :]
+        bc_ref[...] = mix[pl.ds(low_rank, 2 * width), :].astype(F32).T
+        gates.step(seg.lines - 1)
+        keep = pltpu.make_async_copy(gate_src.at[:, 0], gate_out.at[seg.here], local_s)
+        keep.start()
+        gates.finish()
+        keep.wait()
+
+
+def front(shape, taps, history, width, tok, w_x, small_all, head, gate_part, block):
+    lines, fast, seq_lines = shape
+    segs, seqs = lines * fast, seq_lines * 2
+    length, model = tok.shape
+    feats = w_x.shape[1]
+    low_rank = LANES
+    mixes = low_rank + 2 * width
+    steps = length // block
+
+    def whole(*dims):
+        return pl.BlockSpec(dims, lambda i: (0,) * len(dims))
+
+    def rows(columns):
+        return pl.BlockSpec((block, columns), lambda i: (i, 0))
+
+    one = pl.Buffered(1)
+    return pl.pallas_call(
+        functools.partial(front_kernel, shape, steps, taps, history, width),
+        grid=(steps,),
+        in_specs=[
+            rows(model),
+            pl.BlockSpec((model, feats), lambda i: (0, 0), pipeline_mode=one),
+            whole(*small_all.shape), whole(*head.shape), ANY,
+        ],
+        out_specs=[
+            rows(feats), rows(feats), rows(LANES), whole(low_rank, feats), whole(mixes, feats),
+            whole(width + 16, feats), whole(width, feats // LANES, LANES),
+            whole(low_rank, length), whole(length, 2 * width), ANY,
+        ],
+        out_shape=[
+            jax.ShapeDtypeStruct((length, feats), F32),
+            jax.ShapeDtypeStruct((length, feats), BF16),
+            jax.ShapeDtypeStruct((length, LANES), F32),
+            jax.ShapeDtypeStruct((low_rank, feats), BF16),
+            jax.ShapeDtypeStruct((mixes, feats), BF16),
+            jax.ShapeDtypeStruct((width + 16, feats), F32),
+            jax.ShapeDtypeStruct((width, feats // LANES, LANES), F32),
+            jax.ShapeDtypeStruct((low_rank, length), BF16),
+            jax.ShapeDtypeStruct((length, 2 * width), F32),
+            jax.ShapeDtypeStruct((segs, seqs) + gate_part.shape[2:], BF16),
+        ],
+        scratch_shapes=[
+            pltpu.VMEM((block + 8, feats), F32),
+            pltpu.VMEM((mixes, length), F32),
+            pltpu.VMEM((mixes, length), BF16),
+            pltpu.SemaphoreType.DMA,
+            *Gather.semaphores(lines, fast),
+            *sum_scratch(seq_lines, mixes, length),
+        ],
+        compiler_params=comm_params(2),
+        name="front",
+    )(tok, w_x, small_all, head, gate_part)
 
 
 def sum_scratch(seq_lines, rows, width):
@@ -1109,23 +1314,6 @@
         pltpu.VMEM((2, rows, width // 2), BF16),
         dma, dma, dma((seq_lines,)), dma((seq_lines,)), dma, dma,
     ]
-
-
-def total_over_seq(shape, x, collective_id):
-    def kernel(x_ref, out_ref, *scratch):
-        _, seq = grids(shape)
-        meet((seq,))
-        sum_over_seq(seq, x_ref, out_ref, *scratch)
-
-    return pl.pallas_call(
-        kernel,
-        in_specs=[INSIDE],
-        out_specs=INSIDE,
-        out_shape=jax.ShapeDtypeStruct(x.shape, BF16),
-        scratch_shapes=sum_scratch(shape[2], *x.shape),
-        compiler_params=comm_params(collective_id),
-        name="total_over_seq",
-    )(x)
 
 
 def unpack_kernel(
@@ -1227,8 +1415,10 @@
     gain_col = norm_gain.astype(F32)[:, None]
     own_weight = in_proj.astype(F32)
     scaled = (own_weight * gain_col).astype(BF16)
-    scaled = scaled.reshape(own_rows, 2, segs, seqs, part).transpose(3, 1, 0, 2, 4)
-    scaled = scaled.reshape(seqs, 2, own_rows, feats)
+    scaled = scaled.reshape(own_rows, 2, segs, seqs, part)
+    scaled_x = scaled[:, 0].transpose(2, 0, 1, 3).reshape(seqs, own_rows, feats)
+    scaled_g = scaled[:, 1].reshape(own_rows, 2, segs // 2, seqs, part).transpose(3, 1, 0, 2, 4)
+    scaled_g = scaled_g.reshape(seqs, 2, own_rows, feats // 2)
     small = jnp.concatenate(
         [
             dt_proj, x_proj.T, a_log, conv_weight, conv_bias[None], dt_bias[None], d_skip[None],
@@ -1236,43 +1426,25 @@
         axis=0,
     )
     small = jnp.pad(small, ((0, -small.shape[0] % 16), (0, 0)))
-    w_x_half, small_all, tok, g_part = gather_start(shape, scaled, small, tokens[0])
-    w_g_half = lax.all_gather(
-        g_part.reshape(seqs * own_rows, feats), "seg", axis=0, tiled=True
-    )
-
-    small_all = small_all.transpose(1, 0, 2).reshape(small.shape[0], feats)
-    w_dt = small_all[:low_rank]
-    w_xt = small_all[low_rank : low_rank + x_proj.shape[1]]
-    rest = small_all[low_rank + x_proj.shape[1] :].astype(F32)
-    a_mat = -jnp.exp(rest[:width])
-    a2 = (a_mat * LOG2E).reshape(width, planes, LANES)
-    kernel = rest[width : width + taps]
-    b_conv = rest[width + taps][None]
-    b_dt = rest[width + taps + 1][None]
-    skip = rest[width + taps + 2][None]
-
-    tok_float = tok.astype(F32)
-    rstd = lax.rsqrt(jnp.mean(tok_float * tok_float, axis=1, keepdims=True) + EPSILON)
-    x_in = rstd * dot_nn(tok, w_x_half)
+    w_x_half, small_all, tok, g_part = gather_start(shape, scaled_x, scaled_g, small, tokens[0])
     history = init_conv.shape[1]
-    head = mine(init_conv[0])
-    padded = jnp.concatenate([head, x_in], axis=0)
-    conv_out = b_conv + sum(kernel[k] * padded[k : k + length] for k in range(taps))
-    act = jax.nn.silu(conv_out).astype(BF16)
-    mixed_x = total_over_seq(shape, dot_nt(w_xt, act), 2)
-    dt_low = mixed_x[:low_rank]
-    bc = mixed_x[low_rank:].astype(F32).T
-    pre = dot_tn(dt_low, w_dt) + b_dt
+    head = jnp.pad(mine(init_conv[0]), ((8 - history, 0), (0, 0)))
+    x_in, act, rstd, w_dt, w_xt, params, a2, dt_low, bc, w_g_one = front(
+        shape, taps, history, width, tok, w_x_half, small_all, head, g_part, 4 * block
+    )
+    rstd = rstd[:, :1]
     init = mine(init_state[0]).reshape(width, planes, LANES)
-    y_val, checks, final, w_out, cot = forward_scan(
-        shape, pre, act, bc, a2, skip, init, out_proj, cotangent[0], block
+    a_mat = params[:width]
+    kernel = params[width : width + 8]
+    b_conv, b_dt, skip = (params[width + taps + i][None] for i in range(3))
+    y_val, pre, checks, final, gate, gated, w_out, cot, w_g_two = forward_scan(
+        shape, dt_low, w_dt, b_dt, act, bc, a2, skip, init, out_proj, cotangent[0], tok,
+        w_g_one, g_part, 2 * block,
     )
     w_out = w_out.reshape(feats, model)
     cot = cot.reshape(length, model)
-    y_val, w_g_half = lax.optimization_barrier((y_val, w_g_half))
-    gate = rstd * dot_nn(tok, w_g_half)
-    gated = (y_val * jax.nn.silu(gate)).astype(BF16)
+    w_g_one = w_g_one.reshape(model, feats // 2)
+    w_g_two = w_g_two.reshape(model, feats // 2)
     out_part = dot_nn(gated, w_out).astype(BF16)
 
     g_gated = dot_nt(cot, w_out)
@@ -1294,12 +1466,9 @@
     )
     grads, halves, input_grad, ends = finish_all(
         shape, taps, history,
-        (g_actp, x_in, act, tok, w_x_half, w_g_half, gs_gate),
+        (g_actp, x_in, act, tok, w_x_half, w_g_one, w_g_two, gs_gate),
         (
-            g_mixed, w_xt,
-            jnp.pad(head, ((8 - history, 0), (0, 0))),
-            jnp.pad(kernel, ((0, -taps % 8), (0, 0))),
-            b_conv, dtp_grad, a_sum.reshape(width, feats) * a_mat, dtb_grad, skip_grad, g_half,
+            g_mixed, w_xt, head, kernel, b_conv, dtp_grad, a_sum.reshape(width, feats) * a_mat, dtb_grad, skip_grad, g_half,
             tokens[0], cotangent[0],
             final.reshape(width, feats), start.reshape(width, feats),
         ),

time: 486 us -> 461 us (0.949)
  Pallas kernels: 380 us -> 407 us
  matrix products: 54.3 us -> 32.1 us
  between operations: 14.3 us -> 0.91 us
  local copies, waits for them, and re-layouts: 25.3 us -> 16 us
  other arithmetic: 11.2 us -> 3.62 us
    dot_general x3 -> x1, matrix products: 26.4 us -> 6.05 us  [dot_nn(): return jnp.dot(a, b, preferred_element_type=F32)]
    pallas_call x3, Pallas kernels: 191 us -> 208 us  [the longest x1 102 us: finish_all(): pl.pallas_call(kernel, in_specs=[ANY] * 8 + [INSIDE] * 14, out_specs=[INS...]
    pallas_call x1, Pallas kernels: 69.2 us -> 79.8 us  [forward_scan(): pl.pallas_call(functools.partial(forward_kernel, shape, steps), grid=(ste...]
    unnamed x44 -> x35, local copies, waits for them, and re-layouts: 7.43 us -> 0.1 us
    dot_general x3 -> x2, matrix products: 16.3 us -> 12.4 us  [dot_tn(): lax.dot_general(a, b, (((0,), (0,)), ((), ())), preferred_element_type=F32)]
    dot_general x2 -> x1, matrix products: 11.6 us -> 13.6 us  [dot_nt(): lax.dot_general(a, b, (((1,), (1,)), ((), ())), preferred_element_type=F32)]
  transfers between devices with their start and end apart: 1 -> 0, of which waited for: 0 -> 0; matrix products, arithmetic and copies ran while one was open for 9% -> 0% of each run, Pallas kernels for 17% -> 0%
where the time goes in v5:
time: 461 us; the launch traced here: 460 us
  Pallas kernels  407 us (88%)
  matrix products  32.1 us (7%)
  local copies, waits for them, and re-layouts  16 us (3%)
    pallas_call x1, Pallas kernels, backward_scan(): pl.pallas_call(functools.partial(backward_kernel, shape, steps), grid=(st...  114 us
    pallas_call x1, Pallas kernels, finish_all(): pl.pallas_call(kernel, in_specs=[ANY] * 8 + [INSIDE] * 14, out_specs=[INS...  102 us
    pallas_call x1, Pallas kernels, forward_scan(): pl.pallas_call(functools.partial(forward_kernel, shape, steps), grid=(ste...  79.8 us
    pallas_call x1, Pallas kernels, gather_start(): pl.pallas_call(kernel, in_specs=[ANY, ANY, INSIDE, ANY], out_specs=[ANY]...  65.9 us
    pallas_call x1, Pallas kernels, front(): pl.pallas_call(functools.partial(front_kernel, shape, steps, taps, histor...  39.7 us
    dot_general x1, matrix products, dot_nt(): lax.dot_general(a, b, (((1,), (1,)), ((), ())), preferred_element_type=F32)  13.6 us
    dot_general x2, matrix products, dot_tn(): lax.dot_general(a, b, (((0,), (0,)), ((), ())), preferred_element_type=F32)  12.4 us

profile of v5, /device:TPU:1, one launch (start us, length us, event | category | flops | bytes accessed | tf_op | source)
XLA Modules:
  0.0 460.0 jit_solution(13117054257322445019)
XLA Ops:
  0.6 0.0 copy-start
  0.7 0.7 convert_bitcast_fusion
  1.3 1.5 multiply_convert_fusion.1
  2.8 0.8 reshape.82
  3.6 0.0 copy-start.7
  3.6 0.0 copy-start.8
  3.6 0.0 copy-start.9
  3.6 0.0 copy-start.10
  3.6 0.0 copy-start.11
  3.6 0.0 copy-start.12
  3.6 0.0 copy-start.13
  3.7 0.4 fusion
  4.0 0.1 copy.45
  4.1 1.0 reshape.83.refs_0_
  5.1 0.2 copy.46
  5.3 0.4 copy.47
  5.8 1.0 reshape.84.refs_1_
  6.7 0.0 copy-done.7
  6.7 0.0 copy-done.8
  6.7 0.0 copy-done.9
  6.8 0.0 copy-done.10
  6.8 0.0 copy-done.11
  6.8 0.0 copy-done.12
  6.8 0.0 copy-done.13
  6.8 0.1 concatenate.3
  6.9 0.6 pad.8.refs_2_
  7.5 65.9 %gather_start.1 = (bf16[8,4,64,1024]{3,2,1,0:T(8,128)(2,1)}, bf16[8,320,128]{2,1,0:T(8,128)(2,1)}, bf16[4,256,2048]{2,1,0:T(8,128)(2,1)}, bf16[4,2,64,512]{3,2,1,0:T(8,128)(2,1)}) custom-call(bf16[4,64,1024]{2,1,0:T(8,128)(2,1)} %reshape.83.refs_0_, bf16[4,2,64,512]{3,2,1,0:T(8,128)(2,1)} %reshape.84.refs_1_, bf16[320,128]{1,0:T(8,128)(2,1)} %pad.8.refs_2_, ...), custom_call_target="tpu_custom_call" | custom-call | tf_op jit(solution)/shard_map/gather_start/pallas_call | solution.py:1156
  73.4 0.0 copy-done
  73.4 0.6 pad.9.head_ref.refs_10_
  74.1 0.0 copy-start.4
  74.1 39.7 %front.1 = (f32[1024,1024]{1,0:T(8,128)}, bf16[1024,1024]{1,0:T(8,128)(2,1)}, f32[1024,128]{1,0:T(8,128)}, bf16[128,1024]{1,0:T(8,128)(2,1)}, bf16[160,1024]{1,0...) custom-call(bf16[1024,2048]{1,0:T(8,128)(2,1)} %bitcast.57, ...), custom_call_target="tpu_custom_call" | custom-call | tf_op jit(solution)/shard_map/front/pallas_call | solution.py:1270
  113.7 1.5 fusion.1
  115.2 0.0 copy-done.4
  115.2 0.2 reshape_squeeze.11
  115.4 0.7 constant_dynamic-slice_fusion
  116.1 79.8 %scan_forward.1 = (f32[1024,1024]{1,0:T(8,128)}, f32[1024,1024]{1,0:T(8,128)}, f32[128,16,8,128]{3,2,1,0:T(8,128)}, f32[16,8,128]{2,1,0:T(8,128)}, f32[1024,1024...) custom-call(bf16[128,1024]{1,0:T(8,128)(2,1)} %get-tuple-element.57., ...), custom_call_target="tpu_custom_call" | custom-call | flops 134217728 | bytes 25165824 | tf_op jit(solution)/shard_map/scan_forward/pallas_call | solution.py:667
  195.9 1.2 slice_reduce_fusion
  197.2 0.0 copy-start.2
  197.2 13.6 %multiply_convert_fusion = (bf16[1024,1024]{1,0:T(8,128)(2,1)S(1)}, f32[1024,1024]{1,0:T(8,128)}) fusion(f32[1024,1024]{1,0:T(8,128)} %get-tuple-element.67, f32[1024,1024]{1,0:T(8,128)} %get-tuple-element.70, f32[1024]{0:T(1024)S(1)} %slice_reduce_fusion, bf16[1024,2048]{1,0:T(8,128)(2,1)} %bitcast.84, bf16[1024,2048]{1,0:T(8,128)(2,1)} %bitcast.82), kind=kOutput, calls=%fused_computation | convolution fusion | flops 4308598784 | bytes 23072768 | tf_op jit(solution)/shard_map/dot_general | solution.py:27
  210.8 0.0 copy-start.3
  210.8 0.0 copy-done.2
  210.8 0.0 copy-start.15
  210.8 0.0 copy-start.16
  210.8 6.2 %convolution_convert_fusion.2 = bf16[2048,1024]{1,0:T(8,128)(2,1)} fusion(bf16[1024,2048]{1,0:T(8,128)(2,1)S(1)} %bitcast.60, bf16[1024,1024]{1,0:T(8,128)(2,1)S(1)} %get-tuple-element.138.refs_7_), kind=kOutput, calls=%fused_computation.5 | convolution fusion | flops 4297064448 | bytes 10485760 | tf_op jit(solution)/shard_map/dot_general | solution.py:23
  217.0 0.0 copy-done.3
  217.0 0.0 copy-done.15
  217.0 0.0 copy-done.16
  217.0 0.0 copy-start.14
  217.0 6.2 %convolution_convert_fusion.1 = bf16[1024,2048]{1,0:T(8,128)(2,1)} fusion(bf16[1024,1024]{1,0:T(8,128)(2,1)S(1)} %copy-done.16, bf16[1024,2048]{1,0:T(8,128)(2,1)S(1)} %bitcast.85), kind=kOutput, calls=%fused_computation.4 | convolution fusion | flops 4297064448 | bytes 10485760 | tf_op jit(solution)/shard_map/dot_general | solution.py:23
  223.2 0.0 copy-done.14
  223.2 6.1 %convolution_convert_fusion = bf16[1024,2048]{1,0:T(8,128)(2,1)} fusion(bf16[1024,1024]{1,0:T(8,128)(2,1)S(1)} %copy-done.16, bf16[1024,2048]{1,0:T(8,128)(2,1)S(1)} %bitcast.83), kind=kOutput, calls=%fused_computation.3 | convolution fusion | flops 4297064448 | bytes 10485760 | tf_op jit(solution)/shard_map/dot_general | solution.py:19
  229.3 114.4 %scan_backward.1 = (f32[1024,1024]{1,0:T(8,128)}, f32[16,8,128]{2,1,0:T(8,128)}, f32[16,8,128]{2,1,0:T(8,128)}, f32[1,1024]{1,0:T(1,128)}, f32[1,1024]{1,0:T(1,1...) custom-call(f32[1024,1024]{1,0:T(8,128)} %get-tuple-element.64.pre_r, ...), custom_call_target="tpu_custom_call" | custom-call | flops 335544320 | bytes 29360128 | tf_op jit(solution)/shard_map/scan_backward/pallas_call | solution.py:728
  343.7 0.0 copy-done.5
  343.7 0.6 slice.29.refs_11_
  344.3 1.5 bitcast_multiply_fusion.refs_14_
  345.8 0.0 copy-done.6
  345.8 1.5 copy_bitcast_fusion
  347.3 102.0 %finish.1 = (f32[320,128]{1,0:T(8,128)}, bf16[2,4,64,1024]{3,2,1,0:T(8,128)(2,1)}, bf16[256,2048]{1,0:T(8,128)(2,1)}, f32[4,40,256]{2,1,0:T(8,128)}) custom-call(f32[1024,1024]{1,0:T(8,128)} %get-tuple-element.72.refs_0_, f32[1024,1024]{1,0:T(8,128)} %get-tuple-element.73.refs_1_, bf16[1024,1024]{1,0:T(8,128)(2,1)} %get-tuple-element.60.act_ref.refs_2_, ...), custom_call_target="tpu_custom_call" | custom-call | tf_op jit(solution)/shard_map/finish/pallas_call | solution.py:1069
  449.4 0.7 copy.50.gain
  450.1 5.6 %unpack.1 = (bf16[1,256,2048]{2,1,0:T(8,128)(2,1)}, f32[1,16,1024]{2,1,0:T(8,128)}, f32[1,3,1024]{2,1,0:T(4,128)}, bf16[1,256,2048]{2,1,0:T(8,128)(2,1)}, f32[1,...) custom-call(f32[320,128]{1,0:T(8,128)} %get-tuple-element.84.small, ...), custom_call_target="tpu_custom_call" | custom-call | tf_op jit(solution)/shard_map/unpack/pallas_call | solution.py:1373
  455.7 1.3 copy.51
  457.0 1.3 copy.52
  458.4 1.6 copy.53
  460.0 0.0 copy-done.1
  (5 shorter events, 0.0 us)
Async XLA Ops:
  0.6 72.8 %copy-start = (f32[1,3,4096]{2,0,1:T(1,128)S(1)}, f32[1,3,4096]{2,0,1:T(1,128)}, u32[]{:S(2)}) copy-start(f32[1,3,4096]{2,0,1:T(1,128)} %param.26) | copy-start | bytes 147460
  3.6 3.2 copy-start.7
  3.6 3.2 copy-start.8
  3.6 3.2 copy-start.9
  3.6 3.1 copy-start.10
  3.6 3.1 copy-start.11
  3.6 3.1 copy-start.12
  3.6 3.1 copy-start.13
  74.1 41.1 %copy-start.4 = (f32[1,16,4096]{2,1,0:T(8,128)S(1)}, f32[1,16,4096]{2,1,0:T(8,128)}, u32[]{:S(2)}) copy-start(f32[1,16,4096]{2,1,0:T(8,128)} %param.25) | copy-start | bytes 786436
  197.2 13.6 %copy-start.2 = (bf16[4,256,2048]{2,1,0:T(8,128)(2,1)S(1)}, bf16[4,256,2048]{2,1,0:T(8,128)(2,1)}, u32[]{:S(2)}) copy-start(bf16[4,256,2048]{2,1,0:T(8,128)(2,1)} %get-tuple-element.53) | copy-start | bytes 12582916
  210.8 6.2 %copy-start.3 = (bf16[1024,1024]{1,0:T(8,128)(2,1)}, bf16[1024,1024]{1,0:T(8,128)(2,1)S(1)}, u32[]{:S(2)}) copy-start(bf16[1024,1024]{1,0:T(8,128)(2,1)S(1)} %get-tuple-element.138.refs_7_) | copy-start | bytes 6291460
  210.8 6.2 %copy-start.15 = (bf16[4,256,2048]{2,1,0:T(8,128)(2,1)S(1)}, bf16[4,256,2048]{2,1,0:T(8,128)(2,1)}, u32[]{:S(2)}) copy-start(bf16[4,256,2048]{2,1,0:T(8,128)(2,1)} %get-tuple-element.65) | copy-start | bytes 12582916
  210.8 6.2 %copy-start.16 = (bf16[1024,1024]{1,0:T(8,128)(2,1)S(1)}, bf16[1024,1024]{1,0:T(8,128)(2,1)}, u32[]{:S(2)}) copy-start(bf16[1024,1024]{1,0:T(8,128)(2,1)} %get-tuple-element.71) | copy-start | bytes 6291460
  217.0 6.2 %copy-start.14 = (bf16[8,128,2048]{2,1,0:T(8,128)(2,1)S(1)}, bf16[8,128,2048]{2,1,0:T(8,128)(2,1)}, u32[]{:S(2)}) copy-start(bf16[8,128,2048]{2,1,0:T(8,128)(2,1)} %get-tuple-element.66) | copy-start | bytes 12582916
  229.3 114.4 %copy-start.5 = (f32[32,1024]{1,0:T(8,128)S(1)}, f32[32,1024]{1,0:T(8,128)}, u32[]{:S(2)}) copy-start(f32[32,1024]{1,0:T(8,128)} %get-tuple-element.59) | copy-start | bytes 393220
  229.3 116.6 %copy-start.6 = (f32[16,8,128]{2,1,0:T(8,128)S(1)}, f32[16,8,128]{2,1,0:T(8,128)}, u32[]{:S(2)}) copy-start(f32[16,8,128]{2,1,0:T(8,128)} %get-tuple-element.82) | copy-start | bytes 196612
  347.3 112.7 %copy-start.1 = (f32[1,3,4096]{2,0,1:T(1,128)S(1)}, f32[1,3,4096]{2,0,1:T(1,128)}, u32[]{:S(2)}) copy-start(f32[1,3,4096]{2,0,1:T(1,128)} %param.26) | copy-start | bytes 147460

commit v6 on v5

--- a/solution.py
+++ b/solution.py
@@ -36,19 +36,29 @@
 
 
 def to_planes(planes_ref, rows):
-    count = rows.shape[0]
+    groups = planes_ref.shape[0]
     for s in range(rows.shape[1] // LANES):
-        planes_ref[pl.ds(s * count, count), :] = rows[:, s * LANES : (s + 1) * LANES]
-
-
-def from_planes(planes_ref, count, planes):
+        tile = rows[:, s * LANES : (s + 1) * LANES].reshape(groups, UNROLL, LANES)
+        planes_ref[:, pl.ds(s * UNROLL, UNROLL), :] = tile
+
+
+def from_planes(planes_ref):
+    groups, rows, _ = planes_ref.shape
     return jnp.concatenate(
-        [planes_ref[pl.ds(s * count, count), :] for s in range(planes)], axis=1
+        [
+            planes_ref[:, pl.ds(s * UNROLL, UNROLL), :].reshape(groups * UNROLL, LANES)
+            for s in range(rows // UNROLL)
+        ],
+        axis=1,
     )
 
 
+def token_of(planes, i):
+    return pl.ds(i, planes, stride=UNROLL)
+
+
 MESH_ID = pl.DeviceIdType.MESH
-VMEM_MOST = 63 * 1024 * 1024 + 512 * 1024
+VMEM_MOST = 67_043_328
 
 
 class Grid:
@@ -184,6 +194,7 @@
             scratch = scratch[2:]
         self.xbuf, self.stage, self.zbuf, self.acc = scratch[:4]
         self.x_s, self.x_r, self.z_s, self.z_r = scratch[4:]
+        self.last = grid.lines - 1
 
     @staticmethod
     def scratch(lines, fast, shape, inside=False):
@@ -193,42 +204,61 @@
         return loads + [
             pltpu.VMEM((lines, fast - 1) + shape, BF16),
             pltpu.VMEM((lines - 1,) + shape, BF16),
-            pltpu.VMEM((lines - 1,) + shape, BF16),
+            pltpu.VMEM((lines + 1,) + shape, BF16),
             pltpu.VMEM(shape, F32),
-            dma((lines, fast)), dma((lines, fast)), dma((lines,)), dma((lines,)),
+            dma((lines, fast)), dma((lines, fast)), dma((lines,)), dma((lines + 1,)),
         ]
 
-    def index(self, k, e):
-        return self.grid.at(self.grid.line_peer(k), self.grid.lane_peer(e))
-
-    def across(self, k, e):
+    def dest(self, j):
+        line, last = self.grid.line, self.last
+        above, below = last - line, line
+        low = jnp.where(j < above, last - j, j - above)
+        high = jnp.where(j < below, j, last - (j - below))
+        other = jnp.where(2 * line <= last, low, high)
+        return jnp.where(j == last, line, other)
+
+    def index(self, j, e):
+        return self.grid.at(self.dest(j), self.grid.lane_peer(e))
+
+    def across(self, j, e):
         grid = self.grid
         return grid.copy(
-            self.src.at[self.index(k, e)], self.xbuf.at[k, e - 1],
-            self.x_s.at[k, e], self.x_r.at[k, e], grid.at(grid.line, grid.lane_peer(e)),
+            self.src.at[self.index(j, e)], self.xbuf.at[j, e - 1],
+            self.x_s.at[j, e], self.x_r.at[j, e], grid.at(grid.line, grid.lane_peer(e)),
         )
 
-    def local(self, k):
+    def local(self, j):
         return pltpu.make_async_copy(
-            self.src.at[self.index(k, 0)], self.own.at[k], self.o_s.at[k]
+            self.src.at[self.index(j, 0)], self.own.at[j], self.o_s.at[j]
         )
 
-    def along(self, k):
+    def along(self, j):
+        grid = self.grid
+        dest = self.dest(j)
+        up = dest > grid.line
+        to = jnp.clip(jnp.where(up, grid.line + 1, grid.line - 1), 0, self.last)
+        slot = jnp.where(jnp.logical_and(jnp.logical_not(up), dest == to), grid.lines, dest)
+        return grid.copy(
+            self.stage.at[j], self.zbuf.at[slot], self.z_s.at[j], self.z_r.at[slot],
+            grid.at(to, grid.lane),
+        )
+
+    def arrival(self, slot):
         grid = self.grid
         return grid.copy(
-            self.stage.at[k - 1], self.zbuf.at[k - 1], self.z_s.at[k], self.z_r.at[k],
-            grid.at(grid.line_peer(k), grid.lane),
+            self.stage.at[0], self.zbuf.at[slot], self.z_s.at[0], self.z_r.at[slot],
+            grid.at(lax.rem(grid.line + 1, grid.lines), grid.lane),
         )
 
     def order(self):
-        return list(range(self.grid.lines - 1, -1, -1))
+        return list(range(self.grid.lines))
 
     def begin(self):
-        for k in self.order():
+        for j in self.order():
             for e in range(1, self.grid.fast):
-                self.across(k, e).start()
+                self.across(j, e).start()
             if not self.inside:
-                self.local(k).start()
+                self.local(j).start()
 
     def rows(self, step):
         count = self.acc.shape[0]
@@ -240,46 +270,87 @@
 
         lax.fori_loop(0, count // size, run, 0)
 
-    def middle(self, k):
-        for e in range(1, self.grid.fast):
-            self.across(k, e).wait_recv()
+    def middle(self, j):
+        grid = self.grid
+        for e in range(1, grid.fast):
+            self.across(j, e).wait_recv()
         if self.inside:
-            own = self.src.at[self.index(k, 0)]
+            own = self.src.at[self.index(j, 0)]
         else:
-            self.local(k).wait()
-            own = self.own.at[k]
-
-        def add(at):
+            self.local(j).wait()
+            own = self.own.at[j]
+
+        def partial(at):
             total = own[at, :].astype(F32)
-            for e in range(self.grid.fast - 1):
-                total = total + self.xbuf[k, e, at, :].astype(F32)
-            if k > 0:
-                self.stage[k - 1, at, :] = total.astype(BF16)
-            else:
-                self.acc[at, :] = total
-
-        self.rows(add)
-        if k > 0:
-            self.along(k).start()
+            for e in range(grid.fast - 1):
+                total = total + self.xbuf[j, e, at, :].astype(F32)
+            return total
+
+        if j == self.last:
+
+            def keep(at):
+                self.acc[at, :] = partial(at)
+
+            self.rows(keep)
+            return
+        dest = self.dest(j)
+        carried = jnp.where(dest > grid.line, grid.line > 0, grid.line < self.last)
+
+        @pl.when(carried)
+        def _():
+            self.arrival(dest).wait_recv()
+
+            def add(at):
+                total = partial(at) + self.zbuf[dest, at, :].astype(F32)
+                self.stage[j, at, :] = total.astype(BF16)
+
+            self.rows(add)
+
+        @pl.when(jnp.logical_not(carried))
+        def _():
+            def add(at):
+                self.stage[j, at, :] = partial(at).astype(BF16)
+
+            self.rows(add)
+
+        self.along(j).start()
 
     def finish(self, write):
-        for k in range(1, self.grid.lines):
-            self.along(k).wait_recv()
-
-        def add(at):
-            total = self.acc[at, :]
-            for k in range(self.grid.lines - 1):
-                total = total + self.zbuf[k, at, :].astype(F32)
-            write(at, total)
-
-        self.rows(add)
+        line, last = self.grid.line, self.last
+        from_below, from_above = line > 0, line < last
+
+        @pl.when(from_below)
+        def _():
+            self.arrival(line).wait_recv()
+
+        @pl.when(from_above)
+        def _():
+            self.arrival(self.grid.lines).wait_recv()
+
+        def total(at, below, above):
+            result = self.acc[at, :]
+            if below:
+                result = result + self.zbuf[line, at, :].astype(F32)
+            if above:
+                result = result + self.zbuf[last + 1, at, :].astype(F32)
+            write(at, result)
+
+        for when, below, above in (
+            (jnp.logical_and(from_below, from_above), True, True),
+            (jnp.logical_not(from_below), False, True),
+            (jnp.logical_not(from_above), True, False),
+        ):
+
+            @pl.when(when)
+            def _():
+                self.rows(lambda at: total(at, below, above))
 
     def drain(self):
-        for k in self.order():
+        for j in self.order():
             for e in range(1, self.grid.fast):
-                self.across(k, e).wait_send()
-            if k > 0:
-                self.along(k).wait_send()
+                self.across(j, e).wait_send()
+            if j < self.last:
+                self.along(j).wait_send()
 
 
 def into(ref):
@@ -427,8 +498,8 @@
 
     def group(k, carry):
         at = k * UNROLL
-        rates = [rate_pl[pl.ds(at + i, planes, stride=count), :] for i in range(UNROLL)]
-        drives = [drive_pl[pl.ds(at + i, planes, stride=count), :] for i in range(UNROLL)]
+        rates = [rate_pl[k, token_of(planes, i), :] for i in range(UNROLL)]
+        drives = [drive_pl[k, token_of(planes, i), :] for i in range(UNROLL)]
         sums = [None] * UNROLL
         for n in range(width):
             a = a_ref[n]
@@ -440,7 +511,7 @@
                 sums[i] = term if n == 0 else sums[i] + term
             state[n] = h
         for i in range(UNROLL):
-            y_pl[pl.ds(at + i, planes, stride=count), :] = sums[i]
+            y_pl[k, token_of(planes, i), :] = sums[i]
         return carry
 
     ticks = 2 * steps
@@ -467,7 +538,7 @@
 
     lax.fori_loop(0, 2, part_of_step, 0)
     y_ref[pl.ds(pl.multiple_of(step * count, count), count), :] = (
-        from_planes(y_pl, count, planes) + skip_ref[...] * act_ref[...].astype(F32)
+        from_planes(y_pl) + skip_ref[...] * act_ref[...].astype(F32)
     )
 
     @pl.when(step == steps - 1)
@@ -509,27 +580,32 @@
 def backward_kernel(
     shape, steps,
     pre_ref, act_ref, gy_ref, bc_ref, a_ref, skip_ref, check_ref, wdt_ref, low_ref, base_ref,
-    first_src, second_src, third_src,
+    first_src, second_src, gated_src, weight_src,
     gact_ref, agrad_ref, start_ref, dtb_ref, sgrad_ref, dtp_ref, mix_ref,
     first_out, second_out, third_out,
-    carry_s, rate_pl, drive_pl, gy_pl, grate_pl, thr_pl, prod, part, mix_s, *scratch,
+    carry_s, rate_pl, drive_pl, gy_pl, grate_pl, thr_pl, prod, part, mix_s,
+    gated_in, weight_in, third_src, load_s, *scratch,
 ):
     count = pre_ref.shape[0]
     width, planes, _ = a_ref.shape
     low_rank = wdt_ref.shape[0]
     seg, seq = grids(shape)
-    first, second, third = (
-        Scatter(grid, src, scratch[10 * i : 10 * i + 10])
-        for i, (grid, src) in enumerate(((seg, first_src), (seg, second_src), (seq, third_src)))
-    )
+    first = Scatter(seg, first_src, scratch[:10])
+    second = Scatter(seg, second_src, scratch[10:20])
+    third = Scatter(seq, third_src, scratch[20:28], inside=True)
+    loads = [
+        pltpu.make_async_copy(gated_src, gated_in, load_s.at[0]),
+        pltpu.make_async_copy(weight_src, weight_in, load_s.at[1]),
+    ]
     step = pl.program_id(0)
 
     @pl.when(step == 0)
     def _():
         meet((seg, seq))
         first.begin()
-        third.begin()
         second.begin()
+        for load in loads:
+            load.start()
         carry_s[...] = jnp.zeros_like(carry_s)
         agrad_ref[...] = jnp.zeros_like(agrad_ref)
         dtb_ref[...] = jnp.zeros_like(dtb_ref)
@@ -547,9 +623,9 @@
     def group(j, carry):
         k = groups - 1 - j
         at = k * UNROLL
-        rates = [rate_pl[pl.ds(at + i, planes, stride=count), :] for i in range(UNROLL)]
-        drives = [drive_pl[pl.ds(at + i, planes, stride=count), :] for i in range(UNROLL)]
-        gys = [gy_pl[pl.ds(at + i, planes, stride=count), :] for i in range(UNROLL)]
+        rates = [rate_pl[k, token_of(planes, i), :] for i in range(UNROLL)]
+        drives = [drive_pl[k, token_of(planes, i), :] for i in range(UNROLL)]
+        gys = [gy_pl[k, token_of(planes, i), :] for i in range(UNROLL)]
         g_rate = [None] * UNROLL
         through = [None] * UNROLL
         for n in range(width):
@@ -564,10 +640,9 @@
             for i in reversed(range(UNROLL)):
                 lam = lam + bc_ref[at + i, width + n] * gys[i]
                 b_term = bc_ref[at + i, n] * lam
-                prod[pl.ds((i * 2 * width + n) * planes, planes), :] = lam * drives[i]
-                prod[pl.ds((i * 2 * width + width + n) * planes, planes), :] = (
-                    states[i + 1] * gys[i]
-                )
+                region = (i * 2 * width + n) // 8
+                prod[region, token_of(planes, n % 8), :] = lam * drives[i]
+                prod[region + width // 8, token_of(planes, n % 8), :] = states[i + 1] * gys[i]
                 lam = decays[i] * lam
                 weighted = lam * states[i]
                 acc = acc + weighted * rates[i]
@@ -577,13 +652,13 @@
             carry_s[n] = lam
             agrad_ref[n] = acc
         for i in range(UNROLL):
-            grate_pl[pl.ds(at + i, planes, stride=count), :] = g_rate[i]
-            thr_pl[pl.ds(at + i, planes, stride=count), :] = through[i]
+            grate_pl[k, token_of(planes, i), :] = g_rate[i]
+            thr_pl[k, token_of(planes, i), :] = through[i]
             for q in range(2 * width // 8):
-                base = (i * 2 * width + q * 8) * planes
-                total = prod[pl.ds(base, 8, stride=planes), :]
+                region = i * 2 * width // 8 + q
+                total = prod[region, pl.ds(0, 8), :]
                 for s in range(1, planes):
-                    total = total + prod[pl.ds(base + s, 8, stride=planes), :]
+                    total = total + prod[region, pl.ds(s * 8, 8), :]
                 row = pl.multiple_of((at + i) * 2 * width + q * 8, 8)
                 part[pl.ds(row, 8), :] = total
         return carry
@@ -593,13 +668,42 @@
     plan = [[] for _ in range(ticks)]
     for j, event in enumerate(events):
         plan[min(ticks - 1, ticks * (j + 1) // len(events))].append(event)
-    for k in third.order():
-        plan[min(ticks - 1, 2)].append(functools.partial(third.middle, k))
+
+    def output(index):
+        own_len, model = third_src.shape[1:]
+        rows = pl.ds(pl.multiple_of(index * own_len, own_len), own_len)
+
+        def column(c, carry):
+            cols = pl.ds(pl.multiple_of(c * 512, 512), 512)
+            third_src[index, :, cols] = dot_nn(gated_in[rows, :], weight_in[:, cols]).astype(BF16)
+            return carry
+
+        lax.fori_loop(0, model // 512, column, 0)
+
+    def outputs():
+        for load in loads:
+            load.wait()
+
+        def leave(j, carry):
+            output(third.index(j, 1))
+            third.across(j, 1).start()
+            return carry
+
+        def stay(j, carry):
+            output(third.index(j, 0))
+            return carry
+
+        lax.fori_loop(0, seq.lines, leave, 0)
+        lax.fori_loop(0, seq.lines, stay, 0)
+
+    plan[0].append(outputs)
+    for j in third.order():
+        plan[min(ticks - 1, 5 + 2 * j)].append(functools.partial(third.middle, j))
 
     def add_base(at, total):
         third_out[at, :] = (total + base_ref[at, :].astype(F32)).astype(BF16)
 
-    plan[min(ticks - 1, 9)].append(functools.partial(third.finish, add_base))
+    plan[min(ticks - 1, 13)].append(functools.partial(third.finish, add_base))
 
     def part_of_step(h, carry):
         lax.fori_loop(h * (groups // 2), (h + 1) * (groups // 2), group, 0)
@@ -614,8 +718,8 @@
         return carry
 
     lax.fori_loop(0, 2, part_of_step, 0)
-    g_rate = from_planes(grate_pl, count, planes) * (1.0 / LOG2E)
-    through = from_planes(thr_pl, count, planes)
+    g_rate = from_planes(grate_pl) * (1.0 / LOG2E)
+    through = from_planes(thr_pl)
     pre = pre_ref[...]
     rate = softplus(pre)
     act = act_ref[...].astype(F32)
@@ -640,7 +744,7 @@
     @pl.when(step == steps - 1)
     def _():
         start_ref[...] = carry_s[...]
-        sum_over_seq(seq, mix_s, mix_ref, *scratch[30:])
+        sum_over_seq(seq, mix_s, mix_ref, *scratch[28:])
         for event in plan[ticks - 1]:
             event()
         first.finish(into(first_out))
@@ -663,7 +767,7 @@
     def whole(*dims):
         return pl.BlockSpec(dims, lambda i: (0,) * len(dims), pipeline_mode=one)
 
-    plane = pltpu.VMEM((planes * block, LANES), F32)
+    plane = pltpu.VMEM((block // UNROLL, planes * UNROLL, LANES), F32)
     return pl.pallas_call(
         functools.partial(forward_kernel, shape, steps),
         grid=(steps,),
@@ -709,7 +813,8 @@
 
 
 def backward_scan(
-    shape, pre, act, gy, bc, a2, skip, checks, w_dt, dt_low, base, first, second, third, block
+    shape, pre, act, gy, bc, a2, skip, checks, w_dt, dt_low, base, first, second, gated, weight,
+    block,
 ):
     lines, fast, seq_lines = shape
     length, features = pre.shape
@@ -723,7 +828,7 @@
         return pl.BlockSpec((rows, columns), lambda i: (0, 0))
 
     line = all_of(1, features)
-    plane = pltpu.VMEM((planes * block, LANES), F32)
+    plane = pltpu.VMEM((block // UNROLL, planes * UNROLL, LANES), F32)
     mixed = (low_rank + 2 * width, length)
     return pl.pallas_call(
         functools.partial(backward_kernel, shape, steps),
@@ -740,7 +845,7 @@
             all_of(low_rank, features),
             pl.BlockSpec((low_rank, block), lambda i: (0, steps - 1 - i)),
             all_of(*base.shape),
-            ANY, ANY, ANY,
+            ANY, ANY, ANY, ANY,
         ],
         out_specs=[
             rows, whole, whole, line, line, all_of(low_rank, features), all_of(*mixed),
@@ -761,12 +866,16 @@
         scratch_shapes=[pltpu.VMEM((width, planes, LANES), F32)]
         + [plane] * 5
         + [
-            pltpu.VMEM((UNROLL * 2 * width * planes, LANES), F32),
+            pltpu.VMEM((UNROLL * 2 * width // 8, planes * 8, LANES), F32),
             pltpu.VMEM((block * 2 * width, LANES), F32),
             pltpu.VMEM(mixed, F32),
+            pltpu.VMEM(gated.shape, BF16),
+            pltpu.VMEM(weight.shape, BF16),
+            pltpu.VMEM((2 * seq_lines,) + base.shape, BF16),
+            pltpu.SemaphoreType.DMA((2,)),
             *Scatter.scratch(lines, fast, first.shape[1:]),
             *Scatter.scratch(lines, fast, second.shape[1:]),
-            *Scatter.scratch(seq_lines, 2, third.shape[1:]),
+            *Scatter.scratch(seq_lines, 2, base.shape, inside=True),
             *sum_scratch(seq_lines, *mixed),
         ],
         compiler_params=comm_params(6),
@@ -776,7 +885,7 @@
             transcendentals=length * features * width,
         ),
         name="scan_backward",
-    )(pre, act, gy, bc, a2, skip, checks, w_dt, dt_low, base, first, second, third)
+    )(pre, act, gy, bc, a2, skip, checks, w_dt, dt_low, base, first, second, gated, weight)
 
 
 def finish_kernel(shape, taps, history, refs, scratch):
@@ -915,17 +1024,16 @@
             xg[index] = dot_tn(tokb[:, cols], gs_x[...]).astype(BF16)
 
     def leave(j, carry):
-        k = seg.lines - 1 - j
         for e in range(1, seg.fast):
             if by_block:
-                partial(x_sum.index(k, e))
-            x_sum.across(k, e).start()
+                partial(x_sum.index(j, e))
+            x_sum.across(j, e).start()
         return carry
 
     lax.fori_loop(0, seg.lines, leave, 0)
     def stay(j, carry):
         if by_block:
-            partial(x_sum.index(seg.lines - 1 - j, 0))
+            partial(x_sum.index(j, 0))
         return carry
 
     lax.fori_loop(0, seg.lines, stay, 0)
@@ -968,13 +1076,12 @@
         lax.fori_loop(0, model // wide, column, 0)
 
     def leave_q(j, carry):
-        k = seq.lines - 1 - j
-        normed(q_sum.index(k, 1))
-        q_sum.across(k, 1).start()
+        normed(q_sum.index(j, 1))
+        q_sum.across(j, 1).start()
         return carry
 
     def stay_q(j, carry):
-        normed(q_sum.index(seq.lines - 1 - j, 0))
+        normed(q_sum.index(j, 0))
         return carry
 
     lax.fori_loop(0, seq.lines, leave_q, 0)
@@ -1370,21 +1477,30 @@
     model = mixed.shape[1]
     kept = ends.shape[2] * seqs
     f32 = lambda *dims: jax.ShapeDtypeStruct(dims, F32)
+    args = (small, halves, ends, mixed, input_grad, out_grad, weight, gain)
+    outs = [
+        jax.ShapeDtypeStruct((1,) + mixed.shape, BF16),
+        f32(1, width, kept), f32(1, history, kept),
+        jax.ShapeDtypeStruct((1,) + input_grad.shape, BF16),
+        f32(1, width, kept), f32(1, history, kept),
+        f32(own_rows), f32(*weight.shape),
+        f32(taps, part), f32(part), f32(part, low_rank + 2 * width), f32(low_rank, part),
+        f32(part), f32(width, part), f32(part), f32(part, model),
+    ]
+
+    def whole(a):
+        return pl.BlockSpec(
+            a.shape, lambda i: (0,) * len(a.shape), pipeline_mode=pl.Buffered(1)
+        )
+
     return pl.pallas_call(
         functools.partial(unpack_kernel, seqs, taps, history, low_rank, width),
-        in_specs=[INSIDE] * 8,
-        out_specs=[INSIDE] * 16,
-        out_shape=[
-            jax.ShapeDtypeStruct((1,) + mixed.shape, BF16),
-            f32(1, width, kept), f32(1, history, kept),
-            jax.ShapeDtypeStruct((1,) + input_grad.shape, BF16),
-            f32(1, width, kept), f32(1, history, kept),
-            f32(own_rows), f32(*weight.shape),
-            f32(taps, part), f32(part), f32(part, low_rank + 2 * width), f32(low_rank, part),
-            f32(part), f32(width, part), f32(part), f32(part, model),
-        ],
+        grid=(1,),
+        in_specs=[whole(a) for a in args],
+        out_specs=[whole(a) for a in outs],
+        out_shape=outs,
         name="unpack",
-    )(small, halves, ends, mixed, input_grad, out_grad, weight, gain)
+    )(*args)
 
 
 def body(
@@ -1445,8 +1561,6 @@
     cot = cot.reshape(length, model)
     w_g_one = w_g_one.reshape(model, feats // 2)
     w_g_two = w_g_two.reshape(model, feats // 2)
-    out_part = dot_nn(gated, w_out).astype(BF16)
-
     g_gated = dot_nt(cot, w_out)
     sig_gate = jax.nn.sigmoid(gate)
     gy = g_gated * gate * sig_gate
@@ -1460,8 +1574,7 @@
             shape, pre, act, gy, bc, a2, skip, checks, w_dt, dt_low, tokens[0],
             gate_grad.reshape(segs, seqs * own_rows, feats),
             out_grad.reshape(segs, part, model),
-            out_part.reshape(seqs, own_len, model),
-            2 * block,
+            gated, w_out, 2 * block,
         )
     )
     grads, halves, input_grad, ends = finish_all(

time: 461 us -> 458 us (level)
  matrix products: 32.1 us -> 26.3 us
    dot_general x1 -> x0, matrix products: 6.05 us -> none  [dot_nn(): return jnp.dot(a, b, preferred_element_type=F32)]
    pallas_call x1, Pallas kernels: 114 us -> 109 us  [backward_scan(): pl.pallas_call(functools.partial(backward_kernel, shape, steps), grid=(st...]
where the time goes in v6:
time: 458 us; the launch traced here: 453 us
  Pallas kernels  403 us (88%)
  matrix products  26.3 us (6%)
  local copies, waits for them, and re-layouts  19.2 us (4%)
    pallas_call x1, Pallas kernels, backward_scan(): pl.pallas_call(functools.partial(backward_kernel, shape, steps), grid=(st...  109 us
    pallas_call x1, Pallas kernels, finish_all(): pl.pallas_call(kernel, in_specs=[ANY] * 8 + [INSIDE] * 14, out_specs=[INS...  104 us
    pallas_call x1, Pallas kernels, forward_scan(): pl.pallas_call(functools.partial(forward_kernel, shape, steps), grid=(ste...  79.7 us
    pallas_call x1, Pallas kernels, gather_start(): pl.pallas_call(kernel, in_specs=[ANY, ANY, INSIDE, ANY], out_specs=[ANY]...  65.9 us
    pallas_call x1, Pallas kernels, front(): pl.pallas_call(functools.partial(front_kernel, shape, steps, taps, histor...  39.6 us
    dot_general x1, matrix products, dot_nt(): lax.dot_general(a, b, (((1,), (1,)), ((), ())), preferred_element_type=F32)  13.7 us
    dot_general x2, matrix products, dot_tn(): lax.dot_general(a, b, (((0,), (0,)), ((), ())), preferred_element_type=F32)  12.5 us

profile of v6, /device:TPU:1, one launch (start us, length us, event | category | flops | bytes accessed | tf_op | source)
XLA Modules:
  0.0 453.5 jit_solution(6207778966305937490)
XLA Ops:
  0.6 1.2 convert_bitcast_fusion
  1.8 1.5 multiply_convert_fusion.1
  3.3 0.8 reshape.79
  4.1 0.0 copy-start.3
  4.1 0.0 copy-start.4
  4.1 0.0 copy-start.5
  4.1 0.0 copy-start.6
  4.1 0.0 copy-start.7
  4.1 0.0 copy-start.8
  4.1 0.0 copy-start.9
  4.1 0.4 fusion
  4.5 0.1 copy.45
  4.6 1.0 reshape.80.refs_0_
  5.6 0.2 copy.46
  5.8 0.4 copy.47
  6.2 1.0 reshape.81.refs_1_
  7.2 0.0 copy-done.3
  7.2 0.0 copy-done.4
  7.2 0.0 copy-done.5
  7.2 0.0 copy-done.6
  7.2 0.0 copy-done.7
  7.2 0.0 copy-done.8
  7.3 0.0 copy-done.9
  7.3 0.1 concatenate.3
  7.3 0.6 pad.8.refs_2_
  8.0 65.9 %gather_start.1 = (bf16[8,4,64,1024]{3,2,1,0:T(8,128)(2,1)}, bf16[8,320,128]{2,1,0:T(8,128)(2,1)}, bf16[4,256,2048]{2,1,0:T(8,128)(2,1)}, bf16[4,2,64,512]{3,2,1,0:T(8,128)(2,1)}) custom-call(bf16[4,64,1024]{2,1,0:T(8,128)(2,1)} %reshape.80.refs_0_, bf16[4,2,64,512]{3,2,1,0:T(8,128)(2,1)} %reshape.81.refs_1_, bf16[320,128]{1,0:T(8,128)(2,1)} %pad.8.refs_2_, ...), custom_call_target="tpu_custom_call" | custom-call | tf_op jit(solution)/shard_map/gather_start/pallas_call | solution.py:1263
  73.9 0.8 constant_dynamic-slice_fusion.1
  74.7 0.6 pad.9.head_ref.refs_10_
  75.3 39.6 %front.1 = (f32[1024,1024]{1,0:T(8,128)}, bf16[1024,1024]{1,0:T(8,128)(2,1)}, f32[1024,128]{1,0:T(8,128)}, bf16[128,1024]{1,0:T(8,128)(2,1)}, bf16[160,1024]{1,0...) custom-call(bf16[1024,2048]{1,0:T(8,128)(2,1)} %bitcast.53, ...), custom_call_target="tpu_custom_call" | custom-call | tf_op jit(solution)/shard_map/front/pallas_call | solution.py:1377
  115.0 1.5 fusion.1
  116.4 1.1 reshape_squeeze.11
  117.6 0.7 constant_dynamic-slice_fusion
  118.3 79.7 %scan_forward.1 = (f32[1024,1024]{1,0:T(8,128)}, f32[1024,1024]{1,0:T(8,128)}, f32[128,16,8,128]{3,2,1,0:T(8,128)}, f32[16,8,128]{2,1,0:T(8,128)}, f32[1024,1024...) custom-call(bf16[128,1024]{1,0:T(8,128)(2,1)} %get-tuple-element.57., ...), custom_call_target="tpu_custom_call" | custom-call | flops 134217728 | bytes 25165824 | tf_op jit(solution)/shard_map/scan_forward/pallas_call | solution.py:771
  198.0 1.2 slice_reduce_fusion
  199.2 0.0 copy-start
  199.2 13.7 %multiply_convert_fusion = (bf16[1024,1024]{1,0:T(8,128)(2,1)S(1)}, f32[1024,1024]{1,0:T(8,128)}) fusion(f32[1024,1024]{1,0:T(8,128)} %get-tuple-element.67, f32[1024,1024]{1,0:T(8,128)} %get-tuple-element.70, f32[1024]{0:T(1024)S(1)} %slice_reduce_fusion, bf16[1024,2048]{1,0:T(8,128)(2,1)} %bitcast.80, bf16[1024,2048]{1,0:T(8,128)(2,1)} %bitcast.60), kind=kOutput, calls=%fused_computation | convolution fusion | flops 4308598784 | bytes 23072768 | tf_op jit(solution)/shard_map/dot_general | solution.py:27
  213.0 0.0 copy-start.1
  213.0 0.0 copy-done
  213.0 0.0 copy-start.2
  213.0 0.0 copy-start.10
  213.0 6.3 %convolution_convert_fusion.1 = bf16[2048,1024]{1,0:T(8,128)(2,1)} fusion(bf16[1024,2048]{1,0:T(8,128)(2,1)S(1)} %bitcast.56, bf16[1024,1024]{1,0:T(8,128)(2,1)S(1)} %get-tuple-element.138.refs_7_), kind=kOutput, calls=%fused_computation.4 | convolution fusion | flops 4297064448 | bytes 10485760 | tf_op jit(solution)/shard_map/dot_general | solution.py:23
  219.2 0.0 copy-done.1
  219.2 0.0 copy-done.2
  219.2 0.0 copy-done.10
  219.3 6.3 %convolution_convert_fusion = bf16[1024,2048]{1,0:T(8,128)(2,1)} fusion(bf16[1024,1024]{1,0:T(8,128)(2,1)S(1)} %copy-done.2, bf16[1024,2048]{1,0:T(8,128)(2,1)S(1)} %bitcast.81), kind=kOutput, calls=%fused_computation.3 | convolution fusion | flops 4297064448 | bytes 10485760 | tf_op jit(solution)/shard_map/dot_general | solution.py:23
  225.5 108.7 %scan_backward.1 = (f32[1024,1024]{1,0:T(8,128)}, f32[16,8,128]{2,1,0:T(8,128)}, f32[16,8,128]{2,1,0:T(8,128)}, f32[1,1024]{1,0:T(1,128)}, f32[1,1024]{1,0:T(1,1...) custom-call(f32[1024,1024]{1,0:T(8,128)} %get-tuple-element.64.pre_r, ...), custom_call_target="tpu_custom_call" | custom-call | flops 335544320 | bytes 29360128 | tf_op jit(solution)/shard_map/scan_backward/pallas_call | solution.py:833
  334.3 1.4 slice.29.refs_11_
  335.6 1.5 bitcast_multiply_fusion.refs_14_
  337.1 1.5 copy_bitcast_fusion
  338.7 103.5 %finish.1 = (f32[320,128]{1,0:T(8,128)}, bf16[2,4,64,1024]{3,2,1,0:T(8,128)(2,1)}, bf16[256,2048]{1,0:T(8,128)(2,1)}, f32[4,40,256]{2,1,0:T(8,128)}) custom-call(f32[1024,1024]{1,0:T(8,128)} %get-tuple-element.72.refs_0_, f32[1024,1024]{1,0:T(8,128)} %get-tuple-element.73.refs_1_, bf16[1024,1024]{1,0:T(8,128)(2,1)} %get-tuple-element.60.act_ref.refs_2_, ...), custom_call_target="tpu_custom_call" | custom-call | tf_op jit(solution)/shard_map/finish/pallas_call | solution.py:1176
  442.2 1.4 copy.50.gain
  443.6 5.6 %unpack.1 = (bf16[1,256,2048]{2,1,0:T(8,128)(2,1)}, f32[1,16,1024]{2,1,0:T(8,128)}, f32[1,3,1024]{2,1,0:T(4,128)}, bf16[1,256,2048]{2,1,0:T(8,128)(2,1)}, f32[1,...) custom-call(f32[320,128]{1,0:T(8,128)} %get-tuple-element.84.small, ...), custom_call_target="tpu_custom_call" | custom-call | tf_op jit(solution)/shard_map/unpack/pallas_call | solution.py:1496
  449.2 1.3 copy.51
  450.5 1.3 copy.52
  451.9 1.6 copy.53
  (1 shorter events, 0.0 us)
Async XLA Ops:
  4.1 3.2 copy-start.3
  4.1 3.2 copy-start.4
  4.1 3.2 copy-start.5
  4.1 3.1 copy-start.6
  4.1 3.1 copy-start.7
  4.1 3.1 copy-start.8
  4.1 3.1 copy-start.9
  199.2 13.7 %copy-start = (bf16[4,256,2048]{2,1,0:T(8,128)(2,1)S(1)}, bf16[4,256,2048]{2,1,0:T(8,128)(2,1)}, u32[]{:S(2)}) copy-start(bf16[4,256,2048]{2,1,0:T(8,128)(2,1)} %get-tuple-element.53) | copy-start | bytes 12582916
  213.0 6.3 %copy-start.1 = (bf16[1024,1024]{1,0:T(8,128)(2,1)}, bf16[1024,1024]{1,0:T(8,128)(2,1)S(1)}, u32[]{:S(2)}) copy-start(bf16[1024,1024]{1,0:T(8,128)(2,1)S(1)} %get-tuple-element.138.refs_7_) | copy-start | bytes 6291460
  213.0 6.3 %copy-start.2 = (bf16[1024,1024]{1,0:T(8,128)(2,1)S(1)}, bf16[1024,1024]{1,0:T(8,128)(2,1)}, u32[]{:S(2)}) copy-start(bf16[1024,1024]{1,0:T(8,128)(2,1)} %get-tuple-element.71.gated_src) | copy-start | bytes 6291460
  213.0 6.3 %copy-start.10 = (bf16[4,256,2048]{2,1,0:T(8,128)(2,1)S(1)}, bf16[4,256,2048]{2,1,0:T(8,128)(2,1)}, u32[]{:S(2)}) copy-start(bf16[4,256,2048]{2,1,0:T(8,128)(2,1)} %get-tuple-element.65) | copy-start | bytes 12582916

commit v7 on v6

--- a/solution.py
+++ b/solution.py
@@ -457,8 +457,8 @@
 
 
 def forward_kernel(
-    shape, steps,
-    low_ref, wdt_ref, bias_ref, act_ref, bc_ref, a_ref, skip_ref, init_ref, weight_ref, cot_ref,
+    shape, steps, taps,
+    low_ref, wdt_ref, params_ref, act_ref, bc_ref, a_ref, init_ref, weight_ref, cot_ref,
     tok_ref, gate_one, gate_src,
     y_ref, pre_ref, check_ref, final_ref, gate_ref, gated_ref, weights_ref, cots_ref, gate_two,
     state, rate_pl, drive_pl, y_pl, w_one, w_two, local_s, *sems,
@@ -488,7 +488,9 @@
         load_one.start()
         state[...] = init_ref[...]
 
-    pre = dot_tn(low_ref[...], wdt_ref[...]) + bias_ref[...]
+    lines = params_ref[pl.ds(width, 8), :]
+    bias, skip = lines[taps + 1 : taps + 2], lines[taps + 2 : taps + 3]
+    pre = dot_tn(low_ref[...], wdt_ref[...]) + bias
     pre_ref[...] = pre
     rate = softplus(pre)
     act = act_ref[...].astype(F32)
@@ -538,7 +540,7 @@
 
     lax.fori_loop(0, 2, part_of_step, 0)
     y_ref[pl.ds(pl.multiple_of(step * count, count), count), :] = (
-        from_planes(y_pl) + skip_ref[...] * act_ref[...].astype(F32)
+        from_planes(y_pl) + skip * act_ref[...].astype(F32)
     )
 
     @pl.when(step == steps - 1)
@@ -563,8 +565,11 @@
             for j, w in enumerate((w_one, w_two)):
                 cols = pl.ds(j * half, half)
                 gate = rstd * dot_nn(tok_ref[rows, :], w[...].reshape(model, half))
-                gate_ref[rows, cols] = gate
-                gated_ref[rows, cols] = (y_ref[rows, cols] * gate * sigmoid(gate)).astype(BF16)
+                sig = sigmoid(gate)
+                y_val = y_ref[rows, cols]
+                gate_ref[rows, cols] = gate * sig
+                gated_ref[rows, cols] = (y_val * gate * sig).astype(BF16)
+                y_ref[rows, cols] = rstd * y_val * sig * (1.0 + gate * (1.0 - sig))
             return carry
 
         blocks = y_ref.shape[0] // block
@@ -578,8 +583,8 @@
 
 
 def backward_kernel(
-    shape, steps,
-    pre_ref, act_ref, gy_ref, bc_ref, a_ref, skip_ref, check_ref, wdt_ref, low_ref, base_ref,
+    shape, steps, taps,
+    pre_ref, act_ref, gy_ref, bc_ref, a_ref, params_ref, check_ref, wdt_ref, low_ref, base_ref,
     first_src, second_src, gated_src, weight_src,
     gact_ref, agrad_ref, start_ref, dtb_ref, sgrad_ref, dtp_ref, mix_ref,
     first_out, second_out, third_out,
@@ -725,7 +730,8 @@
     act = act_ref[...].astype(F32)
     gy = gy_ref[...]
     g_dtpre = ((g_rate + act * through) * sigmoid(pre)).astype(BF16)
-    gact_ref[...] = gy * skip_ref[...] + rate * through
+    skip = params_ref[pl.ds(width, 8), :][taps + 2 : taps + 3]
+    gact_ref[...] = gy * skip + rate * through
     dtb_ref[...] += jnp.sum(g_dtpre.astype(F32), axis=0, keepdims=True)
     sgrad_ref[...] += jnp.sum(gy * act, axis=0, keepdims=True)
     dtp_ref[...] += dot_nn(low_ref[...], g_dtpre)
@@ -754,7 +760,7 @@
 
 
 def forward_scan(
-    shape, low, w_dt, bias, act, bc, a2, skip, init, weight, cot, tok, gate_one, gate_part, block
+    shape, taps, low, w_dt, params, act, bc, a2, init, weight, cot, tok, gate_one, gate_part, block
 ):
     lines, fast, seq_lines = shape
     length, features = act.shape
@@ -769,13 +775,13 @@
 
     plane = pltpu.VMEM((block // UNROLL, planes * UNROLL, LANES), F32)
     return pl.pallas_call(
-        functools.partial(forward_kernel, shape, steps),
+        functools.partial(forward_kernel, shape, steps, taps),
         grid=(steps,),
         in_specs=[
             pl.BlockSpec((low_rank, block), lambda i: (0, i)),
-            whole(low_rank, features), whole(1, features), rows,
+            whole(low_rank, features), whole(*params.shape), rows,
             pl.BlockSpec((block, 2 * width), lambda i: (i, 0), memory_space=pltpu.SMEM),
-            whole(width, planes, LANES), whole(1, features), whole(width, planes, LANES),
+            whole(width, planes, LANES), whole(width, planes, LANES),
             whole(*weight.shape), whole(*cot.shape), whole(*tok.shape), ANY, ANY,
         ],
         out_specs=[
@@ -809,11 +815,11 @@
             transcendentals=length * features * width,
         ),
         name="scan_forward",
-    )(low, w_dt, bias, act, bc, a2, skip, init, weight, cot, tok, gate_one, gate_part)
+    )(low, w_dt, params, act, bc, a2, init, weight, cot, tok, gate_one, gate_part)
 
 
 def backward_scan(
-    shape, pre, act, gy, bc, a2, skip, checks, w_dt, dt_low, base, first, second, gated, weight,
+    shape, taps, pre, act, gy, bc, a2, params, checks, w_dt, dt_low, base, first, second, gated, weight,
     block,
 ):
     lines, fast, seq_lines = shape
@@ -831,14 +837,14 @@
     plane = pltpu.VMEM((block // UNROLL, planes * UNROLL, LANES), F32)
     mixed = (low_rank + 2 * width, length)
     return pl.pallas_call(
-        functools.partial(backward_kernel, shape, steps),
+        functools.partial(backward_kernel, shape, steps, taps),
         grid=(steps,),
         in_specs=[
             rows, rows, rows,
             pl.BlockSpec(
                 (block, 2 * width), lambda i: (steps - 1 - i, 0), memory_space=pltpu.SMEM
             ),
-            whole, line,
+            whole, all_of(*params.shape),
             pl.BlockSpec(
                 (block // UNROLL, width, planes, LANES), lambda i: (steps - 1 - i, 0, 0, 0)
             ),
@@ -885,13 +891,13 @@
             transcendentals=length * features * width,
         ),
         name="scan_backward",
-    )(pre, act, gy, bc, a2, skip, checks, w_dt, dt_low, base, first, second, gated, weight)
+    )(pre, act, gy, bc, a2, params, checks, w_dt, dt_low, base, first, second, gated, weight)
 
 
 def finish_kernel(shape, taps, history, refs, scratch):
     (
         gact, x_in, act, tok, w_x, w_g, w_h, gs_gate,
-        mix, w_xt, head, kern, b_conv, dtp, a_grad, dtb, sgrad, g_half, own_tok, own_cot,
+        mix, w_xt, head, params, dtp, a_sum, dtb, sgrad, g_half, own_tok, own_cot,
         final, start,
         small_out, halves_out, input_out, ends_out,
     ) = refs
@@ -901,6 +907,9 @@
     ) = scratch[:16]
     seg, seq = grids(shape)
     length, feats = act.shape
+    width = a_sum.shape[0]
+    kern = params.at[pl.ds(width, 8)]
+    b_conv = params.at[pl.ds(width + taps, 1)]
     at = 16
     sets = []
     for inside, size in ((True, 8), (True, 8), (True, 8)):
@@ -994,8 +1003,8 @@
     loads[3].wait()
     low_rank = dtp.shape[0]
     mixes = mix.shape[0]
-    width = a_grad.shape[0]
     part = small_src.shape[2]
+    a_grad = from_states(a_sum) * params[pl.ds(0, width), :]
     xp = dot_nn(mix[...], actb[...])
     for g in range(small_src.shape[0]):
         cols = slice(g * part, (g + 1) * part)
@@ -1039,9 +1048,9 @@
     lax.fori_loop(0, seg.lines, stay, 0)
     ends_in = jnp.concatenate(
         [
-            final[...],
+            from_states(final),
             xb[pl.ds(length, 8), :][8 - history :],
-            start[...],
+            from_states(start),
             sum_head(gc, kern, history, taps),
             jnp.zeros((ends_src.shape[1] - 2 * (width + history), feats), F32),
         ],
@@ -1125,6 +1134,10 @@
         keep.wait()
 
 
+def from_states(ref):
+    return jnp.concatenate([ref[:, s, :] for s in range(ref.shape[1])], axis=1)
+
+
 def sum_head(gc, kern, history, taps):
     top = gc[pl.ds(0, 8), :]
     rows = []
@@ -1139,10 +1152,10 @@
     lines, fast, seq_lines = shape
     segs, seqs = lines * fast, seq_lines * 2
     gact, x_in, act, tok, w_x, w_g, w_h, gs_gate = big
-    mix, w_xt, head, kern, b_conv, dtp, a_grad, dtb, sgrad, g_half, own_tok, own_cot = small[:12]
+    mix, w_xt, head, params, dtp, a_sum, dtb, sgrad, g_half, own_tok, own_cot = small[:11]
     length, feats = act.shape
     own_len, model = own_tok.shape
-    width = a_grad.shape[0]
+    width = a_sum.shape[0]
     rows = dtp.shape[0] + mix.shape[0] + width + 16
     block_rows = model // segs
     own_rows = g_half.shape[0] // seqs
@@ -1171,11 +1184,11 @@
     ]
 
     def kernel(*refs):
-        finish_kernel(shape, taps, history, refs[:26], refs[26:])
+        finish_kernel(shape, taps, history, refs[:25], refs[25:])
 
     return pl.pallas_call(
         kernel,
-        in_specs=[ANY] * 8 + [INSIDE] * 14,
+        in_specs=[ANY] * 8 + [INSIDE] * 13,
         out_specs=[INSIDE] * 4,
         out_shape=[
             jax.ShapeDtypeStruct((rows, feats // segs), F32),
@@ -1288,7 +1301,7 @@
 def front_kernel(
     shape, steps, taps, history, width,
     tok_ref, wx_ref, small_ref, head_ref, gate_src,
-    x_ref, act_ref, rstd_ref, wdt_ref, wxt_ref, par_ref, a2_ref, low_ref, bc_ref, gate_out,
+    x_ref, act_ref, wdt_ref, wxt_ref, par_ref, a2_ref, low_ref, bc_ref, gate_out,
     xb, mix_s, mix, local_s, *scratch,
 ):
     seg, seq = grids(shape)
@@ -1319,7 +1332,6 @@
     kern = par_ref[pl.ds(width, 8), :]
     rows = tok_ref[...].astype(F32)
     rstd = lax.rsqrt(jnp.mean(rows * rows, axis=1, keepdims=True) + EPSILON)
-    rstd_ref[...] = jnp.broadcast_to(rstd, rstd_ref.shape)
     x_in = rstd * dot_nn(tok_ref[...], wx_ref[...])
     x_ref[...] = x_in
     xb[pl.ds(8, count), :] = x_in
@@ -1383,14 +1395,13 @@
             whole(*small_all.shape), whole(*head.shape), ANY,
         ],
         out_specs=[
-            rows(feats), rows(feats), rows(LANES), whole(low_rank, feats), whole(mixes, feats),
+            rows(feats), rows(feats), whole(low_rank, feats), whole(mixes, feats),
             whole(width + 16, feats), whole(width, feats // LANES, LANES),
             whole(low_rank, length), whole(length, 2 * width), ANY,
         ],
         out_shape=[
             jax.ShapeDtypeStruct((length, feats), F32),
             jax.ShapeDtypeStruct((length, feats), BF16),
-            jax.ShapeDtypeStruct((length, LANES), F32),
             jax.ShapeDtypeStruct((low_rank, feats), BF16),
             jax.ShapeDtypeStruct((mixes, feats), BF16),
             jax.ShapeDtypeStruct((width + 16, feats), F32),
@@ -1433,13 +1444,9 @@
     input_o[0] = input_grad[...]
     out_o[...] = out_grad[...]
     part = small.shape[1]
-    columns = xp_o.shape[1]
+    columns = xp_o.shape[0]
     dtp_o[...] = small[pl.ds(0, low_rank), :]
-    turned = small[pl.ds(low_rank, low_rank), :].T
-    xp_o[:, pl.ds(0, low_rank)] = turned
-    xp_o[:, pl.ds(low_rank, columns - low_rank)] = small[
-        pl.ds(2 * low_rank, columns - low_rank), :
-    ].T
+    xp_o[...] = small[pl.ds(low_rank, columns), :]
     at = low_rank + columns
     a_o[...] = small[pl.ds(at, width), :]
     lines = small[pl.ds(at + width, 16), :]
@@ -1454,9 +1461,11 @@
             got = rows[:, g * part : (g + 1) * part]
             cols = pl.ds((g * seqs + s) * part, part)
             final_o[0, :, cols] = got[:width]
-            final_c[0, :, cols] = got[width : width + history]
             start_o[0, :, cols] = got[width + history : 2 * width + history]
-            start_c[0, :, cols] = got[2 * width + history : 2 * (width + history)]
+            for r in range(history):
+                final_c[r, :, cols] = got[width + r : width + r + 1]
+                at = 2 * width + history + r
+                start_c[r, :, cols] = got[at : at + 1]
     scale = gain[...]
     total = jnp.zeros((in_o.shape[0], part), F32)
     groups = halves.shape[3] // part
@@ -1480,11 +1489,11 @@
     args = (small, halves, ends, mixed, input_grad, out_grad, weight, gain)
     outs = [
         jax.ShapeDtypeStruct((1,) + mixed.shape, BF16),
-        f32(1, width, kept), f32(1, history, kept),
+        f32(1, width, kept), f32(history, 1, kept),
         jax.ShapeDtypeStruct((1,) + input_grad.shape, BF16),
-        f32(1, width, kept), f32(1, history, kept),
+        f32(1, width, kept), f32(history, 1, kept),
         f32(own_rows), f32(*weight.shape),
-        f32(taps, part), f32(part), f32(part, low_rank + 2 * width), f32(low_rank, part),
+        f32(taps, part), f32(part), f32(low_rank + 2 * width, part), f32(low_rank, part),
         f32(part), f32(width, part), f32(part), f32(part, model),
     ]
 
@@ -1545,16 +1554,12 @@
     w_x_half, small_all, tok, g_part = gather_start(shape, scaled_x, scaled_g, small, tokens[0])
     history = init_conv.shape[1]
     head = jnp.pad(mine(init_conv[0]), ((8 - history, 0), (0, 0)))
-    x_in, act, rstd, w_dt, w_xt, params, a2, dt_low, bc, w_g_one = front(
+    x_in, act, w_dt, w_xt, params, a2, dt_low, bc, w_g_one = front(
         shape, taps, history, width, tok, w_x_half, small_all, head, g_part, 4 * block
     )
-    rstd = rstd[:, :1]
     init = mine(init_state[0]).reshape(width, planes, LANES)
-    a_mat = params[:width]
-    kernel = params[width : width + 8]
-    b_conv, b_dt, skip = (params[width + taps + i][None] for i in range(3))
-    y_val, pre, checks, final, gate, gated, w_out, cot, w_g_two = forward_scan(
-        shape, dt_low, w_dt, b_dt, act, bc, a2, skip, init, out_proj, cotangent[0], tok,
+    slope, pre, checks, final, gate_act, gated, w_out, cot, w_g_two = forward_scan(
+        shape, taps, dt_low, w_dt, params, act, bc, a2, init, out_proj, cotangent[0], tok,
         w_g_one, g_part, 2 * block,
     )
     w_out = w_out.reshape(feats, model)
@@ -1562,16 +1567,13 @@
     w_g_one = w_g_one.reshape(model, feats // 2)
     w_g_two = w_g_two.reshape(model, feats // 2)
     g_gated = dot_nt(cot, w_out)
-    sig_gate = jax.nn.sigmoid(gate)
-    gy = g_gated * gate * sig_gate
-    gs_gate = (
-        rstd * g_gated * y_val * sig_gate * (1.0 + gate * (1.0 - sig_gate))
-    ).astype(BF16)
+    gy = g_gated * gate_act
+    gs_gate = (g_gated * slope).astype(BF16)
     out_grad = dot_tn(gated, cot).astype(BF16)
     gate_grad = dot_tn(tok, gs_gate).astype(BF16)
     g_actp, a_sum, start, dtb_grad, skip_grad, dtp_grad, g_mixed, g_half, out_grad, mixed_out = (
         backward_scan(
-            shape, pre, act, gy, bc, a2, skip, checks, w_dt, dt_low, tokens[0],
+            shape, taps, pre, act, gy, bc, a2, params, checks, w_dt, dt_low, tokens[0],
             gate_grad.reshape(segs, seqs * own_rows, feats),
             out_grad.reshape(segs, part, model),
             gated, w_out, 2 * block,
@@ -1581,16 +1583,21 @@
         shape, taps, history,
         (g_actp, x_in, act, tok, w_x_half, w_g_one, w_g_two, gs_gate),
         (
-            g_mixed, w_xt, head, kernel, b_conv, dtp_grad, a_sum.reshape(width, feats) * a_mat, dtb_grad, skip_grad, g_half,
-            tokens[0], cotangent[0],
-            final.reshape(width, feats), start.reshape(width, feats),
+            g_mixed, w_xt, head, params, dtp_grad, a_sum, dtb_grad, skip_grad, g_half,
+            tokens[0], cotangent[0], final, start,
         ),
     )
     if part % LANES == 0:
-        return unpack(
-            taps, history, low_rank, width, grads, halves, ends, mixed_out, input_grad, out_grad,
-            in_proj, gain_col,
-        )
+        outs = list(
+            unpack(
+                taps, history, low_rank, width, grads, halves, ends, mixed_out, input_grad,
+                out_grad, in_proj, gain_col,
+            )
+        )
+        outs[2], outs[5], outs[10] = (
+            outs[2].transpose(1, 0, 2), outs[5].transpose(1, 0, 2), outs[10].T
+        )
+        return tuple(outs)
     ends = (
         ends.reshape(seqs, ends.shape[1], segs // seqs, part)
         .transpose(1, 2, 0, 3)

time: 458 us -> 445 us (0.972)
  local copies, waits for them, and re-layouts: 19.2 us -> 9.24 us
where the time goes in v7:
time: 445 us; the launch traced here: 441 us
  Pallas kernels  403 us (91%)
  matrix products  25.1 us (6%)
  local copies, waits for them, and re-layouts  9.24 us (2%)
    pallas_call x1, Pallas kernels, backward_scan(): pl.pallas_call(functools.partial(backward_kernel, shape, steps, taps), gr...  108 us
    pallas_call x1, Pallas kernels, finish_all(): pl.pallas_call(kernel, in_specs=[ANY] * 8 + [INSIDE] * 13, out_specs=[INS...  104 us
    pallas_call x1, Pallas kernels, forward_scan(): pl.pallas_call(functools.partial(forward_kernel, shape, steps, taps), gri...  79.7 us
    pallas_call x1, Pallas kernels, gather_start(): pl.pallas_call(kernel, in_specs=[ANY, ANY, INSIDE, ANY], out_specs=[ANY]...  65.9 us
    pallas_call x1, Pallas kernels, front(): pl.pallas_call(functools.partial(front_kernel, shape, steps, taps, histor...  39.6 us
    dot_general x1, matrix products, dot_nt(): lax.dot_general(a, b, (((1,), (1,)), ((), ())), preferred_element_type=F32)  12.6 us
    dot_general x2, matrix products, dot_tn(): lax.dot_general(a, b, (((0,), (0,)), ((), ())), preferred_element_type=F32)  12.5 us

profile of v7, /device:TPU:1, one launch (start us, length us, event | category | flops | bytes accessed | tf_op | source)
XLA Modules:
  0.0 440.8 jit_solution(9144355737866210271)
XLA Ops:
  0.6 1.2 convert_bitcast_fusion
  1.8 1.5 multiply_convert_fusion.1
  3.3 0.8 reshape.70
  4.1 0.0 copy-start.3
  4.1 0.0 copy-start.4
  4.1 0.0 copy-start.5
  4.1 0.0 copy-start.6
  4.1 0.0 copy-start.7
  4.1 0.0 copy-start.8
  4.1 0.0 copy-start.9
  4.1 0.4 fusion
  4.5 0.1 copy.39
  4.6 1.0 reshape.71.refs_0_
  5.6 0.2 copy.40
  5.8 0.4 copy.41
  6.2 1.0 reshape.72.refs_1_
  7.2 0.0 copy-done.3
  7.2 0.0 copy-done.4
  7.2 0.0 copy-done.5
  7.2 0.0 copy-done.6
  7.2 0.0 copy-done.7
  7.2 0.0 copy-done.8
  7.3 0.0 copy-done.9
  7.3 0.1 concatenate.3
  7.3 0.6 pad.8.refs_2_
  8.0 65.9 %gather_start.1 = (bf16[8,4,64,1024]{3,2,1,0:T(8,128)(2,1)}, bf16[8,320,128]{2,1,0:T(8,128)(2,1)}, bf16[4,256,2048]{2,1,0:T(8,128)(2,1)}, bf16[4,2,64,512]{3,2,1,0:T(8,128)(2,1)}) custom-call(bf16[4,64,1024]{2,1,0:T(8,128)(2,1)} %reshape.71.refs_0_, bf16[4,2,64,512]{3,2,1,0:T(8,128)(2,1)} %reshape.72.refs_1_, bf16[320,128]{1,0:T(8,128)(2,1)} %pad.8.refs_2_, ...), custom_call_target="tpu_custom_call" | custom-call | tf_op jit(solution)/shard_map/gather_start/pallas_call | solution.py:1276
  73.9 0.8 constant_dynamic-slice_fusion.1
  74.7 0.6 pad.9.head_ref.refs_10_
  75.3 39.6 %front.1 = (f32[1024,1024]{1,0:T(8,128)}, bf16[1024,1024]{1,0:T(8,128)(2,1)}, bf16[128,1024]{1,0:T(8,128)(2,1)}, bf16[160,1024]{1,0:T(8,128)(2,1)}, f32[32,1024]...) custom-call(bf16[1024,2048]{1,0:T(8,128)(2,1)} %bitcast.47, ...), custom_call_target="tpu_custom_call" | custom-call | tf_op jit(solution)/shard_map/front/pallas_call | solution.py:1389
  114.9 1.1 reshape_squeeze.11
  116.1 0.7 constant_dynamic-slice_fusion
  116.8 79.7 %scan_forward.1 = (f32[1024,1024]{1,0:T(8,128)}, f32[1024,1024]{1,0:T(8,128)}, f32[128,16,8,128]{3,2,1,0:T(8,128)}, f32[16,8,128]{2,1,0:T(8,128)}, f32[1024,1024...) custom-call(bf16[128,1024]{1,0:T(8,128)(2,1)} %get-tuple-element.72., ...), custom_call_target="tpu_custom_call" | custom-call | flops 134217728 | bytes 25165824 | tf_op jit(solution)/shard_map/scan_forward/pallas_call | solution.py:777
  196.5 0.0 copy-start
  196.5 12.6 %multiply_convert_fusion = (bf16[1024,1024]{1,0:T(8,128)(2,1)S(1)}, f32[1024,1024]{1,0:T(8,128)}) fusion(f32[1024,1024]{1,0:T(8,128)} %get-tuple-element.84, f32[1024,1024]{1,0:T(8,128)} %get-tuple-element.82, bf16[1024,2048]{1,0:T(8,128)(2,1)} %bitcast.74, bf16[1024,2048]{1,0:T(8,128)(2,1)} %bitcast.54), kind=kOutput, calls=%fused_computation | convolution fusion | flops 4298113024 | bytes 23068672 | tf_op jit(solution)/shard_map/dot_general | solution.py:27
  209.1 0.0 copy-start.1
  209.1 0.0 copy-done
  209.1 0.0 copy-start.2
  209.1 0.0 copy-start.10
  209.2 6.3 %convolution_convert_fusion.1 = bf16[2048,1024]{1,0:T(8,128)(2,1)} fusion(bf16[1024,2048]{1,0:T(8,128)(2,1)S(1)} %bitcast.50, bf16[1024,1024]{1,0:T(8,128)(2,1)S(1)} %get-tuple-element.120.refs_7_), kind=kOutput, calls=%fused_computation.2 | convolution fusion | flops 4297064448 | bytes 10485760 | tf_op jit(solution)/shard_map/dot_general | solution.py:23
  215.4 0.0 copy-done.1
  215.4 0.0 copy-done.2
  215.4 0.0 copy-done.10
  215.4 6.3 %convolution_convert_fusion = bf16[1024,2048]{1,0:T(8,128)(2,1)} fusion(bf16[1024,1024]{1,0:T(8,128)(2,1)S(1)} %copy-done.2, bf16[1024,2048]{1,0:T(8,128)(2,1)S(1)} %bitcast.75), kind=kOutput, calls=%fused_computation.1 | convolution fusion | flops 4297064448 | bytes 10485760 | tf_op jit(solution)/shard_map/dot_general | solution.py:23
  221.7 108.4 %scan_backward.1 = (f32[1024,1024]{1,0:T(8,128)}, f32[16,8,128]{2,1,0:T(8,128)}, f32[16,8,128]{2,1,0:T(8,128)}, f32[1,1024]{1,0:T(1,128)}, f32[1,1024]{1,0:T(1,1...) custom-call(f32[1024,1024]{1,0:T(8,128)} %get-tuple-element.79.pre_r, ...), custom_call_target="tpu_custom_call" | custom-call | flops 335544320 | bytes 29360128 | tf_op jit(solution)/shard_map/scan_backward/pallas_call | solution.py:839
  330.1 103.6 %finish.1 = (f32[320,128]{1,0:T(8,128)}, bf16[2,4,64,1024]{3,2,1,0:T(8,128)(2,1)}, bf16[256,2048]{1,0:T(8,128)(2,1)}, f32[4,40,256]{2,1,0:T(8,128)}) custom-call(f32[1024,1024]{1,0:T(8,128)} %get-tuple-element.86.refs_0_, f32[1024,1024]{1,0:T(8,128)} %get-tuple-element.87.refs_1_, bf16[1024,1024]{1,0:T(8,128)(2,1)} %get-tuple-element.75.act_ref.refs_2_, ...), custom_call_target="tpu_custom_call" | custom-call | tf_op jit(solution)/shard_map/finish/pallas_call | solution.py:1189
  433.7 1.4 copy.44.gain
  435.1 5.6 %unpack.1 = (bf16[1,256,2048]{2,1,0:T(8,128)(2,1)}, f32[1,16,1024]{2,1,0:T(8,128)}, f32[3,1,1024]{2,1,0:T(1,128)}, bf16[1,256,2048]{2,1,0:T(8,128)(2,1)}, f32[1,...) custom-call(f32[320,128]{1,0:T(8,128)} %get-tuple-element.98.small, ...), custom_call_target="tpu_custom_call" | custom-call | tf_op jit(solution)/shard_map/unpack/pallas_call | solution.py:1505
  (1 shorter events, 0.0 us)
Async XLA Ops:
  4.1 3.2 copy-start.3
  4.1 3.2 copy-start.4
  4.1 3.2 copy-start.5
  4.1 3.1 copy-start.6
  4.1 3.1 copy-start.7
  4.1 3.1 copy-start.8
  4.1 3.1 copy-start.9
  196.5 12.6 %copy-start = (bf16[4,256,2048]{2,1,0:T(8,128)(2,1)S(1)}, bf16[4,256,2048]{2,1,0:T(8,128)(2,1)}, u32[]{:S(2)}) copy-start(bf16[4,256,2048]{2,1,0:T(8,128)(2,1)} %get-tuple-element.68) | copy-start | bytes 12582916
  209.1 6.3 %copy-start.1 = (bf16[1024,1024]{1,0:T(8,128)(2,1)}, bf16[1024,1024]{1,0:T(8,128)(2,1)S(1)}, u32[]{:S(2)}) copy-start(bf16[1024,1024]{1,0:T(8,128)(2,1)S(1)} %get-tuple-element.120.refs_7_) | copy-start | bytes 6291460
  209.1 6.3 %copy-start.2 = (bf16[1024,1024]{1,0:T(8,128)(2,1)S(1)}, bf16[1024,1024]{1,0:T(8,128)(2,1)}, u32[]{:S(2)}) copy-start(bf16[1024,1024]{1,0:T(8,128)(2,1)} %get-tuple-element.85.gated_src) | copy-start | bytes 6291460
  209.1 6.3 %copy-start.10 = (bf16[4,256,2048]{2,1,0:T(8,128)(2,1)S(1)}, bf16[4,256,2048]{2,1,0:T(8,128)(2,1)}, u32[]{:S(2)}) copy-start(bf16[4,256,2048]{2,1,0:T(8,128)(2,1)} %get-tuple-element.80) | copy-start | bytes 12582916

commit v8 on v7

--- a/solution.py
+++ b/solution.py
@@ -902,23 +902,25 @@
         small_out, halves_out, input_out, ends_out,
     ) = refs
     (
-        gc, xb, actb, tokb, wxb, wgb, gsg, gs_x, xg, q_src, pack, small_src, ends_src, x_half,
+        gc, xb, actb, tokb, wxb, wgb, gsg, gs_x, xg, xh, q_src, pack, small_src, ends_src, x_half,
         in_s, own_s,
-    ) = scratch[:16]
+    ) = scratch[:17]
     seg, seq = grids(shape)
     length, feats = act.shape
     width = a_sum.shape[0]
     kern = params.at[pl.ds(width, 8)]
     b_conv = params.at[pl.ds(width + taps, 1)]
-    at = 16
+    at = 17
     sets = []
-    for inside, size in ((True, 8), (True, 8), (True, 8)):
+    for size in (8, 8, 8, 8):
         sets.append(scratch[at : at + size])
         at += size
     swaps_s = [scratch[at + 2 * i : at + 2 * i + 2] for i in range(3)]
     small = Scatter(seg, small_src, sets[0], inside=True)
-    x_sum = Scatter(seg, xg, sets[1], inside=True)
-    q_sum = Scatter(seq, q_src, sets[2], inside=True)
+    x_sums = [
+        Scatter(seg, xg, sets[1], inside=True), Scatter(seg, xh, sets[2], inside=True)
+    ]
+    q_sum = Scatter(seq, q_src, sets[3], inside=True)
     loads = [
         pltpu.make_async_copy(gact, gc.at[pl.ds(0, length)], in_s.at[0]),
         pltpu.make_async_copy(x_in, xb.at[pl.ds(8, length)], in_s.at[1]),
@@ -957,13 +959,13 @@
     lax.fori_loop(0, length // big, add_mixed, 0)
     loads[1].wait()
     tall = 32
-    chunk = min(512, feats)
+    chunk = feats // 2
     sums_at = 8 * (taps + 1)
     pack[...] = jnp.zeros_like(pack)
 
-    def through_conv(i, carry):
+    def through_conv(side, i, carry):
         t0 = pl.multiple_of(i * tall, tall)
-        for c in range(0, feats, chunk):
+        for c in (side * chunk,):
             cols = pl.ds(c, chunk)
             wide = xb[pl.ds(t0, tall + 8), cols]
             rows = [wide[8 - history + k : 8 - history + k + tall] for k in range(taps)]
@@ -983,14 +985,13 @@
             )
         return carry
 
-    lax.fori_loop(0, length // tall, through_conv, 0)
     loads[2].wait()
 
-    def to_input(i, carry):
+    def to_input(side, i, carry):
         t0 = pl.multiple_of(i * tall, tall)
         lines = tokb[pl.ds(t0, tall), :].astype(F32)
         rstd = lax.rsqrt(jnp.mean(lines * lines, axis=1, keepdims=True) + EPSILON)
-        for c in range(0, feats, chunk):
+        for c in (side * chunk,):
             cols = pl.ds(c, chunk)
             wide = gc[pl.ds(t0, tall + 8), cols]
             g_x = kern[pl.ds(0, 1), cols] * wide[history : history + tall]
@@ -999,7 +1000,47 @@
             gs_x[pl.ds(t0, tall), cols] = (rstd * g_x).astype(BF16)
         return carry
 
-    lax.fori_loop(0, length // tall, to_input, 0)
+    block_rows = xg.shape[1]
+    by_block = block_rows % LANES == 0
+
+    def partial(side, index):
+        cols = pl.ds(pl.multiple_of(index * block_rows, block_rows), block_rows)
+        x_sums[side].src[index] = dot_tn(
+            tokb[:, cols], gs_x[:, pl.ds(side * chunk, chunk)]
+        ).astype(BF16)
+
+    def one_side(side):
+        lax.fori_loop(0, length // tall, functools.partial(through_conv, side), 0)
+        lax.fori_loop(0, length // tall, functools.partial(to_input, side), 0)
+        if not by_block:
+
+            def several(i, carry):
+                cols = pl.ds(pl.multiple_of(i * LANES, LANES), LANES)
+                got = dot_tn(tokb[:, cols], gs_x[:, pl.ds(side * chunk, chunk)])
+                each = LANES // block_rows
+                for p in range(each):
+                    rows = slice(p * block_rows, (p + 1) * block_rows)
+                    x_sums[side].src[i * each + p] = got[rows].astype(BF16)
+                return carry
+
+            lax.fori_loop(0, tokb.shape[1] // LANES, several, 0)
+
+        def leave(j, carry):
+            for e in range(1, seg.fast):
+                if by_block:
+                    partial(side, x_sums[side].index(j, e))
+                x_sums[side].across(j, e).start()
+            return carry
+
+        lax.fori_loop(0, seg.lines, leave, 0)
+
+    def stay(side, j, carry):
+        if by_block:
+            partial(side, x_sums[side].index(j, 0))
+        return carry
+
+    one_side(0)
+    one_side(1)
     loads[3].wait()
     low_rank = dtp.shape[0]
     mixes = mix.shape[0]
@@ -1020,32 +1061,7 @@
         small_src[g, pl.ds(base + width, 16), :] = jnp.concatenate(lines, axis=0).astype(BF16)
     small.begin()
 
-    block_rows = xg.shape[1]
-
-    def partial(index):
-        cols = pl.ds(pl.multiple_of(index * block_rows, block_rows), block_rows)
-        xg[index] = dot_tn(tokb[:, cols], gs_x[...]).astype(BF16)
-
-    by_block = block_rows % LANES == 0
-    if not by_block:
-        for index in range(xg.shape[0]):
-            cols = slice(index * block_rows, (index + 1) * block_rows)
-            xg[index] = dot_tn(tokb[:, cols], gs_x[...]).astype(BF16)
-
-    def leave(j, carry):
-        for e in range(1, seg.fast):
-            if by_block:
-                partial(x_sum.index(j, e))
-            x_sum.across(j, e).start()
-        return carry
-
-    lax.fori_loop(0, seg.lines, leave, 0)
-    def stay(j, carry):
-        if by_block:
-            partial(x_sum.index(j, 0))
-        return carry
-
-    lax.fori_loop(0, seg.lines, stay, 0)
+    lax.fori_loop(0, seg.lines, functools.partial(stay, 0), 0)
     ends_in = jnp.concatenate(
         [
             from_states(final),
@@ -1084,24 +1100,25 @@
 
         lax.fori_loop(0, model // wide, column, 0)
 
-    def leave_q(j, carry):
+    def leave_q(j):
         normed(q_sum.index(j, 1))
         q_sum.across(j, 1).start()
-        return carry
-
-    def stay_q(j, carry):
-        normed(q_sum.index(j, 0))
-        return carry
-
-    lax.fori_loop(0, seq.lines, leave_q, 0)
-    lax.fori_loop(0, seq.lines, stay_q, 0)
-    for k in small.order():
-        small.middle(k)
-    for j, k in enumerate(x_sum.order()):
-        x_sum.middle(k)
-        if j == seg.lines - 2:
-            for m in q_sum.order():
-                q_sum.middle(m)
+
+    rest = [functools.partial(leave_q, j) for j in q_sum.order()]
+    rest += [lambda j=j: normed(q_sum.index(j, 0)) for j in q_sum.order()]
+    turns = x_sums[0].order()
+    for j in turns:
+        x_sums[0].middle(j)
+        for work in rest[j * len(rest) // len(turns) : (j + 1) * len(rest) // len(turns)]:
+            work()
+        if j == 0:
+            lax.fori_loop(0, seg.lines, functools.partial(stay, 1), 0)
+    for j in q_sum.order():
+        q_sum.middle(j)
+    for j in x_sums[1].order():
+        x_sums[1].middle(j)
+    for j in small.order():
+        small.middle(j)
 
     def input_grad(at, total):
         own = own_tok[at, :].astype(F32)
@@ -1112,11 +1129,16 @@
             - own * (square * jnp.mean(total * own, axis=1, keepdims=True))
         ).astype(BF16)
 
+    for side in (0, 1):
+
+        def put(at, total):
+            x_half[at, pl.ds(side * chunk, chunk)] = total.astype(BF16)
+
+        x_sums[side].finish(put)
+    swap_x = swap(0, x_half, swaps_s[0])
+    swap_x.begin()
     q_sum.finish(input_grad)
     small.finish(into(small_out))
-    x_sum.finish(into(x_half))
-    swap_x = swap(0, x_half, swaps_s[0])
-    swap_x.begin()
     own = pl.ds(pl.multiple_of(seq.here * own_rows, own_rows), own_rows)
     keeps = [
         pltpu.make_async_copy(x_half.at[own], halves_out.at[0, seq.here], own_s.at[0]),
@@ -1125,7 +1147,7 @@
     ]
     for keep in keeps:
         keep.start()
-    for scatter in (small, x_sum, q_sum):
+    for scatter in (small, *x_sums, q_sum):
         scatter.drain()
     for exchange in (swap_g, end_swap, swap_x):
         exchange.arrived()
@@ -1170,7 +1192,8 @@
         pltpu.VMEM((2, model, feats // 2), BF16),
         pltpu.VMEM((length, feats), BF16),
         pltpu.VMEM((length, feats), BF16),
-        pltpu.VMEM((segs, block_rows, feats), BF16),
+        pltpu.VMEM((segs, block_rows, feats // 2), BF16),
+        pltpu.VMEM((segs, block_rows, feats // 2), BF16),
         pltpu.VMEM((seqs, own_len, model), BF16),
         pltpu.VMEM((8 * (taps + 1), feats), F32),
         pltpu.VMEM((segs, rows, feats // segs), BF16),
@@ -1178,7 +1201,8 @@
         pltpu.VMEM((block_rows, feats), BF16),
         dma((8,)), dma((3,)),
         *Scatter.scratch(lines, fast, (rows, feats // segs), inside=True),
-        *Scatter.scratch(lines, fast, (block_rows, feats), inside=True),
+        *Scatter.scratch(lines, fast, (block_rows, feats // 2), inside=True),
+        *Scatter.scratch(lines, fast, (block_rows, feats // 2), inside=True),
         *Scatter.scratch(seq_lines, 2, (own_len, model), inside=True),
         *Exchange.semaphores(seqs), *Exchange.semaphores(seqs), *Exchange.semaphores(seqs),
     ]

time: 445 us -> 427 us (0.960)
  Pallas kernels: 403 us -> 385 us
    pallas_call x1, Pallas kernels: 104 us -> 85.9 us  [finish_all(): pl.pallas_call(kernel, in_specs=[ANY] * 8 + [INSIDE] * 13, out_specs=[INS...]
where the time goes in v8:
time: 427 us; the launch traced here: 423 us
  Pallas kernels  385 us (90%)
  matrix products  25.1 us (6%)
  local copies, waits for them, and re-layouts  9.24 us (2%)
    pallas_call x1, Pallas kernels, backward_scan(): pl.pallas_call(functools.partial(backward_kernel, shape, steps, taps), gr...  108 us
    pallas_call x1, Pallas kernels, finish_all(): pl.pallas_call(kernel, in_specs=[ANY] * 8 + [INSIDE] * 13, out_specs=[INS...  85.9 us
    pallas_call x1, Pallas kernels, forward_scan(): pl.pallas_call(functools.partial(forward_kernel, shape, steps, taps), gri...  79.7 us
    pallas_call x1, Pallas kernels, gather_start(): pl.pallas_call(kernel, in_specs=[ANY, ANY, INSIDE, ANY], out_specs=[ANY]...  65.9 us
    pallas_call x1, Pallas kernels, front(): pl.pallas_call(functools.partial(front_kernel, shape, steps, taps, histor...  39.6 us
    dot_general x1, matrix products, dot_nt(): lax.dot_general(a, b, (((1,), (1,)), ((), ())), preferred_element_type=F32)  12.6 us
    dot_general x2, matrix products, dot_tn(): lax.dot_general(a, b, (((0,), (0,)), ((), ())), preferred_element_type=F32)  12.5 us

profile of v8, /device:TPU:1, one launch (start us, length us, event | category | flops | bytes accessed | tf_op | source)
XLA Modules:
  0.0 423.2 jit_solution(4278990679227186704)
XLA Ops:
  0.6 1.2 convert_bitcast_fusion
  1.8 1.5 multiply_convert_fusion.1
  3.3 0.8 reshape.70
  4.1 0.0 copy-start.3
  4.1 0.0 copy-start.4
  4.1 0.0 copy-start.5
  4.1 0.0 copy-start.6
  4.1 0.0 copy-start.7
  4.1 0.0 copy-start.8
  4.1 0.0 copy-start.9
  4.1 0.4 fusion
  4.5 0.1 copy.39
  4.6 1.0 reshape.71.refs_0_
  5.6 0.2 copy.40
  5.8 0.4 copy.41
  6.2 1.0 reshape.72.refs_1_
  7.2 0.0 copy-done.3
  7.2 0.0 copy-done.4
  7.2 0.0 copy-done.5
  7.2 0.0 copy-done.6
  7.2 0.0 copy-done.7
  7.2 0.0 copy-done.8
  7.3 0.0 copy-done.9
  7.3 0.1 concatenate.3
  7.3 0.6 pad.8.refs_2_
  8.0 65.9 %gather_start.1 = (bf16[8,4,64,1024]{3,2,1,0:T(8,128)(2,1)}, bf16[8,320,128]{2,1,0:T(8,128)(2,1)}, bf16[4,256,2048]{2,1,0:T(8,128)(2,1)}, bf16[4,2,64,512]{3,2,1,0:T(8,128)(2,1)}) custom-call(bf16[4,64,1024]{2,1,0:T(8,128)(2,1)} %reshape.71.refs_0_, bf16[4,2,64,512]{3,2,1,0:T(8,128)(2,1)} %reshape.72.refs_1_, bf16[320,128]{1,0:T(8,128)(2,1)} %pad.8.refs_2_, ...), custom_call_target="tpu_custom_call" | custom-call | tf_op jit(solution)/shard_map/gather_start/pallas_call | solution.py:1300
  73.9 0.8 constant_dynamic-slice_fusion.1
  74.7 0.6 pad.9.head_ref.refs_10_
  75.3 39.6 %front.1 = (f32[1024,1024]{1,0:T(8,128)}, bf16[1024,1024]{1,0:T(8,128)(2,1)}, bf16[128,1024]{1,0:T(8,128)(2,1)}, bf16[160,1024]{1,0:T(8,128)(2,1)}, f32[32,1024]...) custom-call(bf16[1024,2048]{1,0:T(8,128)(2,1)} %bitcast.47, ...), custom_call_target="tpu_custom_call" | custom-call | tf_op jit(solution)/shard_map/front/pallas_call | solution.py:1413
  114.9 1.1 reshape_squeeze.11
  116.1 0.7 constant_dynamic-slice_fusion
  116.8 79.7 %scan_forward.1 = (f32[1024,1024]{1,0:T(8,128)}, f32[1024,1024]{1,0:T(8,128)}, f32[128,16,8,128]{3,2,1,0:T(8,128)}, f32[16,8,128]{2,1,0:T(8,128)}, f32[1024,1024...) custom-call(bf16[128,1024]{1,0:T(8,128)(2,1)} %get-tuple-element.72., ...), custom_call_target="tpu_custom_call" | custom-call | flops 134217728 | bytes 25165824 | tf_op jit(solution)/shard_map/scan_forward/pallas_call | solution.py:777
  196.5 0.0 copy-start
  196.5 12.6 %multiply_convert_fusion = (bf16[1024,1024]{1,0:T(8,128)(2,1)S(1)}, f32[1024,1024]{1,0:T(8,128)}) fusion(f32[1024,1024]{1,0:T(8,128)} %get-tuple-element.84, f32[1024,1024]{1,0:T(8,128)} %get-tuple-element.82, bf16[1024,2048]{1,0:T(8,128)(2,1)} %bitcast.74, bf16[1024,2048]{1,0:T(8,128)(2,1)} %bitcast.54), kind=kOutput, calls=%fused_computation | convolution fusion | flops 4298113024 | bytes 23068672 | tf_op jit(solution)/shard_map/dot_general | solution.py:27
  209.1 0.0 copy-start.1
  209.1 0.0 copy-done
  209.1 0.0 copy-start.2
  209.1 0.0 copy-start.10
  209.2 6.3 %convolution_convert_fusion.1 = bf16[2048,1024]{1,0:T(8,128)(2,1)} fusion(bf16[1024,2048]{1,0:T(8,128)(2,1)S(1)} %bitcast.50, bf16[1024,1024]{1,0:T(8,128)(2,1)S(1)} %get-tuple-element.120.refs_7_), kind=kOutput, calls=%fused_computation.2 | convolution fusion | flops 4297064448 | bytes 10485760 | tf_op jit(solution)/shard_map/dot_general | solution.py:23
  215.4 0.0 copy-done.1
  215.4 0.0 copy-done.2
  215.4 0.0 copy-done.10
  215.4 6.3 %convolution_convert_fusion = bf16[1024,2048]{1,0:T(8,128)(2,1)} fusion(bf16[1024,1024]{1,0:T(8,128)(2,1)S(1)} %copy-done.2, bf16[1024,2048]{1,0:T(8,128)(2,1)S(1)} %bitcast.75), kind=kOutput, calls=%fused_computation.1 | convolution fusion | flops 4297064448 | bytes 10485760 | tf_op jit(solution)/shard_map/dot_general | solution.py:23
  221.7 108.4 %scan_backward.1 = (f32[1024,1024]{1,0:T(8,128)}, f32[16,8,128]{2,1,0:T(8,128)}, f32[16,8,128]{2,1,0:T(8,128)}, f32[1,1024]{1,0:T(1,128)}, f32[1,1024]{1,0:T(1,1...) custom-call(f32[1024,1024]{1,0:T(8,128)} %get-tuple-element.79.pre_r, ...), custom_call_target="tpu_custom_call" | custom-call | flops 335544320 | bytes 29360128 | tf_op jit(solution)/shard_map/scan_backward/pallas_call | solution.py:839
  330.1 85.9 %finish.1 = (f32[320,128]{1,0:T(8,128)}, bf16[2,4,64,1024]{3,2,1,0:T(8,128)(2,1)}, bf16[256,2048]{1,0:T(8,128)(2,1)}, f32[4,40,256]{2,1,0:T(8,128)}) custom-call(f32[1024,1024]{1,0:T(8,128)} %get-tuple-element.86.refs_0_, f32[1024,1024]{1,0:T(8,128)} %get-tuple-element.87.refs_1_, bf16[1024,1024]{1,0:T(8,128)(2,1)} %get-tuple-element.75.act_ref.refs_2_, ...), custom_call_target="tpu_custom_call" | custom-call | tf_op jit(solution)/shard_map/finish/pallas_call | solution.py:1213
  416.1 1.4 copy.44.gain
  417.4 5.6 %unpack.1 = (bf16[1,256,2048]{2,1,0:T(8,128)(2,1)}, f32[1,16,1024]{2,1,0:T(8,128)}, f32[3,1,1024]{2,1,0:T(1,128)}, bf16[1,256,2048]{2,1,0:T(8,128)(2,1)}, f32[1,...) custom-call(f32[320,128]{1,0:T(8,128)} %get-tuple-element.98.small, ...), custom_call_target="tpu_custom_call" | custom-call | tf_op jit(solution)/shard_map/unpack/pallas_call | solution.py:1529
  (1 shorter events, 0.0 us)
Async XLA Ops:
  4.1 3.2 copy-start.3
  4.1 3.2 copy-start.4
  4.1 3.2 copy-start.5
  4.1 3.1 copy-start.6
  4.1 3.1 copy-start.7
  4.1 3.1 copy-start.8
  4.1 3.1 copy-start.9
  196.5 12.6 %copy-start = (bf16[4,256,2048]{2,1,0:T(8,128)(2,1)S(1)}, bf16[4,256,2048]{2,1,0:T(8,128)(2,1)}, u32[]{:S(2)}) copy-start(bf16[4,256,2048]{2,1,0:T(8,128)(2,1)} %get-tuple-element.68) | copy-start | bytes 12582916
  209.1 6.3 %copy-start.1 = (bf16[1024,1024]{1,0:T(8,128)(2,1)}, bf16[1024,1024]{1,0:T(8,128)(2,1)S(1)}, u32[]{:S(2)}) copy-start(bf16[1024,1024]{1,0:T(8,128)(2,1)S(1)} %get-tuple-element.120.refs_7_) | copy-start | bytes 6291460
  209.1 6.3 %copy-start.2 = (bf16[1024,1024]{1,0:T(8,128)(2,1)S(1)}, bf16[1024,1024]{1,0:T(8,128)(2,1)}, u32[]{:S(2)}) copy-start(bf16[1024,1024]{1,0:T(8,128)(2,1)} %get-tuple-element.85.gated_src) | copy-start | bytes 6291460
  209.1 6.3 %copy-start.10 = (bf16[4,256,2048]{2,1,0:T(8,128)(2,1)S(1)}, bf16[4,256,2048]{2,1,0:T(8,128)(2,1)}, u32[]{:S(2)}) copy-start(bf16[4,256,2048]{2,1,0:T(8,128)(2,1)} %get-tuple-element.80) | copy-start | bytes 12582916

commit v9 on v8

--- a/solution.py
+++ b/solution.py
@@ -460,8 +460,8 @@
     shape, steps, taps,
     low_ref, wdt_ref, params_ref, act_ref, bc_ref, a_ref, init_ref, weight_ref, cot_ref,
     tok_ref, gate_one, gate_src,
-    y_ref, pre_ref, check_ref, final_ref, gate_ref, gated_ref, weights_ref, cots_ref, gate_two,
-    state, rate_pl, drive_pl, y_pl, w_one, w_two, local_s, *sems,
+    y_out, pre_ref, check_ref, final_ref, gate_out, gated_out, weights_ref, cots_ref, gate_two,
+    y_ref, gate_ref, gated_ref, state, rate_pl, drive_pl, y_pl, w_one, w_two, local_s, *sems,
 ):
     count = pre_ref.shape[0]
     width, planes, _ = a_ref.shape
@@ -576,10 +576,19 @@
         lax.fori_loop(0, blocks // 2, gating, 0)
         late[-1]()
         lax.fori_loop(blocks // 2, blocks, gating, 0)
+        leaving = [
+            pltpu.make_async_copy(y_ref, y_out, local_s.at[4]),
+            pltpu.make_async_copy(gate_ref, gate_out, local_s.at[5]),
+            pltpu.make_async_copy(gated_ref, gated_out, local_s.at[6]),
+        ]
+        for leave in leaving:
+            leave.start()
         weights.finish()
         cots.finish()
         for keep in keeps[:2]:
             keep.wait()
+        for leave in leaving:
+            leave.wait()
 
 
 def backward_kernel(
@@ -672,7 +681,7 @@
     ticks = 2 * steps
     plan = [[] for _ in range(ticks)]
     for j, event in enumerate(events):
-        plan[min(ticks - 1, ticks * (j + 1) // len(events))].append(event)
+        plan[min(ticks - 1, 1 + 5 * ticks * (j + 1) // (4 * len(events)))].append(event)
 
     def output(index):
         own_len, model = third_src.shape[1:]
@@ -750,9 +759,10 @@
     @pl.when(step == steps - 1)
     def _():
         start_ref[...] = carry_s[...]
+        for event in plan[ticks - 1][:-1]:
+            event()
         sum_over_seq(seq, mix_s, mix_ref, *scratch[28:])
-        for event in plan[ticks - 1]:
-            event()
+        plan[ticks - 1][-1]()
         first.finish(into(first_out))
         second.finish(into(second_out))
         for scatter in (first, second, third):
@@ -785,10 +795,9 @@
             whole(*weight.shape), whole(*cot.shape), whole(*tok.shape), ANY, ANY,
         ],
         out_specs=[
-            whole(length, features), rows,
+            ANY, rows,
             pl.BlockSpec((block // UNROLL, width, planes, LANES), lambda i: (i, 0, 0, 0)),
-            whole(width, planes, LANES), whole(length, features), whole(length, features),
-            ANY, ANY, ANY,
+            whole(width, planes, LANES), ANY, ANY, ANY, ANY, ANY,
         ],
         out_shape=[
             jax.ShapeDtypeStruct((length, features), F32),
@@ -802,9 +811,11 @@
             jax.ShapeDtypeStruct(gate_one.shape, BF16),
         ],
         scratch_shapes=[
+            pltpu.VMEM((length, features), F32), pltpu.VMEM((length, features), F32),
+            pltpu.VMEM((length, features), BF16),
             pltpu.VMEM((width, planes, LANES), F32), plane, plane, plane,
             pltpu.VMEM(gate_one.shape, BF16), pltpu.VMEM(gate_one.shape, BF16),
-            pltpu.SemaphoreType.DMA((4,)),
+            pltpu.SemaphoreType.DMA((7,)),
             *Gather.semaphores(lines, fast), *Gather.semaphores(lines, fast),
             *Gather.semaphores(seq_lines, 2),
         ],

time: 427 us -> 422 us (0.988)
  Pallas kernels: 385 us -> 379 us
    pallas_call x1, Pallas kernels: 85.9 us -> 80 us  [finish_all(): pl.pallas_call(kernel, in_specs=[ANY] * 8 + [INSIDE] * 13, out_specs=[INS...]
where the time goes in v9:
time: 422 us; the launch traced here: 417 us
  Pallas kernels  379 us (90%)
  matrix products  25.1 us (6%)
  local copies, waits for them, and re-layouts  9.24 us (2%)
    pallas_call x1, Pallas kernels, backward_scan(): pl.pallas_call(functools.partial(backward_kernel, shape, steps, taps), gr...  112 us
    pallas_call x1, Pallas kernels, finish_all(): pl.pallas_call(kernel, in_specs=[ANY] * 8 + [INSIDE] * 13, out_specs=[INS...  80 us
    pallas_call x1, Pallas kernels, forward_scan(): pl.pallas_call(functools.partial(forward_kernel, shape, steps, taps), gri...  76.6 us
    pallas_call x1, Pallas kernels, gather_start(): pl.pallas_call(kernel, in_specs=[ANY, ANY, INSIDE, ANY], out_specs=[ANY]...  65.9 us
    pallas_call x1, Pallas kernels, front(): pl.pallas_call(functools.partial(front_kernel, shape, steps, taps, histor...  39.6 us
    dot_general x1, matrix products, dot_nt(): lax.dot_general(a, b, (((1,), (1,)), ((), ())), preferred_element_type=F32)  12.6 us
    dot_general x2, matrix products, dot_tn(): lax.dot_general(a, b, (((0,), (0,)), ((), ())), preferred_element_type=F32)  12.5 us

profile of v9, /device:TPU:1, one launch (start us, length us, event | category | flops | bytes accessed | tf_op | source)
XLA Modules:
  0.0 417.5 jit_solution(9932118081355943825)
XLA Ops:
  0.6 1.2 convert_bitcast_fusion
  1.8 1.5 multiply_convert_fusion.1
  3.3 0.8 reshape.70
  4.1 0.0 copy-start.3
  4.1 0.0 copy-start.4
  4.1 0.0 copy-start.5
  4.1 0.0 copy-start.6
  4.1 0.0 copy-start.7
  4.1 0.0 copy-start.8
  4.1 0.0 copy-start.9
  4.1 0.4 fusion
  4.5 0.1 copy.39
  4.6 1.0 reshape.71.refs_0_
  5.6 0.2 copy.40
  5.8 0.4 copy.41
  6.2 1.0 reshape.72.refs_1_
  7.2 0.0 copy-done.3
  7.2 0.0 copy-done.4
  7.2 0.0 copy-done.5
  7.2 0.0 copy-done.6
  7.2 0.0 copy-done.7
  7.2 0.0 copy-done.8
  7.3 0.0 copy-done.9
  7.3 0.1 concatenate.3
  7.3 0.6 pad.8.refs_2_
  8.0 65.9 %gather_start.1 = (bf16[8,4,64,1024]{3,2,1,0:T(8,128)(2,1)}, bf16[8,320,128]{2,1,0:T(8,128)(2,1)}, bf16[4,256,2048]{2,1,0:T(8,128)(2,1)}, bf16[4,2,64,512]{3,2,1,0:T(8,128)(2,1)}) custom-call(bf16[4,64,1024]{2,1,0:T(8,128)(2,1)} %reshape.71.refs_0_, bf16[4,2,64,512]{3,2,1,0:T(8,128)(2,1)} %reshape.72.refs_1_, bf16[320,128]{1,0:T(8,128)(2,1)} %pad.8.refs_2_, ...), custom_call_target="tpu_custom_call" | custom-call | tf_op jit(solution)/shard_map/gather_start/pallas_call | solution.py:1311
  73.9 0.8 constant_dynamic-slice_fusion.1
  74.7 0.6 pad.9.head_ref.refs_10_
  75.3 39.6 %front.1 = (f32[1024,1024]{1,0:T(8,128)}, bf16[1024,1024]{1,0:T(8,128)(2,1)}, bf16[128,1024]{1,0:T(8,128)(2,1)}, bf16[160,1024]{1,0:T(8,128)(2,1)}, f32[32,1024]...) custom-call(bf16[1024,2048]{1,0:T(8,128)(2,1)} %bitcast.47, ...), custom_call_target="tpu_custom_call" | custom-call | tf_op jit(solution)/shard_map/front/pallas_call | solution.py:1424
  114.9 1.1 reshape_squeeze.11
  116.1 0.7 constant_dynamic-slice_fusion
  116.8 76.6 %scan_forward.1 = (f32[1024,1024]{1,0:T(8,128)}, f32[1024,1024]{1,0:T(8,128)}, f32[128,16,8,128]{3,2,1,0:T(8,128)}, f32[16,8,128]{2,1,0:T(8,128)}, f32[1024,1024...) custom-call(bf16[128,1024]{1,0:T(8,128)(2,1)} %get-tuple-element.72., ...), custom_call_target="tpu_custom_call" | custom-call | flops 134217728 | bytes 25165824 | tf_op jit(solution)/shard_map/scan_forward/pallas_call | solution.py:787
  193.3 0.0 copy-start
  193.4 12.6 %multiply_convert_fusion = (bf16[1024,1024]{1,0:T(8,128)(2,1)S(1)}, f32[1024,1024]{1,0:T(8,128)}) fusion(f32[1024,1024]{1,0:T(8,128)} %get-tuple-element.84, f32[1024,1024]{1,0:T(8,128)} %get-tuple-element.82, bf16[1024,2048]{1,0:T(8,128)(2,1)} %bitcast.74, bf16[1024,2048]{1,0:T(8,128)(2,1)} %bitcast.54), kind=kOutput, calls=%fused_computation | convolution fusion | flops 4298113024 | bytes 23068672 | tf_op jit(solution)/shard_map/dot_general | solution.py:27
  206.0 0.0 copy-start.1
  206.0 0.0 copy-done
  206.0 0.0 copy-start.2
  206.0 0.0 copy-start.10
  206.0 6.3 %convolution_convert_fusion.1 = bf16[2048,1024]{1,0:T(8,128)(2,1)} fusion(bf16[1024,2048]{1,0:T(8,128)(2,1)S(1)} %bitcast.50, bf16[1024,1024]{1,0:T(8,128)(2,1)S(1)} %get-tuple-element.120.refs_7_), kind=kOutput, calls=%fused_computation.2 | convolution fusion | flops 4297064448 | bytes 10485760 | tf_op jit(solution)/shard_map/dot_general | solution.py:23
  212.3 0.0 copy-done.1
  212.3 0.0 copy-done.2
  212.3 0.0 copy-done.10
  212.3 6.3 %convolution_convert_fusion = bf16[1024,2048]{1,0:T(8,128)(2,1)} fusion(bf16[1024,1024]{1,0:T(8,128)(2,1)S(1)} %copy-done.2, bf16[1024,2048]{1,0:T(8,128)(2,1)S(1)} %bitcast.75), kind=kOutput, calls=%fused_computation.1 | convolution fusion | flops 4297064448 | bytes 10485760 | tf_op jit(solution)/shard_map/dot_general | solution.py:23
  218.5 111.8 %scan_backward.1 = (f32[1024,1024]{1,0:T(8,128)}, f32[16,8,128]{2,1,0:T(8,128)}, f32[16,8,128]{2,1,0:T(8,128)}, f32[1,1024]{1,0:T(1,128)}, f32[1,1024]{1,0:T(1,1...) custom-call(f32[1024,1024]{1,0:T(8,128)} %get-tuple-element.79.pre_r, ...), custom_call_target="tpu_custom_call" | custom-call | flops 335544320 | bytes 29360128 | tf_op jit(solution)/shard_map/scan_backward/pallas_call | solution.py:850
  330.4 80.0 %finish.1 = (f32[320,128]{1,0:T(8,128)}, bf16[2,4,64,1024]{3,2,1,0:T(8,128)(2,1)}, bf16[256,2048]{1,0:T(8,128)(2,1)}, f32[4,40,256]{2,1,0:T(8,128)}) custom-call(f32[1024,1024]{1,0:T(8,128)} %get-tuple-element.86.refs_0_, f32[1024,1024]{1,0:T(8,128)} %get-tuple-element.87.refs_1_, bf16[1024,1024]{1,0:T(8,128)(2,1)} %get-tuple-element.75.act_ref.refs_2_, ...), custom_call_target="tpu_custom_call" | custom-call | tf_op jit(solution)/shard_map/finish/pallas_call | solution.py:1224
  410.4 1.4 copy.44.gain
  411.7 5.6 %unpack.1 = (bf16[1,256,2048]{2,1,0:T(8,128)(2,1)}, f32[1,16,1024]{2,1,0:T(8,128)}, f32[3,1,1024]{2,1,0:T(1,128)}, bf16[1,256,2048]{2,1,0:T(8,128)(2,1)}, f32[1,...) custom-call(f32[320,128]{1,0:T(8,128)} %get-tuple-element.98.small, ...), custom_call_target="tpu_custom_call" | custom-call | tf_op jit(solution)/shard_map/unpack/pallas_call | solution.py:1540
  (1 shorter events, 0.0 us)
Async XLA Ops:
  4.1 3.2 copy-start.3
  4.1 3.2 copy-start.4
  4.1 3.2 copy-start.5
  4.1 3.1 copy-start.6
  4.1 3.1 copy-start.7
  4.1 3.1 copy-start.8
  4.1 3.1 copy-start.9
  193.3 12.6 %copy-start = (bf16[4,256,2048]{2,1,0:T(8,128)(2,1)S(1)}, bf16[4,256,2048]{2,1,0:T(8,128)(2,1)}, u32[]{:S(2)}) copy-start(bf16[4,256,2048]{2,1,0:T(8,128)(2,1)} %get-tuple-element.68) | copy-start | bytes 12582916
  206.0 6.3 %copy-start.1 = (bf16[1024,1024]{1,0:T(8,128)(2,1)}, bf16[1024,1024]{1,0:T(8,128)(2,1)S(1)}, u32[]{:S(2)}) copy-start(bf16[1024,1024]{1,0:T(8,128)(2,1)S(1)} %get-tuple-element.120.refs_7_) | copy-start | bytes 6291460
  206.0 6.3 %copy-start.2 = (bf16[1024,1024]{1,0:T(8,128)(2,1)S(1)}, bf16[1024,1024]{1,0:T(8,128)(2,1)}, u32[]{:S(2)}) copy-start(bf16[1024,1024]{1,0:T(8,128)(2,1)} %get-tuple-element.85.gated_src) | copy-start | bytes 6291460
  206.0 6.3 %copy-start.10 = (bf16[4,256,2048]{2,1,0:T(8,128)(2,1)S(1)}, bf16[4,256,2048]{2,1,0:T(8,128)(2,1)}, u32[]{:S(2)}) copy-start(bf16[4,256,2048]{2,1,0:T(8,128)(2,1)} %get-tuple-element.80) | copy-start | bytes 12582916
